TPU v7x, 32 devices: a whole 2x2x4 slice. The times are simulated.
32 devices in a mesh: fsdp: 8 (over y, x, core), tp: 4 (over z).
Axes of the slice: x: 2, y: 2, z: 4, core: 2. Of those that a mesh axis runs over, the one named last changes fastest.
Arguments:
- tokens: bfloat16 [8, 1024, 1024], P('fsdp', 'tp'), may hold values from -6 to 6
- lengths: int32 [8], P('fsdp'), may hold values from 256 to 1024, as said below
- norm_gain: bfloat16 [1024], P('fsdp'), may hold values from 0.5 to 1.5
- in_weight: bfloat16 [1024, 2, 2048], P('fsdp', None, 'tp'), may hold values from -0.1875 to 0.1875
- conv_weight: bfloat16 [4, 2048], P(None, ('tp', 'fsdp')), may hold values from -3 to 3
- conv_bias: bfloat16 [2048], P(('tp', 'fsdp')), may hold values from -3 to 3
- x_weight: bfloat16 [2048, 96], P(('tp', 'fsdp')), may hold values from -0.125 to 0.125
- dt_weight: bfloat16 [64, 2048], P('fsdp', 'tp'), may hold values from -0.75 to 0.75
- dt_bias: bfloat16 [2048], P(('tp', 'fsdp')), may hold values from -6.5 to -2.5
- a_log: bfloat16 [16, 2048], P(None, ('tp', 'fsdp')), may hold values from 0 to 2.796875
- d_skip: bfloat16 [2048], P(('tp', 'fsdp')), may hold values from 0.5 to 1.5
- out_weight: bfloat16 [2048, 1024], P('tp', 'fsdp'), may hold values from -0.25 to 0.25
- cotangent: bfloat16 [8, 1024, 1024], P('fsdp', 'tp'), may hold values from -6 to 6
Outputs:
- block_out: bfloat16 [8, 1024, 1024], P('fsdp', 'tp')
- input_grad: float32 [8, 1024, 1024], P('fsdp', 'tp')
- gain_grad: float32 [1024], P('fsdp')
- in_weight_grad: float32 [1024, 2, 2048], P('fsdp', None, 'tp')
- conv_weight_grad: float32 [4, 2048], P(None, ('tp', 'fsdp'))
- conv_bias_grad: float32 [2048], P(('tp', 'fsdp'))
- x_weight_grad: float32 [2048, 96], P(('tp', 'fsdp'))
- dt_weight_grad: float32 [64, 2048], P('fsdp', 'tp')
- dt_bias_grad: float32 [2048], P(('tp', 'fsdp'))
- a_log_grad: float32 [16, 2048], P(None, ('tp', 'fsdp'))
- d_skip_grad: float32 [2048], P(('tp', 'fsdp'))
- out_weight_grad: float32 [2048, 1024], P('tp', 'fsdp')
Inputs may be any that keep to these rules, and one draw needn't show every extreme that they name: lengths[s] is the number of live positions of slot s, counted from its start; at least one slot is full.
All inputs are finite; a program needn't handle non-finite values.
Results may differ from a plain program's by a relative error of at most 0.011.
Values may be sent and summed in bfloat16 or wider, within the bound.
No kernel may reach another device: no remote copies, remote signals or barrier semaphores. Data moves between devices by JAX's collectives and lax.ppermute only.
A program may use at most 192 MiB of HBM per device.

v0:
```python
from functools import partial

import jax
import jax.numpy as jnp
from jax import lax
from jax.sharding import PartitionSpec as P

BLOCK = 64


epsilon = 1e-05


def to_blocks(values, count):
    shaped = values.reshape((values.shape[0], count, values.shape[1] // count) + values.shape[2:])
    return jnp.moveaxis(shaped, (1, 2), (0, 1))


def from_blocks(values):
    merged = jnp.moveaxis(values, (0, 1), (1, 2))
    return merged.reshape((merged.shape[0], merged.shape[1] * merged.shape[2]) + merged.shape[3:])


def silu_grad(values):
    sigma = jax.nn.sigmoid(values)
    return sigma * (1.0 + values * (1.0 - sigma))


def linear_scan(log_decay, pushes_in, carried):
    total_len = log_decay.shape[0]
    span_len = min(8, total_len)
    span_count = total_len // span_len
    span_shape = (span_count, span_len) + log_decay.shape[1:]
    running = jnp.cumsum(log_decay.reshape(span_shape), axis=1)
    pushes = pushes_in.reshape(span_shape)
    positions = jnp.arange(span_len)
    causal = (positions[:, None] >= positions[None, :]).reshape(
        (1, span_len, span_len) + (1,) * (log_decay.ndim - 1)
    )
    between = running[:, :, None] - running[:, None, :]
    factors = jnp.exp(jnp.where(causal, between, -jnp.inf))
    partial_states = jnp.sum(factors * pushes[:, None], axis=2)
    growth = jnp.exp(running)
    arriving = []
    current = carried
    for span_index in range(span_count):
        arriving.append(current)
        current = growth[span_index, -1] * current + partial_states[span_index, -1]
    incoming = jnp.stack(arriving)
    states = partial_states + growth * incoming[:, None]
    return states.reshape(log_decay.shape)


def forward_block(decay_rate, carried, pieces):
    step_size, input_map, output_map, conv_out = pieces
    log_decay = step_size[:, :, None, :] * decay_rate
    drive = (step_size * conv_out)[:, :, None, :] * input_map[:, :, :, None]
    states = linear_scan(log_decay, drive, carried)
    return (states[-1], (jnp.sum(states * output_map[:, :, :, None], axis=2), states))


def backward_block(decay_rate, carried, pieces):
    grad_state, grad_rate = carried
    step_size, input_map, output_map, conv_out, scan_grad, start, states = pieces
    log_decay = step_size[:, :, None, :] * decay_rate
    decay = jnp.exp(log_decay)
    before = jnp.concatenate([start[None], states[:-1]], axis=0)
    following_log = jnp.concatenate([log_decay[1:], jnp.zeros_like(log_decay[:1])], axis=0)
    source = output_map[:, :, :, None] * scan_grad[:, :, None, :]
    source = jnp.concatenate([source[:-1], source[-1:] + grad_state[None]], axis=0)
    state_grad = linear_scan(following_log[::-1], source[::-1], jnp.zeros_like(grad_state))[::-1]
    output_grad = jnp.sum(states * scan_grad[:, :, None, :], axis=3)
    input_grad = jnp.sum(state_grad * (step_size * conv_out)[:, :, None, :], axis=3)
    conv_grad = jnp.sum(state_grad * input_map[:, :, :, None], axis=2) * step_size
    carried_part = state_grad * decay * before
    step_grad = jnp.sum(
        carried_part * decay_rate + state_grad * input_map[:, :, :, None] * conv_out[:, :, None, :],
        axis=2,
    )
    rate_grad = grad_rate + jnp.sum(carried_part * step_size[:, :, None, :], axis=(0, 1))
    return ((decay[0] * state_grad[0], rate_grad), (output_grad, input_grad, conv_grad, step_grad))


def run_forward(decay_rate, pieces, start):

    def plain(carried, piece):
        final, (result, states) = forward_block(decay_rate, carried, piece)
        return (final, (result, carried, states))

    return lax.scan(plain, start, pieces)[1]


def run_backward(decay_rate, pieces, start):
    initial = (start, jnp.zeros(decay_rate.shape, jnp.float32))
    final, results = lax.scan(partial(backward_block, decay_rate), initial, pieces, reverse=True)
    return (final[1], results)


def shards(
    tokens,
    lengths,
    norm_gain,
    in_weight,
    conv_weight,
    conv_bias,
    x_weight,
    dt_weight,
    dt_bias,
    a_log,
    d_skip,
    out_weight,
    cotangent,
):
    gathered = (
        lax.all_gather(norm_gain, "fsdp", axis=0, tiled=True),
        lax.all_gather(in_weight, "fsdp", axis=0, tiled=True),
        lax.all_gather(conv_weight, "fsdp", axis=1, tiled=True),
        lax.all_gather(conv_bias, "fsdp", axis=0, tiled=True),
        lax.all_gather(x_weight, "fsdp", axis=0, tiled=True),
        lax.all_gather(dt_weight, "fsdp", axis=0, tiled=True),
        lax.all_gather(dt_bias, "fsdp", axis=0, tiled=True),
        lax.all_gather(a_log, "fsdp", axis=1, tiled=True),
        lax.all_gather(d_skip, "fsdp", axis=0, tiled=True),
        lax.all_gather(out_weight, "fsdp", axis=1, tiled=True),
    )
    (
        gain_full,
        in_full,
        conv_full,
        conv_bias_full,
        x_full,
        dt_full,
        dt_bias_full,
        rate_full,
        skip_full,
        out_full,
    ) = gathered
    whole = lax.all_gather(tokens, "tp", axis=1, tiled=True)
    seq_count = whole.shape[0]
    seq_len = whole.shape[1]
    kernel = conv_full.shape[0]
    rank = dt_full.shape[0]
    state_width = rate_full.shape[0]
    live_mask = (jnp.arange(seq_len)[None, :] < lengths[:, None]).astype(jnp.float32)[:, :, None]
    values = whole.astype(jnp.float32)
    inverse = lax.rsqrt(jnp.mean(values * values, axis=-1, keepdims=True) + epsilon)
    normed = (values * inverse * gain_full.astype(jnp.float32)).astype(jnp.bfloat16)
    projected = jnp.einsum("bld,dkc->blkc", normed, in_full, preferred_element_type=jnp.float32)
    conv_input = projected[:, :, 0]
    gate_input = projected[:, :, 1]
    conv_weights = conv_full.astype(jnp.float32)
    padded = jnp.pad(conv_input, ((0, 0), (kernel - 1, 0), (0, 0)))
    conv_sum = conv_bias_full.astype(jnp.float32) + sum(
        (conv_weights[offset] * padded[:, offset : offset + seq_len] for offset in range(kernel))
    )
    conv_low = jax.nn.silu(conv_sum).astype(jnp.bfloat16)
    conv_out = conv_low.astype(jnp.float32)
    mapped = lax.psum(
        jnp.einsum("blc,cj->blj", conv_low, x_full, preferred_element_type=jnp.float32), "tp"
    )
    low_rank = mapped[:, :, :rank].astype(jnp.bfloat16)
    input_map = mapped[:, :, rank : rank + state_width]
    output_map = mapped[:, :, rank + state_width :]
    step_pre = jnp.einsum(
        "blr,rc->blc", low_rank, dt_full, preferred_element_type=jnp.float32
    ) + dt_bias_full.astype(jnp.float32)
    step_size = jax.nn.softplus(step_pre) * live_mask
    decay_rate = -jnp.exp(rate_full.astype(jnp.float32))
    count = seq_len // BLOCK
    pieces = (
        to_blocks(step_size, count),
        to_blocks(input_map, count),
        to_blocks(output_map, count),
        to_blocks(conv_out, count),
    )
    start = jnp.zeros((seq_count, state_width, conv_out.shape[2]), jnp.float32)
    scan_blocks, starts, all_states = run_forward(decay_rate, pieces, start)
    scan_out = from_blocks(scan_blocks)
    skip_values = skip_full.astype(jnp.float32)
    gate_act = jax.nn.silu(gate_input)
    before_gate = scan_out + skip_values * conv_out
    mixed = (before_gate * gate_act * live_mask).astype(jnp.bfloat16)
    partial_out = jnp.einsum("blc,cd->bld", mixed, out_full, preferred_element_type=jnp.float32)
    block_sum = lax.psum_scatter(
        partial_out.astype(jnp.bfloat16), "tp", scatter_dimension=1, tiled=True
    ).astype(jnp.float32)
    block_out = (tokens.astype(jnp.float32) + block_sum).astype(jnp.bfloat16)
    regathered = (
        lax.all_gather(norm_gain, "fsdp", axis=0, tiled=True),
        lax.all_gather(in_weight, "fsdp", axis=0, tiled=True),
        lax.all_gather(conv_weight, "fsdp", axis=1, tiled=True),
        lax.all_gather(x_weight, "fsdp", axis=0, tiled=True),
        lax.all_gather(dt_weight, "fsdp", axis=0, tiled=True),
        lax.all_gather(out_weight, "fsdp", axis=1, tiled=True),
    )
    gain_back, in_back, conv_back, x_back, dt_back, out_back = regathered
    grad_whole = lax.all_gather(cotangent, "tp", axis=1, tiled=True)
    mixed_grad = jnp.einsum("bld,cd->blc", grad_whole, out_back, preferred_element_type=jnp.float32)
    out_weight_grad = jnp.einsum(
        "blc,bld->cd", mixed, grad_whole, preferred_element_type=jnp.float32
    )
    masked_grad = mixed_grad * live_mask
    scan_grad = masked_grad * gate_act
    gate_grad = masked_grad * before_gate * silu_grad(gate_input)
    skip_grad = jnp.sum(scan_grad * conv_out, axis=(0, 1))
    grad_pieces = pieces + (to_blocks(scan_grad, count), starts, all_states)
    rate_grad, (output_grad, input_grad, conv_scan_grad, step_grad) = run_backward(
        decay_rate, grad_pieces, start
    )
    a_log_grad = rate_grad * decay_rate
    pre_grad = (from_blocks(step_grad) * live_mask * jax.nn.sigmoid(step_pre)).astype(jnp.bfloat16)
    dt_bias_grad = jnp.sum(pre_grad.astype(jnp.float32), axis=(0, 1))
    dt_weight_grad = jnp.einsum(
        "blr,blc->rc", low_rank, pre_grad, preferred_element_type=jnp.float32
    )
    rank_grad = jnp.einsum("blc,rc->blr", pre_grad, dt_back, preferred_element_type=jnp.float32)
    map_terms = jnp.concatenate(
        [rank_grad, from_blocks(input_grad), from_blocks(output_grad)], axis=2
    )
    map_grad = lax.psum(map_terms.astype(jnp.bfloat16), "tp")
    x_weight_grad = jnp.einsum(
        "blc,blj->cj", conv_low, map_grad, preferred_element_type=jnp.float32
    )
    conv_out_grad = (
        scan_grad * skip_values
        + from_blocks(conv_scan_grad)
        + jnp.einsum("blj,cj->blc", map_grad, x_back, preferred_element_type=jnp.float32)
    )
    sum_grad = conv_out_grad * silu_grad(conv_sum)
    conv_bias_grad = jnp.sum(sum_grad, axis=(0, 1))
    conv_weight_grad = jnp.stack(
        [
            jnp.sum(sum_grad * padded[:, offset : offset + seq_len], axis=(0, 1))
            for offset in range(kernel)
        ]
    )
    padded_grad = jnp.pad(sum_grad, ((0, 0), (0, kernel - 1), (0, 0)))
    conv_back_values = conv_back.astype(jnp.float32)
    conv_input_grad = sum(
        (
            conv_back_values[offset]
            * padded_grad[:, kernel - 1 - offset : kernel - 1 - offset + seq_len]
            for offset in range(kernel)
        )
    )
    projected_grad = jnp.stack([conv_input_grad, gate_grad], axis=2).astype(jnp.bfloat16)
    in_weight_grad = jnp.einsum(
        "bld,blkc->dkc", normed, projected_grad, preferred_element_type=jnp.float32
    )
    normed_part = jnp.einsum(
        "blkc,dkc->bld", projected_grad, in_back, preferred_element_type=jnp.float32
    )
    normed_grad = lax.psum_scatter(
        normed_part.astype(jnp.bfloat16), "tp", scatter_dimension=1, tiled=True
    ).astype(jnp.float32)
    own_values = tokens.astype(jnp.float32)
    own_inverse = lax.rsqrt(jnp.mean(own_values * own_values, axis=-1, keepdims=True) + epsilon)
    own_hat = own_values * own_inverse
    scaled = normed_grad * gain_back.astype(jnp.float32)
    input_grads = cotangent.astype(jnp.float32) + own_inverse * (
        scaled - own_hat * jnp.mean(scaled * own_hat, axis=-1, keepdims=True)
    )
    gain_grad = lax.psum(jnp.sum(normed_grad * own_hat, axis=(0, 1)), "tp")
    reduced = (
        lax.psum_scatter(gain_grad, "fsdp", scatter_dimension=0, tiled=True),
        lax.psum_scatter(in_weight_grad, "fsdp", scatter_dimension=0, tiled=True),
        lax.psum_scatter(conv_weight_grad, "fsdp", scatter_dimension=1, tiled=True),
        lax.psum_scatter(conv_bias_grad, "fsdp", scatter_dimension=0, tiled=True),
        lax.psum_scatter(x_weight_grad, "fsdp", scatter_dimension=0, tiled=True),
        lax.psum_scatter(dt_weight_grad, "fsdp", scatter_dimension=0, tiled=True),
        lax.psum_scatter(dt_bias_grad, "fsdp", scatter_dimension=0, tiled=True),
        lax.psum_scatter(a_log_grad, "fsdp", scatter_dimension=1, tiled=True),
        lax.psum_scatter(skip_grad, "fsdp", scatter_dimension=0, tiled=True),
        lax.psum_scatter(out_weight_grad, "fsdp", scatter_dimension=1, tiled=True),
    )
    return (
        block_out,
        input_grads,
        reduced[0],
        reduced[1],
        reduced[2],
        reduced[3],
        reduced[4],
        reduced[5],
        reduced[6],
        reduced[7],
        reduced[8],
        reduced[9],
    )


def solution(mesh):
    return jax.shard_map(
        shards,
        mesh=mesh,
        in_specs=(
            P("fsdp", "tp", None),
            P("fsdp"),
            P("fsdp"),
            P("fsdp", None, "tp"),
            P(None, ("tp", "fsdp")),
            P(("tp", "fsdp")),
            P(("tp", "fsdp"), None),
            P("fsdp", "tp"),
            P(("tp", "fsdp")),
            P(None, ("tp", "fsdp")),
            P(("tp", "fsdp")),
            P("tp", "fsdp"),
            P("fsdp", "tp", None),
        ),
        out_specs=(
            P("fsdp", "tp", None),
            P("fsdp", "tp", None),
            P("fsdp"),
            P("fsdp", None, "tp"),
            P(None, ("tp", "fsdp")),
            P(("tp", "fsdp")),
            P(("tp", "fsdp"), None),
            P("fsdp", "tp"),
            P(("tp", "fsdp")),
            P(None, ("tp", "fsdp")),
            P(("tp", "fsdp")),
            P("tp", "fsdp"),
        ),
        check_vma=False,
    )
```

profile of v0, /device:TPU:0, one launch (start us, length us, event | category | flops | bytes accessed | tf_op | source)
XLA Modules:
  0.0 1318.7 jit_solution(9680110859214097002)
XLA Ops:
  11.0 10.3 all-gather.1
  25.9 13.9 %all-reduce.11 = (bf16[512]{0:T(512)(128)(2,1)S(1)}, bf16[512]{0:T(512)(128)(2,1)S(1)}, bf16[512]{0:T(512)(128)(2,1)S(1)}) all-reduce(bf16[512]{0:T(512)(128)(2,1)S(1)} %dynamic-update-slice, bf16[512]{0:T(512)(128)(2,1)S(1)} %dynamic-update-slice.1, bf16[512]{0:T(512)(128)(2,1)S(1)} %dynamic-update-slice.2), channel_id=1, replica_groups=mesh['fsdp'=8,'tp'=4] {'fsdp'}, use_global_device_ids=true, to_apply=%add.3 | all-reduce | flops 1536 | bytes 6144
  39.8 8.9 all-gather
  49.4 8.4 all_gather.47
  60.5 26.9 %all-gather.10.cloned.1.call-done = bf16[1024,2,512]{2,0,1:T(8,128)(2,1)} async-done(((bf16[128,2,512]{2,0,1:T(8,128)(2,1)}), bf16[1024,2,512]{2,0,1:T(8,128)(2,1)}) %all-gather.10.cloned.1.call-update) | async-done | bytes 2097168 | tf_op jit(solution)/shard_map/all_gather | solution.py:116
  93.6 19.3 %all-gather.12.cloned.1.call-done = bf16[512,1024]{1,0:T(8,128)(2,1)} async-done(((bf16[512,128]{1,0:T(8,128)(2,1)}), bf16[512,1024]{1,0:T(8,128)(2,1)}) %all-gather.12.cloned.1.call-update) | async-done | bytes 1048592 | tf_op jit(solution)/shard_map/all_gather | solution.py:124
  112.9 47.4 %all-gather.14.cloned.1.call-done = bf16[1,1024,1024]{2,1,0:T(8,128)(2,1)} async-done(((bf16[1,256,1024]{2,1,0:T(8,128)(2,1)}), bf16[1,1024,1024]{2,1,0:T(8,128)(2,1)}) %all-gather.14.cloned.1.call-update) | async-done | bytes 2097168 | tf_op jit(solution)/shard_map/all_gather | solution.py:197
  160.3 8.5 fusion.48
  170.2 9.0 all-gather.2
  179.9 9.1 all_gather.48
  190.7 15.3 %all-reduce.15.cloned.1.call-done = f32[1,1024,96]{1,2,0:T(8,128)} async-done(((f32[1,1024,96]{1,2,0:T(8,128)}), f32[1,1024,96]{1,2,0:T(8,128)}) %all-reduce.15.cloned.1.call-update) | async-done | bytes 393232 | tf_op jit(solution)/shard_map/psum | solution.py:158
  208.1 4.3 fusion.45
  212.7 188.2 %while.41 = (s32[]{:T(128)}, f32[1,16,512]{2,1,0:T(8,128)S(1)}, f32[16,64,1,512]{3,1,2,0:T(8,128)S(1)}, f32[16,1,16,512]{3,2,1,0:T(8,128)}, f32[16,64,1,16,512]{...) while((s32[]{:T(128)}, f32[1,16,512]{2,1,0:T(8,128)S(1)}, ...), condition=%wide.region_6.7_spmd, body=%wide.region_2.6_spmd.sunk | while | flops 24297536 | bytes 34792700 | solution.py:90
  216.1 4.2 multiply_reduce_fusion.13
  227.9 4.2 multiply_reduce_fusion.13
  239.6 4.2 multiply_reduce_fusion.13
  251.4 4.2 multiply_reduce_fusion.13
  405.1 528.0 %while.42 = (s32[]{:T(128)}, f32[1,16,512]{2,1,0:T(8,128)S(1)}, f32[16,512]{1,0:T(8,128)S(1)}, bf16[16,64,1,16]{3,1,2,0:T(8,128)(2,1)S(1)}, bf16[16,64,1,16]{3,1...) while((s32[]{:T(128)}, f32[1,16,512]{2,1,0:T(8,128)S(1)}, ...), condition=%wide.region_17.18_spmd.clone, body=%wide.region_9.17_spmd.clone.sunk | while | flops 31119428 | bytes 71350624 | solution.py:95
  423.3 4.2 multiply_reduce_fusion.15
  456.3 4.2 multiply_reduce_fusion.15
  489.3 4.2 multiply_reduce_fusion.15
  522.3 4.2 multiply_reduce_fusion.15
  555.3 4.2 multiply_reduce_fusion.15
  588.3 4.2 multiply_reduce_fusion.15
  621.3 4.2 multiply_reduce_fusion.15
  654.3 4.2 multiply_reduce_fusion.15
  687.3 4.2 multiply_reduce_fusion.15
  720.3 4.2 multiply_reduce_fusion.15
  753.3 4.2 multiply_reduce_fusion.15
  786.3 4.2 multiply_reduce_fusion.15
  819.3 4.2 multiply_reduce_fusion.15
  852.3 4.2 multiply_reduce_fusion.15
  885.3 4.2 multiply_reduce_fusion.15
  918.3 4.2 multiply_reduce_fusion.15
  938.4 33.6 %all-reduce.17.cloned.1.call-done = bf16[1024,96]{0,1:T(8,128)(2,1)} async-done(((bf16[1024,96]{0,1:T(8,128)(2,1)}), bf16[1024,96]{0,1:T(8,128)(2,1)}) %all-reduce.17.cloned.1.call-update) | async-done | bytes 196624 | tf_op jit(solution)/shard_map/psum | solution.py:220
  978.3 4.9 fusion.99
  984.2 5.9 fusion.69
  994.8 6.6 fusion.73
  1005.6 4.2 fusion.56
  1012.9 33.6 %reduce-scatter.25.cloned.1.call-done = f32[64,4]{1,0:T(8,128)} async-done(((f32[512,4]{1,0:T(8,128)}), f32[64,4]{1,0:T(8,128)}) %reduce-scatter.25.cloned.1.call-update) | async-done | bytes 1040
  1047.9 44.8 %reduce-scatter.15.cloned.1.call-done = bf16[1,256,1024]{2,1,0:T(8,128)(2,1)} async-done(((bf16[1,1024,1024]{2,1,0:T(8,128)(2,1)}), bf16[1,256,1024]{2,1,0:T(8,128)(2,1)}) %reduce-scatter.15.cloned.1.call-update) | async-done | bytes 524304 | tf_op jit(solution)/shard_map/reduce_scatter | solution.py:253
  1094.2 23.9 %all-reduce.10 = (f32[1024]{0:T(1024)S(1)}, f32[512]{0:T(512)S(1)}, f32[512]{0:T(512)S(1)}, f32[512]{0:T(512)S(1)}) all-reduce(f32[1024]{0:T(1024)S(1)} %get-tuple-element.653, f32[512]{0:T(512)S(1)} %get-tuple-element.648, f32[512]{0:T(512)S(1)} %get-tuple-element.731, ...), channel_id=4, replica_groups=mesh['fsdp'=8,'tp'=4] {'fsdp'}, use_global_device_ids=true, to_apply=%region_23.24.clone | all-reduce | flops 2560 | bytes 20480
  1119.9 12.6 psum.24
  1132.5 5.9 reduce-scatter.13.cloned.1.call-done
  1141.2 51.3 %reduce-scatter.17.cloned.1.call-done = f32[128,2,512]{2,0,1:T(8,128)} async-done(((f32[1024,2,512]{2,0,1:T(8,128)}), f32[128,2,512]{2,0,1:T(8,128)}) %reduce-scatter.17.cloned.1.call-update) | async-done | bytes 524304 | tf_op jit(solution)/shard_map/reduce_scatter | solution.py:266
  1194.7 34.9 %reduce-scatter.21.cloned.1.call-done = f32[8,512]{1,0:T(8,128)} async-done(((f32[64,512]{1,0:T(8,128)}), f32[8,512]{1,0:T(8,128)}) %reduce-scatter.21.cloned.1.call-update) | async-done | bytes 16400 | tf_op jit(solution)/shard_map/reduce_scatter | solution.py:270
  1229.6 37.2 %reduce-scatter.19.cloned.1.call-done = f32[64,96]{1,0:T(8,128)} async-done(((f32[512,96]{1,0:T(8,128)}), f32[64,96]{1,0:T(8,128)}) %reduce-scatter.19.cloned.1.call-update) | async-done | bytes 24592 | tf_op jit(solution)/shard_map/reduce_scatter | solution.py:269
  1266.8 45.4 %reduce-scatter.23.cloned.1.call-done = f32[512,128]{1,0:T(8,128)} async-done(((f32[512,1024]{1,0:T(8,128)}), f32[512,128]{1,0:T(8,128)}) %reduce-scatter.23.cloned.1.call-update) | async-done | bytes 262160 | tf_op jit(solution)/shard_map/reduce_scatter | solution.py:274
  (1047 shorter events, 686.2 us)
Async XLA Ops:
  7.2 42.2 %copy-start.22 = (bf16[64,96]{1,0:T(8,128)(2,1)S(1)}, bf16[64,96]{1,0:T(8,128)(2,1)}, u32[]{:S(2)}) copy-start(bf16[64,96]{1,0:T(8,128)(2,1)} %param.23) | copy-start | bytes 36868
  7.2 51.1 %all-gather.8.cloned.1.call-start = ((), (), s32[]{:S(2)}) async-start(), calls=%async_computation.8 | async-start | bytes 2621440 | tf_op jit(solution)/shard_map/all_gather | solution.py:138
  7.9 79.5 %all-gather.10.cloned.1.call-start = ((), (), s32[]{:S(2)}) async-start(), calls=%async_computation.9 | async-start | bytes 2359296 | tf_op jit(solution)/shard_map/all_gather | solution.py:116
  9.7 103.2 %all-gather.12.cloned.1.call-start = ((), (), s32[]{:S(2)}) async-start(), calls=%async_computation.11 | async-start | bytes 1179648 | tf_op jit(solution)/shard_map/all_gather | solution.py:124
  10.4 149.9 %all-gather.14.cloned.1.call-start = ((), (), s32[]{:S(2)}) async-start(), calls=%async_computation.13 | async-start | bytes 2621440 | tf_op jit(solution)/shard_map/all_gather | solution.py:197
  11.0 195.1 %all-reduce.15.cloned.1.call-start = ((), (), s32[]{:S(2)}) async-start(), calls=%async_computation.10 | async-start | bytes 786432 | tf_op jit(solution)/shard_map/psum | solution.py:158
  21.4 66.0 %copy-start.20 = (f32[8,1,128]{2,1,0:T(1,128)}, f32[8,1,128]{2,1,0:T(1,128)S(1)}, u32[]{:S(2)}) copy-start(f32[8,1,128]{2,1,0:T(1,128)S(1)} %convert_element_type.123) | copy-start | bytes 12292
  57.8 111.1 %copy-start.13 = (bf16[512,96]{1,0:T(8,128)(2,1)}, bf16[512,96]{1,0:T(8,128)(2,1)S(1)}, u32[]{:S(2)}) copy-start(bf16[512,96]{1,0:T(8,128)(2,1)S(1)} %all_gather.47) | copy-start | bytes 294916
  57.8 150.3 %copy-start.18 = (f32[1024]{0:T(1024)}, f32[1024]{0:T(1024)S(1)}, u32[]{:S(2)}) copy-start(f32[1024]{0:T(1024)S(1)} %fusion.96) | copy-start | bytes 12292
  57.8 102.5 %copy-start.26 = (f32[1,512]{1,0:T(1,128)}, f32[1,512]{1,0:T(1,128)S(1)}, u32[]{:S(2)}) copy-start(f32[1,512]{1,0:T(1,128)S(1)} %get-tuple-element.751) | copy-start | bytes 6148
  57.8 102.5 %copy-start.28 = (f32[1,512]{1,0:T(1,128)}, f32[1,512]{1,0:T(1,128)S(1)}, u32[]{:S(2)}) copy-start(f32[1,512]{1,0:T(1,128)S(1)} %get-tuple-element.752) | copy-start | bytes 6148
  57.8 102.5 %copy-start.30 = (f32[1,512]{1,0:T(1,128)}, f32[1,512]{1,0:T(1,128)S(1)}, u32[]{:S(2)}) copy-start(f32[1,512]{1,0:T(1,128)S(1)} %get-tuple-element.753) | copy-start | bytes 6148
  57.8 102.4 %copy-start.32 = (f32[1,512]{1,0:T(1,128)}, f32[1,512]{1,0:T(1,128)S(1)}, u32[]{:S(2)}) copy-start(f32[1,512]{1,0:T(1,128)S(1)} %get-tuple-element.754) | copy-start | bytes 6148
  58.3 29.1 %copy-start.10 = (bf16[1,1024,1024]{2,1,0:T(8,128)(2,1)S(1)}, bf16[1,1024,1024]{2,1,0:T(8,128)(2,1)}, u32[]{:S(2)}) copy-start(bf16[1,1024,1024]{2,1,0:T(8,128)(2,1)} %all-gather.8.cloned.1.call-done) | copy-start | bytes 6291460
  60.5 26.9 %copy-start.36 = (f32[1024]{0:T(1024)}, f32[1024]{0:T(1024)S(1)}, u32[]{:S(2)}) copy-start(f32[1024]{0:T(1024)S(1)} %add_rsqrt_fusion) | copy-start | bytes 12292
  93.6 75.3 %copy-start.4 = (f32[1,1024,512]{2,1,0:T(8,128)}, f32[1,1024,512]{2,1,0:T(8,128)S(1)}, u32[]{:S(2)}) copy-start(f32[1,1024,512]{2,1,0:T(8,128)S(1)} %slice_bitcast_fusion.26) | copy-start | bytes 6291460
  160.3 9.9 copy-start.35
  168.8 21.9 %copy-start = (bf16[1,1024,512]{2,1,0:T(8,128)(2,1)}, bf16[1,1024,512]{2,1,0:T(8,128)(2,1)S(1)}, u32[]{:S(2)}) copy-start(bf16[1,1024,512]{2,1,0:T(8,128)(2,1)S(1)} %get-tuple-element.729) | copy-start | bytes 3145732
  168.8 11.1 copy-start.34
  170.1 802.0 %all-reduce.17.cloned.1.call-start = ((), (), s32[]{:S(2)}) async-start(), calls=%async_computation.14 | async-start | bytes 393216 | tf_op jit(solution)/shard_map/psum | solution.py:220
  170.2 38.0 %copy-start.23 = (f32[512]{0:T(512)}, f32[512]{0:T(512)S(1)}, u32[]{:S(2)}) copy-start(f32[512]{0:T(512)S(1)} %convert_element_type.106) | copy-start | bytes 6148
  189.1 19.1 %copy-start.16 = (bf16[64,512]{1,0:T(8,128)(2,1)}, bf16[64,512]{1,0:T(8,128)(2,1)S(1)}, u32[]{:S(2)}) copy-start(bf16[64,512]{1,0:T(8,128)(2,1)S(1)} %all_gather.48) | copy-start | bytes 196612
  400.9 3.4 copy-start.6
  405.1 528.0 %copy-start.19 = (f32[1024]{0:T(1024)S(1)}, f32[1024]{0:T(1024)}, u32[]{:S(2)}) copy-start(f32[1024]{0:T(1024)} %copy-done.18) | copy-start | bytes 12292
  405.1 528.0 %copy-start.24 = (f32[512]{0:T(512)S(1)}, f32[512]{0:T(512)}, u32[]{:S(2)}) copy-start(f32[512]{0:T(512)} %copy-done.23) | copy-start | bytes 6148
  933.1 2.9 copy-start.17
  933.1 3.4 copy-start.12
  936.0 36.0 %copy-start.14 = (bf16[512,96]{1,0:T(8,128)(2,1)S(1)}, bf16[512,96]{1,0:T(8,128)(2,1)}, u32[]{:S(2)}) copy-start(bf16[512,96]{1,0:T(8,128)(2,1)} %copy-done.13) | copy-start | bytes 294916
  936.0 36.0 %copy-start.25 = (f32[512]{0:T(512)S(1)}, f32[512]{0:T(512)}, u32[]{:S(2)}) copy-start(f32[512]{0:T(512)} %convert_element_type.110) | copy-start | bytes 6148
  937.4 74.0 %reduce-scatter.27.cloned.1.call-start = ((), (), s32[]{:S(2)}) async-start(), calls=%async_computation.21 | async-start | bytes 294912
  938.4 108.1 %reduce-scatter.25.cloned.1.call-start = ((), (), s32[]{:S(2)}) async-start(), calls=%async_computation.20 | async-start | bytes 294912
  972.0 4.1 copy-start.1
  972.0 4.4 copy-start.3
  972.0 5.1 copy-start.5
  972.1 5.7 copy-start.7
  972.1 6.3 copy-start.9
  972.1 6.3 copy-start.27
  972.1 6.3 copy-start.29
  972.1 6.2 copy-start.31
  972.1 6.2 copy-start.33
  984.2 108.5 %reduce-scatter.15.cloned.1.call-start = ((), (), s32[]{:S(2)}) async-start(), calls=%async_computation.15 | async-start | bytes 2621440 | tf_op jit(solution)/shard_map/reduce_scatter | solution.py:253
  990.2 148.2 %reduce-scatter.13.cloned.1.call-start = ((), (), s32[]{:S(2)}) async-start(), calls=%async_computation.12 | async-start | bytes 2621440 | tf_op jit(solution)/shard_map/reduce_scatter | solution.py:184
  994.1 198.4 %reduce-scatter.17.cloned.1.call-start = ((), (), s32[]{:S(2)}) async-start(), calls=%async_computation.16 | async-start | bytes 4718592 | tf_op jit(solution)/shard_map/reduce_scatter | solution.py:266
  1001.4 228.1 %reduce-scatter.21.cloned.1.call-start = ((), (), s32[]{:S(2)}) async-start(), calls=%async_computation.18 | async-start | bytes 147456 | tf_op jit(solution)/shard_map/reduce_scatter | solution.py:270
  1003.4 263.5 %reduce-scatter.19.cloned.1.call-start = ((), (), s32[]{:S(2)}) async-start(), calls=%async_computation.17 | async-start | bytes 294912 | tf_op jit(solution)/shard_map/reduce_scatter | solution.py:269
  1005.5 306.6 %reduce-scatter.23.cloned.1.call-start = ((), (), s32[]{:S(2)}) async-start(), calls=%async_computation.19 | async-start | bytes 2359296 | tf_op jit(solution)/shard_map/reduce_scatter | solution.py:274
  1009.8 84.4 %copy-start.38 = (f32[512]{0:T(512)S(1)}, f32[512]{0:T(512)}, u32[]{:S(2)}) copy-start(f32[512]{0:T(512)} %get-tuple-element.727) | copy-start | bytes 6148
  1009.8 128.6 %copy-start.11 = (bf16[1,256,1024]{2,1,0:T(8,128)(2,1)S(1)}, bf16[1,256,1024]{2,1,0:T(8,128)(2,1)}, u32[]{:S(2)}) copy-start(bf16[1,256,1024]{2,1,0:T(8,128)(2,1)} %param.29) | copy-start | bytes 1572868
  (5 other events, 5.8 us)
Sparse Core Ops, SparseCore 0:
  9.6 48.6 all-gather.7
  60.7 26.5 all-gather.9
  89.3 23.5 all-gather.11
  114.3 45.9 all-gather.13
  170.2 35.7 all-reduce.14
  937.6 34.4 all-reduce.16
  975.6 33.2 reduce-scatter.26
  1012.9 33.5 reduce-scatter.24
  1048.8 43.8 reduce-scatter.14
  1094.9 43.4 reduce-scatter.12
  1141.7 50.6 reduce-scatter.16
  1196.2 33.3 reduce-scatter.20
  1233.2 33.6 reduce-scatter.18
  1270.9 41.2 reduce-scatter.22
where the time goes:
time: 1330 us; the launch traced here: 1320 us
  other arithmetic  458 us (34%)
  waiting for transfers between devices  398 us (30%)
  local copies, waits for them, and re-layouts  298 us (22%)
  blocking collectives  96.1 us (7%)
  matrix products  46.1 us (3%)
  between operations  17.1 us (1%)
    reduce_sum x32, other arithmetic, linear_scan(): partial_states = jnp.sum(factors * pushes[:, None], axis=2)  135 us
    dynamic_update_slice x32, other arithmetic, run_forward(): return lax.scan(plain, start, pieces)[1]  58.6 us
    reduce_sum x16, other arithmetic, backward_block(): output_grad = jnp.sum(states * scan_grad[:, :, None, :], axis=3)  56.5 us
    rev x16, local copies, waits for them, and re-layouts, backward_block(): following_log[::-1]  51.4 us
    reduce_scatter x1, waiting for transfers between devices, shards(): lax.psum_scatter(in_weight_grad, 'fsdp', scatter_dimension=0, tiled=True)  51.3 us
    all_gather x1, waiting for transfers between devices, shards(): grad_whole = lax.all_gather(cotangent, 'tp', axis=1, tiled=True)  47.4 us
    reduce_scatter x1, waiting for transfers between devices, shards(): lax.psum_scatter(out_weight_grad, 'fsdp', scatter_dimension=1, tiled=True)  45.4 us
    reduce_scatter x1, waiting for transfers between devices, shards(): lax.psum_scatter(normed_part.astype(jnp.bfloat16), 'tp', scatter_dimensio...  44.8 us
  transfers between devices with their start and end apart: 14, of which 13 were waited for; matrix products, arithmetic and copies ran while one was open for 5% of the time, Pallas kernels for 0%

commit v1 on v0

--- a/solution.py
+++ b/solution.py
@@ -1,24 +1,19 @@
-from functools import partial
+import functools
 
 import jax
 import jax.numpy as jnp
 from jax import lax
+from jax.experimental import pallas as pl
+from jax.experimental.pallas import tpu as pltpu
 from jax.sharding import PartitionSpec as P
 
-BLOCK = 64
+bf16 = jnp.bfloat16
+f32 = jnp.float32
+LOG2E = 1.4426950408889634
+LN2 = 0.6931471805599453
 
 
 epsilon = 1e-05
-
-
-def to_blocks(values, count):
-    shaped = values.reshape((values.shape[0], count, values.shape[1] // count) + values.shape[2:])
-    return jnp.moveaxis(shaped, (1, 2), (0, 1))
-
-
-def from_blocks(values):
-    merged = jnp.moveaxis(values, (0, 1), (1, 2))
-    return merged.reshape((merged.shape[0], merged.shape[1] * merged.shape[2]) + merged.shape[3:])
 
 
 def silu_grad(values):
@@ -26,74 +21,142 @@
     return sigma * (1.0 + values * (1.0 - sigma))
 
 
-def linear_scan(log_decay, pushes_in, carried):
-    total_len = log_decay.shape[0]
-    span_len = min(8, total_len)
-    span_count = total_len // span_len
-    span_shape = (span_count, span_len) + log_decay.shape[1:]
-    running = jnp.cumsum(log_decay.reshape(span_shape), axis=1)
-    pushes = pushes_in.reshape(span_shape)
-    positions = jnp.arange(span_len)
-    causal = (positions[:, None] >= positions[None, :]).reshape(
-        (1, span_len, span_len) + (1,) * (log_decay.ndim - 1)
-    )
-    between = running[:, :, None] - running[:, None, :]
-    factors = jnp.exp(jnp.where(causal, between, -jnp.inf))
-    partial_states = jnp.sum(factors * pushes[:, None], axis=2)
-    growth = jnp.exp(running)
-    arriving = []
-    current = carried
-    for span_index in range(span_count):
-        arriving.append(current)
-        current = growth[span_index, -1] * current + partial_states[span_index, -1]
-    incoming = jnp.stack(arriving)
-    states = partial_states + growth * incoming[:, None]
-    return states.reshape(log_decay.shape)
-
-
-def forward_block(decay_rate, carried, pieces):
-    step_size, input_map, output_map, conv_out = pieces
-    log_decay = step_size[:, :, None, :] * decay_rate
-    drive = (step_size * conv_out)[:, :, None, :] * input_map[:, :, :, None]
-    states = linear_scan(log_decay, drive, carried)
-    return (states[-1], (jnp.sum(states * output_map[:, :, :, None], axis=2), states))
-
-
-def backward_block(decay_rate, carried, pieces):
-    grad_state, grad_rate = carried
-    step_size, input_map, output_map, conv_out, scan_grad, start, states = pieces
-    log_decay = step_size[:, :, None, :] * decay_rate
-    decay = jnp.exp(log_decay)
-    before = jnp.concatenate([start[None], states[:-1]], axis=0)
-    following_log = jnp.concatenate([log_decay[1:], jnp.zeros_like(log_decay[:1])], axis=0)
-    source = output_map[:, :, :, None] * scan_grad[:, :, None, :]
-    source = jnp.concatenate([source[:-1], source[-1:] + grad_state[None]], axis=0)
-    state_grad = linear_scan(following_log[::-1], source[::-1], jnp.zeros_like(grad_state))[::-1]
-    output_grad = jnp.sum(states * scan_grad[:, :, None, :], axis=3)
-    input_grad = jnp.sum(state_grad * (step_size * conv_out)[:, :, None, :], axis=3)
-    conv_grad = jnp.sum(state_grad * input_map[:, :, :, None], axis=2) * step_size
-    carried_part = state_grad * decay * before
-    step_grad = jnp.sum(
-        carried_part * decay_rate + state_grad * input_map[:, :, :, None] * conv_out[:, :, None, :],
-        axis=2,
-    )
-    rate_grad = grad_rate + jnp.sum(carried_part * step_size[:, :, None, :], axis=(0, 1))
-    return ((decay[0] * state_grad[0], rate_grad), (output_grad, input_grad, conv_grad, step_grad))
-
-
-def run_forward(decay_rate, pieces, start):
-
-    def plain(carried, piece):
-        final, (result, states) = forward_block(decay_rate, carried, piece)
-        return (final, (result, carried, states))
-
-    return lax.scan(plain, start, pieces)[1]
-
-
-def run_backward(decay_rate, pieces, start):
-    initial = (start, jnp.zeros(decay_rate.shape, jnp.float32))
-    final, results = lax.scan(partial(backward_block, decay_rate), initial, pieces, reverse=True)
-    return (final[1], results)
+def split(v):
+    hi=v.astype(bf16)
+    return hi,(v-hi.astype(f32)).astype(bf16)
+
+def spread(m, sub):
+    tb,ns=m.shape
+    wide=sub*ns
+    rep=(lax.broadcasted_iota(jnp.int32,(ns,wide),1)%ns==lax.broadcasted_iota(jnp.int32,(ns,wide),0)).astype(bf16)
+    keep=(lax.broadcasted_iota(jnp.int32,(tb,wide),1)//ns==lax.broadcasted_iota(jnp.int32,(tb,wide),0)%sub)
+    out=[]
+    for part in split(m):
+        t=jnp.dot(part,rep,preferred_element_type=f32)
+        out.append(jnp.where(keep,t,0.0).astype(bf16))
+    return out
+
+def outer(eh,el,vh,vl):
+    e=jnp.concatenate([eh,eh,el],0); v=jnp.concatenate([vh,vl,vh],0)
+    return lax.dot_general(e,v,(((0,),(0,)),((),())),preferred_element_type=f32)
+
+def fwd_kernel(sub, dt_ref,x_ref,b_ref,c_ref,rate_ref,y_ref,h_ref, drive, state, eb_h, eb_l, xh, xl):
+    tb,ch=dt_ref.shape; ns=rate_ref.shape[0]; half=ns//2
+    @pl.when(pl.program_id(0)==0)
+    def _(): state[...]=jnp.zeros_like(state)
+    eb_h[...],eb_l[...]=spread(b_ref[...],sub)
+    dtx=dt_ref[...]*x_ref[...].astype(f32)
+    xh[...],xl[...]=split(dtx)
+    for i in range(tb//sub):
+        s=slice(i*sub,(i+1)*sub)
+        drive[i*sub*ns:(i+1)*sub*ns,:]=outer(eb_h[s],eb_l[s],xh[s],xl[s])
+    r0=rate_ref[:half]*LOG2E; r1=rate_ref[half:]*LOG2E
+    U=16
+    def body(j,hs):
+        h0,h1=hs
+        rows=dt_ref[pl.ds(pl.multiple_of(j*U,U),U),:]
+        for k in range(U):
+            dtb=jnp.broadcast_to(rows[k:k+1],(half,ch))
+            a0=jnp.exp2(dtb*r0); a1=jnp.exp2(dtb*r1)
+            base=pl.multiple_of(j*(U*ns),U*ns)+k*ns
+            h0=a0*h0+drive[pl.ds(base,half),:]
+            h1=a1*h1+drive[pl.ds(base+half,half),:]
+            h_ref[pl.ds(base,ns),:]=jnp.concatenate([h0,h1],0).astype(bf16)
+        return h0,h1
+    h0,h1=lax.fori_loop(0,tb//U,body,(state[:half],state[half:]))
+    state[:half]=h0; state[half:]=h1
+    ch_,cl_=spread(c_ref[...],sub)
+    for i in range(tb//sub):
+        s=slice(i*sub,(i+1)*sub)
+        e=jnp.concatenate([ch_[s],cl_[s]],0)
+        o=jnp.dot(e,h_ref[i*sub*ns:(i+1)*sub*ns,:],preferred_element_type=f32)
+        y_ref[s,:]=o[:sub]+o[sub:]
+
+def scan_fwd(dt,x,b,c,rate,tb=128,sub=16):
+    t,ch=dt.shape; ns=rate.shape[0]
+    row=lambda w: pl.BlockSpec((tb,w),lambda i:(i,0))
+    full=lambda a: pl.BlockSpec(a.shape,lambda i:(0,0))
+    return pl.pallas_call(functools.partial(fwd_kernel,sub),
+        grid=(t//tb,),
+        in_specs=[row(ch),row(ch),row(ns),row(ns),full(rate)],
+        out_specs=[row(ch),pl.BlockSpec((tb*ns,ch),lambda i:(i,0))],
+        out_shape=[jax.ShapeDtypeStruct((t,ch),f32),jax.ShapeDtypeStruct((t*ns,ch),bf16)],
+        scratch_shapes=[pltpu.VMEM((tb*ns,ch),f32),pltpu.VMEM((ns,ch),f32),pltpu.VMEM((tb,sub*ns),bf16),pltpu.VMEM((tb,sub*ns),bf16),pltpu.VMEM((tb,ch),bf16),pltpu.VMEM((tb,ch),bf16)],
+        compiler_params=pltpu.CompilerParams(vmem_limit_bytes=56*2**20),
+        name="scan_fwd")(dt,x,b,c,rate)
+
+def bwd_kernel(sub, dt_ref,x_ref,b_ref,c_ref,dy_ref,h_ref,hp_ref,rate_ref,
+               w_ref,q_ref,ib_ref,oc_ref,acc_ref, drive, carry, gs, vs):
+    tb,ch=dt_ref.shape; ns=rate_ref.shape[0]; half=ns//2
+    step=pl.program_id(0); nb=pl.num_programs(0)
+    @pl.when(step==0)
+    def _():
+        carry[...]=jnp.zeros_like(carry); acc_ref[...]=jnp.zeros_like(acc_ref)
+    ech,ecl=spread(c_ref[...],sub)
+    dy=dy_ref[...]
+    yh,yl=split(dy)
+    for i in range(tb//sub):
+        s=slice(i*sub,(i+1)*sub)
+        drive[i*sub*ns:(i+1)*sub*ns,:]=outer(ech[s],ecl[s],yh[s],yl[s])
+    r0=rate_ref[:half]*LOG2E; r1=rate_ref[half:]*LOG2E
+    before=jnp.where(step==nb-1,jnp.zeros_like(hp_ref[...]),hp_ref[...])
+    U=16
+    def body(jj,cs):
+        q0,q1,s0,s1=cs
+        j=tb//U-1-jj
+        rows=dt_ref[pl.ds(pl.multiple_of(j*U,U),U),:]
+        for k in reversed(range(U)):
+            dtb=jnp.broadcast_to(rows[k:k+1],(half,ch))
+            a0=jnp.exp2(dtb*r0); a1=jnp.exp2(dtb*r1)
+            base=pl.multiple_of(j*(U*ns),U*ns)+k*ns
+            g0=drive[pl.ds(base,half),:]+q0
+            g1=drive[pl.ds(base+half,half),:]+q1
+            gs[pl.ds(base,ns),:]=jnp.concatenate([g0,g1],0).astype(bf16)
+            q0=a0*g0; q1=a1*g1
+            if k==0:
+                prev=h_ref[pl.ds(pl.multiple_of(jnp.maximum(base-ns,0),ns),ns),:]
+                prev=jnp.where(j==0,before,prev)
+            else:
+                prev=h_ref[pl.ds(base-ns,ns),:]
+            prev=prev.astype(f32)
+            m0=r0*(q0*prev[:half]); m1=r1*(q1*prev[half:])
+            s0=s0+dtb*m0; s1=s1+dtb*m1
+            vs[pl.ds(base,ns),:]=jnp.concatenate([m0,m1],0).astype(bf16)
+        return q0,q1,s0,s1
+    q0,q1,s0,s1=lax.fori_loop(0,tb//U,body,(carry[:half],carry[half:],acc_ref[:half],acc_ref[half:]))
+    carry[:half]=q0; carry[half:]=q1; acc_ref[:half]=s0; acc_ref[half:]=s1
+    ebh,ebl=spread(b_ref[...],sub)
+    wide=sub*ns
+    ones=(lax.broadcasted_iota(jnp.int32,(sub,wide),1)//ns==lax.broadcasted_iota(jnp.int32,(sub,wide),0))
+    one_b=ones.astype(bf16)
+    rep=(lax.broadcasted_iota(jnp.int32,(wide,ns),0)%ns==lax.broadcasted_iota(jnp.int32,(wide,ns),1)).astype(bf16)
+    dxh=(dt_ref[...]*x_ref[...].astype(f32)).astype(bf16)
+    nt=(((1,),(1,)),((),()))
+    for i in range(tb//sub):
+        s=slice(i*sub,(i+1)*sub); big=slice(i*sub*ns,(i+1)*sub*ns)
+        g=gs[big,:]
+        o=jnp.dot(jnp.concatenate([ebh[s],ebl[s]],0),g,preferred_element_type=f32)
+        w_ref[s,:]=o[:sub]+o[sub:]
+        q_ref[s,:]=jnp.dot(one_b,vs[big,:],preferred_element_type=f32)*LN2
+        zb=lax.dot_general(dxh[s],g,nt,preferred_element_type=f32)
+        zc=lax.dot_general(yh[s],h_ref[big,:],nt,preferred_element_type=f32)
+        z=jnp.where(jnp.concatenate([ones,ones],0),jnp.concatenate([zb,zc],0),0.0).astype(bf16)
+        z=jnp.dot(z,rep,preferred_element_type=f32)
+        ib_ref[s,:]=z[:sub]; oc_ref[s,:]=z[sub:]
+
+def scan_bwd(dt,x,b,c,dy,h,rate,tb=128,sub=16):
+    t,ch=dt.shape; ns=rate.shape[0]; nb=t//tb
+    row=lambda w: pl.BlockSpec((tb,w),lambda i:(nb-1-i,0))
+    full=lambda a: pl.BlockSpec(a.shape,lambda i:(0,0))
+    return pl.pallas_call(functools.partial(bwd_kernel,sub),
+        grid=(nb,),
+        in_specs=[row(ch),row(ch),row(ns),row(ns),row(ch),pl.BlockSpec((tb*ns,ch),lambda i:(nb-1-i,0)),
+                  pl.BlockSpec((ns,ch),lambda i:(jnp.maximum((nb-1-i)*tb-1,0),0)),full(rate)],
+        out_specs=[row(ch),row(ch),row(ns),row(ns),full(rate)],
+        out_shape=[jax.ShapeDtypeStruct((t,ch),f32),jax.ShapeDtypeStruct((t,ch),f32),jax.ShapeDtypeStruct((t,ns),f32),jax.ShapeDtypeStruct((t,ns),f32),jax.ShapeDtypeStruct((ns,ch),f32)],
+        scratch_shapes=[pltpu.VMEM((tb*ns,ch),f32),pltpu.VMEM((ns,ch),f32),pltpu.VMEM((tb*ns,ch),bf16),pltpu.VMEM((tb*ns,ch),bf16)],
+        compiler_params=pltpu.CompilerParams(vmem_limit_bytes=56*2**20),
+        name="scan_bwd")(dt,x,b,c,dy,h,h,rate)
 
 
 def shards(
@@ -166,16 +229,11 @@
     ) + dt_bias_full.astype(jnp.float32)
     step_size = jax.nn.softplus(step_pre) * live_mask
     decay_rate = -jnp.exp(rate_full.astype(jnp.float32))
-    count = seq_len // BLOCK
-    pieces = (
-        to_blocks(step_size, count),
-        to_blocks(input_map, count),
-        to_blocks(output_map, count),
-        to_blocks(conv_out, count),
-    )
-    start = jnp.zeros((seq_count, state_width, conv_out.shape[2]), jnp.float32)
-    scan_blocks, starts, all_states = run_forward(decay_rate, pieces, start)
-    scan_out = from_blocks(scan_blocks)
+    scans = [
+        scan_fwd(step_size[s], conv_low[s], input_map[s], output_map[s], decay_rate)
+        for s in range(seq_count)
+    ]
+    scan_out = jnp.stack([s[0] for s in scans])
     skip_values = skip_full.astype(jnp.float32)
     gate_act = jax.nn.silu(gate_input)
     before_gate = scan_out + skip_values * conv_out
@@ -203,19 +261,32 @@
     scan_grad = masked_grad * gate_act
     gate_grad = masked_grad * before_gate * silu_grad(gate_input)
     skip_grad = jnp.sum(scan_grad * conv_out, axis=(0, 1))
-    grad_pieces = pieces + (to_blocks(scan_grad, count), starts, all_states)
-    rate_grad, (output_grad, input_grad, conv_scan_grad, step_grad) = run_backward(
-        decay_rate, grad_pieces, start
-    )
-    a_log_grad = rate_grad * decay_rate
-    pre_grad = (from_blocks(step_grad) * live_mask * jax.nn.sigmoid(step_pre)).astype(jnp.bfloat16)
+    backs = [
+        scan_bwd(
+            step_size[s],
+            conv_low[s],
+            input_map[s],
+            output_map[s],
+            scan_grad[s],
+            scans[s][1],
+            decay_rate,
+        )
+        for s in range(seq_count)
+    ]
+    weighted, step_part, input_grad, output_grad = (
+        jnp.stack([s[i] for s in backs]) for i in range(4)
+    )
+    conv_scan_grad = weighted * step_size
+    step_grad = step_part + weighted * conv_out
+    a_log_grad = sum(s[4] for s in backs) * LN2
+    pre_grad = (step_grad * live_mask * jax.nn.sigmoid(step_pre)).astype(jnp.bfloat16)
     dt_bias_grad = jnp.sum(pre_grad.astype(jnp.float32), axis=(0, 1))
     dt_weight_grad = jnp.einsum(
         "blr,blc->rc", low_rank, pre_grad, preferred_element_type=jnp.float32
     )
     rank_grad = jnp.einsum("blc,rc->blr", pre_grad, dt_back, preferred_element_type=jnp.float32)
     map_terms = jnp.concatenate(
-        [rank_grad, from_blocks(input_grad), from_blocks(output_grad)], axis=2
+        [rank_grad, input_grad, output_grad], axis=2
     )
     map_grad = lax.psum(map_terms.astype(jnp.bfloat16), "tp")
     x_weight_grad = jnp.einsum(
@@ -223,7 +294,7 @@
     )
     conv_out_grad = (
         scan_grad * skip_values
-        + from_blocks(conv_scan_grad)
+        + conv_scan_grad
         + jnp.einsum("blj,cj->blc", map_grad, x_back, preferred_element_type=jnp.float32)
     )
     sum_grad = conv_out_grad * silu_grad(conv_sum)

time: 1330 us -> 665 us (0.50)
  other arithmetic: 458 us -> 15.4 us
  local copies, waits for them, and re-layouts: 298 us -> 21.8 us
  Pallas kernels: 0 us -> 65.8 us
    reduce_sum x80 -> x0, other arithmetic: 247 us -> none  [the longest x32 135 us: linear_scan(): partial_states = jnp.sum(factors * pushes[:, None], axis=2)]
    rev x32 -> x0, local copies, waits for them, and re-layouts: 79.8 us -> none  [the longest x16 51.4 us: backward_block(): following_log[::-1]]
    pallas_call x0 -> x2, Pallas kernels: none -> 65.8 us  [the longest x1 45.4 us: scan_bwd(): pl.pallas_call(functools.partial(bwd_kernel, sub), grid=(nb,), in_specs=[...]
    mul x112 -> x0, local copies, waits for them, and re-layouts: 62.1 us -> none  [the longest x32 27 us: backward_block(): source = output_map[:, :, :, None] * scan_grad[:, :, None, :]]
    slice x49 -> x0, local copies, waits for them, and re-layouts: 60.8 us -> none  [the longest x16 29.2 us: backward_block(): log_decay[1:]]
    dynamic_update_slice x32 -> x0, other arithmetic: 58.6 us -> none  [run_forward(): return lax.scan(plain, start, pieces)[1]]
    mul x65 -> x1, other arithmetic: 47.5 us -> 0.01 us  [shards(): a_log_grad = sum((s[4] for s in backs)) * LN2]
    another operation x65 -> x1, other arithmetic: 35 us -> 0.7 us  [the longest x32 34 us: linear_scan(): running = jnp.cumsum(log_decay.reshape(span_shape), axis=1)]
  transfers between devices with their start and end apart: 14 -> 14, of which waited for: 13 -> 13; matrix products, arithmetic and copies ran while one was open for 5% -> 9% of each run, Pallas kernels for 0% -> 0%
where the time goes in v1:
time: 665 us; the launch traced here: 664 us
  waiting for transfers between devices  403 us (61%)
  blocking collectives  96.2 us (14%)
  Pallas kernels  65.8 us (10%)
  matrix products  44.1 us (7%)
  local copies, waits for them, and re-layouts  21.8 us (3%)
  between operations  16.9 us (3%)
  other arithmetic  15.4 us (2%)
    reduce_scatter x1, waiting for transfers between devices, shards(): lax.psum_scatter(in_weight_grad, 'fsdp', scatter_dimension=0, tiled=True)  51.6 us
    all_gather x1, waiting for transfers between devices, shards(): grad_whole = lax.all_gather(cotangent, 'tp', axis=1, tiled=True)  47.4 us
    pallas_call x1, Pallas kernels, scan_bwd(): pl.pallas_call(functools.partial(bwd_kernel, sub), grid=(nb,), in_specs=[...  45.4 us
    reduce_scatter x1, waiting for transfers between devices, shards(): lax.psum_scatter(out_weight_grad, 'fsdp', scatter_dimension=1, tiled=True)  45 us
    reduce_scatter x1, waiting for transfers between devices, shards(): lax.psum_scatter(normed_part.astype(jnp.bfloat16), 'tp', scatter_dimensio...  44.9 us
    unnamed x2, blocking collectives  38.9 us
    reduce_scatter x1, waiting for transfers between devices, shards(): lax.psum_scatter(x_weight_grad, 'fsdp', scatter_dimension=0, tiled=True)  37.5 us
    unnamed x16, waiting for transfers between devices  37.5 us
  transfers between devices with their start and end apart: 14, of which 13 were waited for; matrix products, arithmetic and copies ran while one was open for 9% of the time, Pallas kernels for 0%

profile of v1, /device:TPU:0, one launch (start us, length us, event | category | flops | bytes accessed | tf_op | source)
XLA Modules:
  0.0 664.1 jit_solution(5368952233993876361)
XLA Ops:
  8.0 1.7 copy.49
  11.0 10.3 %all-gather.1 = bf16[8,1,128]{2,1,0:T(2,128)(2,1)S(1)} all-gather(bf16[1,1,128]{2,1,0:T(2,128)(2,1)} %bitcast.205), channel_id=1, replica_groups=mesh['fsdp'=8,'tp'=4] {'fsdp'}, dimensions={0}, use_global_device_ids=true | all-gather | bytes 2304 | tf_op jit(solution)/shard_map/all_gather | solution.py:178
  21.4 1.3 fusion.66
  23.3 0.9 dynamic-update-slice
  24.2 0.8 dynamic-update-slice.1
  25.9 13.9 %all-reduce.10 = (bf16[512]{0:T(512)(128)(2,1)S(1)}, bf16[512]{0:T(512)(128)(2,1)S(1)}, bf16[512]{0:T(512)(128)(2,1)S(1)}) all-reduce(bf16[512]{0:T(512)(128)(2,1)S(1)} %dynamic-update-slice, bf16[512]{0:T(512)(128)(2,1)S(1)} %dynamic-update-slice.1, bf16[512]{0:T(512)(128)(2,1)S(1)} %dynamic-update-slice.2), channel_id=1, replica_groups=mesh['fsdp'=8,'tp'=4] {'fsdp'}, use_global_device_ids=true, to_apply=%add.2 | all-reduce | flops 1536 | bytes 6144
  39.8 8.9 %all-gather = bf16[8,64,4]{1,2,0:T(4,128)(2,1)S(1)} all-gather(bf16[1,64,4]{1,2,0:T(4,128)(2,1)} %bitcast.204), channel_id=1, replica_groups=mesh['fsdp'=8,'tp'=4] {'fsdp'}, dimensions={0}, use_global_device_ids=true | all-gather | bytes 4608 | tf_op jit(solution)/shard_map/all_gather | solution.py:180
  49.4 8.4 %all_gather.47 = bf16[512,96]{1,0:T(8,128)(2,1)S(1)} all-gather(bf16[64,96]{1,0:T(8,128)(2,1)S(1)} %copy-done.17), channel_id=1, replica_groups=mesh['fsdp'=8,'tp'=4] {'fsdp'}, dimensions={0}, use_global_device_ids=true | all-gather | bytes 110592 | tf_op jit(solution)/shard_map/all_gather | solution.py:182
  58.3 2.2 fusion
  60.5 26.9 %all-gather.10.cloned.1.call-done = bf16[1024,2,512]{2,0,1:T(8,128)(2,1)} async-done(((bf16[128,2,512]{2,0,1:T(8,128)(2,1)}), bf16[1024,2,512]{2,0,1:T(8,128)(2,1)}) %all-gather.10.cloned.1.call-update) | async-done | bytes 2097168 | tf_op jit(solution)/shard_map/all_gather | solution.py:179
  87.4 4.0 convolution_bitcast_fusion
  91.4 1.9 copy-done.2
  93.5 19.4 %all-gather.12.cloned.1.call-done = bf16[512,1024]{1,0:T(8,128)(2,1)} async-done(((bf16[512,128]{1,0:T(8,128)(2,1)}), bf16[512,1024]{1,0:T(8,128)(2,1)}) %all-gather.12.cloned.1.call-update) | async-done | bytes 1048592 | tf_op jit(solution)/shard_map/all_gather | solution.py:187
  112.9 47.4 %all-gather.14.cloned.1.call-done = bf16[1,1024,1024]{2,1,0:T(8,128)(2,1)} async-done(((bf16[1,256,1024]{2,1,0:T(8,128)(2,1)}), bf16[1,1024,1024]{2,1,0:T(8,128)(2,1)}) %all-gather.14.cloned.1.call-update) | async-done | bytes 2097168 | tf_op jit(solution)/shard_map/all_gather | solution.py:255
  160.3 8.0 %fusion.8 = (f32[512]{0:T(512)S(1)}, f32[1024,512]{1,0:T(8,128)}, bf16[1,1024,512]{2,1,0:T(8,128)(2,1)S(1)}, f32[1,1024,512]{2,1,0:T(8,128)}, f32[1024,512]{1,0:T(8,128)}) fusion(f32[1,1024,2,512]{3,1,2,0:T(8,128)} %copy-done.2, f32[1024]{0:T(1024)S(1)} %fusion.56, f32[1,1024,512]{2,1,0:T(8,128)S(1)} %slice_bitcast_fusion, f32[512]{0:T(512)S(1)} %bitcast.193, ...), kind=kOutput, calls=%fused_computation.16 | convolution fusion | flops 1085275648 | bytes 14696448 | tf_op jit(solution)/shard_map/bld,cd->blc/dot_general | solution.py:256
  168.3 1.2 convolution_bitcast_fusion.1
  169.6 9.0 %all-gather.2 = bf16[8,64,16]{1,2,0:T(8,128)(2,1)S(1)} all-gather(bf16[1,64,16]{1,2,0:T(8,128)(2,1)S(1)} %bitcast.203), channel_id=1, replica_groups=mesh['fsdp'=8,'tp'=4] {'fsdp'}, dimensions={0}, use_global_device_ids=true | all-gather | bytes 18432 | tf_op jit(solution)/shard_map/all_gather | solution.py:185
  179.4 9.3 %all_gather.48 = bf16[64,512]{1,0:T(8,128)(2,1)S(1)} all-gather(bf16[8,512]{1,0:T(8,128)(2,1)S(1)} %copy-done.18), channel_id=1, replica_groups=mesh['fsdp'=8,'tp'=4] {'fsdp'}, dimensions={0}, use_global_device_ids=true | all-gather | bytes 73728 | tf_op jit(solution)/shard_map/all_gather | solution.py:183
  188.7 18.0 %all-reduce.14.cloned.1.call-done = f32[1,1024,96]{2,1,0:T(8,128)} async-done(((f32[1,1024,96]{2,1,0:T(8,128)}), f32[1,1024,96]{2,1,0:T(8,128)}) %all-reduce.14.cloned.1.call-update) | async-done | bytes 393232 | tf_op jit(solution)/shard_map/psum | solution.py:221
  206.7 2.6 slice_bitcast_fusion.1
  209.3 2.7 fusion.10
  212.0 20.4 %scan_fwd.1 = (f32[1024,512]{1,0:T(8,128)}, bf16[16384,512]{1,0:T(8,128)(2,1)}) custom-call(f32[1024,512]{1,0:T(8,128)} %get-tuple-element.113.dt_ref, bf16[1024,512]{1,0:T(8,128)(2,1)} %bitcast.178, f32[1024,16]{1,0:T(8,128)} %get-tuple-element.105.b_ref, f32[1024,16]{1,0:T(8,128)} %get-tuple-element.104.c_ref, f32[16,512]{1,0:T(8,128)} %bitcast.182), custom_call_target="tpu_custom_call" | custom-call | tf_op jit(solution)/shard_map/scan_fwd/pallas_call | solution.py:79
  232.5 45.4 %scan_bwd.1 = (f32[1024,512]{1,0:T(8,128)}, f32[1024,512]{1,0:T(8,128)}, f32[1024,16]{1,0:T(8,128)}, f32[1024,16]{1,0:T(8,128)}, f32[16,512]{1,0:T(8,128)}) custom-call(f32[1024,512]{1,0:T(8,128)} %get-tuple-element.113.dt_ref, bf16[1024,512]{1,0:T(8,128)(2,1)} %bitcast.179, f32[1024,16]{1,0:T(8,128)} %get-tuple-element.105.b_ref, ...), custom_call_target="tpu_custom_call" | custom-call | tf_op jit(solution)/shard_map/scan_bwd/pallas_call | solution.py:151
  277.9 3.1 convert_reduce_fusion
  283.5 34.0 %all-reduce.16.cloned.1.call-done = bf16[1024,96]{0,1:T(8,128)(2,1)} async-done(((bf16[1024,96]{0,1:T(8,128)(2,1)}), bf16[1024,96]{0,1:T(8,128)(2,1)}) %all-reduce.16.cloned.1.call-update) | async-done | bytes 196624 | tf_op jit(solution)/shard_map/psum | solution.py:291
  317.5 4.7 bitcast_multiply_fusion.1
  324.1 4.8 fusion.62
  328.8 0.9 copy.59
  329.8 6.0 fusion.30
  336.0 4.1 convert_bitcast_fusion
  340.2 6.6 fusion.34
  347.0 1.0 fusion.43
  348.0 1.2 fusion.59
  349.3 4.2 fusion.17
  355.2 1.4 copy.62
  356.6 35.4 %reduce-scatter.25.cloned.1.call-done = f32[64,4]{1,0:T(8,128)} async-done(((f32[512,4]{1,0:T(8,128)}), f32[64,4]{1,0:T(8,128)}) %reduce-scatter.25.cloned.1.call-update) | async-done | bytes 1040
  392.0 1.4 copy.60
  393.4 44.9 %reduce-scatter.15.cloned.1.call-done = bf16[1,256,1024]{2,1,0:T(8,128)(2,1)} async-done(((bf16[1,1024,1024]{2,1,0:T(8,128)(2,1)}), bf16[1,256,1024]{2,1,0:T(8,128)(2,1)}) %reduce-scatter.15.cloned.1.call-update) | async-done | bytes 524304 | tf_op jit(solution)/shard_map/reduce_scatter | solution.py:324
  438.3 1.5 fusion.40
  439.8 25.0 %all-reduce.9 = (f32[1024]{0:T(1024)S(1)}, f32[512]{0:T(512)S(1)}, f32[512]{0:T(512)S(1)}, f32[512]{0:T(512)S(1)}) all-reduce(f32[1024]{0:T(1024)S(1)} %get-tuple-element.82, f32[512]{0:T(512)S(1)} %get-tuple-element.77, f32[512]{0:T(512)S(1)} %get-tuple-element.95, ...), channel_id=4, replica_groups=mesh['fsdp'=8,'tp'=4] {'fsdp'}, use_global_device_ids=true, to_apply=%region_9.10.clone | all-reduce | flops 2560 | bytes 20480
  466.6 11.4 %psum.24 = f32[128]{0:T(128)} all-reduce(f32[128]{0:T(128)S(1)} %dynamic-slice.4), channel_id=1, replica_groups=mesh['fsdp'=8,'tp'=4] {'tp'}, use_global_device_ids=true, to_apply=%region_8.9 | all-reduce | flops 128 | bytes 1024 | tf_op jit(solution)/shard_map/psum | solution.py:334
  478.0 5.9 reduce-scatter.13.cloned.1.call-done
  483.9 2.8 fusion.38
  486.7 51.6 %reduce-scatter.17.cloned.1.call-done = f32[128,2,512]{2,0,1:T(8,128)} async-done(((f32[1024,2,512]{2,0,1:T(8,128)}), f32[128,2,512]{2,0,1:T(8,128)}) %reduce-scatter.17.cloned.1.call-update) | async-done | bytes 524304 | tf_op jit(solution)/shard_map/reduce_scatter | solution.py:337
  538.3 2.2 copy.55
  540.5 34.6 %reduce-scatter.21.cloned.1.call-done = f32[8,512]{1,0:T(8,128)} async-done(((f32[64,512]{1,0:T(8,128)}), f32[8,512]{1,0:T(8,128)}) %reduce-scatter.21.cloned.1.call-update) | async-done | bytes 16400 | tf_op jit(solution)/shard_map/reduce_scatter | solution.py:341
  575.1 37.5 %reduce-scatter.19.cloned.1.call-done = f32[64,96]{1,0:T(8,128)} async-done(((f32[512,96]{1,0:T(8,128)}), f32[64,96]{1,0:T(8,128)}) %reduce-scatter.19.cloned.1.call-update) | async-done | bytes 24592 | tf_op jit(solution)/shard_map/reduce_scatter | solution.py:340
  612.6 45.0 %reduce-scatter.23.cloned.1.call-done = f32[512,128]{1,0:T(8,128)} async-done(((f32[512,1024]{1,0:T(8,128)}), f32[512,128]{1,0:T(8,128)}) %reduce-scatter.23.cloned.1.call-update) | async-done | bytes 262160 | tf_op jit(solution)/shard_map/reduce_scatter | solution.py:345
  (101 shorter events, 11.5 us)
Async XLA Ops:
  7.2 42.2 %copy-start.17 = (bf16[64,96]{1,0:T(8,128)(2,1)S(1)}, bf16[64,96]{1,0:T(8,128)(2,1)}, u32[]{:S(2)}) copy-start(bf16[64,96]{1,0:T(8,128)(2,1)} %param.19) | copy-start | bytes 36868
  7.2 51.1 %all-gather.8.cloned.1.call-start = ((), (), s32[]{:S(2)}) async-start(), calls=%async_computation.8 | async-start | bytes 2621440 | tf_op jit(solution)/shard_map/all_gather | solution.py:201
  7.9 79.5 %all-gather.10.cloned.1.call-start = ((), (), s32[]{:S(2)}) async-start(), calls=%async_computation.9 | async-start | bytes 2359296 | tf_op jit(solution)/shard_map/all_gather | solution.py:179
  9.7 103.2 %all-gather.12.cloned.1.call-start = ((), (), s32[]{:S(2)}) async-start(), calls=%async_computation.11 | async-start | bytes 1179648 | tf_op jit(solution)/shard_map/all_gather | solution.py:187
  10.4 149.9 %all-gather.14.cloned.1.call-start = ((), (), s32[]{:S(2)}) async-start(), calls=%async_computation.13 | async-start | bytes 2621440 | tf_op jit(solution)/shard_map/all_gather | solution.py:255
  11.0 195.7 %all-reduce.14.cloned.1.call-start = ((), (), s32[]{:S(2)}) async-start(), calls=%async_computation.10 | async-start | bytes 1048576 | tf_op jit(solution)/shard_map/psum | solution.py:221
  58.3 29.1 %copy-start.11 = (bf16[1,1024,1024]{2,1,0:T(8,128)(2,1)S(1)}, bf16[1,1024,1024]{2,1,0:T(8,128)(2,1)}, u32[]{:S(2)}) copy-start(bf16[1,1024,1024]{2,1,0:T(8,128)(2,1)} %all-gather.8.cloned.1.call-done) | copy-start | bytes 6291460
  91.3 1.9 copy-start.2
  93.5 74.8 %copy-start.4 = (f32[1,1024,512]{2,1,0:T(8,128)}, f32[1,1024,512]{2,1,0:T(8,128)S(1)}, u32[]{:S(2)}) copy-start(f32[1,1024,512]{2,1,0:T(8,128)S(1)} %slice_bitcast_fusion) | copy-start | bytes 6291460
  168.3 41.0 %copy-start = (bf16[1,1024,512]{2,1,0:T(8,128)(2,1)}, bf16[1,1024,512]{2,1,0:T(8,128)(2,1)S(1)}, u32[]{:S(2)}) copy-start(bf16[1,1024,512]{2,1,0:T(8,128)(2,1)S(1)} %get-tuple-element.93) | copy-start | bytes 3145732
  168.3 1.3 copy-start.19
  168.3 11.1 %copy-start.18 = (bf16[8,512]{1,0:T(8,128)(2,1)S(1)}, bf16[8,512]{1,0:T(8,128)(2,1)}, u32[]{:S(2)}) copy-start(bf16[8,512]{1,0:T(8,128)(2,1)} %param.20) | copy-start | bytes 24580
  169.5 147.9 %all-reduce.16.cloned.1.call-start = ((), (), s32[]{:S(2)}) async-start(), calls=%async_computation.14 | async-start | bytes 393216 | tf_op jit(solution)/shard_map/psum | solution.py:291
  206.7 2.6 copy-start.7
  232.5 45.4 %copy-start.1 = (bf16[1,1024,512]{2,1,0:T(8,128)(2,1)S(1)}, bf16[1,1024,512]{2,1,0:T(8,128)(2,1)}, u32[]{:S(2)}) copy-start(bf16[1,1024,512]{2,1,0:T(8,128)(2,1)} %copy-done) | copy-start | bytes 3145732
  277.9 3.6 copy-start.13
  277.9 3.6 copy-start.14
  281.0 1.6 copy-start.16
  282.5 72.7 %reduce-scatter.27.cloned.1.call-start = ((), (), s32[]{:S(2)}) async-start(), calls=%async_computation.21 | async-start | bytes 294912
  283.4 108.6 %reduce-scatter.25.cloned.1.call-start = ((), (), s32[]{:S(2)}) async-start(), calls=%async_computation.20 | async-start | bytes 294912
  317.5 4.7 copy-start.3
  317.5 5.4 copy-start.5
  317.5 6.0 copy-start.9
  317.5 6.6 copy-start.10
  329.7 108.5 %reduce-scatter.15.cloned.1.call-start = ((), (), s32[]{:S(2)}) async-start(), calls=%async_computation.15 | async-start | bytes 2621440 | tf_op jit(solution)/shard_map/reduce_scatter | solution.py:324
  335.8 148.1 %reduce-scatter.13.cloned.1.call-start = ((), (), s32[]{:S(2)}) async-start(), calls=%async_computation.12 | async-start | bytes 2621440 | tf_op jit(solution)/shard_map/reduce_scatter | solution.py:242
  340.2 198.1 %reduce-scatter.17.cloned.1.call-start = ((), (), s32[]{:S(2)}) async-start(), calls=%async_computation.16 | async-start | bytes 4718592 | tf_op jit(solution)/shard_map/reduce_scatter | solution.py:337
  346.9 1.1 copy-start.15
  346.9 228.2 %reduce-scatter.21.cloned.1.call-start = ((), (), s32[]{:S(2)}) async-start(), calls=%async_computation.18 | async-start | bytes 147456 | tf_op jit(solution)/shard_map/reduce_scatter | solution.py:341
  347.9 1.3 copy-start.8
  348.0 264.7 %reduce-scatter.19.cloned.1.call-start = ((), (), s32[]{:S(2)}) async-start(), calls=%async_computation.17 | async-start | bytes 294912 | tf_op jit(solution)/shard_map/reduce_scatter | solution.py:340
  349.2 308.4 %reduce-scatter.23.cloned.1.call-start = ((), (), s32[]{:S(2)}) async-start(), calls=%async_computation.19 | async-start | bytes 2359296 | tf_op jit(solution)/shard_map/reduce_scatter | solution.py:345
  353.5 1.4 copy-start.6
  353.5 130.4 %copy-start.12 = (bf16[1,256,1024]{2,1,0:T(8,128)(2,1)S(1)}, bf16[1,256,1024]{2,1,0:T(8,128)(2,1)}, u32[]{:S(2)}) copy-start(bf16[1,256,1024]{2,1,0:T(8,128)(2,1)} %param.25) | copy-start | bytes 1572868
Sparse Core Ops, SparseCore 0:
  9.6 48.6 all-gather.7
  60.7 26.5 all-gather.9
  89.3 23.5 all-gather.11
  114.3 45.9 all-gather.13
  169.7 36.9 all-reduce.13
  282.6 34.8 all-reduce.15
  321.4 33.3 reduce-scatter.26
  358.3 33.6 reduce-scatter.24
  394.4 43.8 reduce-scatter.14
  440.4 43.4 reduce-scatter.12
  487.6 50.6 reduce-scatter.16
  541.7 33.3 reduce-scatter.20
  579.0 33.6 reduce-scatter.18
  616.3 41.2 reduce-scatter.22

commit v2 on v0

v2 whole, which is shorter than its diff:
```python
import functools

import jax
import jax.numpy as jnp
from jax import lax
from jax.experimental import pallas as pl
from jax.experimental.pallas import tpu as pltpu
from jax.sharding import PartitionSpec as P

bf16 = jnp.bfloat16
f32 = jnp.float32
LOG2E = 1.4426950408889634
LN2 = 0.6931471805599453
SUB = 16
ROWS = 128
UNROLL = 16
NT = (((1,), (1,)), ((), ()))
TN = (((0,), (0,)), ((), ()))
epsilon = 1e-05
VMEM_LIMIT = 56 * 2**20


def dot(a, b, dims=(((1,), (0,)), ((), ()))):
    return lax.dot_general(a, b, dims, preferred_element_type=f32)


def shape(dims, kind):
    return jax.ShapeDtypeStruct(dims, kind)


def iota(dims, axis):
    return lax.broadcasted_iota(jnp.int32, dims, axis)


def params():
    return pltpu.CompilerParams(vmem_limit_bytes=VMEM_LIMIT)


def halves(values):
    high = values.astype(bf16)
    return high, (values - high.astype(f32)).astype(bf16)


def spread(parts, first, width, positions):
    rows, cols = parts[0].shape
    wide = positions * width
    pick = (iota((cols, wide), 1) % width + first == iota((cols, wide), 0)).astype(bf16)
    keep = iota((rows, wide), 1) // width == iota((rows, wide), 0) % positions
    return [jnp.where(keep, dot(part, pick), 0.0).astype(bf16) for part in parts]


def outer(e_high, e_low, v_high, v_low):
    left = jnp.concatenate([e_high, e_high, e_low], 0)
    right = jnp.concatenate([v_high, v_low, v_high], 0)
    return dot(left, right, TN)


def live_rows(length, first, rows):
    return (iota((rows, 1), 0) + first < length).astype(f32)


def front_kernel(
    pieces, order, place, tokens, gain, conv_w, conv_b, x_w, *refs
):
    piece_refs = refs[:pieces]
    normed_ref, w_ref, input_ref, gate_ref, sum_ref, low_ref, map_ref, halo = refs[pieces:]
    rows = tokens.shape[1]
    chans = conv_w.shape[1]
    taps = conv_w.shape[0]

    @pl.when(pl.program_id(0) == 0)
    def _():
        for index in range(pieces):
            depth = piece_refs[index].shape[0]
            start = pl.multiple_of(place[index] * depth, depth)
            w_ref[pl.ds(start, depth), :] = piece_refs[index][...]
        halo[:8] = jnp.zeros_like(halo[:8])

    values = tokens[0].astype(f32)
    inverse = lax.rsqrt(jnp.mean(values * values, axis=-1, keepdims=True) + epsilon)
    normed = (values * inverse * gain[...]).astype(bf16)
    normed_ref[...] = normed
    projected = dot(normed, w_ref[...])
    conv_in = projected[:, :chans]
    input_ref[...] = conv_in
    gate_ref[...] = projected[:, chans:]
    halo[8:] = conv_in
    total = conv_b[...]
    for tap in range(taps):
        first = 8 - taps + 1 + tap
        total = total + conv_w[tap : tap + 1] * halo[first : first + rows]
    halo[:8] = conv_in[rows - 8 :]
    sum_ref[...] = total
    low = (total * jax.nn.sigmoid(total)).astype(bf16)
    low_ref[...] = low
    map_ref[...] = dot(low, x_w[...], NT)


def front(order, place, stack, gain, conv_w, conv_b, x_w, pieces):
    count, rows, depth = stack.shape
    total = count * rows
    chans = conv_w.shape[1]
    maps = x_w.shape[0]
    full = lambda a: pl.BlockSpec(a.shape, lambda i, *_: (0,) * a.ndim)
    row = lambda w: pl.BlockSpec((rows, w), lambda i, *_: (i, 0))
    both = pieces[0].shape[1]
    return pl.pallas_call(
        functools.partial(front_kernel, len(pieces)),
        grid_spec=pltpu.PrefetchScalarGridSpec(
            num_scalar_prefetch=2,
            grid=(count,),
            in_specs=[pl.BlockSpec((1, rows, depth), lambda i, o, p: (o[i], 0, 0))]
            + [full(a) for a in (gain, conv_w, conv_b, x_w)]
            + [full(a) for a in pieces],
            out_specs=[
                row(depth),
                pl.BlockSpec((depth, both), lambda i, *_: (0, 0)),
                row(chans),
                row(chans),
                row(chans),
                row(chans),
                row(maps),
            ],
            scratch_shapes=[pltpu.VMEM((rows + 8, chans), f32)],
        ),
        out_shape=[
            shape((total, depth), bf16),
            shape((depth, both), bf16),
            shape((total, chans), f32),
            shape((total, chans), f32),
            shape((total, chans), f32),
            shape((total, chans), bf16),
            shape((total, maps), f32),
        ],
        compiler_params=params(),
        name="front",
    )(order, place, stack, gain, conv_w, conv_b, x_w, *pieces)


def forward_kernel(
    length, own, got, low, gate, dt_w, dt_b, a_log, skip,
    mixed_ref, before_ref, step_ref, h_ref, drive, state,
):
    rows, chans = low.shape
    width = a_log.shape[0]
    rank = dt_w.shape[0] - 2 * width
    half = width // 2
    first = pl.program_id(0) * rows

    @pl.when(pl.program_id(0) == 0)
    def _():
        state[...] = jnp.zeros_like(state)

    live = live_rows(length[0], first, rows)
    mapped = own[...] + got[...].astype(f32)
    parts = halves(mapped)
    step = jax.nn.softplus(dot(parts[0], dt_w[...]) + dt_b[...]) * live
    step_ref[...] = step
    conv_out = low[...].astype(f32)
    b_high, b_low = spread(parts, rank, width, SUB)
    x_high, x_low = halves(step * conv_out)
    for index in range(rows // SUB):
        s = slice(index * SUB, (index + 1) * SUB)
        drive[index * SUB * width : (index + 1) * SUB * width, :] = outer(
            b_high[s], b_low[s], x_high[s], x_low[s]
        )
    rate = -jnp.exp(a_log[...]) * LOG2E
    rate_0, rate_1 = rate[:half], rate[half:]

    def body(block, carried):
        h_0, h_1 = carried
        steps = step_ref[pl.ds(pl.multiple_of(block * UNROLL, UNROLL), UNROLL), :]
        for k in range(UNROLL):
            wide = jnp.broadcast_to(steps[k : k + 1], (half, chans))
            base = pl.multiple_of(block * (UNROLL * width), UNROLL * width) + k * width
            h_0 = jnp.exp2(wide * rate_0) * h_0 + drive[pl.ds(base, half), :]
            h_1 = jnp.exp2(wide * rate_1) * h_1 + drive[pl.ds(base + half, half), :]
            h_ref[pl.ds(base, width), :] = jnp.concatenate([h_0, h_1], 0).astype(bf16)
        return h_0, h_1

    h_0, h_1 = lax.fori_loop(0, rows // UNROLL, body, (state[:half], state[half:]))
    state[:half] = h_0
    state[half:] = h_1
    c_high, c_low = spread(parts, rank + width, width, SUB)
    scan = []
    for index in range(rows // SUB):
        s = slice(index * SUB, (index + 1) * SUB)
        both = dot(
            jnp.concatenate([c_high[s], c_low[s]], 0),
            h_ref[index * SUB * width : (index + 1) * SUB * width, :],
        )
        scan.append(both[:SUB] + both[SUB:])
    before = jnp.concatenate(scan, 0) + skip[...] * conv_out
    before_ref[...] = before
    gates = gate[...]
    mixed_ref[...] = (before * (gates * jax.nn.sigmoid(gates)) * live).astype(bf16)


def forward(length, own, got, low, gate, dt_w, dt_b, a_log, skip):
    total, chans = low.shape
    width = a_log.shape[0]
    row = lambda w: pl.BlockSpec((ROWS, w), lambda i, *_: (i, 0))
    full = lambda a: pl.BlockSpec(a.shape, lambda i, *_: (0,) * a.ndim)
    maps = own.shape[1]
    return pl.pallas_call(
        forward_kernel,
        grid_spec=pltpu.PrefetchScalarGridSpec(
            num_scalar_prefetch=1,
            grid=(total // ROWS,),
            in_specs=[row(maps), row(maps), row(chans), row(chans)]
            + [full(a) for a in (dt_w, dt_b, a_log, skip)],
            out_specs=[
                row(chans),
                row(chans),
                row(chans),
                pl.BlockSpec((ROWS * width, chans), lambda i, *_: (i, 0)),
            ],
            scratch_shapes=[
                pltpu.VMEM((ROWS * width, chans), f32),
                pltpu.VMEM((width, chans), f32),
            ],
        ),
        out_shape=[
            shape((total, chans), bf16),
            shape((total, chans), f32),
            shape((total, chans), f32),
            shape((total * width, chans), bf16),
        ],
        compiler_params=params(),
        name="forward",
    )(length, own, got, low, gate, dt_w, dt_b, a_log, skip)


def gate_kernel(length, grad, out_w, gate, before, low, scan_ref, gate_ref, skip_ref):
    rows = grad.shape[0]
    live = live_rows(length[0], pl.program_id(0) * rows, rows)
    masked = dot(grad[...], out_w[...], NT) * live
    gates = gate[...]
    sigma = jax.nn.sigmoid(gates)
    scan_grad = masked * (gates * sigma)
    scan_ref[...] = scan_grad
    gate_ref[...] = (masked * before[...] * (sigma * (1.0 + gates * (1.0 - sigma)))).astype(bf16)

    @pl.when(pl.program_id(0) == 0)
    def _():
        skip_ref[...] = jnp.zeros_like(skip_ref)

    skip_ref[...] += jnp.sum(scan_grad * low[...].astype(f32), axis=0, keepdims=True)


def gate_back(length, grad, out_w, gate, before, low):
    total, chans = low.shape
    rows = 256
    row = lambda w: pl.BlockSpec((rows, w), lambda i, *_: (i, 0))
    full = lambda a: pl.BlockSpec(a.shape, lambda i, *_: (0,) * a.ndim)
    return pl.pallas_call(
        gate_kernel,
        grid_spec=pltpu.PrefetchScalarGridSpec(
            num_scalar_prefetch=1,
            grid=(total // rows,),
            in_specs=[row(grad.shape[1]), full(out_w), row(chans), row(chans), row(chans)],
            out_specs=[row(chans), row(chans), pl.BlockSpec((1, chans), lambda i, *_: (0, 0))],
        ),
        out_shape=[shape((total, chans), f32), shape((total, chans), bf16), shape((1, chans), f32)],
        compiler_params=params(),
        name="gate_back",
    )(length, grad, out_w, gate, before, low)


def backward_kernel(
    length, own, got, low, step_ref, scan_grad_ref, h_ref, last_ref, dt_w, dt_b, a_log, skip,
    map_ref, out_ref, rate_ref, dt_w_ref, dt_b_ref, drive, carry, grads, terms,
):
    rows, chans = low.shape
    width = a_log.shape[0]
    rank = dt_w.shape[0] - 2 * width
    half = width // 2
    turn = pl.program_id(0)
    turns = pl.num_programs(0)

    @pl.when(turn == 0)
    def _():
        carry[...] = jnp.zeros_like(carry)
        rate_ref[...] = jnp.zeros_like(rate_ref)
        dt_w_ref[...] = jnp.zeros_like(dt_w_ref)
        dt_b_ref[...] = jnp.zeros_like(dt_b_ref)

    mapped = own[...] + got[...].astype(f32)
    parts = halves(mapped)
    c_high, c_low = spread(parts, rank + width, width, SUB)
    scan_grad = scan_grad_ref[...]
    y_high, y_low = halves(scan_grad)
    for index in range(rows // SUB):
        s = slice(index * SUB, (index + 1) * SUB)
        drive[index * SUB * width : (index + 1) * SUB * width, :] = outer(
            c_high[s], c_low[s], y_high[s], y_low[s]
        )
    rate = -jnp.exp(a_log[...]) * LOG2E
    rate_0, rate_1 = rate[:half], rate[half:]
    before = jnp.where(turn == turns - 1, jnp.zeros_like(last_ref[...]), last_ref[...])

    def body(back, carried):
        q_0, q_1, sum_0, sum_1 = carried
        block = rows // UNROLL - 1 - back
        steps = step_ref[pl.ds(pl.multiple_of(block * UNROLL, UNROLL), UNROLL), :]
        for k in reversed(range(UNROLL)):
            wide = jnp.broadcast_to(steps[k : k + 1], (half, chans))
            base = pl.multiple_of(block * (UNROLL * width), UNROLL * width) + k * width
            g_0 = drive[pl.ds(base, half), :] + q_0
            g_1 = drive[pl.ds(base + half, half), :] + q_1
            grads[pl.ds(base, width), :] = jnp.concatenate([g_0, g_1], 0).astype(bf16)
            q_0 = jnp.exp2(wide * rate_0) * g_0
            q_1 = jnp.exp2(wide * rate_1) * g_1
            if k == 0:
                start = pl.multiple_of(jnp.maximum(base - width, 0), width)
                past = jnp.where(block == 0, before, h_ref[pl.ds(start, width), :])
            else:
                past = h_ref[pl.ds(base - width, width), :]
            past = past.astype(f32)
            m_0 = rate_0 * (q_0 * past[:half])
            m_1 = rate_1 * (q_1 * past[half:])
            sum_0 = sum_0 + wide * m_0
            sum_1 = sum_1 + wide * m_1
            terms[pl.ds(base, width), :] = jnp.concatenate([m_0, m_1], 0).astype(bf16)
        return q_0, q_1, sum_0, sum_1

    q_0, q_1, sum_0, sum_1 = lax.fori_loop(
        0, rows // UNROLL, body, (carry[:half], carry[half:], rate_ref[:half], rate_ref[half:])
    )
    carry[:half] = q_0
    carry[half:] = q_1
    rate_ref[:half] = sum_0
    rate_ref[half:] = sum_1
    b_high, b_low = spread(parts, rank, width, SUB)
    wide = SUB * width
    own_group = iota((SUB, wide), 1) // width == iota((SUB, wide), 0)
    ones = own_group.astype(bf16)
    maps = rank + 2 * width
    pick_b = (iota((wide, maps), 0) % width + rank == iota((wide, maps), 1)).astype(bf16)
    pick_c = (iota((wide, maps), 0) % width + rank + width == iota((wide, maps), 1)).astype(bf16)
    steps = step_ref[...]
    conv_out = low[...].astype(f32)
    drive_low = (steps * conv_out).astype(bf16)
    weighted, stepped, crossed = [], [], []
    for index in range(rows // SUB):
        s = slice(index * SUB, (index + 1) * SUB)
        big = slice(index * SUB * width, (index + 1) * SUB * width)
        grad = grads[big, :]
        both = dot(jnp.concatenate([b_high[s], b_low[s]], 0), grad)
        weighted.append(both[:SUB] + both[SUB:])
        stepped.append(dot(ones, terms[big, :]))
        on_b = jnp.where(own_group, dot(drive_low[s], grad, NT), 0.0).astype(bf16)
        on_c = jnp.where(own_group, dot(y_high[s], h_ref[big, :], NT), 0.0).astype(bf16)
        crossed.append(dot(on_b, pick_b) + dot(on_c, pick_c))
    weighted = jnp.concatenate(weighted, 0)
    step_grad = jnp.concatenate(stepped, 0) * LN2 + conv_out * weighted
    live = live_rows(length[0], (turns - 1 - turn) * rows, rows)
    step_pre = dot(parts[0], dt_w[...]) + dt_b[...]
    pre_grad = (step_grad * live * jax.nn.sigmoid(step_pre)).astype(bf16)
    dt_b_ref[...] += jnp.sum(pre_grad.astype(f32), axis=0, keepdims=True)
    dt_w_ref[...] += dot(parts[0], pre_grad, TN)
    map_ref[...] = jnp.concatenate(crossed, 0) + dot(pre_grad, dt_w[...], NT)
    out_ref[...] = scan_grad * skip[...] + steps * weighted


def backward(length, own, got, low, step, scan_grad, h, dt_w, dt_b, a_log, skip):
    total, chans = low.shape
    width = a_log.shape[0]
    turns = total // ROWS
    at = lambda i: turns - 1 - i
    row = lambda w: pl.BlockSpec((ROWS, w), lambda i, *_: (at(i), 0))
    full = lambda a: pl.BlockSpec(a.shape, lambda i, *_: (0,) * a.ndim)
    maps = own.shape[1]
    return pl.pallas_call(
        backward_kernel,
        grid_spec=pltpu.PrefetchScalarGridSpec(
            num_scalar_prefetch=1,
            grid=(turns,),
            in_specs=[
                row(maps),
                row(maps),
                row(chans),
                row(chans),
                row(chans),
                pl.BlockSpec((ROWS * width, chans), lambda i, *_: (at(i), 0)),
                pl.BlockSpec((width, chans), lambda i, *_: (jnp.maximum(at(i) * ROWS - 1, 0), 0)),
            ]
            + [full(a) for a in (dt_w, dt_b, a_log, skip)],
            out_specs=[row(maps), row(chans), full(a_log), full(dt_w), full(dt_b)],
            scratch_shapes=[
                pltpu.VMEM((ROWS * width, chans), f32),
                pltpu.VMEM((width, chans), f32),
                pltpu.VMEM((ROWS * width, chans), bf16),
                pltpu.VMEM((ROWS * width, chans), bf16),
            ],
        ),
        out_shape=[
            shape((total, maps), f32),
            shape((total, chans), f32),
            shape(a_log.shape, f32),
            shape(dt_w.shape, f32),
            shape(dt_b.shape, f32),
        ],
        compiler_params=params(),
        name="backward",
    )(length, own, got, low, step, scan_grad, h, h, dt_w, dt_b, a_log, skip)


def back_kernel(
    slot, own, got, x_w, out_grad, conv_sum, conv_in, low, conv_w, gate_grad, normed, tokens, w,
    part_ref, weight_ref, x_ref, conv_w_ref, conv_b_ref, gain_ref, halo, total,
):
    rows, chans = low.shape
    taps = conv_w.shape[0]
    turn = pl.program_id(0)

    @pl.when(turn == 0)
    def _():
        halo[rows:] = jnp.zeros_like(halo[rows:])
        total[...] = jnp.zeros_like(total)
        for ref in (x_ref, conv_w_ref, conv_b_ref, gain_ref):
            ref[...] = jnp.zeros_like(ref)

    map_grad = (own[...] + got[...].astype(f32)).astype(bf16)
    x_ref[...] += dot(map_grad, low[...], TN)
    values = conv_sum[...]
    sigma = jax.nn.sigmoid(values)
    sum_grad = (out_grad[...] + dot(map_grad, x_w[...])) * (sigma * (1.0 + values * (1.0 - sigma)))
    conv_b_ref[...] += jnp.sum(sum_grad, axis=0, keepdims=True)
    halo[:rows] = sum_grad
    inputs = conv_in[...]
    input_grad = jnp.zeros_like(inputs)
    for tap in range(taps):
        first = taps - 1 - tap
        moved = halo[first : first + rows]
        input_grad = input_grad + conv_w[tap : tap + 1] * moved
        conv_w_ref[tap : tap + 1] += jnp.sum(inputs * moved, axis=0, keepdims=True)
    halo[rows:] = sum_grad[:8]
    input_grad = input_grad.astype(bf16)
    total[...] += dot(normed[...], input_grad, TN)
    part = dot(jnp.concatenate([input_grad, gate_grad[...]], 1), w[...], NT)
    part_ref[0] = part.astype(bf16)
    values = tokens[0].astype(f32)
    inverse = lax.rsqrt(jnp.mean(values * values, axis=-1, keepdims=True) + epsilon)
    gain_ref[...] += jnp.sum(part * (values * inverse), axis=0, keepdims=True)

    @pl.when(turn == pl.num_programs(0) - 1)
    def _():
        weight_ref[...] = total[...].astype(bf16)


def back(slot, order, own, got, x_w, out_grad, conv_sum, conv_in, low, conv_w, gate_grad, normed, stack, w):
    chans = low.shape[1]
    count, rows, depth = stack.shape
    at = lambda i: count - 1 - i
    row = lambda a: pl.BlockSpec((rows, a.shape[1]), lambda i, *_: (at(i), 0))
    full = lambda a: pl.BlockSpec(a.shape, lambda i, *_: (0,) * len(a.shape))
    outs = [
        shape((count, rows, depth), bf16),
        shape((depth, chans), bf16),
        shape(x_w.shape, f32),
        shape(conv_w.shape, f32),
        shape((1, chans), f32),
        shape((1, depth), f32),
    ]

    def kernel(slot, order, *refs):
        back_kernel(slot, *refs)

    return pl.pallas_call(
        kernel,
        grid_spec=pltpu.PrefetchScalarGridSpec(
            num_scalar_prefetch=2,
            grid=(count,),
            in_specs=[
                row(own),
                row(got),
                full(x_w),
                row(out_grad),
                row(conv_sum),
                row(conv_in),
                row(low),
                full(conv_w),
                row(gate_grad),
                row(normed),
                pl.BlockSpec((1, rows, depth), lambda i, s, o: (o[at(i)], 0, 0)),
                full(w),
            ],
            out_specs=[pl.BlockSpec((1, rows, depth), lambda i, s, o: (s[at(i)], 0, 0))]
            + [full(a) for a in outs[1:]],
            scratch_shapes=[pltpu.VMEM((rows + 8, chans), f32), pltpu.VMEM((depth, chans), f32)],
        ),
        out_shape=outs,
        compiler_params=params(),
        name="back",
    )(slot, order, own, got, x_w, out_grad, conv_sum, conv_in, low, conv_w, gate_grad, normed, stack, w)


def project_kernel(slot, mixed, out_w, part_ref):
    part_ref[0] = dot(mixed[...], out_w[...]).astype(bf16)


def project(slot, mixed, out_w, count):
    total, chans = mixed.shape
    rows = total // count
    depth = out_w.shape[1]
    return pl.pallas_call(
        project_kernel,
        grid_spec=pltpu.PrefetchScalarGridSpec(
            num_scalar_prefetch=1,
            grid=(count,),
            in_specs=[
                pl.BlockSpec((rows, chans), lambda i, s: (i, 0)),
                pl.BlockSpec(out_w.shape, lambda i, s: (0, 0)),
            ],
            out_specs=pl.BlockSpec((1, rows, depth), lambda i, s: (s[i], 0, 0)),
        ),
        out_shape=shape((count, rows, depth), bf16),
        compiler_params=params(),
        name="project",
    )(slot, mixed, out_w)


def exchange(values, axis, size, bits):
    return lax.ppermute(values, axis, [(i, i ^ bits) for i in range(size)])


def relay(values, axis, size, cuts):
    me = lax.axis_index(axis)
    rows = values.shape[0] // cuts
    found = []
    for cut in range(cuts):
        piece = values[cut * rows : (cut + 1) * rows]
        up, down = [piece], [piece]
        for hop in range(1, size):
            pairs = range(hop - 1, size - 1)
            up.append(lax.ppermute(up[-1], axis, [(i, i + 1) for i in pairs]))
            down.append(lax.ppermute(down[-1], axis, [(size - 1 - i, size - 2 - i) for i in pairs]))
        found.append([piece] + [jnp.where(me >= k, up[k], down[size - k]) for k in range(1, size)])
    return jnp.stack([jnp.concatenate([part[k] for part in found], 0) for k in range(size)])


def gather_pieces(values, axis, size):
    even = [values] + [exchange(values, axis, size, m) for m in range(2, size, 2)]
    odd = [exchange(piece, axis, size, 1) for piece in even]
    return [piece for pair in zip(even, odd) for piece in pair]


def scatter_sum(values, axis, size):
    me = lax.axis_index(axis)
    pairs = values.reshape((size // 2, 2) + values.shape[1:])
    core = me % 2
    keep = lax.dynamic_index_in_dim(pairs, core, 1, False)
    send = lax.dynamic_index_in_dim(pairs, 1 - core, 1, False)
    summed = keep + exchange(send, axis, size, 1)
    place = me // 2
    total = lax.dynamic_index_in_dim(summed, place, 0, False).astype(f32)
    for m in range(1, size // 2):
        piece = lax.dynamic_index_in_dim(summed, place ^ m, 0, False)
        total = total + exchange(piece, axis, size, 2 * m).astype(f32)
    return total


def sum_all(values, axis, size):
    bits = 1
    while bits < size:
        got = exchange(values.astype(bf16), axis, size, 2 * bits - 1)
        bits *= 2
        if bits < size:
            values = values + got.astype(f32)
    return values, got


def shards(
    fsdp, tp, tokens, lengths, norm_gain, in_weight, conv_weight, conv_bias, x_weight, dt_weight,
    dt_bias, a_log, d_skip, out_weight, cotangent,
):
    tp_me = lax.axis_index("tp")
    fs_me = lax.axis_index("fsdp")
    chunks = jnp.arange(tp)
    order = ((tp_me - chunks) % tp).astype(jnp.int32)
    slot = ((chunks - tp_me) % tp).astype(jnp.int32)
    place = (fs_me ^ jnp.arange(fsdp)).astype(jnp.int32)
    depth = tokens.shape[2]
    part = conv_weight.shape[1]
    chans = part * fsdp
    taps = conv_weight.shape[0]
    width = a_log.shape[0]
    maps = x_weight.shape[1]
    rank = maps - 2 * width

    stack = relay(tokens[0], "tp", tp, 2)
    pieces = gather_pieces(in_weight.reshape(in_weight.shape[0], 2 * chans), "fsdp", fsdp)
    small = jnp.concatenate(
        [
            conv_weight,
            conv_bias[None],
            dt_bias[None],
            d_skip[None],
            a_log,
            x_weight.T,
            dt_weight.reshape(-1, part),
            norm_gain.reshape(-1, part),
        ],
        0,
    )
    gathered = lax.all_gather(small, "fsdp", axis=0)
    top = taps + 3 + width + maps
    by_chan = gathered[:, :top].transpose(1, 0, 2).reshape(top, chans)
    conv_w = by_chan[:taps].astype(f32)
    conv_b, dt_b, skip = (by_chan[taps + i : taps + i + 1].astype(f32) for i in range(3))
    logs = by_chan[taps + 3 : taps + 3 + width].astype(f32)
    x_w = by_chan[taps + 3 + width :]
    dt_rows = rank * chans // part // fsdp
    dt_w = gathered[:, top : top + dt_rows].reshape(rank, chans)
    dt_w = jnp.pad(dt_w, ((0, 2 * width), (0, 0)))
    gain = gathered[:, top + dt_rows :].reshape(1, depth).astype(f32)
    out_w = lax.all_gather(out_weight, "fsdp", axis=1, tiled=True)
    grad_whole = lax.all_gather(cotangent[0], "tp", axis=0, tiled=True)

    normed, w, conv_in, gate, conv_sum, low, map_part = front(
        order, place, stack, gain, conv_w, conv_b, x_w, pieces
    )
    own, got = sum_all(map_part, "tp", tp)
    mixed, before, step, h = forward(lengths, own, got, low, gate, dt_w, dt_b, logs, skip)

    sent = project(slot, mixed, out_w, tp)
    block_out = tokens.astype(f32) + scatter_chunks(sent, "tp", tp)[None]
    scan_grad, gate_grad, skip_grad = gate_back(lengths, grad_whole, out_w, gate, before, low)
    out_grad = dot(grad_whole, mixed, TN).astype(bf16)
    out_weight_grad = scatter_sum(out_grad.reshape(fsdp, -1, chans), "fsdp", fsdp)
    gate_weight = dot(normed, gate_grad, TN).astype(bf16)
    gate_weight_grad = scatter_sum(gate_weight.reshape(fsdp, -1, chans), "fsdp", fsdp)

    map_part, conv_grad, rate_grad, dt_w_grad, dt_b_grad = backward(
        lengths, own, got, low, step, scan_grad, h, dt_w, dt_b, logs, skip
    )
    own_grad, got_grad = sum_all(map_part, "tp", tp)
    sent_back, conv_weight_half, x_w_grad, conv_w_grad, conv_b_grad, gain_grad = back(
        slot, order, own_grad, got_grad, x_w, conv_grad, conv_sum, conv_in, low, conv_w,
        gate_grad, normed, stack, w,
    )
    normed_grad = scatter_chunks(sent_back, "tp", tp)
    conv_half_grad = scatter_sum(conv_weight_half.reshape(fsdp, -1, chans), "fsdp", fsdp)
    a_log_grad = rate_grad * LN2
    rows = jnp.concatenate(
        [conv_w_grad, conv_b_grad, dt_b_grad, skip_grad, a_log_grad, x_w_grad], 0
    )
    packed = jnp.concatenate(
        [
            rows.reshape(top, fsdp, part).transpose(1, 0, 2),
            dt_w_grad[:rank].reshape(fsdp, -1, part),
            gain_grad.reshape(fsdp, -1, part),
        ],
        1,
    )
    small_grad = lax.psum_scatter(packed, "fsdp", scatter_dimension=0, tiled=False)
    gain_out = lax.psum(small_grad[top + dt_rows :].reshape(-1), "tp")

    own_values = tokens.astype(f32)
    own_inverse = lax.rsqrt(jnp.mean(own_values * own_values, axis=-1, keepdims=True) + epsilon)
    own_hat = own_values * own_inverse
    scaled = normed_grad[None] * gain[None]
    input_grads = cotangent.astype(f32) + own_inverse * (
        scaled - own_hat * jnp.mean(scaled * own_hat, axis=-1, keepdims=True)
    )
    return (
        block_out.astype(bf16),
        input_grads,
        gain_out,
        jnp.stack([conv_half_grad, gate_weight_grad], 1),
        small_grad[:taps],
        small_grad[taps],
        small_grad[taps + 3 + width : top].T,
        small_grad[top : top + dt_rows].reshape(-1, chans),
        small_grad[taps + 1],
        small_grad[taps + 3 : taps + 3 + width],
        small_grad[taps + 2],
        out_weight_grad.T,
    )


def scatter_chunks(sent, axis, size):
    total = sent[0].astype(f32)
    for s in range(1, size):
        total = total + lax.ppermute(
            sent[s], axis, [(i, (i + s) % size) for i in range(size)]
        ).astype(f32)
    return total


def solution(mesh):
    sizes = dict(mesh.shape)
    return jax.shard_map(
        functools.partial(shards, sizes["fsdp"], sizes["tp"]),
        mesh=mesh,
        in_specs=(
            P("fsdp", "tp", None),
            P("fsdp"),
            P("fsdp"),
            P("fsdp", None, "tp"),
            P(None, ("tp", "fsdp")),
            P(("tp", "fsdp")),
            P(("tp", "fsdp"), None),
            P("fsdp", "tp"),
            P(("tp", "fsdp")),
            P(None, ("tp", "fsdp")),
            P(("tp", "fsdp")),
            P("tp", "fsdp"),
            P("fsdp", "tp", None),
        ),
        out_specs=(
            P("fsdp", "tp", None),
            P("fsdp", "tp", None),
            P("fsdp"),
            P("fsdp", None, "tp"),
            P(None, ("tp", "fsdp")),
            P(("tp", "fsdp")),
            P(("tp", "fsdp"), None),
            P("fsdp", "tp"),
            P(("tp", "fsdp")),
            P(None, ("tp", "fsdp")),
            P(("tp", "fsdp")),
            P("tp", "fsdp"),
        ),
        check_vma=False,
    )
```

time: 1330 us -> 399 us (0.30)
  other arithmetic: 458 us -> 19.5 us
  waiting for transfers between devices: 398 us -> 136 us
  local copies, waits for them, and re-layouts: 298 us -> 36.5 us
  Pallas kernels: 0 us -> 106 us
  blocking collectives: 96.1 us -> 20.4 us
  starting transfers between devices: 0.57 us -> 59.2 us
  matrix products: 46.1 us -> 3.92 us
    reduce_sum x84 -> x1, other arithmetic: 259 us -> 0.5 us  [shards(): jnp.mean(scaled * own_hat, axis=-1, keepdims=True)]
    reduce_scatter x6 -> x1, waiting for transfers between devices: 219 us -> 0.01 us  [shards(): lax.psum_scatter(packed, 'fsdp', scatter_dimension=0, tiled=False)]
    ppermute x0 -> x41, waiting for transfers between devices: none -> 136 us  [the longest x6 65.6 us: scatter_chunks(): lax.ppermute(sent[s], axis, [(i, (i + s) % size) for i in range(size)])]
    pallas_call x0 -> x6, Pallas kernels: none -> 106 us  [the longest x1 48.7 us: backward(): pl.pallas_call(backward_kernel, grid_spec=pltpu.PrefetchScalarGridSpec(nu...]
    all_gather x4 -> x2, waiting for transfers between devices: 94 us -> 0.02 us  [the longest x1 0.02 us: shards(): out_w = lax.all_gather(out_weight, 'fsdp', axis=1, tiled=True)]
    rev x32 -> x0, local copies, waits for them, and re-layouts: 79.8 us -> none  [the longest x16 51.4 us: backward_block(): following_log[::-1]]
    mul x112 -> x0, local copies, waits for them, and re-layouts: 62.1 us -> none  [the longest x32 27 us: backward_block(): source = output_map[:, :, :, None] * scan_grad[:, :, None, :]]
    ppermute x0 -> x41, starting transfers between devices: none -> 59.1 us  [the longest x23 25.2 us: exchange(): return lax.ppermute(values, axis, [(i, i ^ bits) for i in range(size)])]
  transfers between devices with their start and end apart: 14 -> 44, of which waited for: 13 -> 12; matrix products, arithmetic and copies ran while one was open for 5% -> 13% of each run, Pallas kernels for 0% -> 13%
where the time goes in v2:
time: 399 us; the launch traced here: 397 us
  waiting for transfers between devices  136 us (34%)
  Pallas kernels  106 us (27%)
  starting transfers between devices  59.2 us (15%)
  local copies, waits for them, and re-layouts  36.5 us (9%)
  blocking collectives  20.4 us (5%)
  other arithmetic  19.5 us (5%)
  between operations  15.4 us (4%)
    ppermute x6, waiting for transfers between devices, scatter_chunks(): lax.ppermute(sent[s], axis, [(i, (i + s) % size) for i in range(size)])  65.6 us
    ppermute x6, waiting for transfers between devices, relay(): lax.ppermute(down[-1], axis, [(size - 1 - i, size - 2 - i) for i in pairs])  49 us
    pallas_call x1, Pallas kernels, backward(): pl.pallas_call(backward_kernel, grid_spec=pltpu.PrefetchScalarGridSpec(nu...  48.7 us
    ppermute x23, starting transfers between devices, exchange(): return lax.ppermute(values, axis, [(i, i ^ bits) for i in range(size)])  25.2 us
    pallas_call x1, Pallas kernels, forward(): pl.pallas_call(forward_kernel, grid_spec=pltpu.PrefetchScalarGridSpec(num...  22.2 us
    ppermute x23, waiting for transfers between devices, exchange(): return lax.ppermute(values, axis, [(i, i ^ bits) for i in range(size)])  21.2 us
    ppermute x6, starting transfers between devices, relay(): up.append(lax.ppermute(up[-1], axis, [(i, i + 1) for i in pairs]))  13.6 us
    pallas_call x1, Pallas kernels, back(): pl.pallas_call(kernel, grid_spec=pltpu.PrefetchScalarGridSpec(num_scalar_...  13.3 us
  transfers between devices with their start and end apart: 44, of which 12 were waited for; matrix products, arithmetic and copies ran while one was open for 13% of the time, Pallas kernels for 13%

profile of v2, /device:TPU:0, one launch (start us, length us, event | category | flops | bytes accessed | tf_op | source)
XLA Modules:
  0.0 397.2 jit_solution(1213400387811630278)
XLA Ops:
  9.1 4.9 %collective-permute-start.4 = (bf16[128,1024]{1,0:T(8,128)(2,1)S(1)}, bf16[128,1024]{1,0:T(8,128)(2,1)S(1)}, u32[]{:S(2)}, u32[]{:S(2)}) collective-permute-start(bf16[128,1024]{1,0:T(8,128)(2,1)S(1)} %get-tuple-element.161), channel_id=1, source_target_pairs={{0,1},{1,2},{2,3},{4,5},{5,6},{6,7},{8,9},{9,10},{10,11},{12,13},{... | collective-permute-start | bytes 786440 | tf_op jit(solution)/shard_map/ppermute | solution.py:537
  14.1 1.3 collective-permute-start.5
  15.4 4.6 %collective-permute-start = (bf16[128,1024]{1,0:T(8,128)(2,1)S(1)}, bf16[128,1024]{1,0:T(8,128)(2,1)S(1)}, u32[]{:S(2)}, u32[]{:S(2)}) collective-permute-start(bf16[128,1024]{1,0:T(8,128)(2,1)S(1)} %get-tuple-element.160), channel_id=1, source_target_pairs={{0,1},{1,2},{2,3},{4,5},{5,6},{6,7},{8,9},{9,10},{10,11},{12,13},{... | collective-permute-start | bytes 786440 | tf_op jit(solution)/shard_map/ppermute | solution.py:537
  22.2 1.6 collective-permute-start.13
  25.0 9.8 %all-gather.2 = bf16[8,185,64]{1,2,0:T(8,128)(2,1)S(1)} all-gather(bf16[1,185,64]{1,2,0:T(8,128)(2,1)S(1)} %bitcast.141), channel_id=2, replica_groups=mesh['fsdp'=8,'tp'=4] {'fsdp'}, dimensions={0}, use_global_device_ids=true | all-gather | bytes 213120 | tf_op jit(solution)/shard_map/all_gather | solution.py:607
  35.0 1.4 collective-permute-start.9
  38.3 1.4 collective-permute-start.8
  45.9 7.5 %collective-permute-done.6 = bf16[128,1024]{1,0:T(8,128)(2,1)S(1)} collective-permute-done((bf16[128,1024]{1,0:T(8,128)(2,1)S(1)}, bf16[128,1024]{1,0:T(8,128)(2,1)S(1)}, u32[]{:S(2)}, u32[]{:S(2)}) %collective-permute-start.6) | collective-permute-done | bytes 262176 | tf_op jit(solution)/shard_map/ppermute | solution.py:538
  54.2 13.9 %collective-permute-done.2 = bf16[128,1024]{1,0:T(8,128)(2,1)} collective-permute-done((bf16[128,1024]{1,0:T(8,128)(2,1)S(1)}, bf16[128,1024]{1,0:T(8,128)(2,1)}, u32[]{:S(2)}, u32[]{:S(2)}) %collective-permute-start.2) | collective-permute-done | bytes 262176 | tf_op jit(solution)/shard_map/ppermute | solution.py:538
  71.2 1.5 collective-permute-start.3
  73.5 22.7 %collective-permute-done.7 = bf16[128,1024]{1,0:T(8,128)(2,1)S(1)} collective-permute-done((bf16[128,1024]{1,0:T(8,128)(2,1)S(1)}, bf16[128,1024]{1,0:T(8,128)(2,1)S(1)}, u32[]{:S(2)}, u32[]{:S(2)}) %collective-permute-start.7) | collective-permute-done | bytes 262176 | tf_op jit(solution)/shard_map/ppermute | solution.py:538
  96.3 4.7 %collective-permute-done.3 = bf16[128,1024]{1,0:T(8,128)(2,1)S(1)} collective-permute-done((bf16[128,1024]{1,0:T(8,128)(2,1)}, bf16[128,1024]{1,0:T(8,128)(2,1)S(1)}, u32[]{:S(2)}, u32[]{:S(2)}) %collective-permute-start.3) | collective-permute-done | bytes 262176 | tf_op jit(solution)/shard_map/ppermute | solution.py:538
  101.1 1.6 pad_maximum_fusion.tokens.refs_10_
  104.3 9.0 %front.1 = (bf16[1024,1024]{1,0:T(8,128)(2,1)}, bf16[1024,1024]{1,0:T(8,128)(2,1)}, f32[1024,512]{1,0:T(8,128)}, f32[1024,512]{1,0:T(8,128)}, f32[1024,512]{1,0:...) custom-call(s32[4]{0:T(128)} %and_select_fusion.order, s32[8]{0:T(128)} %iota_xor_fusion.place, ...), custom_call_target="tpu_custom_call" | custom-call | tf_op jit(solution)/shard_map/front/pallas_call | solution.py:107
  119.1 3.0 collective-permute-done.19
  122.9 2.8 collective-permute-start.20
  125.7 5.8 %collective-permute-done.20.got = bf16[1024,96]{1,0:T(8,128)(2,1)S(1)} collective-permute-done((bf16[1024,96]{1,0:T(8,128)(2,1)S(1)}, bf16[1024,96]{1,0:T(8,128)(2,1)S(1)}, u32[]{:S(2)}, u32[]{:S(2)}) %collective-permute-start.20) | collective-permute-done | bytes 196640 | tf_op jit(solution)/shard_map/ppermute | solution.py:525
  132.3 22.2 %forward.1 = (bf16[1024,512]{1,0:T(8,128)(2,1)}, f32[1024,512]{1,0:T(8,128)}, f32[1024,512]{1,0:T(8,128)}, bf16[16384,512]{1,0:T(8,128)(2,1)}) custom-call(s32[1]{0:T(128)S(6)} %copy.166.length, f32[1024,96]{1,0:T(8,128)} %get-tuple-element.140.own, bf16[1024,96]{1,0:T(8,128)(2,1)} %copy-done.8, bf16[1024,512]{1,0:T(8,128)(2,1)} %get-tuple-element.38.low.refs_6_, ...), custom_call_target="tpu_custom_call" | custom-call | tf_op jit(solution)/shard_map/forward/pallas_call | solution.py:205
  154.5 5.5 %project.1 = bf16[4,256,1024]{2,1,0:T(8,128)(2,1)} custom-call(s32[4]{0:T(128)} %and_select_fusion.1.slot, bf16[1024,512]{1,0:T(8,128)(2,1)} %get-tuple-element.40.mixed, bf16[512,1024]{1,0:T(8,128)(2,1)} %all-gather.6.cloned.1.call-done.out_w), custom_call_target="tpu_custom_call" | custom-call | tf_op jit(solution)/shard_map/project/pallas_call | solution.py:507
  159.9 2.6 slice_bitcast_fusion.2
  162.5 7.0 %gate_back.1 = (f32[1024,512]{1,0:T(8,128)}, bf16[1024,512]{1,0:T(8,128)(2,1)}, f32[1,512]{1,0:T(1,128)}) custom-call(s32[1]{0:T(128)S(6)} %copy.166.length, bf16[1024,1024]{1,0:T(8,128)(2,1)} %bitcast.124, bf16[512,1024]{1,0:T(8,128)(2,1)} %all-gather.6.cloned.1.call-done.out_w, f32[1024,512]{1,0:T(8,128)} %get-tuple-element.39.gate, ...), custom_call_target="tpu_custom_call" | custom-call | tf_op jit(solution)/shard_map/gate_back/pallas_call | solution.py:256
  169.5 48.7 %backward.1 = (f32[1024,96]{1,0:T(8,128)}, f32[1024,512]{1,0:T(8,128)}, f32[16,512]{1,0:T(8,128)}, f32[96,512]{1,0:T(8,128)}, f32[1,512]{1,0:T(1,128)}) custom-call(s32[1]{0:T(128)S(6)} %copy.166.length, f32[1024,96]{1,0:T(8,128)} %get-tuple-element.140.own, bf16[1024,96]{1,0:T(8,128)(2,1)} %copy-done.8, bf16[1024,512]{1,0:T(8,128)(2,1)} %get-tuple-element.38.low.refs_6_, ...), custom_call_target="tpu_custom_call" | custom-call | tf_op jit(solution)/shard_map/backward/pallas_call | solution.py:374
  218.2 1.8 convert_element_type.171
  219.9 5.2 %collective-permute-start.24 = (bf16[1024,96]{1,0:T(8,128)(2,1)}, bf16[1024,96]{1,0:T(8,128)(2,1)}, u32[]{:S(2)}, u32[]{:S(2)}) collective-permute-start(bf16[1024,96]{1,0:T(8,128)(2,1)} %convert_element_type.171), channel_id=1, source_target_pairs={{0,1},{1,0},{2,3},{3,2},{4,5},{5,4},{6,7},{7,6},{8,9},{9,8},{10,11... | collective-permute-start | bytes 589832 | tf_op jit(solution)/shard_map/ppermute | solution.py:525
  226.3 2.7 convolution_convert_fusion.1
  232.4 2.2 constant_dynamic-slice_fusion.1
  235.8 1.8 fusion.28
  237.6 2.7 collective-permute-start.25
  240.3 7.6 %collective-permute-done.25.refs_1_ = bf16[1024,96]{1,0:T(8,128)(2,1)S(1)} collective-permute-done((bf16[1024,96]{1,0:T(8,128)(2,1)S(1)}, bf16[1024,96]{1,0:T(8,128)(2,1)S(1)}, u32[]{:S(2)}, u32[]{:S(2)}) %collective-permute-start.25) | collective-permute-done | bytes 196640 | tf_op jit(solution)/shard_map/ppermute | solution.py:525
  248.7 13.3 %back.1 = (bf16[4,256,1024]{2,1,0:T(8,128)(2,1)}, bf16[1024,512]{1,0:T(8,128)(2,1)}, f32[96,512]{1,0:T(8,128)}, f32[4,512]{1,0:T(4,128)}, f32[1,512]{1,0:T(1,128)}, /*index=5*/f32[1,1024]{1,0:T(1,128)}) custom-call(s32[4]{0:T(128)} %and_select_fusion.1.slot, s32[4]{0:T(128)} %and_select_fusion.order, f32[1024,96]{1,0:T(8,128)} %get-tuple-element.138.refs_0_, ...), custom_call_target="tpu_custom_call" | custom-call | tf_op jit(solution)/shard_map/back/pallas_call | solution.py:470
  262.0 2.6 slice_bitcast_fusion.6
  264.6 2.7 collective-permute-start.28
  272.9 1.5 collective-permute-start.36
  276.5 1.3 bitcast_add_fusion
  277.9 2.4 collective-permute-done.36
  280.2 1.5 collective-permute-start.40
  284.7 1.5 collective-permute-done.40
  286.2 3.7 collective-permute-start.23
  289.9 1.6 collective-permute-start.27
  291.5 1.7 collective-permute-start.26
  294.1 2.7 collective-permute-start.21
  296.8 60.9 %collective-permute-done.27 = bf16[256,1024]{1,0:T(8,128)(2,1)S(1)} collective-permute-done((bf16[256,1024]{1,0:T(8,128)(2,1)S(1)}, bf16[256,1024]{1,0:T(8,128)(2,1)S(1)}, u32[]{:S(2)}, u32[]{:S(2)}) %collective-permute-start.27) | collective-permute-done | bytes 524320 | tf_op jit(solution)/shard_map/ppermute | solution.py:686
  357.8 1.6 collective-permute-start.32
  361.8 4.6 %collective-permute-done.22 = bf16[256,1024]{1,0:T(8,128)(2,1)S(1)} collective-permute-done((bf16[256,1024]{1,0:T(8,128)(2,1)S(1)}, bf16[256,1024]{1,0:T(8,128)(2,1)S(1)}, u32[]{:S(2)}, u32[]{:S(2)}) %collective-permute-start.22) | collective-permute-done | bytes 524320 | tf_op jit(solution)/shard_map/ppermute | solution.py:686
  366.4 3.5 fusion.6
  370.7 1.4 slice_bitcast_fusion.10
  377.0 10.7 %psum.7 = f32[128]{0:T(128)} all-reduce(f32[128]{0:T(128)S(1)} %reshape.183), channel_id=1, replica_groups=mesh['fsdp'=8,'tp'=4] {'tp'}, use_global_device_ids=true, to_apply=%region_3.4 | all-reduce | flops 128 | bytes 1024 | tf_op jit(solution)/shard_map/psum | solution.py:658
  387.7 1.6 slice_reduce_fusion
  (231 shorter events, 53.7 us)
Async XLA Ops:
  7.3 147.2 %all-gather.6.cloned.1.call-start = ((), (), s32[]{:S(2)}) async-start(), calls=%async_computation.1 | async-start | bytes 1179648 | tf_op jit(solution)/shard_map/all_gather | solution.py:618
  8.0 154.5 %all-gather.8.cloned.1.call-start = ((), (), s32[]{:S(2)}) async-start(), calls=%async_computation.3 | async-start | bytes 2621440 | tf_op jit(solution)/shard_map/all_gather | solution.py:619
  9.1 25.9 %collective-permute-start.4 = (bf16[128,1024]{1,0:T(8,128)(2,1)S(1)}, bf16[128,1024]{1,0:T(8,128)(2,1)S(1)}, u32[]{:S(2)}, u32[]{:S(2)}) collective-permute-start(bf16[128,1024]{1,0:T(8,128)(2,1)S(1)} %get-tuple-element.161), channel_id=1, source_target_pairs={{0,1},{1,2},{2,3},{4,5},{5,6},{6,7},{8,9},{9,10},{10,11},{12,13},{... | collective-permute-start | bytes 786440 | tf_op jit(solution)/shard_map/ppermute | solution.py:537
  14.1 22.4 %collective-permute-start.5 = (bf16[128,1024]{1,0:T(8,128)(2,1)S(1)}, bf16[128,1024]{1,0:T(8,128)(2,1)S(1)}, u32[]{:S(2)}, u32[]{:S(2)}) collective-permute-start(bf16[128,1024]{1,0:T(8,128)(2,1)S(1)} %get-tuple-element.161), channel_id=1, source_target_pairs={{3,2},{2,1},{1,0},{7,6},{6,5},{5,4},{11,10},{10,9},{9,8},{15,14},{... | collective-permute-start | bytes 786440 | tf_op jit(solution)/shard_map/ppermute | solution.py:538
  15.4 22.9 %collective-permute-start = (bf16[128,1024]{1,0:T(8,128)(2,1)S(1)}, bf16[128,1024]{1,0:T(8,128)(2,1)S(1)}, u32[]{:S(2)}, u32[]{:S(2)}) collective-permute-start(bf16[128,1024]{1,0:T(8,128)(2,1)S(1)} %get-tuple-element.160), channel_id=1, source_target_pairs={{0,1},{1,2},{2,3},{4,5},{5,6},{6,7},{8,9},{9,10},{10,11},{12,13},{... | collective-permute-start | bytes 786440 | tf_op jit(solution)/shard_map/ppermute | solution.py:537
  19.9 19.7 %collective-permute-start.1 = (bf16[128,1024]{1,0:T(8,128)(2,1)S(1)}, bf16[128,1024]{1,0:T(8,128)(2,1)S(1)}, u32[]{:S(2)}, u32[]{:S(2)}) collective-permute-start(bf16[128,1024]{1,0:T(8,128)(2,1)S(1)} %get-tuple-element.160), channel_id=1, source_target_pairs={{3,2},{2,1},{1,0},{7,6},{6,5},{5,4},{11,10},{10,9},{9,8},{15,14},{... | collective-permute-start | bytes 786440 | tf_op jit(solution)/shard_map/ppermute | solution.py:538
  22.2 50.6 %copy-start.9 = (bf16[16,8,2,512]{3,1,2,0:T(8,128)(2,1)}, bf16[16,8,2,512]{3,1,2,0:T(8,128)(2,1)S(1)}, u32[]{:S(2)}) copy-start(bf16[16,8,2,512]{3,1,2,0:T(8,128)(2,1)S(1)} %copy.162) | copy-start | bytes 786436
  22.2 50.5 %collective-permute-start.13 = (bf16[128,1024]{1,0:T(8,128)(2,1)S(1)}, bf16[128,1024]{1,0:T(8,128)(2,1)S(1)}, u32[]{:S(2)}, u32[]{:S(2)}) collective-permute-start(bf16[128,1024]{1,0:T(8,128)(2,1)S(1)} %bitcast.125), channel_id=1, source_target_pairs={{0,8},{4,12},{8,0},{12,4},{16,24},{20,28},{24,16},{28,20},{1,9},{5... | collective-permute-start | bytes 786440 | tf_op jit(solution)/shard_map/ppermute | solution.py:525
  23.8 346.1 %reduce-scatter.2.cloned.1.call-start = ((), (), s32[]{:S(2)}) async-start(), calls=%async_computation.2 | async-start | bytes 589824 | tf_op jit(solution)/shard_map/reduce_scatter | solution.py:657
  35.0 9.6 %collective-permute-start.9 = (bf16[128,1024]{1,0:T(8,128)(2,1)S(1)}, bf16[128,1024]{1,0:T(8,128)(2,1)}, u32[]{:S(2)}, u32[]{:S(2)}) collective-permute-start(bf16[128,1024]{1,0:T(8,128)(2,1)S(1)} %collective-permute-done.4), channel_id=1, source_target_pairs={{1,2},{2,3},{5,6},{6,7},{9,10},{10,11},{13,14},{14,15},{17,18},{18... | collective-permute-start | bytes 786440 | tf_op jit(solution)/shard_map/ppermute | solution.py:537
  36.4 17.0 %collective-permute-start.6 = (bf16[128,1024]{1,0:T(8,128)(2,1)S(1)}, bf16[128,1024]{1,0:T(8,128)(2,1)S(1)}, u32[]{:S(2)}, u32[]{:S(2)}) collective-permute-start(bf16[128,1024]{1,0:T(8,128)(2,1)S(1)} %collective-permute-done.5), channel_id=1, source_target_pairs={{2,1},{1,0},{6,5},{5,4},{10,9},{9,8},{14,13},{13,12},{18,17},{17,1... | collective-permute-start | bytes 786440 | tf_op jit(solution)/shard_map/ppermute | solution.py:538
  38.3 15.2 %collective-permute-start.8 = (bf16[128,1024]{1,0:T(8,128)(2,1)S(1)}, bf16[128,1024]{1,0:T(8,128)(2,1)}, u32[]{:S(2)}, u32[]{:S(2)}) collective-permute-start(bf16[128,1024]{1,0:T(8,128)(2,1)S(1)} %collective-permute-done), channel_id=1, source_target_pairs={{1,2},{2,3},{5,6},{6,7},{9,10},{10,11},{13,14},{14,15},{17,18},{18... | collective-permute-start | bytes 786440 | tf_op jit(solution)/shard_map/ppermute | solution.py:537
  39.7 28.5 %collective-permute-start.2 = (bf16[128,1024]{1,0:T(8,128)(2,1)S(1)}, bf16[128,1024]{1,0:T(8,128)(2,1)}, u32[]{:S(2)}, u32[]{:S(2)}) collective-permute-start(bf16[128,1024]{1,0:T(8,128)(2,1)S(1)} %collective-permute-done.1), channel_id=1, source_target_pairs={{2,1},{1,0},{6,5},{5,4},{10,9},{9,8},{14,13},{13,12},{18,17},{17,1... | collective-permute-start | bytes 786440 | tf_op jit(solution)/shard_map/ppermute | solution.py:538
  44.7 28.2 %collective-permute-start.15 = (bf16[128,1024]{1,0:T(8,128)(2,1)S(1)}, bf16[128,1024]{1,0:T(8,128)(2,1)S(1)}, u32[]{:S(2)}, u32[]{:S(2)}) collective-permute-start(bf16[128,1024]{1,0:T(8,128)(2,1)S(1)} %bitcast.126), channel_id=1, source_target_pairs={{0,16},{4,20},{8,24},{12,28},{16,0},{20,4},{24,8},{28,12},{1,17},{... | collective-permute-start | bytes 786440 | tf_op jit(solution)/shard_map/ppermute | solution.py:525
  53.5 19.9 %collective-permute-start.17 = (bf16[128,1024]{1,0:T(8,128)(2,1)S(1)}, bf16[128,1024]{1,0:T(8,128)(2,1)S(1)}, u32[]{:S(2)}, u32[]{:S(2)}) collective-permute-start(bf16[128,1024]{1,0:T(8,128)(2,1)S(1)} %bitcast.127), channel_id=1, source_target_pairs={{0,24},{4,28},{8,16},{12,20},{16,8},{20,12},{24,0},{28,4},{1,25},{... | collective-permute-start | bytes 786440 | tf_op jit(solution)/shard_map/ppermute | solution.py:525
  53.5 16.3 %collective-permute-start.11 = (bf16[128,1024]{1,0:T(8,128)(2,1)}, bf16[128,1024]{1,0:T(8,128)(2,1)S(1)}, u32[]{:S(2)}, u32[]{:S(2)}) collective-permute-start(bf16[128,1024]{1,0:T(8,128)(2,1)} %collective-permute-done.9), channel_id=1, source_target_pairs={{2,3},{6,7},{10,11},{14,15},{18,19},{22,23},{26,27},{30,31}} | collective-permute-start | bytes 786440 | tf_op jit(solution)/shard_map/ppermute | solution.py:537
  68.1 3.1 collective-permute-start.10
  69.9 26.4 %collective-permute-start.7 = (bf16[128,1024]{1,0:T(8,128)(2,1)S(1)}, bf16[128,1024]{1,0:T(8,128)(2,1)S(1)}, u32[]{:S(2)}, u32[]{:S(2)}) collective-permute-start(bf16[128,1024]{1,0:T(8,128)(2,1)S(1)} %collective-permute-done.6), channel_id=1, source_target_pairs={{1,0},{5,4},{9,8},{13,12},{17,16},{21,20},{25,24},{29,28}} | collective-permute-start | bytes 786440 | tf_op jit(solution)/shard_map/ppermute | solution.py:538
  71.2 29.8 %collective-permute-start.3 = (bf16[128,1024]{1,0:T(8,128)(2,1)}, bf16[128,1024]{1,0:T(8,128)(2,1)S(1)}, u32[]{:S(2)}, u32[]{:S(2)}) collective-permute-start(bf16[128,1024]{1,0:T(8,128)(2,1)} %collective-permute-done.2), channel_id=1, source_target_pairs={{1,0},{5,4},{9,8},{13,12},{17,16},{21,20},{25,24},{29,28}} | collective-permute-start | bytes 786440 | tf_op jit(solution)/shard_map/ppermute | solution.py:538
  72.8 29.9 %collective-permute-start.12 = (bf16[128,1024]{1,0:T(8,128)(2,1)S(1)}, bf16[128,1024]{1,0:T(8,128)(2,1)S(1)}, u32[]{:S(2)}, u32[]{:S(2)}) collective-permute-start(bf16[128,1024]{1,0:T(8,128)(2,1)S(1)} %bitcast.128), channel_id=1, source_target_pairs={{0,4},{4,0},{8,12},{12,8},{16,20},{20,16},{24,28},{28,24},{1,5},{5... | collective-permute-start | bytes 786440 | tf_op jit(solution)/shard_map/ppermute | solution.py:525
  72.9 29.8 %collective-permute-start.14 = (bf16[128,1024]{1,0:T(8,128)(2,1)S(1)}, bf16[128,1024]{1,0:T(8,128)(2,1)S(1)}, u32[]{:S(2)}, u32[]{:S(2)}) collective-permute-start(bf16[128,1024]{1,0:T(8,128)(2,1)S(1)} %collective-permute-done.13.refs_2_), channel_id=1, source_target_pairs={{0,4},{4,0},{8,12},{12,8},{16,20},{20,16},{24,28},{28,24},{1,5},{5... | collective-permute-start | bytes 786440 | tf_op jit(solution)/shard_map/ppermute | solution.py:525
  73.4 29.4 %collective-permute-start.16 = (bf16[128,1024]{1,0:T(8,128)(2,1)S(1)}, bf16[128,1024]{1,0:T(8,128)(2,1)S(1)}, u32[]{:S(2)}, u32[]{:S(2)}) collective-permute-start(bf16[128,1024]{1,0:T(8,128)(2,1)S(1)} %collective-permute-done.15.refs_4_), channel_id=1, source_target_pairs={{0,4},{4,0},{8,12},{12,8},{16,20},{20,16},{24,28},{28,24},{1,5},{5... | collective-permute-start | bytes 786440 | tf_op jit(solution)/shard_map/ppermute | solution.py:525
  96.2 6.6 %collective-permute-start.18 = (bf16[128,1024]{1,0:T(8,128)(2,1)S(1)}, bf16[128,1024]{1,0:T(8,128)(2,1)S(1)}, u32[]{:S(2)}, u32[]{:S(2)}) collective-permute-start(bf16[128,1024]{1,0:T(8,128)(2,1)S(1)} %collective-permute-done.17.refs_6_), channel_id=1, source_target_pairs={{0,4},{4,0},{8,12},{12,8},{16,20},{20,16},{24,28},{28,24},{1,5},{5... | collective-permute-start | bytes 786440 | tf_op jit(solution)/shard_map/ppermute | solution.py:525
  114.5 7.6 %collective-permute-start.19 = (bf16[1024,96]{1,0:T(8,128)(2,1)S(1)}, bf16[1024,96]{1,0:T(8,128)(2,1)S(1)}, u32[]{:S(2)}, u32[]{:S(2)}) collective-permute-start(bf16[1024,96]{1,0:T(8,128)(2,1)S(1)} %convert_element_type.155), channel_id=1, source_target_pairs={{0,1},{1,0},{2,3},{3,2},{4,5},{5,4},{6,7},{7,6},{8,9},{9,8},{10,11... | collective-permute-start | bytes 589832 | tf_op jit(solution)/shard_map/ppermute | solution.py:525
  122.9 8.6 %collective-permute-start.20 = (bf16[1024,96]{1,0:T(8,128)(2,1)S(1)}, bf16[1024,96]{1,0:T(8,128)(2,1)S(1)}, u32[]{:S(2)}, u32[]{:S(2)}) collective-permute-start(bf16[1024,96]{1,0:T(8,128)(2,1)S(1)} %get-tuple-element.139), channel_id=1, source_target_pairs={{0,3},{1,2},{2,1},{3,0},{4,7},{5,6},{6,5},{7,4},{8,11},{9,10},{10,... | collective-permute-start | bytes 589832 | tf_op jit(solution)/shard_map/ppermute | solution.py:525
  169.5 56.8 %copy-start.4 = (bf16[1024,1024]{1,0:T(8,128)(2,1)S(1)}, bf16[1024,1024]{1,0:T(8,128)(2,1)}, u32[]{:S(2)}) copy-start(bf16[1024,1024]{1,0:T(8,128)(2,1)} %get-tuple-element.50.refs_9_) | copy-start | bytes 6291460
  219.9 15.9 %collective-permute-start.24 = (bf16[1024,96]{1,0:T(8,128)(2,1)}, bf16[1024,96]{1,0:T(8,128)(2,1)}, u32[]{:S(2)}, u32[]{:S(2)}) collective-permute-start(bf16[1024,96]{1,0:T(8,128)(2,1)} %convert_element_type.171), channel_id=1, source_target_pairs={{0,1},{1,0},{2,3},{3,2},{4,5},{5,4},{6,7},{7,6},{8,9},{9,8},{10,11... | collective-permute-start | bytes 589832 | tf_op jit(solution)/shard_map/ppermute | solution.py:525
  229.9 41.6 %collective-permute-start.33 = (bf16[4,128,512]{2,1,0:T(8,128)(2,1)}, bf16[4,128,512]{2,1,0:T(8,128)(2,1)}, u32[]{:S(2)}, u32[]{:S(2)}) collective-permute-start(bf16[4,128,512]{2,1,0:T(8,128)(2,1)} %dynamic-slice_bitcast_fusion), channel_id=1, source_target_pairs={{0,4},{4,0},{8,12},{12,8},{16,20},{20,16},{24,28},{28,24},{1,5},{5... | collective-permute-start | bytes 1572872 | tf_op jit(solution)/shard_map/ppermute | solution.py:525
  235.5 40.0 %collective-permute-start.37 = (bf16[4,128,512]{1,2,0:T(8,128)(2,1)}, bf16[4,128,512]{1,2,0:T(8,128)(2,1)}, u32[]{:S(2)}, u32[]{:S(2)}) collective-permute-start(bf16[4,128,512]{1,2,0:T(8,128)(2,1)} %bitcast.123), channel_id=1, source_target_pairs={{0,4},{4,0},{8,12},{12,8},{16,20},{20,16},{24,28},{28,24},{1,5},{5... | collective-permute-start | bytes 1572872 | tf_op jit(solution)/shard_map/ppermute | solution.py:525
  237.6 10.3 %collective-permute-start.25 = (bf16[1024,96]{1,0:T(8,128)(2,1)S(1)}, bf16[1024,96]{1,0:T(8,128)(2,1)S(1)}, u32[]{:S(2)}, u32[]{:S(2)}) collective-permute-start(bf16[1024,96]{1,0:T(8,128)(2,1)S(1)} %get-tuple-element.137), channel_id=1, source_target_pairs={{0,3},{1,2},{2,1},{3,0},{4,7},{5,6},{6,5},{7,4},{8,11},{9,10},{10,... | collective-permute-start | bytes 589832 | tf_op jit(solution)/shard_map/ppermute | solution.py:525
  264.6 29.5 %collective-permute-start.28 = (bf16[256,1024]{1,0:T(8,128)(2,1)}, bf16[256,1024]{1,0:T(8,128)(2,1)S(1)}, u32[]{:S(2)}, u32[]{:S(2)}) collective-permute-start(bf16[256,1024]{1,0:T(8,128)(2,1)} %get-tuple-element.142), channel_id=1, source_target_pairs={{0,3},{1,0},{2,1},{3,2},{4,7},{5,4},{6,5},{7,6},{8,11},{9,8},{10,9... | collective-permute-start | bytes 1572872 | tf_op jit(solution)/shard_map/ppermute | solution.py:686
  271.5 22.5 %collective-permute-start.29 = (bf16[4,128,512]{2,1,0:T(8,128)(2,1)S(1)}, bf16[4,128,512]{2,1,0:T(8,128)(2,1)S(1)}, u32[]{:S(2)}, u32[]{:S(2)}) collective-permute-start(bf16[4,128,512]{2,1,0:T(8,128)(2,1)S(1)} %dynamic-slice_bitcast_fusion.1), channel_id=1, source_target_pairs={{0,4},{4,0},{8,12},{12,8},{16,20},{20,16},{24,28},{28,24},{1,5},{5... | collective-permute-start | bytes 1572872 | tf_op jit(solution)/shard_map/ppermute | solution.py:525
  272.9 7.3 %collective-permute-start.36 = (bf16[128,512]{1,0:T(8,128)(2,1)S(1)}, bf16[128,512]{1,0:T(8,128)(2,1)S(1)}, u32[]{:S(2)}, u32[]{:S(2)}) collective-permute-start(bf16[128,512]{1,0:T(8,128)(2,1)S(1)} %get-tuple-element.156), channel_id=1, source_target_pairs={{0,24},{4,28},{8,16},{12,20},{16,8},{20,12},{24,0},{28,4},{1,25},{... | collective-permute-start | bytes 393224 | tf_op jit(solution)/shard_map/ppermute | solution.py:525
  274.5 8.1 %collective-permute-start.35 = (bf16[128,512]{1,0:T(8,128)(2,1)S(1)}, bf16[128,512]{1,0:T(8,128)(2,1)S(1)}, u32[]{:S(2)}, u32[]{:S(2)}) collective-permute-start(bf16[128,512]{1,0:T(8,128)(2,1)S(1)} %get-tuple-element.157), channel_id=1, source_target_pairs={{0,16},{4,20},{8,24},{12,28},{16,0},{20,4},{24,8},{28,12},{1,17},{... | collective-permute-start | bytes 393224 | tf_op jit(solution)/shard_map/ppermute | solution.py:525
  275.5 8.1 %collective-permute-start.34 = (bf16[128,512]{1,0:T(8,128)(2,1)S(1)}, bf16[128,512]{1,0:T(8,128)(2,1)S(1)}, u32[]{:S(2)}, u32[]{:S(2)}) collective-permute-start(bf16[128,512]{1,0:T(8,128)(2,1)S(1)} %get-tuple-element.155), channel_id=1, source_target_pairs={{0,8},{4,12},{8,0},{12,4},{16,24},{20,28},{24,16},{28,20},{1,9},{5... | collective-permute-start | bytes 393224 | tf_op jit(solution)/shard_map/ppermute | solution.py:525
  277.8 82.5 %copy-start.3 = (bf16[4,256,1024]{2,1,0:T(8,128)(2,1)S(1)}, bf16[4,256,1024]{2,1,0:T(8,128)(2,1)}, u32[]{:S(2)}) copy-start(bf16[4,256,1024]{2,1,0:T(8,128)(2,1)} %get-tuple-element.52) | copy-start | bytes 6291460
  280.2 6.0 %collective-permute-start.40 = (bf16[128,512]{0,1:T(8,128)(2,1)S(1)}, bf16[128,512]{0,1:T(8,128)(2,1)S(1)}, u32[]{:S(2)}, u32[]{:S(2)}) collective-permute-start(bf16[128,512]{0,1:T(8,128)(2,1)S(1)} %get-tuple-element.150), channel_id=1, source_target_pairs={{0,24},{4,28},{8,16},{12,20},{16,8},{20,12},{24,0},{28,4},{1,25},{... | collective-permute-start | bytes 393224 | tf_op jit(solution)/shard_map/ppermute | solution.py:525
  282.6 7.3 %collective-permute-start.39 = (bf16[128,512]{0,1:T(8,128)(2,1)S(1)}, bf16[128,512]{0,1:T(8,128)(2,1)S(1)}, u32[]{:S(2)}, u32[]{:S(2)}) collective-permute-start(bf16[128,512]{0,1:T(8,128)(2,1)S(1)} %get-tuple-element.151), channel_id=1, source_target_pairs={{0,16},{4,20},{8,24},{12,28},{16,0},{20,4},{24,8},{28,12},{1,17},{... | collective-permute-start | bytes 393224 | tf_op jit(solution)/shard_map/ppermute | solution.py:525
  283.7 7.8 %collective-permute-start.38 = (bf16[128,512]{0,1:T(8,128)(2,1)S(1)}, bf16[128,512]{0,1:T(8,128)(2,1)S(1)}, u32[]{:S(2)}, u32[]{:S(2)}) collective-permute-start(bf16[128,512]{0,1:T(8,128)(2,1)S(1)} %get-tuple-element.149), channel_id=1, source_target_pairs={{0,8},{4,12},{8,0},{12,4},{16,24},{20,28},{24,16},{28,20},{1,9},{5... | collective-permute-start | bytes 393224 | tf_op jit(solution)/shard_map/ppermute | solution.py:525
  286.2 74.6 %collective-permute-start.23 = (bf16[256,1024]{1,0:T(8,128)(2,1)S(1)}, bf16[256,1024]{1,0:T(8,128)(2,1)S(1)}, u32[]{:S(2)}, u32[]{:S(2)}) collective-permute-start(bf16[256,1024]{1,0:T(8,128)(2,1)S(1)} %copy-done.14), channel_id=1, source_target_pairs={{0,3},{1,0},{2,1},{3,2},{4,7},{5,4},{6,5},{7,6},{8,11},{9,8},{10,9... | collective-permute-start | bytes 1572872 | tf_op jit(solution)/shard_map/ppermute | solution.py:686
  289.9 67.9 %collective-permute-start.27 = (bf16[256,1024]{1,0:T(8,128)(2,1)S(1)}, bf16[256,1024]{1,0:T(8,128)(2,1)S(1)}, u32[]{:S(2)}, u32[]{:S(2)}) collective-permute-start(bf16[256,1024]{1,0:T(8,128)(2,1)S(1)} %copy-done.16), channel_id=1, source_target_pairs={{0,2},{1,3},{2,0},{3,1},{4,6},{5,7},{6,4},{7,5},{8,10},{9,11},{10,... | collective-permute-start | bytes 1572872 | tf_op jit(solution)/shard_map/ppermute | solution.py:686
  291.5 67.9 %collective-permute-start.26 = (bf16[256,1024]{1,0:T(8,128)(2,1)S(1)}, bf16[256,1024]{1,0:T(8,128)(2,1)S(1)}, u32[]{:S(2)}, u32[]{:S(2)}) collective-permute-start(bf16[256,1024]{1,0:T(8,128)(2,1)S(1)} %copy-done.15), channel_id=1, source_target_pairs={{0,1},{1,2},{2,3},{3,0},{4,5},{5,6},{6,7},{7,4},{8,9},{9,10},{10,1... | collective-permute-start | bytes 1572872 | tf_op jit(solution)/shard_map/ppermute | solution.py:686
  294.0 72.5 %collective-permute-start.22 = (bf16[256,1024]{1,0:T(8,128)(2,1)S(1)}, bf16[256,1024]{1,0:T(8,128)(2,1)S(1)}, u32[]{:S(2)}, u32[]{:S(2)}) collective-permute-start(bf16[256,1024]{1,0:T(8,128)(2,1)S(1)} %copy-done.13), channel_id=1, source_target_pairs={{0,2},{1,3},{2,0},{3,1},{4,6},{5,7},{6,4},{7,5},{8,10},{9,11},{10,... | collective-permute-start | bytes 1572872 | tf_op jit(solution)/shard_map/ppermute | solution.py:686
  294.1 72.3 %copy-start.7 = (bf16[1,256,1024]{2,1,0:T(8,128)(2,1)S(1)}, bf16[1,256,1024]{2,1,0:T(8,128)(2,1)}, u32[]{:S(2)}) copy-start(bf16[1,256,1024]{2,1,0:T(8,128)(2,1)} %param.25) | copy-start | bytes 1572868
  294.1 72.3 %collective-permute-start.21 = (bf16[256,1024]{1,0:T(8,128)(2,1)S(1)}, bf16[256,1024]{1,0:T(8,128)(2,1)S(1)}, u32[]{:S(2)}, u32[]{:S(2)}) collective-permute-start(bf16[256,1024]{1,0:T(8,128)(2,1)S(1)} %copy-done.12), channel_id=1, source_target_pairs={{0,1},{1,2},{2,3},{3,0},{4,5},{5,6},{6,7},{7,4},{8,9},{9,10},{10,1... | collective-permute-start | bytes 1572872 | tf_op jit(solution)/shard_map/ppermute | solution.py:686
  357.8 31.5 %collective-permute-start.32 = (bf16[128,512]{1,0:T(8,128)(2,1)S(1)}, bf16[128,512]{1,0:T(8,128)(2,1)S(1)}, u32[]{:S(2)}, u32[]{:S(2)}) collective-permute-start(bf16[128,512]{1,0:T(8,128)(2,1)S(1)} %get-tuple-element.153), channel_id=1, source_target_pairs={{0,24},{4,28},{8,16},{12,20},{16,8},{20,12},{24,0},{28,4},{1,25},{... | collective-permute-start | bytes 393224 | tf_op jit(solution)/shard_map/ppermute | solution.py:525
  359.4 29.9 %collective-permute-start.31 = (bf16[128,512]{1,0:T(8,128)(2,1)S(1)}, bf16[128,512]{1,0:T(8,128)(2,1)S(1)}, u32[]{:S(2)}, u32[]{:S(2)}) collective-permute-start(bf16[128,512]{1,0:T(8,128)(2,1)S(1)} %get-tuple-element.154), channel_id=1, source_target_pairs={{0,16},{4,20},{8,24},{12,28},{16,0},{20,4},{24,8},{28,12},{1,17},{... | collective-permute-start | bytes 393224 | tf_op jit(solution)/shard_map/ppermute | solution.py:525
  360.8 28.5 %collective-permute-start.30 = (bf16[128,512]{1,0:T(8,128)(2,1)S(1)}, bf16[128,512]{1,0:T(8,128)(2,1)S(1)}, u32[]{:S(2)}, u32[]{:S(2)}) collective-permute-start(bf16[128,512]{1,0:T(8,128)(2,1)S(1)} %get-tuple-element.152), channel_id=1, source_target_pairs={{0,8},{4,12},{8,0},{12,4},{16,24},{20,28},{24,16},{28,20},{1,9},{5... | collective-permute-start | bytes 393224 | tf_op jit(solution)/shard_map/ppermute | solution.py:525
  (36 other events, 412.9 us)
Sparse Core Ops, SparseCore 0:
  10.0 26.6 all-gather.5
  38.3 53.6 all-gather.7
  270.5 34.4 reduce-scatter.1

commit v3 on v2

v3 whole, which is shorter than its diff:
```python
import functools

import jax
import jax.numpy as jnp
from jax import lax
from jax.experimental import pallas as pl
from jax.experimental.pallas import tpu as pltpu
from jax.sharding import PartitionSpec as P

bf16 = jnp.bfloat16
f32 = jnp.float32
LOG2E = 1.4426950408889634
LN2 = 0.6931471805599453
ROWS = 128
STEPS = 16
LANES = 128
NT = (((1,), (1,)), ((), ()))
TN = (((0,), (0,)), ((), ()))
epsilon = 1e-05
VMEM_LIMIT = 56 * 2**20


def dot(a, b, dims=(((1,), (0,)), ((), ()))):
    return lax.dot_general(a, b, dims, preferred_element_type=f32)


def shape(dims, kind):
    return jax.ShapeDtypeStruct(dims, kind)


def iota(dims, axis):
    return lax.broadcasted_iota(jnp.int32, dims, axis)


def params():
    return pltpu.CompilerParams(vmem_limit_bytes=VMEM_LIMIT)


def cost(micros):
    return pl.CostEstimate(
        flops=int(micros * 1e9), bytes_accessed=int(micros * 3e6), transcendentals=0
    )


def halves(values):
    high = values.astype(bf16)
    return high, (values - high.astype(f32)).astype(bf16)


def spread(columns):
    width, rows = columns.shape
    wide = STEPS * width
    pick = (iota((width, wide), 1) % width == iota((width, wide), 0)).astype(bf16)
    keep = iota((rows, wide), 1) // width == iota((rows, wide), 0) % STEPS
    return jnp.where(keep, dot(columns, pick, TN), 0.0).astype(bf16)


def to_lanes(target, columns):
    width, rows = columns.shape
    wide = STEPS * width
    parts = [spread(part) for part in halves(columns)]
    ones = jnp.ones((2 * STEPS, LANES), bf16)
    for index in range(rows // STEPS):
        s = slice(index * STEPS, (index + 1) * STEPS)
        both = jnp.concatenate([part[s] for part in parts], 0)
        target[index * wide : (index + 1) * wide, :] = dot(both, ones, TN)


def across(values, chans):
    return jnp.concatenate([values] * (chans // LANES), 1)


def row_of(ref, index, count):
    return ref[pl.ds(index, count, stride=0), :]


def twice(values):
    return jnp.concatenate([values, values], 0).astype(bf16)


def fold(values):
    return sum(values[:, i : i + LANES] for i in range(0, values.shape[1], LANES))


def lane_sums(values, width):
    rows = values.shape[0] // width
    sums = dot(values, jnp.ones((LANES, rows), bf16))
    lane = iota((width, rows), 1)
    kept = [jnp.zeros((width, rows), f32)] * 4
    for t in range(rows):
        kept[t % 4] = jnp.where(lane == t, sums[t * width : (t + 1) * width], kept[t % 4])
    return (kept[0] + kept[1]) + (kept[2] + kept[3])


def live_rows(length, first, rows):
    return (iota((rows, 1), 0) + first < length).astype(f32)


def full(array):
    return pl.BlockSpec(array.shape, lambda *_: (0,) * len(array.shape))


class Rows:
    def __init__(self, maps, width, taps):
        self.maps = maps
        self.width = width
        self.taps = taps
        self.rank = maps - 2 * width
        self.first = maps + width
        self.count = -(-(self.first + taps + 3) // 16) * 16

    def x_w(self, ref):
        return ref[: self.maps, :]

    def a_log(self, ref):
        return ref[self.maps : self.first, :].astype(f32)

    def rest(self, ref):
        return ref[self.first :, :].astype(f32)


def front_kernel(lay, shards, pieces, order, place, gain, small, *refs):
    token_refs = refs[:shards]
    piece_refs = refs[shards : shards + pieces]
    (
        normed_ref, w_ref, input_ref, gate_ref, sum_ref, low_ref, map_ref, send_ref, halo, tokens,
    ) = refs[shards + pieces :]
    rows = tokens.shape[0]
    chans = small.shape[1]
    taps = lay.taps
    turn = pl.program_id(0)

    @pl.when(turn == 0)
    def _():
        for index in range(pieces):
            depth = piece_refs[index].shape[0]
            start = pl.multiple_of(place[index] * depth, depth)
            w_ref[pl.ds(start, depth), :] = piece_refs[index][...]
        halo[:8] = jnp.zeros_like(halo[:8])

    for index in range(shards):

        @pl.when(order[turn] == index)
        def _(index=index):
            tokens[...] = token_refs[index][...].astype(f32)

    values = tokens[...]
    inverse = lax.rsqrt(jnp.mean(values * values, axis=-1, keepdims=True) + epsilon)
    normed = (values * inverse * gain[...]).astype(bf16)
    normed_ref[...] = normed
    projected = dot(normed, w_ref[...])
    conv_in = projected[:, :chans]
    input_ref[...] = conv_in
    gate_ref[...] = projected[:, chans:]
    halo[8:] = conv_in
    rest = lay.rest(small)
    total = rest[taps : taps + 1]
    for tap in range(taps):
        first = 8 - taps + 1 + tap
        total = total + rest[tap : tap + 1] * halo[first : first + rows]
    halo[:8] = conv_in[rows - 8 :]
    sum_ref[...] = total
    low = (total * jax.nn.sigmoid(total)).astype(bf16)
    low_ref[...] = low
    mapped = dot(lay.x_w(small), low, NT)
    map_ref[...] = mapped
    send_ref[...] = mapped.astype(bf16)


def front(lay, order, place, shards, gain, small, pieces):
    rows, depth = shards[0].shape
    total = len(shards) * rows
    chans = small.shape[1]
    row = lambda w: pl.BlockSpec((rows, w), lambda i, *_: (i, 0))
    column = lambda w: pl.BlockSpec((w, rows), lambda i, *_: (0, i))
    both = pieces[0].shape[1]
    return pl.pallas_call(
        functools.partial(front_kernel, lay, len(shards), len(pieces)),
        grid_spec=pltpu.PrefetchScalarGridSpec(
            num_scalar_prefetch=2,
            grid=(len(shards),),
            in_specs=[full(a) for a in (gain, small, *shards, *pieces)],
            out_specs=[
                row(depth),
                pl.BlockSpec((depth, both), lambda i, *_: (0, 0)),
                row(chans),
                row(chans),
                row(chans),
                row(chans),
                column(lay.maps),
                column(lay.maps),
            ],
            scratch_shapes=[pltpu.VMEM((rows + 8, chans), f32), pltpu.VMEM((rows, depth), f32)],
        ),
        out_shape=[
            shape((total, depth), bf16),
            shape((depth, both), bf16),
            shape((total, chans), f32),
            shape((total, chans), f32),
            shape((total, chans), f32),
            shape((total, chans), bf16),
            shape((lay.maps, total), f32),
            shape((lay.maps, total), bf16),
        ],
        compiler_params=params(),
        cost_estimate=cost(9),
        name="front",
    )(order, place, gain, small, *shards, *pieces)


def forward_kernel(
    lay, length, slot, own, got, low, gate, dt_w, small, out_w,
    mixed_ref, before_ref, step_ref, h_ref, sent_ref, state, drive, lanes, step_rows, drive_rows,
):
    rows, chans = low.shape
    width, rank, taps = lay.width, lay.rank, lay.taps
    half = width // 2
    wide = STEPS * width

    @pl.when(pl.program_id(0) == 0)
    def _():
        state[...] = jnp.zeros_like(state)

    live = live_rows(length[0], pl.program_id(0) * rows, rows)
    mapped = own[...] + got[...].astype(f32)
    rest = lay.rest(small)
    step_pre = dot(mapped[:rank].astype(bf16), dt_w[...], TN) + rest[taps + 1 : taps + 2]
    step = jax.nn.softplus(step_pre) * live
    step_ref[...] = step
    conv_out = low[...].astype(f32)
    drive[...] = step * conv_out
    to_lanes(lanes, mapped[rank : rank + width])
    rate = -jnp.exp(lay.a_log(small)) * LOG2E
    rate_0, rate_1 = rate[:half], rate[half:]

    def body(block, carried):
        h_0, h_1 = carried
        s = pl.ds(pl.multiple_of(block * STEPS, STEPS), STEPS)
        step_rows[...] = step_ref[s, :]
        drive_rows[...] = drive[s, :]
        for k in range(STEPS):
            steps = row_of(step_rows, k, half)
            drives = row_of(drive_rows, k, half)
            base = pl.multiple_of(block * wide, wide) + k * width
            b_0 = across(lanes[pl.ds(base, half), :], chans)
            b_1 = across(lanes[pl.ds(base + half, half), :], chans)
            h_0 = jnp.exp2(steps * rate_0) * h_0 + drives * b_0
            h_1 = jnp.exp2(steps * rate_1) * h_1 + drives * b_1
            h_ref[pl.ds(base, width), :] = jnp.concatenate([h_0, h_1], 0).astype(bf16)
        return h_0, h_1

    h_0, h_1 = lax.fori_loop(0, rows // STEPS, body, (state[:half], state[half:]))
    state[:half] = h_0
    state[half:] = h_1
    outs = spread(mapped[rank + width :].astype(bf16))
    scan = [
        dot(outs[i * STEPS : (i + 1) * STEPS], h_ref[i * wide : (i + 1) * wide, :])
        for i in range(rows // STEPS)
    ]
    before = jnp.concatenate(scan, 0) + rest[taps + 2 : taps + 3] * conv_out
    before_ref[...] = before
    gates = gate[...]
    mixed = (before * (gates * jax.nn.sigmoid(gates)) * live).astype(bf16)
    mixed_ref[...] = mixed
    sent_ref[0] = dot(mixed, out_w[...]).astype(bf16)


def forward(lay, length, slot, own, got, low, gate, dt_w, small, out_w):
    total, chans = low.shape
    count = slot.shape[0]
    part = total // count
    blocks = part // ROWS
    depth = out_w.shape[1]
    width = lay.width
    row = lambda w: pl.BlockSpec((ROWS, w), lambda i, *_: (i, 0))
    column = lambda w: pl.BlockSpec((w, ROWS), lambda i, *_: (0, i))
    return pl.pallas_call(
        functools.partial(forward_kernel, lay),
        grid_spec=pltpu.PrefetchScalarGridSpec(
            num_scalar_prefetch=2,
            grid=(total // ROWS,),
            in_specs=[column(lay.maps), column(lay.maps), row(chans), row(chans)]
            + [full(a) for a in (dt_w, small, out_w)],
            out_specs=[
                row(chans),
                row(chans),
                row(chans),
                pl.BlockSpec((ROWS * width, chans), lambda i, *_: (i, 0)),
                pl.BlockSpec((1, ROWS, depth), lambda i, n, s: (s[i // blocks], i % blocks, 0)),
            ],
            scratch_shapes=[
                pltpu.VMEM((width, chans), f32),
                pltpu.VMEM((ROWS, chans), f32),
                pltpu.VMEM((ROWS * width, LANES), f32),
                pltpu.VMEM((STEPS, chans), f32),
                pltpu.VMEM((STEPS, chans), f32),
            ],
        ),
        out_shape=[
            shape((total, chans), bf16),
            shape((total, chans), f32),
            shape((total, chans), f32),
            shape((total * width, chans), bf16),
            shape((count, part, depth), bf16),
        ],
        compiler_params=params(),
        cost_estimate=cost(24),
        name="forward",
    )(length, slot, own, got, low, gate, dt_w, small, out_w)


def backward_kernel(
    lay, length, own, got, low, gate, before_ref, step_ref, grad, h_ref, last_ref, dt_w, small, out_w,
    map_ref, send_ref, out_ref, gate_ref, rate_ref, dt_w_ref, bias_ref,
    carry, grads, terms, drive, scan_grad, lanes, cross_b, cross_c, step_rows, drive_rows, grad_rows,
):
    rows, chans = low.shape
    width, rank, taps = lay.width, lay.rank, lay.taps
    half = width // 2
    wide = STEPS * width
    turn = pl.program_id(0)
    turns = pl.num_programs(0)

    @pl.when(turn == 0)
    def _():
        for ref in (carry, rate_ref, dt_w_ref, bias_ref):
            ref[...] = jnp.zeros_like(ref)

    live = live_rows(length[0], (turns - 1 - turn) * rows, rows)
    rest = lay.rest(small)
    conv_out = low[...].astype(f32)
    masked = dot(grad[...], out_w[...], NT) * live
    gates = gate[...]
    sigma = jax.nn.sigmoid(gates)
    gate_ref[...] = (
        masked * before_ref[...] * (sigma * (1.0 + gates * (1.0 - sigma)))
    ).astype(bf16)
    out_scan = masked * (gates * sigma)
    scan_grad[...] = out_scan
    bias_ref[1:2] += jnp.sum(out_scan * conv_out, axis=0, keepdims=True)
    mapped = own[...] + got[...].astype(f32)
    to_lanes(lanes, mapped[rank + width :])
    drive[...] = step_ref[...] * conv_out
    rate = -jnp.exp(lay.a_log(small)) * LOG2E
    rate_0, rate_1 = rate[:half], rate[half:]
    rate_low = rate.astype(bf16)
    first = jnp.where(turn == turns - 1, jnp.zeros_like(last_ref[...]), last_ref[...])

    def body(back, carried):
        q_0, q_1, total, h = carried
        block = rows // STEPS - 1 - back
        s = pl.ds(pl.multiple_of(block * STEPS, STEPS), STEPS)
        step_rows[...] = step_ref[s, :]
        drive_rows[...] = drive[s, :]
        grad_rows[...] = scan_grad[s, :]
        part = jnp.zeros((width, chans), bf16)
        for k in reversed(range(STEPS)):
            steps = row_of(step_rows, k, half)
            drives = row_of(drive_rows, k, half)
            outs = row_of(grad_rows, k, half)
            base = pl.multiple_of(block * wide, wide) + k * width
            g_0 = outs * across(lanes[pl.ds(base, half), :], chans) + q_0
            g_1 = outs * across(lanes[pl.ds(base + half, half), :], chans) + q_1
            g = jnp.concatenate([g_0, g_1], 0).astype(bf16)
            grads[pl.ds(base, width), :] = g
            cross_b[pl.ds(base, width), :] = fold(g * twice(drives))
            cross_c[pl.ds(base, width), :] = fold(h * twice(outs))
            q_0 = jnp.exp2(steps * rate_0) * g_0
            q_1 = jnp.exp2(steps * rate_1) * g_1
            if k == 0:
                start = pl.multiple_of(jnp.maximum(base - width, 0), width)
                h = jnp.where(block == 0, first, h_ref[pl.ds(start, width), :])
            else:
                h = h_ref[pl.ds(base - width, width), :]
            term = jnp.concatenate([q_0, q_1], 0).astype(bf16) * h * rate_low
            terms[pl.ds(base, width), :] = term
            part = part + twice(steps) * term
        return q_0, q_1, total + part.astype(f32), h

    start = (carry[:half], carry[half:], rate_ref[...], h_ref[(rows - 1) * width :, :])
    q_0, q_1, total, _ = lax.fori_loop(0, rows // STEPS, body, start)
    carry[:half] = q_0
    carry[half:] = q_1
    rate_ref[...] = total
    ins = spread(mapped[rank : rank + width].astype(bf16))
    ones = (iota((STEPS, wide), 1) // width == iota((STEPS, wide), 0)).astype(bf16)
    weighted, stepped = [], []
    for i in range(rows // STEPS):
        big = slice(i * wide, (i + 1) * wide)
        weighted.append(dot(ins[i * STEPS : (i + 1) * STEPS], grads[big, :]))
        stepped.append(dot(ones, terms[big, :]))
    weighted = jnp.concatenate(weighted, 0)
    step_grad = jnp.concatenate(stepped, 0) * LN2 + conv_out * weighted
    map_low = mapped[:rank].astype(bf16)
    step_pre = dot(map_low, dt_w[...], TN) + rest[taps + 1 : taps + 2]
    pre_grad = (step_grad * live * jax.nn.sigmoid(step_pre)).astype(bf16)
    bias_ref[0:1] += jnp.sum(pre_grad.astype(f32), axis=0, keepdims=True)
    dt_w_ref[...] += dot(map_low, pre_grad)
    map_grad = jnp.concatenate(
        [dot(dt_w[...], pre_grad, NT), lane_sums(cross_b[...], width), lane_sums(cross_c[...], width)],
        0,
    )
    map_ref[...] = map_grad
    send_ref[...] = map_grad.astype(bf16)
    out_ref[...] = out_scan * rest[taps + 2 : taps + 3] + step_ref[...] * weighted


def backward(lay, length, own, got, low, gate, before, step, grad, h, dt_w, small, out_w):
    total, chans = low.shape
    width = lay.width
    turns = total // ROWS
    at = lambda i: turns - 1 - i
    row = lambda w: pl.BlockSpec((ROWS, w), lambda i, *_: (at(i), 0))
    column = lambda w: pl.BlockSpec((w, ROWS), lambda i, *_: (0, at(i)))
    outs = [
        shape((lay.maps, total), f32),
        shape((lay.maps, total), bf16),
        shape((total, chans), f32),
        shape((total, chans), bf16),
        shape((width, chans), f32),
        shape(dt_w.shape, f32),
        shape((8, chans), f32),
    ]
    return pl.pallas_call(
        functools.partial(backward_kernel, lay),
        grid_spec=pltpu.PrefetchScalarGridSpec(
            num_scalar_prefetch=1,
            grid=(turns,),
            in_specs=[
                column(lay.maps),
                column(lay.maps),
                row(chans),
                row(chans),
                row(chans),
                row(chans),
                row(grad.shape[1]),
                pl.BlockSpec((ROWS * width, chans), lambda i, *_: (at(i), 0)),
                pl.BlockSpec((width, chans), lambda i, *_: (jnp.maximum(at(i) * ROWS - 1, 0), 0)),
            ]
            + [full(a) for a in (dt_w, small, out_w)],
            out_specs=[column(lay.maps), column(lay.maps), row(chans), row(chans)]
            + [full(a) for a in outs[4:]],
            scratch_shapes=[
                pltpu.VMEM((width, chans), f32),
                pltpu.VMEM((ROWS * width, chans), bf16),
                pltpu.VMEM((ROWS * width, chans), bf16),
                pltpu.VMEM((ROWS, chans), f32),
                pltpu.VMEM((ROWS, chans), f32),
                pltpu.VMEM((ROWS * width, LANES), f32),
                pltpu.VMEM((ROWS * width, LANES), bf16),
                pltpu.VMEM((ROWS * width, LANES), bf16),
                pltpu.VMEM((STEPS, chans), f32),
                pltpu.VMEM((STEPS, chans), f32),
                pltpu.VMEM((STEPS, chans), f32),
            ],
        ),
        out_shape=outs,
        compiler_params=params(),
        cost_estimate=cost(40),
        name="backward",
    )(length, own, got, low, gate, before, step, grad, h, h, dt_w, small, out_w)


def back_kernel(
    lay, shards, slot, order, own, got, small, out_grad, conv_sum, conv_in, low, gate_grad, normed, w,
    *refs,
):
    token_refs = refs[:shards]
    part_ref, weight_ref, x_ref, conv_ref, gain_ref, halo, total, tokens = refs[shards:]
    rows, chans = low.shape
    taps = lay.taps
    turn = pl.program_id(0)

    @pl.when(turn == 0)
    def _():
        halo[rows:] = jnp.zeros_like(halo[rows:])
        for ref in (total, x_ref, conv_ref, gain_ref):
            ref[...] = jnp.zeros_like(ref)

    for index in range(shards):

        @pl.when(order[shards - 1 - turn] == index)
        def _(index=index):
            tokens[...] = token_refs[index][...].astype(f32)

    rest = lay.rest(small)
    map_grad = (own[...] + got[...].astype(f32)).astype(bf16)
    x_ref[...] += dot(map_grad, low[...])
    values = conv_sum[...]
    sigma = jax.nn.sigmoid(values)
    sum_grad = (out_grad[...] + dot(map_grad, lay.x_w(small), TN)) * (
        sigma * (1.0 + values * (1.0 - sigma))
    )
    conv_ref[taps : taps + 1] += jnp.sum(sum_grad, axis=0, keepdims=True)
    halo[:rows] = sum_grad
    inputs = conv_in[...]
    input_grad = jnp.zeros_like(inputs)
    for tap in range(taps):
        first = taps - 1 - tap
        moved = halo[first : first + rows]
        input_grad = input_grad + rest[tap : tap + 1] * moved
        conv_ref[tap : tap + 1] += jnp.sum(inputs * moved, axis=0, keepdims=True)
    halo[rows:] = sum_grad[:8]
    input_grad = input_grad.astype(bf16)
    total[...] += dot(normed[...], input_grad, TN)
    part = dot(jnp.concatenate([input_grad, gate_grad[...]], 1), w[...], NT)
    part_ref[0] = part.astype(bf16)
    values = tokens[...]
    inverse = lax.rsqrt(jnp.mean(values * values, axis=-1, keepdims=True) + epsilon)
    gain_ref[...] += jnp.sum(part * (values * inverse), axis=0, keepdims=True)

    @pl.when(turn == pl.num_programs(0) - 1)
    def _():
        weight_ref[...] = total[...].astype(bf16)


def back(lay, slot, order, own, got, small, out_grad, conv_sum, conv_in, low, gate_grad, normed, w, tokens):
    chans = low.shape[1]
    count = len(tokens)
    rows, depth = tokens[0].shape
    at = lambda i: count - 1 - i
    row = lambda a: pl.BlockSpec((rows, a.shape[1]), lambda i, *_: (at(i), 0))
    column = lambda a: pl.BlockSpec((a.shape[0], rows), lambda i, *_: (0, at(i)))
    outs = [
        shape((count, rows, depth), bf16),
        shape((depth, chans), bf16),
        shape((lay.maps, chans), f32),
        shape((8, chans), f32),
        shape((1, depth), f32),
    ]
    return pl.pallas_call(
        functools.partial(back_kernel, lay, count),
        grid_spec=pltpu.PrefetchScalarGridSpec(
            num_scalar_prefetch=2,
            grid=(count,),
            in_specs=[
                column(own),
                column(got),
                full(small),
                row(out_grad),
                row(conv_sum),
                row(conv_in),
                row(low),
                row(gate_grad),
                row(normed),
                full(w),
            ]
            + [full(a) for a in tokens],
            out_specs=[pl.BlockSpec((1, rows, depth), lambda i, s, o: (s[at(i)], 0, 0))]
            + [full(a) for a in outs[1:]],
            scratch_shapes=[
                pltpu.VMEM((rows + 8, chans), f32),
                pltpu.VMEM((depth, chans), f32),
                pltpu.VMEM((rows, depth), f32),
            ],
        ),
        out_shape=outs,
        compiler_params=params(),
        cost_estimate=cost(13),
        name="back",
    )(slot, order, own, got, small, out_grad, conv_sum, conv_in, low, gate_grad, normed, w, *tokens)


def exchange(values, axis, size, bits):
    return lax.ppermute(values, axis, [(i, i ^ bits) for i in range(size)])


def relay(values, axis, size, beside):
    me = lax.axis_index(axis)
    up, down = [values], [values]
    for hop in range(1, size):
        pairs = range(hop - 1, size - 1)
        up.append(lax.ppermute(up[-1], axis, [(i, i + 1) for i in pairs]))
        down.append(lax.ppermute(down[-1], axis, [(size - 1 - i, size - 2 - i) for i in pairs]))
        if hop == 1:
            up[1], down[1], beside = lax.optimization_barrier((up[1], down[1], beside))
    return up, down, beside


def chain_terms(sent, axis, size):
    up, down = sent[size - 1], sent[1]
    for hop in range(1, size):
        up = lax.ppermute(up, axis, [(i, i + 1) for i in range(hop)])
        down = lax.ppermute(down, axis, [(size - 1 - i, size - 2 - i) for i in range(hop)])
        if hop < size - 1:
            up = up + sent[size - 1 - hop]
            down = down + sent[hop + 1]
    return [sent[0], up, down]


def gather_pieces(values, axis, size):
    even = [values] + [exchange(values, axis, size, m) for m in range(2, size, 2)]
    odd = [exchange(piece, axis, size, 1) for piece in even]
    return [piece for pair in zip(even, odd) for piece in pair]


def pair_sum(values, axis, size):
    pairs = values.reshape((size // 2, 2) + values.shape[1:])
    core = lax.axis_index(axis) % 2
    keep = lax.dynamic_index_in_dim(pairs, core, 1, False)
    send = lax.dynamic_index_in_dim(pairs, 1 - core, 1, False)
    return keep + exchange(send, axis, size, 1)


def chip_terms(summed, axis, size):
    place = lax.axis_index(axis) // 2
    terms = [lax.dynamic_index_in_dim(summed, place, 0, False)]
    for m in range(1, size // 2):
        piece = lax.dynamic_index_in_dim(summed, place ^ m, 0, False)
        terms.append(exchange(piece, axis, size, 2 * m))
    return terms


def chunk_terms(sent, axis, size):
    return [sent[0]] + [
        lax.ppermute(sent[s], axis, [(i, (i + s) % size) for i in range(size)])
        for s in range(1, size)
    ]


def total(terms):
    return sum(term.astype(f32) for term in terms)


def sum_all(values, send, axis, size):
    bits = 1
    while bits < size:
        got = exchange(send, axis, size, 2 * bits - 1)
        bits *= 2
        if bits < size:
            values = values + got.astype(f32)
            send = values.astype(bf16)
    return values, got


def shards(
    fsdp, tp, tokens, lengths, norm_gain, in_weight, conv_weight, conv_bias, x_weight, dt_weight,
    dt_bias, a_log, d_skip, out_weight, cotangent,
):
    tp_me = lax.axis_index("tp")
    fs_me = lax.axis_index("fsdp")
    chunks = jnp.arange(tp)
    order = ((tp_me - chunks) % tp).astype(jnp.int32)
    slot = ((chunks - tp_me) % tp).astype(jnp.int32)
    place = (fs_me ^ jnp.arange(fsdp)).astype(jnp.int32)
    depth = tokens.shape[2]
    part = conv_weight.shape[1]
    chans = part * fsdp
    lay = Rows(x_weight.shape[1], a_log.shape[0], conv_weight.shape[0])
    maps, width, taps, rank, first = lay.maps, lay.width, lay.taps, lay.rank, lay.first

    pieces = gather_pieces(in_weight.reshape(in_weight.shape[0], 2 * chans), "fsdp", fsdp)
    packed = jnp.concatenate(
        [
            x_weight.T,
            a_log,
            conv_weight,
            conv_bias[None],
            dt_bias[None],
            d_skip[None],
            jnp.zeros((lay.count - first - taps - 3, part), bf16),
            dt_weight.reshape(-1, part),
            norm_gain.reshape(-1, part),
        ],
        0,
    )
    gathered = lax.all_gather(packed, "fsdp", axis=0)
    up, down, gathered = relay(tokens[0], "tp", tp, gathered)
    token_shards = up[:1] + [jnp.where(tp_me >= k, up[k], down[tp - k]) for k in range(1, tp)]
    small = gathered[:, : lay.count].transpose(1, 0, 2).reshape(lay.count, chans)
    dt_rows = dt_weight.size // part
    dt_w = gathered[:, lay.count : lay.count + dt_rows].reshape(rank, chans)
    gain = gathered[:, lay.count + dt_rows :].reshape(1, depth).astype(f32)
    out_w = lax.all_gather(out_weight, "fsdp", axis=1, tiled=True)
    token_shards, held = lax.optimization_barrier((token_shards, cotangent[0]))
    grad_whole = lax.all_gather(held, "tp", axis=0, tiled=True)

    normed, w, conv_in, gate, conv_sum, low, map_part, map_send = front(
        lay, order, place, token_shards, gain, small, pieces
    )
    own, got = sum_all(map_part, map_send, "tp", tp)
    mixed, before, step, h, sent = forward(
        lay, lengths, slot, own, got, low, gate, dt_w, small, out_w
    )
    block_terms = chunk_terms(sent, "tp", tp)
    out_grad = dot(grad_whole, mixed, TN).astype(bf16)

    map_part, map_send, conv_grad, gate_grad, rate_grad, dt_w_grad, bias_grad = backward(
        lay, lengths, own, got, low, gate, before, step, grad_whole, h, dt_w, small, out_w
    )
    map_part, map_send, block_terms[0] = lax.optimization_barrier(
        (map_part, map_send, block_terms[0])
    )
    own_grad, got_grad = sum_all(map_part, map_send, "tp", tp)
    block_out = (tokens.astype(f32) + total(block_terms)[None]).astype(bf16)
    gate_weight = dot(normed, gate_grad, TN).astype(bf16)
    out_terms = chip_terms(pair_sum(out_grad.reshape(fsdp, -1, chans), "fsdp", fsdp), "fsdp", fsdp)
    gate_terms = chip_terms(
        pair_sum(gate_weight.reshape(fsdp, -1, chans), "fsdp", fsdp), "fsdp", fsdp
    )
    own_grad, got_grad, block_out, out_terms, gate_terms = lax.optimization_barrier(
        (own_grad, got_grad, block_out, out_terms, gate_terms)
    )
    sent_back, conv_weight_half, x_w_grad, taps_grad, gain_grad = back(
        lay, slot, order, own_grad, got_grad, small, conv_grad, conv_sum, conv_in, low,
        gate_grad, normed, w, token_shards,
    )
    normed_grad = total(chain_terms(sent_back, "tp", tp))
    conv_pairs = pair_sum(conv_weight_half.reshape(fsdp, -1, chans), "fsdp", fsdp)
    rows = jnp.concatenate(
        [x_w_grad, rate_grad * LN2, taps_grad[: taps + 1], bias_grad[:2]], 0
    ).astype(bf16)
    top = rows.shape[0]
    packed = jnp.concatenate(
        [
            rows.reshape(top, fsdp, part).transpose(1, 0, 2),
            dt_w_grad.astype(bf16).reshape(fsdp, -1, part),
            gain_grad.astype(bf16).reshape(fsdp, -1, part),
        ],
        1,
    )
    small_grad = total(chip_terms(pair_sum(packed, "fsdp", fsdp), "fsdp", fsdp))
    gain_out = small_grad[top + dt_rows :].reshape(-1, 2 * part)
    bits = 1
    while bits < tp:
        gain_out = gain_out + exchange(gain_out, "tp", tp, 2 * bits - 1)
        bits *= 2
    out_weight_grad = total(out_terms).T
    conv_terms = chip_terms(conv_pairs, "fsdp", fsdp)
    in_weight_grad = jnp.stack([total(conv_terms), total(gate_terms)], 1)

    own_values = tokens.astype(f32)
    own_inverse = lax.rsqrt(jnp.mean(own_values * own_values, axis=-1, keepdims=True) + epsilon)
    own_hat = own_values * own_inverse
    scaled = normed_grad[None] * gain[None]
    input_grads = cotangent.astype(f32) + own_inverse * (
        scaled - own_hat * jnp.mean(scaled * own_hat, axis=-1, keepdims=True)
    )
    return (
        block_out,
        input_grads,
        gain_out.reshape(-1),
        in_weight_grad,
        small_grad[first : first + taps],
        small_grad[first + taps],
        small_grad[:maps].T,
        small_grad[top : top + dt_rows].reshape(-1, chans),
        small_grad[first + taps + 1],
        small_grad[maps:first],
        small_grad[first + taps + 2],
        out_weight_grad,
    )


def solution(mesh):
    sizes = dict(mesh.shape)
    return jax.shard_map(
        functools.partial(shards, sizes["fsdp"], sizes["tp"]),
        mesh=mesh,
        in_specs=(
            P("fsdp", "tp", None),
            P("fsdp"),
            P("fsdp"),
            P("fsdp", None, "tp"),
            P(None, ("tp", "fsdp")),
            P(("tp", "fsdp")),
            P(("tp", "fsdp"), None),
            P("fsdp", "tp"),
            P(("tp", "fsdp")),
            P(None, ("tp", "fsdp")),
            P(("tp", "fsdp")),
            P("tp", "fsdp"),
            P("fsdp", "tp", None),
        ),
        out_specs=(
            P("fsdp", "tp", None),
            P("fsdp", "tp", None),
            P("fsdp"),
            P("fsdp", None, "tp"),
            P(None, ("tp", "fsdp")),
            P(("tp", "fsdp")),
            P(("tp", "fsdp"), None),
            P("fsdp", "tp"),
            P(("tp", "fsdp")),
            P(None, ("tp", "fsdp")),
            P(("tp", "fsdp")),
            P("tp", "fsdp"),
        ),
        check_vma=False,
    )
```

time: 399 us -> 300 us (0.75)
  waiting for transfers between devices: 136 us -> 61.2 us
  Pallas kernels: 106 us -> 86.3 us
  blocking collectives: 20.4 us -> 9.76 us
  starting transfers between devices: 59.2 us -> 65.8 us
  other arithmetic: 19.5 us -> 23.7 us
    ppermute x6 -> x9, waiting for transfers between devices: 65.6 us -> 11.4 us  [the longest x3 7.2 us: chain_terms(): up = lax.ppermute(up, axis, [(i, i + 1) for i in range(hop)])]
    ppermute x6 -> x3, waiting for transfers between devices: 49 us -> 19.7 us  [relay(): lax.ppermute(down[-1], axis, [(size - 1 - i, size - 2 - i) for i in pairs])]
    ppermute x6 -> x9, starting transfers between devices: 12.4 us -> 33.5 us  [the longest x3 15.7 us: chain_terms(): up = lax.ppermute(up, axis, [(i, i + 1) for i in range(hop)])]
    pallas_call x6 -> x4, Pallas kernels: 106 us -> 86.3 us  [the longest x1 39.5 us: backward(): pl.pallas_call(functools.partial(backward_kernel, lay), grid_spec=pltpu.P...]
    psum x1 -> x0, blocking collectives: 10.7 us -> none  [shards(): gain_out = lax.psum(small_grad[top + dt_rows:].reshape(-1), 'tp')]
    ppermute x6 -> x3, starting transfers between devices: 13.6 us -> 6.96 us  [relay(): up.append(lax.ppermute(up[-1], axis, [(i, i + 1) for i in pairs]))]
    all_gather x1, waiting for transfers between devices: 0.01 us -> 5.07 us  [shards(): grad_whole = lax.all_gather(held, 'tp', axis=0, tiled=True)]
    add x3 -> x8, other arithmetic: 2.62 us -> 7.25 us  [the longest x2 3.56 us: chain_terms(): up = up + sent[size - 1 - hop]]
  transfers between devices with their start and end apart: 44 -> 46, of which waited for: 12 -> 13; matrix products, arithmetic and copies ran while one was open for 13% -> 17% of each run, Pallas kernels for 13% -> 24%
where the time goes in v3:
time: 300 us; the launch traced here: 299 us
  Pallas kernels  86.3 us (29%)
  starting transfers between devices  65.8 us (22%)
  waiting for transfers between devices  61.2 us (20%)
  local copies, waits for them, and re-layouts  32.7 us (11%)
  other arithmetic  23.7 us (8%)
  between operations  15.3 us (5%)
  blocking collectives  9.76 us (3%)
  matrix products  4.48 us (1%)
    pallas_call x1, Pallas kernels, backward(): pl.pallas_call(functools.partial(backward_kernel, lay), grid_spec=pltpu.P...  39.5 us
    ppermute x29, waiting for transfers between devices, exchange(): return lax.ppermute(values, axis, [(i, i ^ bits) for i in range(size)])  25.1 us
    pallas_call x1, Pallas kernels, forward(): pl.pallas_call(functools.partial(forward_kernel, lay), grid_spec=pltpu.Pr...  22.8 us
    ppermute x29, starting transfers between devices, exchange(): return lax.ppermute(values, axis, [(i, i ^ bits) for i in range(size)])  21.4 us
    ppermute x3, waiting for transfers between devices, relay(): lax.ppermute(down[-1], axis, [(size - 1 - i, size - 2 - i) for i in pairs])  19.7 us
    ppermute x3, starting transfers between devices, chain_terms(): up = lax.ppermute(up, axis, [(i, i + 1) for i in range(hop)])  15.7 us
    pallas_call x1, Pallas kernels, back(): pl.pallas_call(functools.partial(back_kernel, lay, count), grid_spec=pltp...  13.7 us
    ppermute x3, starting transfers between devices, chunk_terms(): lax.ppermute(sent[s], axis, [(i, (i + s) % size) for i in range(size)])  13.6 us
  transfers between devices with their start and end apart: 46, of which 13 were waited for; matrix products, arithmetic and copies ran while one was open for 17% of the time, Pallas kernels for 24%

profile of v3, /device:TPU:0, one launch (start us, length us, event | category | flops | bytes accessed | tf_op | source)
XLA Modules:
  0.0 299.2 jit_solution(6063186265996567163)
XLA Ops:
  7.2 1.3 collective-permute-start.1
  8.5 5.6 %collective-permute-start = (bf16[256,1024]{1,0:T(8,128)(2,1)}, bf16[256,1024]{1,0:T(8,128)(2,1)S(1)}, u32[]{:S(2)}, u32[]{:S(2)}) collective-permute-start(bf16[256,1024]{1,0:T(8,128)(2,1)} %bitcast.130), channel_id=1, source_target_pairs={{0,1},{1,2},{2,3},{4,5},{5,6},{6,7},{8,9},{9,10},{10,11},{12,13},{... | collective-permute-start | bytes 1572872 | tf_op jit(solution)/shard_map/ppermute | solution.py:573
  20.6 9.8 %all-gather.1 = bf16[8,194,64]{1,2,0:T(8,128)(2,1)S(1)} all-gather(bf16[1,194,64]{1,2,0:T(8,128)(2,1)S(1)} %bitcast.148), channel_id=2, replica_groups=mesh['fsdp'=8,'tp'=4] {'fsdp'}, dimensions={0}, use_global_device_ids=true | all-gather | bytes 223488 | tf_op jit(solution)/shard_map/all_gather | solution.py:667
  31.0 1.3 collective-permute-start.2
  32.3 1.7 copy.151
  34.0 1.5 collective-permute-start.11
  35.5 1.5 collective-permute-start.9
  41.1 8.4 %collective-permute-done.2 = bf16[256,1024]{1,0:T(8,128)(2,1)S(1)} collective-permute-done((bf16[256,1024]{1,0:T(8,128)(2,1)S(1)}, bf16[256,1024]{1,0:T(8,128)(2,1)S(1)}, u32[]{:S(2)}, u32[]{:S(2)}) %collective-permute-start.2) | collective-permute-done | bytes 524320 | tf_op jit(solution)/shard_map/ppermute | solution.py:574
  49.5 1.3 collective-permute-start.3
  53.6 11.3 %collective-permute-done.3 = bf16[256,1024]{1,0:T(8,128)(2,1)S(1)} collective-permute-done((bf16[256,1024]{1,0:T(8,128)(2,1)S(1)}, bf16[256,1024]{1,0:T(8,128)(2,1)S(1)}, u32[]{:S(2)}, u32[]{:S(2)}) %collective-permute-start.3) | collective-permute-done | bytes 524320 | tf_op jit(solution)/shard_map/ppermute | solution.py:574
  67.2 10.2 %front.1 = (bf16[1024,1024]{1,0:T(8,128)(2,1)}, bf16[1024,1024]{1,0:T(8,128)(2,1)}, f32[1024,512]{1,0:T(8,128)}, f32[1024,512]{1,0:T(8,128)}, f32[1024,512]{1,0:...) custom-call(s32[4]{0:T(128)} %and_select_fusion.1.order, s32[8]{0:T(128)} %iota_xor_fusion.place, ...), custom_call_target="tpu_custom_call" | custom-call | flops 8999999488 | bytes 27000000 | tf_op jit(solution)/shard_map/front/pallas_call | solution.py:177
  77.5 5.8 %collective-permute-done.13 = bf16[96,1024]{1,0:T(8,128)(2,1)S(1)} collective-permute-done((bf16[96,1024]{1,0:T(8,128)(2,1)}, bf16[96,1024]{1,0:T(8,128)(2,1)S(1)}, u32[]{:S(2)}, u32[]{:S(2)}) %collective-permute-start.13) | collective-permute-done | bytes 196640 | tf_op jit(solution)/shard_map/ppermute | solution.py:565
  83.3 1.9 fusion.21
  85.2 1.9 collective-permute-start.14
  89.9 7.5 %collective-permute-done.14.got = bf16[96,1024]{1,0:T(8,128)(2,1)S(1)} collective-permute-done((bf16[96,1024]{1,0:T(8,128)(2,1)S(1)}, bf16[96,1024]{1,0:T(8,128)(2,1)S(1)}, u32[]{:S(2)}, u32[]{:S(2)}) %collective-permute-start.14) | collective-permute-done | bytes 196640 | tf_op jit(solution)/shard_map/ppermute | solution.py:565
  98.1 22.8 %forward.1 = (bf16[1024,512]{1,0:T(8,128)(2,1)}, f32[1024,512]{1,0:T(8,128)}, f32[1024,512]{1,0:T(8,128)}, bf16[16384,512]{1,0:T(8,128)(2,1)}, bf16[4,256,1024]{2,1,0:T(8,128)(2,1)}) custom-call(s32[1]{0:T(128)S(6)} %copy.152.length, s32[4]{0:T(128)} %and_select_fusion.slot, f32[96,1024]{1,0:T(8,128)} %get-tuple-element.169.own, ...), custom_call_target="tpu_custom_call" | custom-call | flops 24000000000 | bytes 72000000 | tf_op jit(solution)/shard_map/forward/pallas_call | solution.py:277
  120.9 2.7 slice_bitcast_fusion.4
  123.6 10.9 %collective-permute-start.17 = (bf16[256,1024]{1,0:T(8,128)(2,1)}, bf16[256,1024]{1,0:T(8,128)(2,1)S(1)}, u32[]{:S(2)}, u32[]{:S(2)}) collective-permute-start(bf16[256,1024]{1,0:T(8,128)(2,1)} %get-tuple-element.176), channel_id=1, source_target_pairs={{0,1},{1,2},{2,3},{3,0},{4,5},{5,6},{6,7},{7,4},{8,9},{9,10},{10,1... | collective-permute-start | bytes 1572872 | tf_op jit(solution)/shard_map/ppermute | solution.py:616
  134.5 2.7 collective-permute-start.18
  137.2 5.1 %all-gather.7.cloned.1.call-done.grad = bf16[1024,1024]{1,0:T(8,128)(2,1)} async-done(((bf16[256,1024]{1,0:T(8,128)(2,1)}), bf16[1024,1024]{1,0:T(8,128)(2,1)}) %all-gather.7.cloned.1.call-update) | async-done | bytes 2097168 | tf_op jit(solution)/shard_map/all_gather | solution.py:676
  142.3 39.5 %backward.1 = (f32[96,1024]{1,0:T(8,128)}, bf16[96,1024]{1,0:T(8,128)(2,1)}, f32[1024,512]{1,0:T(8,128)}, bf16[1024,512]{1,0:T(8,128)(2,1)}, f32[16,512]{1,0:T(8...) custom-call(s32[1]{0:T(128)S(6)} %copy.152.length, f32[96,1024]{1,0:T(8,128)} %get-tuple-element.169.own, ...), custom_call_target="tpu_custom_call" | custom-call | flops 40000000000 | bytes 120000000 | tf_op jit(solution)/shard_map/backward/pallas_call | solution.py:424
  182.6 1.3 convolution_convert_fusion.1
  185.4 3.2 %convolution_convert_fusion = bf16[1024,512]{1,0:T(8,128)(2,1)S(1)} fusion(bf16[1024,1024]{1,0:T(8,128)(2,1)} %get-tuple-element.81.normed, bf16[1024,512]{1,0:T(8,128)(2,1)} %get-tuple-element.82.gate_grad), kind=kOutput, calls=%fused_computation.3 | convolution fusion | flops 1074266112 | bytes 4194304 | tf_op jit(solution)/shard_map/dot_general | solution.py:24
  189.3 2.4 fusion.7
  191.7 4.5 %collective-permute-done.15 = bf16[96,1024]{1,0:T(8,128)(2,1)S(1)} collective-permute-done((bf16[96,1024]{1,0:T(8,128)(2,1)S(1)}, bf16[96,1024]{1,0:T(8,128)(2,1)S(1)}, u32[]{:S(2)}, u32[]{:S(2)}) %collective-permute-start.15) | collective-permute-done | bytes 196640 | tf_op jit(solution)/shard_map/ppermute | solution.py:565
  198.1 1.8 collective-permute-start.22
  201.8 3.1 %collective-permute-done.16.got = bf16[96,1024]{1,0:T(8,128)(2,1)S(1)} collective-permute-done((bf16[96,1024]{1,0:T(8,128)(2,1)S(1)}, bf16[96,1024]{1,0:T(8,128)(2,1)S(1)}, u32[]{:S(2)}, u32[]{:S(2)}) %collective-permute-start.16) | collective-permute-done | bytes 196640 | tf_op jit(solution)/shard_map/ppermute | solution.py:565
  204.9 1.2 collective-permute-start.26
  207.5 2.1 collective-permute-done.27
  209.6 1.3 collective-permute-done.26
  211.1 13.7 %back.1 = (bf16[4,256,1024]{2,1,0:T(8,128)(2,1)}, bf16[1024,512]{1,0:T(8,128)(2,1)}, f32[96,512]{1,0:T(8,128)}, f32[8,512]{1,0:T(8,128)}, f32[1,1024]{1,0:T(1,128)}) custom-call(s32[4]{0:T(128)} %and_select_fusion.slot, s32[4]{0:T(128)} %and_select_fusion.1.order, f32[96,1024]{1,0:T(8,128)} %get-tuple-element.84.own, bf16[96,1024]{1,0:T(8,128)(2,1)} %copy-done.19, ...), custom_call_target="tpu_custom_call" | custom-call | flops 12999999488 | bytes 39000000 | tf_op jit(solution)/shard_map/back/pallas_call | solution.py:531
  229.7 5.7 %collective-permute-start.28 = (bf16[256,1024]{1,0:T(8,128)(2,1)}, bf16[256,1024]{1,0:T(8,128)(2,1)}, u32[]{:S(2)}, u32[]{:S(2)}) collective-permute-start(bf16[256,1024]{1,0:T(8,128)(2,1)} %get-tuple-element.174), channel_id=1, source_target_pairs={{0,1},{4,5},{8,9},{12,13},{16,17},{20,21},{24,25},{28,29}} | collective-permute-start | bytes 1572872 | tf_op jit(solution)/shard_map/ppermute | solution.py:583
  235.4 1.5 collective-permute-start.31
  240.7 2.0 collective-permute-start.37
  242.7 1.2 collective-permute-start.36
  243.9 1.9 dynamic-slice_bitcast_fusion
  248.7 1.3 reshape.123
  250.0 2.3 bitcast_add_fusion.3
  252.3 4.7 %collective-permute-start.29 = (bf16[256,1024]{1,0:T(8,128)(2,1)}, bf16[256,1024]{1,0:T(8,128)(2,1)}, u32[]{:S(2)}, u32[]{:S(2)}) collective-permute-start(bf16[256,1024]{1,0:T(8,128)(2,1)} %get-tuple-element.172), channel_id=1, source_target_pairs={{0,1},{1,2},{4,5},{5,6},{8,9},{9,10},{12,13},{13,14},{16,17},{17,1... | collective-permute-start | bytes 1572872 | tf_op jit(solution)/shard_map/ppermute | solution.py:583
  257.0 1.5 collective-permute-start.32
  261.5 1.4 reshape.125
  266.9 1.5 collective-permute-start.43
  269.3 1.3 fusion.19
  270.7 5.2 %collective-permute-start.30 = (bf16[256,1024]{1,0:T(8,128)(2,1)S(1)}, bf16[256,1024]{1,0:T(8,128)(2,1)S(1)}, u32[]{:S(2)}, u32[]{:S(2)}) collective-permute-start(bf16[256,1024]{1,0:T(8,128)(2,1)S(1)} %get-tuple-element.170), channel_id=1, source_target_pairs={{0,1},{1,2},{2,3},{4,5},{5,6},{6,7},{8,9},{9,10},{10,11},{12,13},{... | collective-permute-start | bytes 1572872 | tf_op jit(solution)/shard_map/ppermute | solution.py:583
  275.9 1.3 collective-permute-start.33
  279.1 7.2 %collective-permute-done.30 = bf16[256,1024]{1,0:T(8,128)(2,1)S(1)} collective-permute-done((bf16[256,1024]{1,0:T(8,128)(2,1)S(1)}, bf16[256,1024]{1,0:T(8,128)(2,1)S(1)}, u32[]{:S(2)}, u32[]{:S(2)}) %collective-permute-start.30) | collective-permute-done | bytes 524320 | tf_op jit(solution)/shard_map/ppermute | solution.py:583
  286.3 4.2 %collective-permute-done.33 = bf16[256,1024]{1,0:T(8,128)(2,1)S(1)} collective-permute-done((bf16[256,1024]{1,0:T(8,128)(2,1)S(1)}, bf16[256,1024]{1,0:T(8,128)(2,1)S(1)}, u32[]{:S(2)}, u32[]{:S(2)}) %collective-permute-start.33) | collective-permute-done | bytes 524320 | tf_op jit(solution)/shard_map/ppermute | solution.py:584
  290.9 1.4 fusion.5
  (184 shorter events, 49.1 us)
Async XLA Ops:
  7.2 82.8 %all-gather.5.cloned.1.call-start = ((), (), s32[]{:S(2)}) async-start(), calls=%async_computation | async-start | bytes 1179648 | tf_op jit(solution)/shard_map/all_gather | solution.py:674
  7.2 23.1 %collective-permute-start.1 = (bf16[256,1024]{1,0:T(8,128)(2,1)}, bf16[256,1024]{1,0:T(8,128)(2,1)S(1)}, u32[]{:S(2)}, u32[]{:S(2)}) collective-permute-start(bf16[256,1024]{1,0:T(8,128)(2,1)} %bitcast.129), channel_id=1, source_target_pairs={{3,2},{2,1},{1,0},{7,6},{6,5},{5,4},{11,10},{10,9},{9,8},{15,14},{... | collective-permute-start | bytes 1572872 | tf_op jit(solution)/shard_map/ppermute | solution.py:574
  8.5 21.8 %collective-permute-start = (bf16[256,1024]{1,0:T(8,128)(2,1)}, bf16[256,1024]{1,0:T(8,128)(2,1)S(1)}, u32[]{:S(2)}, u32[]{:S(2)}) collective-permute-start(bf16[256,1024]{1,0:T(8,128)(2,1)} %bitcast.130), channel_id=1, source_target_pairs={{0,1},{1,2},{2,3},{4,5},{5,6},{6,7},{8,9},{9,10},{10,11},{12,13},{... | collective-permute-start | bytes 1572872 | tf_op jit(solution)/shard_map/ppermute | solution.py:573
  30.3 7.8 %collective-permute-start.4 = (bf16[256,1024]{1,0:T(8,128)(2,1)S(1)}, bf16[256,1024]{1,0:T(8,128)(2,1)S(1)}, u32[]{:S(2)}, u32[]{:S(2)}) collective-permute-start(bf16[256,1024]{1,0:T(8,128)(2,1)S(1)} %collective-permute-done), channel_id=1, source_target_pairs={{1,2},{2,3},{5,6},{6,7},{9,10},{10,11},{13,14},{14,15},{17,18},{18... | collective-permute-start | bytes 1572872 | tf_op jit(solution)/shard_map/ppermute | solution.py:573
  31.0 18.5 %collective-permute-start.2 = (bf16[256,1024]{1,0:T(8,128)(2,1)S(1)}, bf16[256,1024]{1,0:T(8,128)(2,1)S(1)}, u32[]{:S(2)}, u32[]{:S(2)}) collective-permute-start(bf16[256,1024]{1,0:T(8,128)(2,1)S(1)} %collective-permute-done.1), channel_id=1, source_target_pairs={{2,1},{1,0},{6,5},{5,4},{10,9},{9,8},{14,13},{13,12},{18,17},{17,1... | collective-permute-start | bytes 1572872 | tf_op jit(solution)/shard_map/ppermute | solution.py:574
  34.0 17.7 %collective-permute-start.11 = (bf16[128,1024]{1,0:T(8,128)(2,1)}, bf16[128,1024]{1,0:T(8,128)(2,1)}, u32[]{:S(2)}, u32[]{:S(2)}) collective-permute-start(bf16[128,1024]{1,0:T(8,128)(2,1)} %bitcast.70.refs_4_), channel_id=1, source_target_pairs={{0,24},{4,28},{8,16},{12,20},{16,8},{20,12},{24,0},{28,4},{1,25},{... | collective-permute-start | bytes 786440 | tf_op jit(solution)/shard_map/ppermute | solution.py:565
  35.5 16.2 %collective-permute-start.9 = (bf16[128,1024]{1,0:T(8,128)(2,1)}, bf16[128,1024]{1,0:T(8,128)(2,1)}, u32[]{:S(2)}, u32[]{:S(2)}) collective-permute-start(bf16[128,1024]{1,0:T(8,128)(2,1)} %bitcast.70.refs_4_), channel_id=1, source_target_pairs={{0,16},{4,20},{8,24},{12,28},{16,0},{20,4},{24,8},{28,12},{1,17},{... | collective-permute-start | bytes 786440 | tf_op jit(solution)/shard_map/ppermute | solution.py:565
  37.0 15.2 %collective-permute-start.7 = (bf16[128,1024]{1,0:T(8,128)(2,1)}, bf16[128,1024]{1,0:T(8,128)(2,1)}, u32[]{:S(2)}, u32[]{:S(2)}) collective-permute-start(bf16[128,1024]{1,0:T(8,128)(2,1)} %bitcast.70.refs_4_), channel_id=1, source_target_pairs={{0,8},{4,12},{8,0},{12,4},{16,24},{20,28},{24,16},{28,20},{1,9},{5... | collective-permute-start | bytes 786440 | tf_op jit(solution)/shard_map/ppermute | solution.py:565
  37.5 104.8 %all-gather.7.cloned.1.call-start = ((), (), s32[]{:S(2)}) async-start(), calls=%async_computation.1 | async-start | bytes 2621440 | tf_op jit(solution)/shard_map/all_gather | solution.py:676
  38.1 14.2 %collective-permute-start.5 = (bf16[256,1024]{1,0:T(8,128)(2,1)S(1)}, bf16[256,1024]{1,0:T(8,128)(2,1)S(1)}, u32[]{:S(2)}, u32[]{:S(2)}) collective-permute-start(bf16[256,1024]{1,0:T(8,128)(2,1)S(1)} %collective-permute-done.4), channel_id=1, source_target_pairs={{2,3},{6,7},{10,11},{14,15},{18,19},{22,23},{26,27},{30,31}} | collective-permute-start | bytes 1572872 | tf_op jit(solution)/shard_map/ppermute | solution.py:573
  49.5 15.4 %collective-permute-start.3 = (bf16[256,1024]{1,0:T(8,128)(2,1)S(1)}, bf16[256,1024]{1,0:T(8,128)(2,1)S(1)}, u32[]{:S(2)}, u32[]{:S(2)}) collective-permute-start(bf16[256,1024]{1,0:T(8,128)(2,1)S(1)} %collective-permute-done.2), channel_id=1, source_target_pairs={{1,0},{5,4},{9,8},{13,12},{17,16},{21,20},{25,24},{29,28}} | collective-permute-start | bytes 1572872 | tf_op jit(solution)/shard_map/ppermute | solution.py:574
  51.7 14.0 %collective-permute-start.6 = (bf16[128,1024]{1,0:T(8,128)(2,1)}, bf16[128,1024]{1,0:T(8,128)(2,1)S(1)}, u32[]{:S(2)}, u32[]{:S(2)}) collective-permute-start(bf16[128,1024]{1,0:T(8,128)(2,1)} %bitcast.70.refs_4_), channel_id=1, source_target_pairs={{0,4},{4,0},{8,12},{12,8},{16,20},{20,16},{24,28},{28,24},{1,5},{5... | collective-permute-start | bytes 786440 | tf_op jit(solution)/shard_map/ppermute | solution.py:565
  51.7 14.0 %collective-permute-start.12 = (bf16[128,1024]{1,0:T(8,128)(2,1)}, bf16[128,1024]{1,0:T(8,128)(2,1)S(1)}, u32[]{:S(2)}, u32[]{:S(2)}) collective-permute-start(bf16[128,1024]{1,0:T(8,128)(2,1)} %collective-permute-done.11.refs_10_), channel_id=1, source_target_pairs={{0,4},{4,0},{8,12},{12,8},{16,20},{20,16},{24,28},{28,24},{1,5},{5... | collective-permute-start | bytes 786440 | tf_op jit(solution)/shard_map/ppermute | solution.py:565
  52.2 13.5 %collective-permute-start.10 = (bf16[128,1024]{1,0:T(8,128)(2,1)}, bf16[128,1024]{1,0:T(8,128)(2,1)}, u32[]{:S(2)}, u32[]{:S(2)}) collective-permute-start(bf16[128,1024]{1,0:T(8,128)(2,1)} %collective-permute-done.9.refs_8_), channel_id=1, source_target_pairs={{0,4},{4,0},{8,12},{12,8},{16,20},{20,16},{24,28},{28,24},{1,5},{5... | collective-permute-start | bytes 786440 | tf_op jit(solution)/shard_map/ppermute | solution.py:565
  52.3 13.4 %collective-permute-start.8 = (bf16[128,1024]{1,0:T(8,128)(2,1)}, bf16[128,1024]{1,0:T(8,128)(2,1)S(1)}, u32[]{:S(2)}, u32[]{:S(2)}) collective-permute-start(bf16[128,1024]{1,0:T(8,128)(2,1)} %collective-permute-done.7.refs_6_), channel_id=1, source_target_pairs={{0,4},{4,0},{8,12},{12,8},{16,20},{20,16},{24,28},{28,24},{1,5},{5... | collective-permute-start | bytes 786440 | tf_op jit(solution)/shard_map/ppermute | solution.py:565
  77.4 5.9 %collective-permute-start.13 = (bf16[96,1024]{1,0:T(8,128)(2,1)}, bf16[96,1024]{1,0:T(8,128)(2,1)S(1)}, u32[]{:S(2)}, u32[]{:S(2)}) collective-permute-start(bf16[96,1024]{1,0:T(8,128)(2,1)} %get-tuple-element.67), channel_id=1, source_target_pairs={{0,1},{1,0},{2,3},{3,2},{4,5},{5,4},{6,7},{7,6},{8,9},{9,8},{10,11... | collective-permute-start | bytes 589832 | tf_op jit(solution)/shard_map/ppermute | solution.py:565
  85.2 12.2 %collective-permute-start.14 = (bf16[96,1024]{1,0:T(8,128)(2,1)S(1)}, bf16[96,1024]{1,0:T(8,128)(2,1)S(1)}, u32[]{:S(2)}, u32[]{:S(2)}) collective-permute-start(bf16[96,1024]{1,0:T(8,128)(2,1)S(1)} %get-tuple-element.168), channel_id=1, source_target_pairs={{0,3},{1,2},{2,1},{3,0},{4,7},{5,6},{6,5},{7,4},{8,11},{9,10},{10,... | collective-permute-start | bytes 589832 | tf_op jit(solution)/shard_map/ppermute | solution.py:565
  123.6 65.6 %collective-permute-start.17 = (bf16[256,1024]{1,0:T(8,128)(2,1)}, bf16[256,1024]{1,0:T(8,128)(2,1)S(1)}, u32[]{:S(2)}, u32[]{:S(2)}) collective-permute-start(bf16[256,1024]{1,0:T(8,128)(2,1)} %get-tuple-element.176), channel_id=1, source_target_pairs={{0,1},{1,2},{2,3},{3,0},{4,5},{5,6},{6,7},{7,4},{8,9},{9,10},{10,1... | collective-permute-start | bytes 1572872 | tf_op jit(solution)/shard_map/ppermute | solution.py:616
  134.5 54.7 %collective-permute-start.19 = (bf16[256,1024]{1,0:T(8,128)(2,1)}, bf16[256,1024]{1,0:T(8,128)(2,1)}, u32[]{:S(2)}, u32[]{:S(2)}) collective-permute-start(bf16[256,1024]{1,0:T(8,128)(2,1)} %get-tuple-element.177), channel_id=1, source_target_pairs={{0,3},{1,0},{2,1},{3,2},{4,7},{5,4},{6,5},{7,6},{8,11},{9,8},{10,9... | collective-permute-start | bytes 1572872 | tf_op jit(solution)/shard_map/ppermute | solution.py:616
  134.5 54.7 %collective-permute-start.18 = (bf16[256,1024]{1,0:T(8,128)(2,1)}, bf16[256,1024]{1,0:T(8,128)(2,1)}, u32[]{:S(2)}, u32[]{:S(2)}) collective-permute-start(bf16[256,1024]{1,0:T(8,128)(2,1)} %get-tuple-element.178), channel_id=1, source_target_pairs={{0,2},{1,3},{2,0},{3,1},{4,6},{5,7},{6,4},{7,5},{8,10},{9,11},{10,... | collective-permute-start | bytes 1572872 | tf_op jit(solution)/shard_map/ppermute | solution.py:616
  142.3 40.3 %copy-start.14 = (bf16[1024,1024]{1,0:T(8,128)(2,1)S(1)}, bf16[1024,1024]{1,0:T(8,128)(2,1)}, u32[]{:S(2)}) copy-start(bf16[1024,1024]{1,0:T(8,128)(2,1)} %all-gather.7.cloned.1.call-done.grad) | copy-start | bytes 6291460
  142.3 40.3 %copy-start.21 = (bf16[1024,512]{1,0:T(8,128)(2,1)S(1)}, bf16[1024,512]{1,0:T(8,128)(2,1)}, u32[]{:S(2)}) copy-start(bf16[1024,512]{1,0:T(8,128)(2,1)} %get-tuple-element.80) | copy-start | bytes 3145732
  185.3 11.6 %collective-permute-start.20 = (bf16[4,128,512]{2,1,0:T(8,128)(2,1)S(1)}, bf16[4,128,512]{2,1,0:T(8,128)(2,1)S(1)}, u32[]{:S(2)}, u32[]{:S(2)}) collective-permute-start(bf16[4,128,512]{2,1,0:T(8,128)(2,1)S(1)} %dynamic-slice_bitcast_fusion.2), channel_id=1, source_target_pairs={{0,4},{4,0},{8,12},{12,8},{16,20},{20,16},{24,28},{28,24},{1,5},{5... | collective-permute-start | bytes 1572872 | tf_op jit(solution)/shard_map/ppermute | solution.py:565
  188.7 11.9 %collective-permute-start.24 = (bf16[4,128,512]{2,1,0:T(8,128)(2,1)S(1)}, bf16[4,128,512]{2,1,0:T(8,128)(2,1)S(1)}, u32[]{:S(2)}, u32[]{:S(2)}) collective-permute-start(bf16[4,128,512]{2,1,0:T(8,128)(2,1)S(1)} %dynamic-slice_bitcast_fusion.1), channel_id=1, source_target_pairs={{0,4},{4,0},{8,12},{12,8},{16,20},{20,16},{24,28},{28,24},{1,5},{5... | collective-permute-start | bytes 1572872 | tf_op jit(solution)/shard_map/ppermute | solution.py:565
  189.2 6.9 %collective-permute-start.15 = (bf16[96,1024]{1,0:T(8,128)(2,1)S(1)}, bf16[96,1024]{1,0:T(8,128)(2,1)S(1)}, u32[]{:S(2)}, u32[]{:S(2)}) collective-permute-start(bf16[96,1024]{1,0:T(8,128)(2,1)S(1)} %copy-done.20), channel_id=1, source_target_pairs={{0,1},{1,0},{2,3},{3,2},{4,5},{5,4},{6,7},{7,6},{8,9},{9,8},{10,11... | collective-permute-start | bytes 589832 | tf_op jit(solution)/shard_map/ppermute | solution.py:565
  196.9 8.0 %collective-permute-start.16 = (bf16[96,1024]{1,0:T(8,128)(2,1)S(1)}, bf16[96,1024]{1,0:T(8,128)(2,1)S(1)}, u32[]{:S(2)}, u32[]{:S(2)}) collective-permute-start(bf16[96,1024]{1,0:T(8,128)(2,1)S(1)} %get-tuple-element.166), channel_id=1, source_target_pairs={{0,3},{1,2},{2,1},{3,0},{4,7},{5,6},{6,5},{7,4},{8,11},{9,10},{10,... | collective-permute-start | bytes 589832 | tf_op jit(solution)/shard_map/ppermute | solution.py:565
  197.1 9.1 %collective-permute-start.23 = (bf16[128,512]{1,0:T(8,128)(2,1)S(1)}, bf16[128,512]{1,0:T(8,128)(2,1)S(1)}, u32[]{:S(2)}, u32[]{:S(2)}) collective-permute-start(bf16[128,512]{1,0:T(8,128)(2,1)S(1)} %get-tuple-element.189), channel_id=1, source_target_pairs={{0,24},{4,28},{8,16},{12,20},{16,8},{20,12},{24,0},{28,4},{1,25},{... | collective-permute-start | bytes 393224 | tf_op jit(solution)/shard_map/ppermute | solution.py:565
  198.1 9.4 %collective-permute-start.22 = (bf16[128,512]{1,0:T(8,128)(2,1)S(1)}, bf16[128,512]{1,0:T(8,128)(2,1)S(1)}, u32[]{:S(2)}, u32[]{:S(2)}) collective-permute-start(bf16[128,512]{1,0:T(8,128)(2,1)S(1)} %get-tuple-element.190), channel_id=1, source_target_pairs={{0,16},{4,20},{8,24},{12,28},{16,0},{20,4},{24,8},{28,12},{1,17},{... | collective-permute-start | bytes 393224 | tf_op jit(solution)/shard_map/ppermute | solution.py:565
  199.9 7.6 %collective-permute-start.21 = (bf16[128,512]{1,0:T(8,128)(2,1)S(1)}, bf16[128,512]{1,0:T(8,128)(2,1)S(1)}, u32[]{:S(2)}, u32[]{:S(2)}) collective-permute-start(bf16[128,512]{1,0:T(8,128)(2,1)S(1)} %get-tuple-element.191), channel_id=1, source_target_pairs={{0,8},{4,12},{8,0},{12,4},{16,24},{20,28},{24,16},{28,20},{1,9},{5... | collective-permute-start | bytes 393224 | tf_op jit(solution)/shard_map/ppermute | solution.py:565
  200.7 8.9 %collective-permute-start.27 = (bf16[128,512]{1,0:T(8,128)(2,1)S(1)}, bf16[128,512]{1,0:T(8,128)(2,1)S(1)}, u32[]{:S(2)}, u32[]{:S(2)}) collective-permute-start(bf16[128,512]{1,0:T(8,128)(2,1)S(1)} %get-tuple-element.185), channel_id=1, source_target_pairs={{0,24},{4,28},{8,16},{12,20},{16,8},{20,12},{24,0},{28,4},{1,25},{... | collective-permute-start | bytes 393224 | tf_op jit(solution)/shard_map/ppermute | solution.py:565
  204.9 6.0 %collective-permute-start.26 = (bf16[128,512]{1,0:T(8,128)(2,1)S(1)}, bf16[128,512]{1,0:T(8,128)(2,1)S(1)}, u32[]{:S(2)}, u32[]{:S(2)}) collective-permute-start(bf16[128,512]{1,0:T(8,128)(2,1)S(1)} %get-tuple-element.186), channel_id=1, source_target_pairs={{0,16},{4,20},{8,24},{12,28},{16,0},{20,4},{24,8},{28,12},{1,17},{... | collective-permute-start | bytes 393224 | tf_op jit(solution)/shard_map/ppermute | solution.py:565
  206.1 5.0 %collective-permute-start.25 = (bf16[128,512]{1,0:T(8,128)(2,1)S(1)}, bf16[128,512]{1,0:T(8,128)(2,1)S(1)}, u32[]{:S(2)}, u32[]{:S(2)}) collective-permute-start(bf16[128,512]{1,0:T(8,128)(2,1)S(1)} %get-tuple-element.187), channel_id=1, source_target_pairs={{0,8},{4,12},{8,0},{12,4},{16,24},{20,28},{24,16},{28,20},{1,9},{5... | collective-permute-start | bytes 393224 | tf_op jit(solution)/shard_map/ppermute | solution.py:565
  228.6 9.6 %collective-permute-start.34 = (bf16[4,185,64]{2,1,0:T(8,128)(2,1)S(1)}, bf16[4,185,64]{2,1,0:T(8,128)(2,1)}, u32[]{:S(2)}, u32[]{:S(2)}) collective-permute-start(bf16[4,185,64]{2,1,0:T(8,128)(2,1)S(1)} %bitcast.147), channel_id=1, source_target_pairs={{0,4},{4,0},{8,12},{12,8},{16,20},{20,16},{24,28},{28,24},{1,5},{5... | collective-permute-start | bytes 284168 | tf_op jit(solution)/shard_map/ppermute | solution.py:565
  229.7 20.3 %collective-permute-start.28 = (bf16[256,1024]{1,0:T(8,128)(2,1)}, bf16[256,1024]{1,0:T(8,128)(2,1)}, u32[]{:S(2)}, u32[]{:S(2)}) collective-permute-start(bf16[256,1024]{1,0:T(8,128)(2,1)} %get-tuple-element.174), channel_id=1, source_target_pairs={{0,1},{4,5},{8,9},{12,13},{16,17},{20,21},{24,25},{28,29}} | collective-permute-start | bytes 1572872 | tf_op jit(solution)/shard_map/ppermute | solution.py:583
  235.4 14.7 %collective-permute-start.31 = (bf16[256,1024]{1,0:T(8,128)(2,1)}, bf16[256,1024]{1,0:T(8,128)(2,1)}, u32[]{:S(2)}, u32[]{:S(2)}) collective-permute-start(bf16[256,1024]{1,0:T(8,128)(2,1)} %get-tuple-element.175), channel_id=1, source_target_pairs={{3,2},{7,6},{11,10},{15,14},{19,18},{23,22},{27,26},{31,30}} | collective-permute-start | bytes 1572872 | tf_op jit(solution)/shard_map/ppermute | solution.py:584
  240.5 6.2 %collective-permute-start.35 = (bf16[185,64]{1,0:T(8,128)(2,1)}, bf16[185,64]{1,0:T(8,128)(2,1)S(1)}, u32[]{:S(2)}, u32[]{:S(2)}) collective-permute-start(bf16[185,64]{1,0:T(8,128)(2,1)} %get-tuple-element.195), channel_id=1, source_target_pairs={{0,8},{4,12},{8,0},{12,4},{16,24},{20,28},{24,16},{28,20},{1,9},{5... | collective-permute-start | bytes 71048 | tf_op jit(solution)/shard_map/ppermute | solution.py:565
  240.7 5.9 %collective-permute-start.37 = (bf16[185,64]{1,0:T(8,128)(2,1)}, bf16[185,64]{1,0:T(8,128)(2,1)S(1)}, u32[]{:S(2)}, u32[]{:S(2)}) collective-permute-start(bf16[185,64]{1,0:T(8,128)(2,1)} %get-tuple-element.196), channel_id=1, source_target_pairs={{0,24},{4,28},{8,16},{12,20},{16,8},{20,12},{24,0},{28,4},{1,25},{... | collective-permute-start | bytes 71048 | tf_op jit(solution)/shard_map/ppermute | solution.py:565
  242.7 4.6 %collective-permute-start.36 = (bf16[185,64]{1,0:T(8,128)(2,1)S(1)}, bf16[185,64]{1,0:T(8,128)(2,1)}, u32[]{:S(2)}, u32[]{:S(2)}) collective-permute-start(bf16[185,64]{1,0:T(8,128)(2,1)S(1)} %get-tuple-element.197), channel_id=1, source_target_pairs={{0,16},{4,20},{8,24},{12,28},{16,0},{20,4},{24,8},{28,12},{1,17},{... | collective-permute-start | bytes 71048 | tf_op jit(solution)/shard_map/ppermute | solution.py:565
  246.7 18.0 %collective-permute-start.40 = (bf16[4,128,512]{2,1,0:T(8,128)(2,1)}, bf16[4,128,512]{2,1,0:T(8,128)(2,1)}, u32[]{:S(2)}, u32[]{:S(2)}) collective-permute-start(bf16[4,128,512]{2,1,0:T(8,128)(2,1)} %dynamic-slice_bitcast_fusion), channel_id=1, source_target_pairs={{0,4},{4,0},{8,12},{12,8},{16,20},{20,16},{24,28},{28,24},{1,5},{5... | collective-permute-start | bytes 1572872 | tf_op jit(solution)/shard_map/ppermute | solution.py:565
  250.0 12.9 %collective-permute-start.38 = (f32[1,128]{1,0:T(1,128)}, f32[1,128]{1,0:T(1,128)}, u32[]{:S(2)}, u32[]{:S(2)}) collective-permute-start(f32[1,128]{1,0:T(1,128)} %reshape.123), channel_id=1, source_target_pairs={{0,1},{1,0},{2,3},{3,2},{4,5},{5,4},{6,7},{7,6},{8,9},{9,8},{10,11... | collective-permute-start | bytes 1544 | tf_op jit(solution)/shard_map/ppermute | solution.py:565
  252.3 16.1 %collective-permute-start.29 = (bf16[256,1024]{1,0:T(8,128)(2,1)}, bf16[256,1024]{1,0:T(8,128)(2,1)}, u32[]{:S(2)}, u32[]{:S(2)}) collective-permute-start(bf16[256,1024]{1,0:T(8,128)(2,1)} %get-tuple-element.172), channel_id=1, source_target_pairs={{0,1},{1,2},{4,5},{5,6},{8,9},{9,10},{12,13},{13,14},{16,17},{17,1... | collective-permute-start | bytes 1572872 | tf_op jit(solution)/shard_map/ppermute | solution.py:583
  257.0 12.3 %collective-permute-start.32 = (bf16[256,1024]{1,0:T(8,128)(2,1)}, bf16[256,1024]{1,0:T(8,128)(2,1)}, u32[]{:S(2)}, u32[]{:S(2)}) collective-permute-start(bf16[256,1024]{1,0:T(8,128)(2,1)} %get-tuple-element.173), channel_id=1, source_target_pairs={{3,2},{2,1},{7,6},{6,5},{11,10},{10,9},{15,14},{14,13},{19,18},{18... | collective-permute-start | bytes 1572872 | tf_op jit(solution)/shard_map/ppermute | solution.py:584
  263.6 12.3 %collective-permute-start.39 = (f32[1,128]{1,0:T(1,128)S(1)}, f32[1,128]{1,0:T(1,128)S(1)}, u32[]{:S(2)}, u32[]{:S(2)}) collective-permute-start(f32[1,128]{1,0:T(1,128)S(1)} %add.193), channel_id=1, source_target_pairs={{0,3},{1,2},{2,1},{3,0},{4,7},{5,6},{6,5},{7,4},{8,11},{9,10},{10,... | collective-permute-start | bytes 1544 | tf_op jit(solution)/shard_map/ppermute | solution.py:565
  265.8 12.0 %collective-permute-start.41 = (bf16[128,512]{1,0:T(8,128)(2,1)S(1)}, bf16[128,512]{1,0:T(8,128)(2,1)S(1)}, u32[]{:S(2)}, u32[]{:S(2)}) collective-permute-start(bf16[128,512]{1,0:T(8,128)(2,1)S(1)} %get-tuple-element.180), channel_id=1, source_target_pairs={{0,8},{4,12},{8,0},{12,4},{16,24},{20,28},{24,16},{28,20},{1,9},{5... | collective-permute-start | bytes 393224 | tf_op jit(solution)/shard_map/ppermute | solution.py:565
  266.9 10.9 %collective-permute-start.43 = (bf16[128,512]{1,0:T(8,128)(2,1)S(1)}, bf16[128,512]{1,0:T(8,128)(2,1)S(1)}, u32[]{:S(2)}, u32[]{:S(2)}) collective-permute-start(bf16[128,512]{1,0:T(8,128)(2,1)S(1)} %get-tuple-element.181), channel_id=1, source_target_pairs={{0,24},{4,28},{8,16},{12,20},{16,8},{20,12},{24,0},{28,4},{1,25},{... | collective-permute-start | bytes 393224 | tf_op jit(solution)/shard_map/ppermute | solution.py:565
  268.4 9.4 %collective-permute-start.42 = (bf16[128,512]{1,0:T(8,128)(2,1)S(1)}, bf16[128,512]{1,0:T(8,128)(2,1)S(1)}, u32[]{:S(2)}, u32[]{:S(2)}) collective-permute-start(bf16[128,512]{1,0:T(8,128)(2,1)S(1)} %get-tuple-element.182), channel_id=1, source_target_pairs={{0,16},{4,20},{8,24},{12,28},{16,0},{20,4},{24,8},{28,12},{1,17},{... | collective-permute-start | bytes 393224 | tf_op jit(solution)/shard_map/ppermute | solution.py:565
  270.7 15.6 %collective-permute-start.30 = (bf16[256,1024]{1,0:T(8,128)(2,1)S(1)}, bf16[256,1024]{1,0:T(8,128)(2,1)S(1)}, u32[]{:S(2)}, u32[]{:S(2)}) collective-permute-start(bf16[256,1024]{1,0:T(8,128)(2,1)S(1)} %get-tuple-element.170), channel_id=1, source_target_pairs={{0,1},{1,2},{2,3},{4,5},{5,6},{6,7},{8,9},{9,10},{10,11},{12,13},{... | collective-permute-start | bytes 1572872 | tf_op jit(solution)/shard_map/ppermute | solution.py:583
  275.9 14.5 %collective-permute-start.33 = (bf16[256,1024]{1,0:T(8,128)(2,1)S(1)}, bf16[256,1024]{1,0:T(8,128)(2,1)S(1)}, u32[]{:S(2)}, u32[]{:S(2)}) collective-permute-start(bf16[256,1024]{1,0:T(8,128)(2,1)S(1)} %get-tuple-element.171), channel_id=1, source_target_pairs={{3,2},{2,1},{1,0},{7,6},{6,5},{5,4},{11,10},{10,9},{9,8},{15,14},{... | collective-permute-start | bytes 1572872 | tf_op jit(solution)/shard_map/ppermute | solution.py:584
  (20 other events, 164.7 us)
Sparse Core Ops, SparseCore 0:
  37.7 27.3 all-gather.4
  77.6 64.6 all-gather.6

commit v4 on v3

--- a/solution.py
+++ b/solution.py
@@ -14,6 +14,7 @@
 ROWS = 128
 STEPS = 16
 LANES = 128
+SCALE = 1.0
 NT = (((1,), (1,)), ((), ()))
 TN = (((0,), (0,)), ((), ()))
 epsilon = 1e-05
@@ -38,7 +39,7 @@
 
 def cost(micros):
     return pl.CostEstimate(
-        flops=int(micros * 1e9), bytes_accessed=int(micros * 3e6), transcendentals=0
+        flops=int(micros * SCALE * 1e9), bytes_accessed=int(micros * SCALE * 3e6), transcendentals=0
     )
 
 
@@ -169,7 +170,8 @@
 
 def front(lay, order, place, shards, gain, small, pieces):
     rows, depth = shards[0].shape
-    total = len(shards) * rows
+    count = order.shape[0]
+    total = count * rows
     chans = small.shape[1]
     row = lambda w: pl.BlockSpec((rows, w), lambda i, *_: (i, 0))
     column = lambda w: pl.BlockSpec((w, rows), lambda i, *_: (0, i))
@@ -178,7 +180,7 @@
         functools.partial(front_kernel, lay, len(shards), len(pieces)),
         grid_spec=pltpu.PrefetchScalarGridSpec(
             num_scalar_prefetch=2,
-            grid=(len(shards),),
+            grid=(count,),
             in_specs=[full(a) for a in (gain, small, *shards, *pieces)],
             out_specs=[
                 row(depth),
@@ -209,9 +211,11 @@
 
 
 def forward_kernel(
-    lay, length, slot, own, got, low, gate, dt_w, small, out_w,
-    mixed_ref, before_ref, step_ref, h_ref, sent_ref, state, drive, lanes, step_rows, drive_rows,
+    lay, count, length, slot, own, got, low, gate, dt_w, small, out_w,
+    mixed_ref, before_ref, step_ref, h_ref, *refs,
 ):
+    sent_refs = refs[:count]
+    state, drive, lanes, step_rows, drive_rows = refs[count:]
     rows, chans = low.shape
     width, rank, taps = lay.width, lay.rank, lay.taps
     half = width // 2
@@ -262,20 +266,26 @@
     gates = gate[...]
     mixed = (before * (gates * jax.nn.sigmoid(gates)) * live).astype(bf16)
     mixed_ref[...] = mixed
-    sent_ref[0] = dot(mixed, out_w[...]).astype(bf16)
+    part = dot(mixed, out_w[...]).astype(bf16)
+    blocks = sent_refs[0].shape[0] // rows
+    turn = pl.program_id(0)
+    for index in range(count):
+
+        @pl.when(slot[turn // blocks] == index)
+        def _(index=index):
+            sent_refs[index][pl.ds(pl.multiple_of(turn % blocks * rows, rows), rows), :] = part
 
 
 def forward(lay, length, slot, own, got, low, gate, dt_w, small, out_w):
     total, chans = low.shape
     count = slot.shape[0]
     part = total // count
-    blocks = part // ROWS
     depth = out_w.shape[1]
     width = lay.width
     row = lambda w: pl.BlockSpec((ROWS, w), lambda i, *_: (i, 0))
     column = lambda w: pl.BlockSpec((w, ROWS), lambda i, *_: (0, i))
     return pl.pallas_call(
-        functools.partial(forward_kernel, lay),
+        functools.partial(forward_kernel, lay, count),
         grid_spec=pltpu.PrefetchScalarGridSpec(
             num_scalar_prefetch=2,
             grid=(total // ROWS,),
@@ -286,8 +296,8 @@
                 row(chans),
                 row(chans),
                 pl.BlockSpec((ROWS * width, chans), lambda i, *_: (i, 0)),
-                pl.BlockSpec((1, ROWS, depth), lambda i, n, s: (s[i // blocks], i % blocks, 0)),
-            ],
+            ]
+            + [pl.BlockSpec((part, depth), lambda i, *_: (0, 0))] * count,
             scratch_shapes=[
                 pltpu.VMEM((width, chans), f32),
                 pltpu.VMEM((ROWS, chans), f32),
@@ -301,8 +311,8 @@
             shape((total, chans), f32),
             shape((total, chans), f32),
             shape((total * width, chans), bf16),
-            shape((count, part, depth), bf16),
-        ],
+        ]
+        + [shape((part, depth), bf16)] * count,
         compiler_params=params(),
         cost_estimate=cost(24),
         name="forward",
@@ -462,11 +472,10 @@
 
 
 def back_kernel(
-    lay, shards, slot, order, own, got, small, out_grad, conv_sum, conv_in, low, gate_grad, normed, w,
-    *refs,
+    lay, count, slot, place, own, got, small, out_grad, conv_sum, conv_in, low, gate_grad, normed, w, *refs
 ):
-    token_refs = refs[:shards]
-    part_ref, weight_ref, x_ref, conv_ref, gain_ref, halo, total, tokens = refs[shards:]
+    part_refs = refs[:count]
+    keep_ref, send_ref, x_ref, conv_ref, halo, total = refs[count:]
     rows, chans = low.shape
     taps = lay.taps
     turn = pl.program_id(0)
@@ -474,14 +483,8 @@
     @pl.when(turn == 0)
     def _():
         halo[rows:] = jnp.zeros_like(halo[rows:])
-        for ref in (total, x_ref, conv_ref, gain_ref):
+        for ref in (total, x_ref, conv_ref):
             ref[...] = jnp.zeros_like(ref)
-
-    for index in range(shards):
-
-        @pl.when(order[shards - 1 - turn] == index)
-        def _(index=index):
-            tokens[...] = token_refs[index][...].astype(f32)
 
     rest = lay.rest(small)
     map_grad = (own[...] + got[...].astype(f32)).astype(bf16)
@@ -504,29 +507,35 @@
     input_grad = input_grad.astype(bf16)
     total[...] += dot(normed[...], input_grad, TN)
     part = dot(jnp.concatenate([input_grad, gate_grad[...]], 1), w[...], NT)
-    part_ref[0] = part.astype(bf16)
-    values = tokens[...]
-    inverse = lax.rsqrt(jnp.mean(values * values, axis=-1, keepdims=True) + epsilon)
-    gain_ref[...] += jnp.sum(part * (values * inverse), axis=0, keepdims=True)
+    for index in range(count):
+
+        @pl.when(slot[pl.num_programs(0) - 1 - turn] == index)
+        def _(index=index):
+            part_refs[index][...] = part.astype(bf16)
 
     @pl.when(turn == pl.num_programs(0) - 1)
     def _():
-        weight_ref[...] = total[...].astype(bf16)
-
-
-def back(lay, slot, order, own, got, small, out_grad, conv_sum, conv_in, low, gate_grad, normed, w, tokens):
+        depth = keep_ref.shape[1]
+        for index in range(2 * keep_ref.shape[0]):
+            start = pl.multiple_of(place[index] * depth, depth)
+            values = total[pl.ds(start, depth), :].astype(bf16)
+            (send_ref if index % 2 else keep_ref)[index // 2] = values
+
+
+def back(lay, slot, place, own, got, small, out_grad, conv_sum, conv_in, low, gate_grad, normed, w):
     chans = low.shape[1]
-    count = len(tokens)
-    rows, depth = tokens[0].shape
+    count = slot.shape[0]
+    total, depth = normed.shape
+    rows = total // count
     at = lambda i: count - 1 - i
     row = lambda a: pl.BlockSpec((rows, a.shape[1]), lambda i, *_: (at(i), 0))
     column = lambda a: pl.BlockSpec((a.shape[0], rows), lambda i, *_: (0, at(i)))
-    outs = [
-        shape((count, rows, depth), bf16),
-        shape((depth, chans), bf16),
+    half = place.shape[0] // 2
+    outs = [shape((rows, depth), bf16)] * count + [
+        shape((half, depth // half // 2, chans), bf16),
+        shape((half, depth // half // 2, chans), bf16),
         shape((lay.maps, chans), f32),
         shape((8, chans), f32),
-        shape((1, depth), f32),
     ]
     return pl.pallas_call(
         functools.partial(back_kernel, lay, count),
@@ -544,21 +553,15 @@
                 row(gate_grad),
                 row(normed),
                 full(w),
-            ]
-            + [full(a) for a in tokens],
-            out_specs=[pl.BlockSpec((1, rows, depth), lambda i, s, o: (s[at(i)], 0, 0))]
-            + [full(a) for a in outs[1:]],
-            scratch_shapes=[
-                pltpu.VMEM((rows + 8, chans), f32),
-                pltpu.VMEM((depth, chans), f32),
-                pltpu.VMEM((rows, depth), f32),
             ],
+            out_specs=[full(a) for a in outs],
+            scratch_shapes=[pltpu.VMEM((rows + 8, chans), f32), pltpu.VMEM((depth, chans), f32)],
         ),
         out_shape=outs,
         compiler_params=params(),
-        cost_estimate=cost(13),
+        cost_estimate=cost(11),
         name="back",
-    )(slot, order, own, got, small, out_grad, conv_sum, conv_in, low, gate_grad, normed, w, *tokens)
+    )(slot, place, own, got, small, out_grad, conv_sum, conv_in, low, gate_grad, normed, w)
 
 
 def exchange(values, axis, size, bits):
@@ -566,49 +569,47 @@
 
 
 def relay(values, axis, size, beside):
-    me = lax.axis_index(axis)
     up, down = [values], [values]
+    beside = list(beside)
     for hop in range(1, size):
         pairs = range(hop - 1, size - 1)
         up.append(lax.ppermute(up[-1], axis, [(i, i + 1) for i in pairs]))
         down.append(lax.ppermute(down[-1], axis, [(size - 1 - i, size - 2 - i) for i in pairs]))
-        if hop == 1:
-            up[1], down[1], beside = lax.optimization_barrier((up[1], down[1], beside))
+        if hop <= len(beside):
+            up[-1], down[-1], beside[hop - 1] = lax.optimization_barrier(
+                (up[-1], down[-1], beside[hop - 1])
+            )
     return up, down, beside
 
 
-def chain_terms(sent, axis, size):
+def chain_terms(sent, axis, size, after):
     up, down = sent[size - 1], sent[1]
     for hop in range(1, size):
         up = lax.ppermute(up, axis, [(i, i + 1) for i in range(hop)])
         down = lax.ppermute(down, axis, [(size - 1 - i, size - 2 - i) for i in range(hop)])
+        if hop == size - 2:
+            up, down, after = lax.optimization_barrier((up, down, after))
         if hop < size - 1:
             up = up + sent[size - 1 - hop]
             down = down + sent[hop + 1]
-    return [sent[0], up, down]
-
-
-def gather_pieces(values, axis, size):
-    even = [values] + [exchange(values, axis, size, m) for m in range(2, size, 2)]
+    return [sent[0], up, down], after
+
+
+def even_pieces(values, axis, size):
+    return [values] + [exchange(values, axis, size, m) for m in range(2, size, 2)]
+
+
+def all_pieces(even, axis, size):
     odd = [exchange(piece, axis, size, 1) for piece in even]
     return [piece for pair in zip(even, odd) for piece in pair]
 
 
-def pair_sum(values, axis, size):
-    pairs = values.reshape((size // 2, 2) + values.shape[1:])
-    core = lax.axis_index(axis) % 2
-    keep = lax.dynamic_index_in_dim(pairs, core, 1, False)
-    send = lax.dynamic_index_in_dim(pairs, 1 - core, 1, False)
+def pair_sum(keep, send, axis, size):
     return keep + exchange(send, axis, size, 1)
 
 
 def chip_terms(summed, axis, size):
-    place = lax.axis_index(axis) // 2
-    terms = [lax.dynamic_index_in_dim(summed, place, 0, False)]
-    for m in range(1, size // 2):
-        piece = lax.dynamic_index_in_dim(summed, place ^ m, 0, False)
-        terms.append(exchange(piece, axis, size, 2 * m))
-    return terms
+    return [summed[0]] + [exchange(summed[m], axis, size, 2 * m) for m in range(1, size // 2)]
 
 
 def chunk_terms(sent, axis, size):
@@ -622,15 +623,17 @@
     return sum(term.astype(f32) for term in terms)
 
 
-def sum_all(values, send, axis, size):
+def sum_all(values, send, axis, size, beside):
     bits = 1
     while bits < size:
         got = exchange(send, axis, size, 2 * bits - 1)
+        if bits == 1:
+            got, beside = lax.optimization_barrier((got, beside))
         bits *= 2
         if bits < size:
             values = values + got.astype(f32)
             send = values.astype(bf16)
-    return values, got
+    return values, got, beside
 
 
 def shards(
@@ -649,7 +652,7 @@
     lay = Rows(x_weight.shape[1], a_log.shape[0], conv_weight.shape[0])
     maps, width, taps, rank, first = lay.maps, lay.width, lay.taps, lay.rank, lay.first
 
-    pieces = gather_pieces(in_weight.reshape(in_weight.shape[0], 2 * chans), "fsdp", fsdp)
+    even = even_pieces(in_weight.reshape(in_weight.shape[0], 2 * chans), "fsdp", fsdp)
     packed = jnp.concatenate(
         [
             x_weight.T,
@@ -665,48 +668,47 @@
         0,
     )
     gathered = lax.all_gather(packed, "fsdp", axis=0)
-    up, down, gathered = relay(tokens[0], "tp", tp, gathered)
-    token_shards = up[:1] + [jnp.where(tp_me >= k, up[k], down[tp - k]) for k in range(1, tp)]
+    up, down, (gathered, even) = relay(tokens[0], "tp", tp, (gathered, even))
+    pieces = all_pieces(even, "fsdp", fsdp)
+    token_shards = up + down[1:]
+    source = jnp.where(chunks <= tp_me, tp_me - chunks, chunks - tp_me + tp - 1).astype(jnp.int32)
     small = gathered[:, : lay.count].transpose(1, 0, 2).reshape(lay.count, chans)
     dt_rows = dt_weight.size // part
     dt_w = gathered[:, lay.count : lay.count + dt_rows].reshape(rank, chans)
     gain = gathered[:, lay.count + dt_rows :].reshape(1, depth).astype(f32)
     out_w = lax.all_gather(out_weight, "fsdp", axis=1, tiled=True)
-    token_shards, held = lax.optimization_barrier((token_shards, cotangent[0]))
+
+    normed, w, conv_in, gate, conv_sum, low, map_part, map_send = front(
+        lay, source, place, token_shards, gain, small, pieces
+    )
+    map_send, held = lax.optimization_barrier((map_send, cotangent[0]))
     grad_whole = lax.all_gather(held, "tp", axis=0, tiled=True)
-
-    normed, w, conv_in, gate, conv_sum, low, map_part, map_send = front(
-        lay, order, place, token_shards, gain, small, pieces
-    )
-    own, got = sum_all(map_part, map_send, "tp", tp)
-    mixed, before, step, h, sent = forward(
+    own, got, _ = sum_all(map_part, map_send, "tp", tp, ())
+    mixed, before, step, h, *sent = forward(
         lay, lengths, slot, own, got, low, gate, dt_w, small, out_w
     )
+    sent, grad_whole = lax.optimization_barrier((sent, grad_whole))
     block_terms = chunk_terms(sent, "tp", tp)
-    out_grad = dot(grad_whole, mixed, TN).astype(bf16)
 
     map_part, map_send, conv_grad, gate_grad, rate_grad, dt_w_grad, bias_grad = backward(
         lay, lengths, own, got, low, gate, before, step, grad_whole, h, dt_w, small, out_w
     )
-    map_part, map_send, block_terms[0] = lax.optimization_barrier(
-        (map_part, map_send, block_terms[0])
-    )
-    own_grad, got_grad = sum_all(map_part, map_send, "tp", tp)
+    map_part, map_send, block_terms = lax.optimization_barrier((map_part, map_send, block_terms))
+    own_grad, got_grad, held = sum_all(map_part, map_send, "tp", tp, gate_grad)
+    pair = [
+        dot(a, b, TN).reshape(fsdp, 1, -1, chans)
+        for a, b in ((normed, held), (grad_whole, mixed))
+    ]
+    gate_half, out_weight_grad = lax.psum_scatter(
+        jnp.concatenate(pair, 1).astype(bf16), "fsdp", scatter_dimension=0, tiled=False
+    )
     block_out = (tokens.astype(f32) + total(block_terms)[None]).astype(bf16)
-    gate_weight = dot(normed, gate_grad, TN).astype(bf16)
-    out_terms = chip_terms(pair_sum(out_grad.reshape(fsdp, -1, chans), "fsdp", fsdp), "fsdp", fsdp)
-    gate_terms = chip_terms(
-        pair_sum(gate_weight.reshape(fsdp, -1, chans), "fsdp", fsdp), "fsdp", fsdp
-    )
-    own_grad, got_grad, block_out, out_terms, gate_terms = lax.optimization_barrier(
-        (own_grad, got_grad, block_out, out_terms, gate_terms)
-    )
-    sent_back, conv_weight_half, x_w_grad, taps_grad, gain_grad = back(
-        lay, slot, order, own_grad, got_grad, small, conv_grad, conv_sum, conv_in, low,
-        gate_grad, normed, w, token_shards,
-    )
-    normed_grad = total(chain_terms(sent_back, "tp", tp))
-    conv_pairs = pair_sum(conv_weight_half.reshape(fsdp, -1, chans), "fsdp", fsdp)
+    own_grad, got_grad, block_out = lax.optimization_barrier((own_grad, got_grad, block_out))
+    *sent_back, keep, send, x_w_grad, taps_grad = back(
+        lay, slot, place, own_grad, got_grad, small, conv_grad, conv_sum, conv_in, low,
+        gate_grad, normed, w,
+    )
+    conv_half = total(chip_terms(pair_sum(keep, send, "fsdp", fsdp), "fsdp", fsdp))
     rows = jnp.concatenate(
         [x_w_grad, rate_grad * LN2, taps_grad[: taps + 1], bias_grad[:2]], 0
     ).astype(bf16)
@@ -715,19 +717,23 @@
         [
             rows.reshape(top, fsdp, part).transpose(1, 0, 2),
             dt_w_grad.astype(bf16).reshape(fsdp, -1, part),
-            gain_grad.astype(bf16).reshape(fsdp, -1, part),
         ],
         1,
-    )
-    small_grad = total(chip_terms(pair_sum(packed, "fsdp", fsdp), "fsdp", fsdp))
-    gain_out = small_grad[top + dt_rows :].reshape(-1, 2 * part)
+    )[place]
+    pairs = pair_sum(packed[0::2], packed[1::2], "fsdp", fsdp)
+    small_grad = total(chip_terms(pairs, "fsdp", fsdp))
+    chain, (small_grad, gate_half, out_weight_grad) = chain_terms(
+        sent_back, "tp", tp, (small_grad, gate_half, out_weight_grad)
+    )
+    normed_grad = total(chain)
+    in_weight_grad = jnp.stack([conv_half, gate_half.astype(f32)], 1)
+    out_weight_grad = out_weight_grad.astype(f32).T
+    gain_out = jnp.sum(in_weight_grad * in_weight.astype(f32), axis=(1, 2), keepdims=True)
+    gain_out = (gain_out[:, 0] / norm_gain.astype(f32)[:, None]).reshape(1, -1)
     bits = 1
     while bits < tp:
         gain_out = gain_out + exchange(gain_out, "tp", tp, 2 * bits - 1)
         bits *= 2
-    out_weight_grad = total(out_terms).T
-    conv_terms = chip_terms(conv_pairs, "fsdp", fsdp)
-    in_weight_grad = jnp.stack([total(conv_terms), total(gate_terms)], 1)
 
     own_values = tokens.astype(f32)
     own_inverse = lax.rsqrt(jnp.mean(own_values * own_values, axis=-1, keepdims=True) + epsilon)

time: 300 us -> 283 us (0.943)
  local copies, waits for them, and re-layouts: 32.7 us -> 23.4 us
  starting transfers between devices: 65.8 us -> 56.9 us
  other arithmetic: 23.7 us -> 16.9 us
  waiting for transfers between devices: 61.2 us -> 67.6 us
    ppermute x29 -> x21, waiting for transfers between devices: 25.1 us -> 35 us  [exchange(): return lax.ppermute(values, axis, [(i, i ^ bits) for i in range(size)])]
    squeeze x10 -> x2, local copies, waits for them, and re-layouts: 7.03 us -> 0.04 us  [chip_terms(): summed[m]]
    ppermute x3, waiting for transfers between devices: 19.7 us -> 13.3 us  [relay(): lax.ppermute(down[-1], axis, [(size - 1 - i, size - 2 - i) for i in pairs])]
    ppermute x3, waiting for transfers between devices: 7.2 us -> 13.5 us  [chain_terms(): up = lax.ppermute(up, axis, [(i, i + 1) for i in range(hop)])]
    ppermute x3, starting transfers between devices: 13.6 us -> 8.38 us  [chunk_terms(): lax.ppermute(sent[s], axis, [(i, (i + s) % size) for i in range(size)])]
    ppermute x3, waiting for transfers between devices: 4.16 us -> 0.01 us  [chain_terms(): lax.ppermute(down, axis, [(size - 1 - i, size - 2 - i) for i in range(hop)])]
    ppermute x29 -> x21, starting transfers between devices: 21.4 us -> 20 us  [exchange(): return lax.ppermute(values, axis, [(i, i ^ bits) for i in range(size)])]
    unnamed x50 -> x49, local copies, waits for them, and re-layouts: 9.46 us -> 8.04 us
  transfers between devices with their start and end apart: 46 -> 39, of which waited for: 13 -> 13; matrix products, arithmetic and copies ran while one was open for 17% -> 13% of each run, Pallas kernels for 24% -> 31%
where the time goes in v4:
time: 283 us; the launch traced here: 282 us
  Pallas kernels  87.7 us (31%)
  waiting for transfers between devices  67.6 us (24%)
  starting transfers between devices  56.9 us (20%)
  local copies, waits for them, and re-layouts  23.4 us (8%)
  other arithmetic  16.9 us (6%)
  between operations  15 us (5%)
  blocking collectives  9.76 us (3%)
  matrix products  4.57 us (2%)
    pallas_call x1, Pallas kernels, backward(): pl.pallas_call(functools.partial(backward_kernel, lay), grid_spec=pltpu.P...  39.4 us
    ppermute x21, waiting for transfers between devices, exchange(): return lax.ppermute(values, axis, [(i, i ^ bits) for i in range(size)])  35 us
    pallas_call x1, Pallas kernels, forward(): pl.pallas_call(functools.partial(forward_kernel, lay, count), grid_spec=p...  23.9 us
    ppermute x21, starting transfers between devices, exchange(): return lax.ppermute(values, axis, [(i, i ^ bits) for i in range(size)])  20 us
    pallas_call x1, Pallas kernels, back(): pl.pallas_call(functools.partial(back_kernel, lay, count), grid_spec=pltp...  13.5 us
    ppermute x3, waiting for transfers between devices, chain_terms(): up = lax.ppermute(up, axis, [(i, i + 1) for i in range(hop)])  13.5 us
    ppermute x3, starting transfers between devices, chain_terms(): up = lax.ppermute(up, axis, [(i, i + 1) for i in range(hop)])  13.4 us
    ppermute x3, waiting for transfers between devices, relay(): lax.ppermute(down[-1], axis, [(size - 1 - i, size - 2 - i) for i in pairs])  13.3 us
  transfers between devices with their start and end apart: 39, of which 13 were waited for; matrix products, arithmetic and copies ran while one was open for 13% of the time, Pallas kernels for 31%

profile of v4, /device:TPU:0, one launch (start us, length us, event | category | flops | bytes accessed | tf_op | source)
XLA Modules:
  0.0 282.0 jit_solution(67771314274507403)
XLA Ops:
  7.2 1.3 collective-permute-start.1
  8.5 5.6 %collective-permute-start = (bf16[256,1024]{1,0:T(8,128)(2,1)}, bf16[256,1024]{1,0:T(8,128)(2,1)S(1)}, u32[]{:S(2)}, u32[]{:S(2)}) collective-permute-start(bf16[256,1024]{1,0:T(8,128)(2,1)} %bitcast.71), channel_id=1, source_target_pairs={{0,1},{1,2},{2,3},{4,5},{5,6},{6,7},{8,9},{9,10},{10,11},{12,13},{... | collective-permute-start | bytes 1572872 | tf_op jit(solution)/shard_map/ppermute | solution.py:576
  20.6 9.8 %all-gather.1 = bf16[8,194,64]{1,2,0:T(8,128)(2,1)S(1)} all-gather(bf16[1,194,64]{1,2,0:T(8,128)(2,1)S(1)} %bitcast.87), channel_id=2, replica_groups=mesh['fsdp'=8,'tp'=4] {'fsdp'}, dimensions={0}, use_global_device_ids=true | all-gather | bytes 223488 | tf_op jit(solution)/shard_map/all_gather | solution.py:670
  31.0 1.3 collective-permute-start.3
  32.4 1.0 copy.142
  33.4 1.5 collective-permute-start.6
  35.0 1.5 collective-permute-start.5
  37.0 6.6 %collective-permute-done.6.refs_13_ = bf16[128,1024]{1,0:T(8,128)(2,1)S(1)} collective-permute-done((bf16[128,1024]{1,0:T(8,128)(2,1)S(1)}, bf16[128,1024]{1,0:T(8,128)(2,1)S(1)}, u32[]{:S(2)}, u32[]{:S(2)}) %collective-permute-start.6) | collective-permute-done | bytes 262176 | tf_op jit(solution)/shard_map/ppermute | solution.py:568
  43.6 6.5 %collective-permute-done.5.refs_11_ = bf16[128,1024]{1,0:T(8,128)(2,1)} collective-permute-done((bf16[128,1024]{1,0:T(8,128)(2,1)S(1)}, bf16[128,1024]{1,0:T(8,128)(2,1)}, u32[]{:S(2)}, u32[]{:S(2)}) %collective-permute-start.5) | collective-permute-done | bytes 262176 | tf_op jit(solution)/shard_map/ppermute | solution.py:568
  50.2 1.5 collective-permute-start.7
  51.7 1.3 collective-permute-start.8
  57.0 13.3 %collective-permute-done.8.refs_6_ = bf16[256,1024]{1,0:T(8,128)(2,1)} collective-permute-done((bf16[256,1024]{1,0:T(8,128)(2,1)S(1)}, bf16[256,1024]{1,0:T(8,128)(2,1)}, u32[]{:S(2)}, u32[]{:S(2)}) %collective-permute-start.8) | collective-permute-done | bytes 524320 | tf_op jit(solution)/shard_map/ppermute | solution.py:577
  70.4 10.9 %front.1 = (bf16[1024,1024]{1,0:T(8,128)(2,1)}, bf16[1024,1024]{1,0:T(8,128)(2,1)}, f32[1024,512]{1,0:T(8,128)}, f32[1024,512]{1,0:T(8,128)}, f32[1024,512]{1,0:...) custom-call(s32[4]{0:T(128)} %compare_select_fusion.3.order, ...), custom_call_target="tpu_custom_call" | custom-call | flops 8999999488 | bytes 27000000 | tf_op jit(solution)/shard_map/front/pallas_call | solution.py:179
  82.6 5.7 %collective-permute-done.13 = bf16[96,1024]{1,0:T(8,128)(2,1)S(1)} collective-permute-done((bf16[96,1024]{1,0:T(8,128)(2,1)}, bf16[96,1024]{1,0:T(8,128)(2,1)S(1)}, u32[]{:S(2)}, u32[]{:S(2)}) %collective-permute-start.13) | collective-permute-done | bytes 196640 | tf_op jit(solution)/shard_map/ppermute | solution.py:568
  88.4 1.8 fusion.17
  90.2 1.2 collective-permute-start.14
  92.5 10.8 %collective-permute-done.14.got = bf16[96,1024]{1,0:T(8,128)(2,1)S(1)} collective-permute-done((bf16[96,1024]{1,0:T(8,128)(2,1)S(1)}, bf16[96,1024]{1,0:T(8,128)(2,1)S(1)}, u32[]{:S(2)}, u32[]{:S(2)}) %collective-permute-start.14) | collective-permute-done | bytes 196640 | tf_op jit(solution)/shard_map/ppermute | solution.py:568
  104.0 23.9 %forward.1 = (bf16[1024,512]{1,0:T(8,128)(2,1)}, f32[1024,512]{1,0:T(8,128)}, f32[1024,512]{1,0:T(8,128)}, bf16[16384,512]{1,0:T(8,128)(2,1)}, bf16[256,1024]{1,...) custom-call(s32[1]{0:T(128)S(6)} %copy.144.length, ...), custom_call_target="tpu_custom_call" | custom-call | flops 24000000000 | bytes 72000000 | tf_op jit(solution)/shard_map/forward/pallas_call | solution.py:287
  127.9 5.7 %all-gather.7.cloned.1.call-done.grad = bf16[1024,1024]{1,0:T(8,128)(2,1)} async-done(((bf16[256,1024]{1,0:T(8,128)(2,1)}), bf16[1024,1024]{1,0:T(8,128)(2,1)}) %all-gather.7.cloned.1.call-update) | async-done | bytes 2097168 | tf_op jit(solution)/shard_map/all_gather | solution.py:685
  133.6 4.8 %collective-permute-start.15 = (bf16[256,1024]{1,0:T(8,128)(2,1)}, bf16[256,1024]{1,0:T(8,128)(2,1)S(1)}, u32[]{:S(2)}, u32[]{:S(2)}) collective-permute-start(bf16[256,1024]{1,0:T(8,128)(2,1)} %get-tuple-element.101), channel_id=1, source_target_pairs={{0,1},{1,2},{2,3},{3,0},{4,5},{5,6},{6,7},{7,4},{8,9},{9,10},{10,1... | collective-permute-start | bytes 1572872 | tf_op jit(solution)/shard_map/ppermute | solution.py:617
  139.1 2.8 %collective-permute-start.17 = (bf16[256,1024]{1,0:T(8,128)(2,1)}, bf16[256,1024]{1,0:T(8,128)(2,1)S(1)}, u32[]{:S(2)}, u32[]{:S(2)}) collective-permute-start(bf16[256,1024]{1,0:T(8,128)(2,1)} %get-tuple-element.103), channel_id=1, source_target_pairs={{0,3},{1,0},{2,1},{3,2},{4,7},{5,4},{6,5},{7,6},{8,11},{9,8},{10,9... | collective-permute-start | bytes 1572872 | tf_op jit(solution)/shard_map/ppermute | solution.py:617
  142.0 39.4 %backward.1 = (f32[96,1024]{1,0:T(8,128)}, bf16[96,1024]{1,0:T(8,128)(2,1)}, f32[1024,512]{1,0:T(8,128)}, bf16[1024,512]{1,0:T(8,128)(2,1)}, f32[16,512]{1,0:T(8...) custom-call(s32[1]{0:T(128)S(6)} %copy.144.length, f32[96,1024]{1,0:T(8,128)} %get-tuple-element.204.own, ...), custom_call_target="tpu_custom_call" | custom-call | flops 40000000000 | bytes 120000000 | tf_op jit(solution)/shard_map/backward/pallas_call | solution.py:434
  184.5 3.3 %convolution_convert_fusion = bf16[1024,512]{1,0:T(8,128)(2,1)S(1)} fusion(bf16[1024,1024]{1,0:T(8,128)(2,1)} %all-gather.7.cloned.1.call-done.grad, bf16[1024,512]{1,0:T(8,128)(2,1)} %get-tuple-element.130), kind=kOutput, calls=%fused_computation.5 | convolution fusion | flops 1074266112 | bytes 4194304 | tf_op jit(solution)/shard_map/dot_general | solution.py:25
  187.8 2.5 collective-permute-done.18
  191.2 1.5 collective-permute-start.19
  192.7 1.3 convolution_convert_fusion.1
  194.0 1.5 pad_maximum_fusion
  195.5 1.0 copy-done
  196.7 1.3 fusion.7
  198.9 13.5 %back.1 = (bf16[256,1024]{1,0:T(8,128)(2,1)}, bf16[256,1024]{1,0:T(8,128)(2,1)}, bf16[256,1024]{1,0:T(8,128)(2,1)}, bf16[256,1024]{1,0:T(8,128)(2,1)}, bf16[4,12...) custom-call(s32[4]{0:T(128)} %and_select_fusion.slot, ...), custom_call_target="tpu_custom_call" | custom-call | flops 11000000512 | bytes 33000000 | tf_op jit(solution)/shard_map/back/pallas_call | solution.py:540
  216.0 3.8 %collective-permute-start.20 = (bf16[256,1024]{1,0:T(8,128)(2,1)S(1)}, bf16[256,1024]{1,0:T(8,128)(2,1)S(1)}, u32[]{:S(2)}, u32[]{:S(2)}) collective-permute-start(bf16[256,1024]{1,0:T(8,128)(2,1)S(1)} %copy-done.4), channel_id=1, source_target_pairs={{0,1},{4,5},{8,9},{12,13},{16,17},{20,21},{24,25},{28,29}} | collective-permute-start | bytes 1572872 | tf_op jit(solution)/shard_map/ppermute | solution.py:588
  220.6 1.5 collective-permute-start.25
  222.1 2.3 collective-permute-start.27
  225.1 6.1 %collective-permute-done.20 = bf16[256,1024]{1,0:T(8,128)(2,1)S(1)} collective-permute-done((bf16[256,1024]{1,0:T(8,128)(2,1)S(1)}, bf16[256,1024]{1,0:T(8,128)(2,1)S(1)}, u32[]{:S(2)}, u32[]{:S(2)}) %collective-permute-start.20) | collective-permute-done | bytes 524320 | tf_op jit(solution)/shard_map/ppermute | solution.py:588
  231.2 1.4 collective-permute-start.31
  232.7 2.2 collective-permute-start.33
  235.6 1.5 collective-permute-start.23
  237.1 5.0 %collective-permute-start.21 = (bf16[256,1024]{1,0:T(8,128)(2,1)S(1)}, bf16[256,1024]{1,0:T(8,128)(2,1)}, u32[]{:S(2)}, u32[]{:S(2)}) collective-permute-start(bf16[256,1024]{1,0:T(8,128)(2,1)S(1)} %get-tuple-element.213), channel_id=1, source_target_pairs={{0,1},{1,2},{4,5},{5,6},{8,9},{9,10},{12,13},{13,14},{16,17},{17,1... | collective-permute-start | bytes 1572872 | tf_op jit(solution)/shard_map/ppermute | solution.py:588
  243.0 1.0 slice_bitcast_fusion.4
  244.0 7.4 %collective-permute-done.21 = bf16[256,1024]{1,0:T(8,128)(2,1)} collective-permute-done((bf16[256,1024]{1,0:T(8,128)(2,1)S(1)}, bf16[256,1024]{1,0:T(8,128)(2,1)}, u32[]{:S(2)}, u32[]{:S(2)}) %collective-permute-start.21) | collective-permute-done | bytes 524320 | tf_op jit(solution)/shard_map/ppermute | solution.py:588
  251.4 2.1 add.118
  253.4 2.0 add.120
  255.6 2.7 collective-permute-start.34
  258.3 1.3 collective-permute-start.29
  259.6 4.6 %collective-permute-start.28 = (bf16[256,1024]{1,0:T(8,128)(2,1)}, bf16[256,1024]{1,0:T(8,128)(2,1)S(1)}, u32[]{:S(2)}, u32[]{:S(2)}) collective-permute-start(bf16[256,1024]{1,0:T(8,128)(2,1)} %add.118), channel_id=1, source_target_pairs={{0,1},{1,2},{2,3},{4,5},{5,6},{6,7},{8,9},{9,10},{10,11},{12,13},{... | collective-permute-start | bytes 1572872 | tf_op jit(solution)/shard_map/ppermute | solution.py:588
  269.9 1.2 copy.135
  271.9 1.1 collective-permute-done.35
  274.0 1.4 fusion.5
  (159 shorter events, 34.2 us)
Async XLA Ops:
  7.2 85.3 %all-gather.5.cloned.1.call-start = ((), (), s32[]{:S(2)}) async-start(), calls=%async_computation.1 | async-start | bytes 1179648 | tf_op jit(solution)/shard_map/all_gather | solution.py:679
  7.2 23.1 %collective-permute-start.1 = (bf16[256,1024]{1,0:T(8,128)(2,1)}, bf16[256,1024]{1,0:T(8,128)(2,1)S(1)}, u32[]{:S(2)}, u32[]{:S(2)}) collective-permute-start(bf16[256,1024]{1,0:T(8,128)(2,1)} %bitcast.70), channel_id=1, source_target_pairs={{3,2},{2,1},{1,0},{7,6},{6,5},{5,4},{11,10},{10,9},{9,8},{15,14},{... | collective-permute-start | bytes 1572872 | tf_op jit(solution)/shard_map/ppermute | solution.py:577
  8.5 21.8 %collective-permute-start = (bf16[256,1024]{1,0:T(8,128)(2,1)}, bf16[256,1024]{1,0:T(8,128)(2,1)S(1)}, u32[]{:S(2)}, u32[]{:S(2)}) collective-permute-start(bf16[256,1024]{1,0:T(8,128)(2,1)} %bitcast.71), channel_id=1, source_target_pairs={{0,1},{1,2},{2,3},{4,5},{5,6},{6,7},{8,9},{9,10},{10,11},{12,13},{... | collective-permute-start | bytes 1572872 | tf_op jit(solution)/shard_map/ppermute | solution.py:576
  30.3 40.1 %copy-start.11 = (bf16[256,1024]{1,0:T(8,128)(2,1)}, bf16[256,1024]{1,0:T(8,128)(2,1)S(1)}, u32[]{:S(2)}) copy-start(bf16[256,1024]{1,0:T(8,128)(2,1)S(1)} %collective-permute-done.1.refs_4_) | copy-start | bytes 1572868
  30.3 40.1 %copy-start.12 = (bf16[256,1024]{1,0:T(8,128)(2,1)}, bf16[256,1024]{1,0:T(8,128)(2,1)S(1)}, u32[]{:S(2)}) copy-start(bf16[256,1024]{1,0:T(8,128)(2,1)S(1)} %collective-permute-done.refs_1_) | copy-start | bytes 1572868
  30.3 19.8 %collective-permute-start.2 = (bf16[256,1024]{1,0:T(8,128)(2,1)S(1)}, bf16[256,1024]{1,0:T(8,128)(2,1)S(1)}, u32[]{:S(2)}, u32[]{:S(2)}) collective-permute-start(bf16[256,1024]{1,0:T(8,128)(2,1)S(1)} %collective-permute-done.refs_1_), channel_id=1, source_target_pairs={{1,2},{2,3},{5,6},{6,7},{9,10},{10,11},{13,14},{14,15},{17,18},{18... | collective-permute-start | bytes 1572872 | tf_op jit(solution)/shard_map/ppermute | solution.py:576
  31.0 19.1 %collective-permute-start.3 = (bf16[256,1024]{1,0:T(8,128)(2,1)S(1)}, bf16[256,1024]{1,0:T(8,128)(2,1)S(1)}, u32[]{:S(2)}, u32[]{:S(2)}) collective-permute-start(bf16[256,1024]{1,0:T(8,128)(2,1)S(1)} %collective-permute-done.1.refs_4_), channel_id=1, source_target_pairs={{2,1},{1,0},{6,5},{5,4},{10,9},{9,8},{14,13},{13,12},{18,17},{17,1... | collective-permute-start | bytes 1572872 | tf_op jit(solution)/shard_map/ppermute | solution.py:577
  32.4 101.2 %all-gather.7.cloned.1.call-start = ((), (), s32[]{:S(2)}) async-start(), calls=%async_computation.2 | async-start | bytes 2621440 | tf_op jit(solution)/shard_map/all_gather | solution.py:685
  33.4 37.0 %copy-start.10 = (bf16[16,8,2,512]{3,1,2,0:T(8,128)(2,1)}, bf16[16,8,2,512]{3,1,2,0:T(8,128)(2,1)S(1)}, u32[]{:S(2)}) copy-start(bf16[16,8,2,512]{3,1,2,0:T(8,128)(2,1)S(1)} %copy.142) | copy-start | bytes 786436
  33.4 10.1 %collective-permute-start.6 = (bf16[128,1024]{1,0:T(8,128)(2,1)S(1)}, bf16[128,1024]{1,0:T(8,128)(2,1)S(1)}, u32[]{:S(2)}, u32[]{:S(2)}) collective-permute-start(bf16[128,1024]{1,0:T(8,128)(2,1)S(1)} %bitcast.82), channel_id=1, source_target_pairs={{0,24},{4,28},{8,16},{12,20},{16,8},{20,12},{24,0},{28,4},{1,25},{... | collective-permute-start | bytes 786440 | tf_op jit(solution)/shard_map/ppermute | solution.py:568
  35.0 15.1 %collective-permute-start.5 = (bf16[128,1024]{1,0:T(8,128)(2,1)S(1)}, bf16[128,1024]{1,0:T(8,128)(2,1)}, u32[]{:S(2)}, u32[]{:S(2)}) collective-permute-start(bf16[128,1024]{1,0:T(8,128)(2,1)S(1)} %bitcast.83), channel_id=1, source_target_pairs={{0,16},{4,20},{8,24},{12,28},{16,0},{20,4},{24,8},{28,12},{1,17},{... | collective-permute-start | bytes 786440 | tf_op jit(solution)/shard_map/ppermute | solution.py:568
  36.4 13.7 %collective-permute-start.4 = (bf16[128,1024]{1,0:T(8,128)(2,1)S(1)}, bf16[128,1024]{1,0:T(8,128)(2,1)}, u32[]{:S(2)}, u32[]{:S(2)}) collective-permute-start(bf16[128,1024]{1,0:T(8,128)(2,1)S(1)} %bitcast.84), channel_id=1, source_target_pairs={{0,8},{4,12},{8,0},{12,4},{16,24},{20,28},{24,16},{28,20},{1,9},{5... | collective-permute-start | bytes 786440 | tf_op jit(solution)/shard_map/ppermute | solution.py:568
  43.6 26.8 %copy-start.15 = (bf16[128,1024]{1,0:T(8,128)(2,1)}, bf16[128,1024]{1,0:T(8,128)(2,1)S(1)}, u32[]{:S(2)}) copy-start(bf16[128,1024]{1,0:T(8,128)(2,1)S(1)} %collective-permute-done.6.refs_13_) | copy-start | bytes 786436
  50.2 20.3 %copy-start.13 = (bf16[256,1024]{1,0:T(8,128)(2,1)}, bf16[256,1024]{1,0:T(8,128)(2,1)S(1)}, u32[]{:S(2)}) copy-start(bf16[256,1024]{1,0:T(8,128)(2,1)S(1)} %collective-permute-done.2.refs_2_) | copy-start | bytes 1572868
  50.2 20.3 %copy-start.14 = (bf16[256,1024]{1,0:T(8,128)(2,1)}, bf16[256,1024]{1,0:T(8,128)(2,1)S(1)}, u32[]{:S(2)}) copy-start(bf16[256,1024]{1,0:T(8,128)(2,1)S(1)} %collective-permute-done.3.refs_5_) | copy-start | bytes 1572868
  50.2 3.9 %collective-permute-start.9 = (bf16[128,1024]{1,0:T(8,128)(2,1)S(1)}, bf16[128,1024]{1,0:T(8,128)(2,1)S(1)}, u32[]{:S(2)}, u32[]{:S(2)}) collective-permute-start(bf16[128,1024]{1,0:T(8,128)(2,1)S(1)} %bitcast.85), channel_id=1, source_target_pairs={{0,4},{4,0},{8,12},{12,8},{16,20},{20,16},{24,28},{28,24},{1,5},{5... | collective-permute-start | bytes 786440 | tf_op jit(solution)/shard_map/ppermute | solution.py:568
  50.2 6.8 %collective-permute-start.7 = (bf16[256,1024]{1,0:T(8,128)(2,1)S(1)}, bf16[256,1024]{1,0:T(8,128)(2,1)}, u32[]{:S(2)}, u32[]{:S(2)}) collective-permute-start(bf16[256,1024]{1,0:T(8,128)(2,1)S(1)} %collective-permute-done.2.refs_2_), channel_id=1, source_target_pairs={{2,3},{6,7},{10,11},{14,15},{18,19},{22,23},{26,27},{30,31}} | collective-permute-start | bytes 1572872 | tf_op jit(solution)/shard_map/ppermute | solution.py:576
  51.7 18.7 %collective-permute-start.8 = (bf16[256,1024]{1,0:T(8,128)(2,1)S(1)}, bf16[256,1024]{1,0:T(8,128)(2,1)}, u32[]{:S(2)}, u32[]{:S(2)}) collective-permute-start(bf16[256,1024]{1,0:T(8,128)(2,1)S(1)} %collective-permute-done.3.refs_5_), channel_id=1, source_target_pairs={{1,0},{5,4},{9,8},{13,12},{17,16},{21,20},{25,24},{29,28}} | collective-permute-start | bytes 1572872 | tf_op jit(solution)/shard_map/ppermute | solution.py:577
  53.5 3.5 %collective-permute-start.10 = (bf16[128,1024]{1,0:T(8,128)(2,1)}, bf16[128,1024]{1,0:T(8,128)(2,1)}, u32[]{:S(2)}, u32[]{:S(2)}) collective-permute-start(bf16[128,1024]{1,0:T(8,128)(2,1)} %collective-permute-done.4.refs_9_), channel_id=1, source_target_pairs={{0,4},{4,0},{8,12},{12,8},{16,20},{20,16},{24,28},{28,24},{1,5},{5... | collective-permute-start | bytes 786440 | tf_op jit(solution)/shard_map/ppermute | solution.py:568
  54.0 3.0 %collective-permute-start.11 = (bf16[128,1024]{1,0:T(8,128)(2,1)}, bf16[128,1024]{1,0:T(8,128)(2,1)}, u32[]{:S(2)}, u32[]{:S(2)}) collective-permute-start(bf16[128,1024]{1,0:T(8,128)(2,1)} %collective-permute-done.5.refs_11_), channel_id=1, source_target_pairs={{0,4},{4,0},{8,12},{12,8},{16,20},{20,16},{24,28},{28,24},{1,5},{5... | collective-permute-start | bytes 786440 | tf_op jit(solution)/shard_map/ppermute | solution.py:568
  54.0 3.0 %collective-permute-start.12 = (bf16[128,1024]{1,0:T(8,128)(2,1)S(1)}, bf16[128,1024]{1,0:T(8,128)(2,1)}, u32[]{:S(2)}, u32[]{:S(2)}) collective-permute-start(bf16[128,1024]{1,0:T(8,128)(2,1)S(1)} %collective-permute-done.6.refs_13_), channel_id=1, source_target_pairs={{0,4},{4,0},{8,12},{12,8},{16,20},{20,16},{24,28},{28,24},{1,5},{5... | collective-permute-start | bytes 786440 | tf_op jit(solution)/shard_map/ppermute | solution.py:568
  81.3 161.6 %reduce-scatter.2.cloned.1.call-start = ((), (), s32[]{:S(2)}) async-start(), calls=%async_computation.3 | async-start | bytes 2359296 | tf_op jit(solution)/shard_map/reduce_scatter | solution.py:702
  81.4 7.0 %collective-permute-start.13 = (bf16[96,1024]{1,0:T(8,128)(2,1)}, bf16[96,1024]{1,0:T(8,128)(2,1)S(1)}, u32[]{:S(2)}, u32[]{:S(2)}) collective-permute-start(bf16[96,1024]{1,0:T(8,128)(2,1)} %get-tuple-element.86), channel_id=1, source_target_pairs={{0,1},{1,0},{2,3},{3,2},{4,5},{5,4},{6,7},{7,6},{8,9},{9,8},{10,11... | collective-permute-start | bytes 589832 | tf_op jit(solution)/shard_map/ppermute | solution.py:568
  90.2 13.1 %collective-permute-start.14 = (bf16[96,1024]{1,0:T(8,128)(2,1)S(1)}, bf16[96,1024]{1,0:T(8,128)(2,1)S(1)}, u32[]{:S(2)}, u32[]{:S(2)}) collective-permute-start(bf16[96,1024]{1,0:T(8,128)(2,1)S(1)} %get-tuple-element.203), channel_id=1, source_target_pairs={{0,3},{1,2},{2,1},{3,0},{4,7},{5,6},{6,5},{7,4},{8,11},{9,10},{10,... | collective-permute-start | bytes 589832 | tf_op jit(solution)/shard_map/ppermute | solution.py:568
  133.6 50.8 %collective-permute-start.15 = (bf16[256,1024]{1,0:T(8,128)(2,1)}, bf16[256,1024]{1,0:T(8,128)(2,1)S(1)}, u32[]{:S(2)}, u32[]{:S(2)}) collective-permute-start(bf16[256,1024]{1,0:T(8,128)(2,1)} %get-tuple-element.101), channel_id=1, source_target_pairs={{0,1},{1,2},{2,3},{3,0},{4,5},{5,6},{6,7},{7,4},{8,9},{9,10},{10,1... | collective-permute-start | bytes 1572872 | tf_op jit(solution)/shard_map/ppermute | solution.py:617
  138.4 46.0 %collective-permute-start.16 = (bf16[256,1024]{1,0:T(8,128)(2,1)}, bf16[256,1024]{1,0:T(8,128)(2,1)S(1)}, u32[]{:S(2)}, u32[]{:S(2)}) collective-permute-start(bf16[256,1024]{1,0:T(8,128)(2,1)} %get-tuple-element.102), channel_id=1, source_target_pairs={{0,2},{1,3},{2,0},{3,1},{4,6},{5,7},{6,4},{7,5},{8,10},{9,11},{10,... | collective-permute-start | bytes 1572872 | tf_op jit(solution)/shard_map/ppermute | solution.py:617
  139.1 45.3 %collective-permute-start.17 = (bf16[256,1024]{1,0:T(8,128)(2,1)}, bf16[256,1024]{1,0:T(8,128)(2,1)S(1)}, u32[]{:S(2)}, u32[]{:S(2)}) collective-permute-start(bf16[256,1024]{1,0:T(8,128)(2,1)} %get-tuple-element.103), channel_id=1, source_target_pairs={{0,3},{1,0},{2,1},{3,2},{4,7},{5,4},{6,5},{7,6},{8,11},{9,8},{10,9... | collective-permute-start | bytes 1572872 | tf_op jit(solution)/shard_map/ppermute | solution.py:617
  184.4 5.9 %collective-permute-start.18 = (bf16[96,1024]{1,0:T(8,128)(2,1)}, bf16[96,1024]{1,0:T(8,128)(2,1)S(1)}, u32[]{:S(2)}, u32[]{:S(2)}) collective-permute-start(bf16[96,1024]{1,0:T(8,128)(2,1)} %get-tuple-element.105), channel_id=1, source_target_pairs={{0,1},{1,0},{2,3},{3,2},{4,5},{5,4},{6,7},{7,6},{8,9},{9,8},{10,11... | collective-permute-start | bytes 589832 | tf_op jit(solution)/shard_map/ppermute | solution.py:568
  191.2 7.7 %collective-permute-start.19 = (bf16[96,1024]{1,0:T(8,128)(2,1)S(1)}, bf16[96,1024]{1,0:T(8,128)(2,1)}, u32[]{:S(2)}, u32[]{:S(2)}) collective-permute-start(bf16[96,1024]{1,0:T(8,128)(2,1)S(1)} %get-tuple-element.201), channel_id=1, source_target_pairs={{0,3},{1,2},{2,1},{3,0},{4,7},{5,6},{6,5},{7,4},{8,11},{9,10},{10,... | collective-permute-start | bytes 589832 | tf_op jit(solution)/shard_map/ppermute | solution.py:568
  214.9 20.0 %copy-start.6 = (bf16[256,1024]{1,0:T(8,128)(2,1)S(1)}, bf16[256,1024]{1,0:T(8,128)(2,1)}, u32[]{:S(2)}) copy-start(bf16[256,1024]{1,0:T(8,128)(2,1)} %get-tuple-element.122) | copy-start | bytes 1572868
  215.5 5.1 %collective-permute-start.24 = (bf16[4,183,64]{1,2,0:T(8,128)(2,1)S(1)}, bf16[4,183,64]{1,2,0:T(8,128)(2,1)S(1)}, u32[]{:S(2)}, u32[]{:S(2)}) collective-permute-start(bf16[4,183,64]{1,2,0:T(8,128)(2,1)S(1)} %slice.76), channel_id=1, source_target_pairs={{0,4},{4,0},{8,12},{12,8},{16,20},{20,16},{24,28},{28,24},{1,5},{5... | collective-permute-start | bytes 281096 | tf_op jit(solution)/shard_map/ppermute | solution.py:568
  215.5 8.9 %collective-permute-start.30 = (bf16[4,128,512]{2,1,0:T(8,128)(2,1)}, bf16[4,128,512]{2,1,0:T(8,128)(2,1)S(1)}, u32[]{:S(2)}, u32[]{:S(2)}) collective-permute-start(bf16[4,128,512]{2,1,0:T(8,128)(2,1)} %get-tuple-element.134), channel_id=1, source_target_pairs={{0,4},{4,0},{8,12},{12,8},{16,20},{20,16},{24,28},{28,24},{1,5},{5... | collective-permute-start | bytes 1572872 | tf_op jit(solution)/shard_map/ppermute | solution.py:568
  216.0 15.2 %collective-permute-start.20 = (bf16[256,1024]{1,0:T(8,128)(2,1)S(1)}, bf16[256,1024]{1,0:T(8,128)(2,1)S(1)}, u32[]{:S(2)}, u32[]{:S(2)}) collective-permute-start(bf16[256,1024]{1,0:T(8,128)(2,1)S(1)} %copy-done.4), channel_id=1, source_target_pairs={{0,1},{4,5},{8,9},{12,13},{16,17},{20,21},{24,25},{28,29}} | collective-permute-start | bytes 1572872 | tf_op jit(solution)/shard_map/ppermute | solution.py:588
  219.9 12.8 %collective-permute-start.22 = (bf16[256,1024]{1,0:T(8,128)(2,1)S(1)}, bf16[256,1024]{1,0:T(8,128)(2,1)S(1)}, u32[]{:S(2)}, u32[]{:S(2)}) collective-permute-start(bf16[256,1024]{1,0:T(8,128)(2,1)S(1)} %copy-done.5), channel_id=1, source_target_pairs={{3,2},{7,6},{11,10},{15,14},{19,18},{23,22},{27,26},{31,30}} | collective-permute-start | bytes 1572872 | tf_op jit(solution)/shard_map/ppermute | solution.py:589
  220.6 14.4 %collective-permute-start.25 = (bf16[183,64]{0,1:T(8,128)(2,1)S(1)}, bf16[183,64]{0,1:T(8,128)(2,1)S(1)}, u32[]{:S(2)}, u32[]{:S(2)}) collective-permute-start(bf16[183,64]{0,1:T(8,128)(2,1)S(1)} %get-tuple-element.216), channel_id=1, source_target_pairs={{0,8},{4,12},{8,0},{12,4},{16,24},{20,28},{24,16},{28,20},{1,9},{5... | collective-permute-start | bytes 70280 | tf_op jit(solution)/shard_map/ppermute | solution.py:568
  222.1 13.5 %collective-permute-start.27 = (bf16[183,64]{0,1:T(8,128)(2,1)S(1)}, bf16[183,64]{0,1:T(8,128)(2,1)S(1)}, u32[]{:S(2)}, u32[]{:S(2)}) collective-permute-start(bf16[183,64]{0,1:T(8,128)(2,1)S(1)} %get-tuple-element.217), channel_id=1, source_target_pairs={{0,24},{4,28},{8,16},{12,20},{16,8},{20,12},{24,0},{28,4},{1,25},{... | collective-permute-start | bytes 70280 | tf_op jit(solution)/shard_map/ppermute | solution.py:568
  224.4 12.7 %collective-permute-start.26 = (bf16[183,64]{0,1:T(8,128)(2,1)S(1)}, bf16[183,64]{0,1:T(8,128)(2,1)S(1)}, u32[]{:S(2)}, u32[]{:S(2)}) collective-permute-start(bf16[183,64]{0,1:T(8,128)(2,1)S(1)} %get-tuple-element.218), channel_id=1, source_target_pairs={{0,16},{4,20},{8,24},{12,28},{16,0},{20,4},{24,8},{28,12},{1,17},{... | collective-permute-start | bytes 70280 | tf_op jit(solution)/shard_map/ppermute | solution.py:568
  231.2 10.9 %collective-permute-start.31 = (bf16[128,512]{1,0:T(8,128)(2,1)S(1)}, bf16[128,512]{1,0:T(8,128)(2,1)S(1)}, u32[]{:S(2)}, u32[]{:S(2)}) collective-permute-start(bf16[128,512]{1,0:T(8,128)(2,1)S(1)} %get-tuple-element.207), channel_id=1, source_target_pairs={{0,8},{4,12},{8,0},{12,4},{16,24},{20,28},{24,16},{28,20},{1,9},{5... | collective-permute-start | bytes 393224 | tf_op jit(solution)/shard_map/ppermute | solution.py:568
  232.7 10.2 %collective-permute-start.33 = (bf16[128,512]{1,0:T(8,128)(2,1)S(1)}, bf16[128,512]{1,0:T(8,128)(2,1)S(1)}, u32[]{:S(2)}, u32[]{:S(2)}) collective-permute-start(bf16[128,512]{1,0:T(8,128)(2,1)S(1)} %get-tuple-element.208), channel_id=1, source_target_pairs={{0,24},{4,28},{8,16},{12,20},{16,8},{20,12},{24,0},{28,4},{1,25},{... | collective-permute-start | bytes 393224 | tf_op jit(solution)/shard_map/ppermute | solution.py:568
  235.0 7.8 %collective-permute-start.32 = (bf16[128,512]{1,0:T(8,128)(2,1)S(1)}, bf16[128,512]{1,0:T(8,128)(2,1)S(1)}, u32[]{:S(2)}, u32[]{:S(2)}) collective-permute-start(bf16[128,512]{1,0:T(8,128)(2,1)S(1)} %get-tuple-element.209), channel_id=1, source_target_pairs={{0,16},{4,20},{8,24},{12,28},{16,0},{20,4},{24,8},{28,12},{1,17},{... | collective-permute-start | bytes 393224 | tf_op jit(solution)/shard_map/ppermute | solution.py:568
  235.6 8.3 %collective-permute-start.23 = (bf16[256,1024]{1,0:T(8,128)(2,1)S(1)}, bf16[256,1024]{1,0:T(8,128)(2,1)}, u32[]{:S(2)}, u32[]{:S(2)}) collective-permute-start(bf16[256,1024]{1,0:T(8,128)(2,1)S(1)} %get-tuple-element.212), channel_id=1, source_target_pairs={{3,2},{2,1},{7,6},{6,5},{11,10},{10,9},{15,14},{14,13},{19,18},{18... | collective-permute-start | bytes 1572872 | tf_op jit(solution)/shard_map/ppermute | solution.py:589
  237.1 14.2 %collective-permute-start.21 = (bf16[256,1024]{1,0:T(8,128)(2,1)S(1)}, bf16[256,1024]{1,0:T(8,128)(2,1)}, u32[]{:S(2)}, u32[]{:S(2)}) collective-permute-start(bf16[256,1024]{1,0:T(8,128)(2,1)S(1)} %get-tuple-element.213), channel_id=1, source_target_pairs={{0,1},{1,2},{4,5},{5,6},{8,9},{9,10},{12,13},{13,14},{16,17},{17,1... | collective-permute-start | bytes 1572872 | tf_op jit(solution)/shard_map/ppermute | solution.py:588
  242.9 12.5 %copy-start.3 = (bf16[128,2,512]{2,1,0:T(2,128)(2,1)S(1)}, bf16[128,2,512]{2,1,0:T(2,128)(2,1)}, u32[]{:S(2)}) copy-start(bf16[128,2,512]{2,1,0:T(2,128)(2,1)} %param.16) | copy-start | bytes 786436
  255.4 18.1 %copy-start.1 = (bf16[256,1024]{1,0:T(8,128)(2,1)S(1)}, bf16[256,1024]{1,0:T(8,128)(2,1)}, u32[]{:S(2)}) copy-start(bf16[256,1024]{1,0:T(8,128)(2,1)} %get-tuple-element.120) | copy-start | bytes 1572868
  255.6 9.9 %collective-permute-start.34 = (f32[1,128]{1,0:T(1,128)S(1)}, f32[1,128]{1,0:T(1,128)S(1)}, u32[]{:S(2)}, u32[]{:S(2)}) collective-permute-start(f32[1,128]{1,0:T(1,128)S(1)} %fusion.15), channel_id=1, source_target_pairs={{0,1},{1,0},{2,3},{3,2},{4,5},{5,4},{6,7},{7,6},{8,9},{9,8},{10,11... | collective-permute-start | bytes 1544 | tf_op jit(solution)/shard_map/ppermute | solution.py:568
  258.3 15.2 %collective-permute-start.29 = (bf16[256,1024]{1,0:T(8,128)(2,1)}, bf16[256,1024]{1,0:T(8,128)(2,1)S(1)}, u32[]{:S(2)}, u32[]{:S(2)}) collective-permute-start(bf16[256,1024]{1,0:T(8,128)(2,1)} %add.120), channel_id=1, source_target_pairs={{3,2},{2,1},{1,0},{7,6},{6,5},{5,4},{11,10},{10,9},{9,8},{15,14},{... | collective-permute-start | bytes 1572872 | tf_op jit(solution)/shard_map/ppermute | solution.py:589
  259.6 13.9 %collective-permute-start.28 = (bf16[256,1024]{1,0:T(8,128)(2,1)}, bf16[256,1024]{1,0:T(8,128)(2,1)S(1)}, u32[]{:S(2)}, u32[]{:S(2)}) collective-permute-start(bf16[256,1024]{1,0:T(8,128)(2,1)} %add.118), channel_id=1, source_target_pairs={{0,1},{1,2},{2,3},{4,5},{5,6},{6,7},{8,9},{9,10},{10,11},{12,13},{... | collective-permute-start | bytes 1572872 | tf_op jit(solution)/shard_map/ppermute | solution.py:588
  265.6 7.5 %collective-permute-start.35 = (f32[1,128]{1,0:T(1,128)S(1)}, f32[1,128]{1,0:T(1,128)S(1)}, u32[]{:S(2)}, u32[]{:S(2)}) collective-permute-start(f32[1,128]{1,0:T(1,128)S(1)} %add.127), channel_id=1, source_target_pairs={{0,3},{1,2},{2,1},{3,0},{4,7},{5,6},{6,5},{7,4},{8,11},{9,10},{10,... | collective-permute-start | bytes 1544 | tf_op jit(solution)/shard_map/ppermute | solution.py:568
  (12 other events, 62.9 us)
Sparse Core Ops, SparseCore 0:
  32.5 28.2 all-gather.4
  81.5 52.0 all-gather.6
  195.6 44.1 reduce-scatter.1

commit v5 on v4

--- a/solution.py
+++ b/solution.py
@@ -120,36 +120,23 @@
         return ref[self.first :, :].astype(f32)
 
 
-def front_kernel(lay, shards, pieces, order, place, gain, small, *refs):
-    token_refs = refs[:shards]
-    piece_refs = refs[shards : shards + pieces]
-    (
-        normed_ref, w_ref, input_ref, gate_ref, sum_ref, low_ref, map_ref, send_ref, halo, tokens,
-    ) = refs[shards + pieces :]
+def front_kernel(
+    lay, tokens, gain, small, w,
+    normed_ref, input_ref, gate_ref, sum_ref, low_ref, map_ref, send_ref, halo,
+):
     rows = tokens.shape[0]
     chans = small.shape[1]
     taps = lay.taps
-    turn = pl.program_id(0)
-
-    @pl.when(turn == 0)
+
+    @pl.when(pl.program_id(0) == 0)
     def _():
-        for index in range(pieces):
-            depth = piece_refs[index].shape[0]
-            start = pl.multiple_of(place[index] * depth, depth)
-            w_ref[pl.ds(start, depth), :] = piece_refs[index][...]
         halo[:8] = jnp.zeros_like(halo[:8])
 
-    for index in range(shards):
-
-        @pl.when(order[turn] == index)
-        def _(index=index):
-            tokens[...] = token_refs[index][...].astype(f32)
-
-    values = tokens[...]
+    values = tokens[...].astype(f32)
     inverse = lax.rsqrt(jnp.mean(values * values, axis=-1, keepdims=True) + epsilon)
     normed = (values * inverse * gain[...]).astype(bf16)
     normed_ref[...] = normed
-    projected = dot(normed, w_ref[...])
+    projected = dot(normed, w[...])
     conv_in = projected[:, :chans]
     input_ref[...] = conv_in
     gate_ref[...] = projected[:, chans:]
@@ -168,35 +155,19 @@
     send_ref[...] = mapped.astype(bf16)
 
 
-def front(lay, order, place, shards, gain, small, pieces):
-    rows, depth = shards[0].shape
-    count = order.shape[0]
-    total = count * rows
+def front(lay, tokens, gain, small, w):
+    total, depth = tokens.shape
+    rows = 256
     chans = small.shape[1]
-    row = lambda w: pl.BlockSpec((rows, w), lambda i, *_: (i, 0))
-    column = lambda w: pl.BlockSpec((w, rows), lambda i, *_: (0, i))
-    both = pieces[0].shape[1]
+    row = lambda w: pl.BlockSpec((rows, w), lambda i: (i, 0))
+    column = lambda w: pl.BlockSpec((w, rows), lambda i: (0, i))
     return pl.pallas_call(
-        functools.partial(front_kernel, lay, len(shards), len(pieces)),
-        grid_spec=pltpu.PrefetchScalarGridSpec(
-            num_scalar_prefetch=2,
-            grid=(count,),
-            in_specs=[full(a) for a in (gain, small, *shards, *pieces)],
-            out_specs=[
-                row(depth),
-                pl.BlockSpec((depth, both), lambda i, *_: (0, 0)),
-                row(chans),
-                row(chans),
-                row(chans),
-                row(chans),
-                column(lay.maps),
-                column(lay.maps),
-            ],
-            scratch_shapes=[pltpu.VMEM((rows + 8, chans), f32), pltpu.VMEM((rows, depth), f32)],
-        ),
+        functools.partial(front_kernel, lay),
+        grid=(total // rows,),
+        in_specs=[row(depth)] + [full(a) for a in (gain, small, w)],
+        out_specs=[row(depth)] + [row(chans)] * 4 + [column(lay.maps)] * 2,
         out_shape=[
             shape((total, depth), bf16),
-            shape((depth, both), bf16),
             shape((total, chans), f32),
             shape((total, chans), f32),
             shape((total, chans), f32),
@@ -204,18 +175,17 @@
             shape((lay.maps, total), f32),
             shape((lay.maps, total), bf16),
         ],
+        scratch_shapes=[pltpu.VMEM((rows + 8, chans), f32)],
         compiler_params=params(),
         cost_estimate=cost(9),
         name="front",
-    )(order, place, gain, small, *shards, *pieces)
+    )(tokens, gain, small, w)
 
 
 def forward_kernel(
-    lay, count, length, slot, own, got, low, gate, dt_w, small, out_w,
-    mixed_ref, before_ref, step_ref, h_ref, *refs,
+    lay, length, own, got, low, gate, dt_w, small, out_w,
+    mixed_ref, before_ref, step_ref, h_ref, sent_ref, state, drive, lanes, step_rows, drive_rows,
 ):
-    sent_refs = refs[:count]
-    state, drive, lanes, step_rows, drive_rows = refs[count:]
     rows, chans = low.shape
     width, rank, taps = lay.width, lay.rank, lay.taps
     half = width // 2
@@ -266,28 +236,19 @@
     gates = gate[...]
     mixed = (before * (gates * jax.nn.sigmoid(gates)) * live).astype(bf16)
     mixed_ref[...] = mixed
-    part = dot(mixed, out_w[...]).astype(bf16)
-    blocks = sent_refs[0].shape[0] // rows
-    turn = pl.program_id(0)
-    for index in range(count):
-
-        @pl.when(slot[turn // blocks] == index)
-        def _(index=index):
-            sent_refs[index][pl.ds(pl.multiple_of(turn % blocks * rows, rows), rows), :] = part
-
-
-def forward(lay, length, slot, own, got, low, gate, dt_w, small, out_w):
+    sent_ref[...] = dot(mixed, out_w[...]).astype(bf16)
+
+
+def forward(lay, length, own, got, low, gate, dt_w, small, out_w):
     total, chans = low.shape
-    count = slot.shape[0]
-    part = total // count
     depth = out_w.shape[1]
     width = lay.width
     row = lambda w: pl.BlockSpec((ROWS, w), lambda i, *_: (i, 0))
     column = lambda w: pl.BlockSpec((w, ROWS), lambda i, *_: (0, i))
     return pl.pallas_call(
-        functools.partial(forward_kernel, lay, count),
+        functools.partial(forward_kernel, lay),
         grid_spec=pltpu.PrefetchScalarGridSpec(
-            num_scalar_prefetch=2,
+            num_scalar_prefetch=1,
             grid=(total // ROWS,),
             in_specs=[column(lay.maps), column(lay.maps), row(chans), row(chans)]
             + [full(a) for a in (dt_w, small, out_w)],
@@ -296,8 +257,8 @@
                 row(chans),
                 row(chans),
                 pl.BlockSpec((ROWS * width, chans), lambda i, *_: (i, 0)),
-            ]
-            + [pl.BlockSpec((part, depth), lambda i, *_: (0, 0))] * count,
+                row(depth),
+            ],
             scratch_shapes=[
                 pltpu.VMEM((width, chans), f32),
                 pltpu.VMEM((ROWS, chans), f32),
@@ -311,12 +272,12 @@
             shape((total, chans), f32),
             shape((total, chans), f32),
             shape((total * width, chans), bf16),
-        ]
-        + [shape((part, depth), bf16)] * count,
+            shape((total, depth), bf16),
+        ],
         compiler_params=params(),
         cost_estimate=cost(24),
         name="forward",
-    )(length, slot, own, got, low, gate, dt_w, small, out_w)
+    )(length, own, got, low, gate, dt_w, small, out_w)
 
 
 def backward_kernel(
@@ -472,10 +433,9 @@
 
 
 def back_kernel(
-    lay, count, slot, place, own, got, small, out_grad, conv_sum, conv_in, low, gate_grad, normed, w, *refs
+    lay, own, got, small, out_grad, conv_sum, conv_in, low, gate_grad, w,
+    part_ref, input_ref, x_ref, conv_ref, halo,
 ):
-    part_refs = refs[:count]
-    keep_ref, send_ref, x_ref, conv_ref, halo, total = refs[count:]
     rows, chans = low.shape
     taps = lay.taps
     turn = pl.program_id(0)
@@ -483,7 +443,7 @@
     @pl.when(turn == 0)
     def _():
         halo[rows:] = jnp.zeros_like(halo[rows:])
-        for ref in (total, x_ref, conv_ref):
+        for ref in (x_ref, conv_ref):
             ref[...] = jnp.zeros_like(ref)
 
     rest = lay.rest(small)
@@ -505,94 +465,115 @@
         conv_ref[tap : tap + 1] += jnp.sum(inputs * moved, axis=0, keepdims=True)
     halo[rows:] = sum_grad[:8]
     input_grad = input_grad.astype(bf16)
-    total[...] += dot(normed[...], input_grad, TN)
+    input_ref[...] = input_grad
     part = dot(jnp.concatenate([input_grad, gate_grad[...]], 1), w[...], NT)
-    for index in range(count):
-
-        @pl.when(slot[pl.num_programs(0) - 1 - turn] == index)
-        def _(index=index):
-            part_refs[index][...] = part.astype(bf16)
-
-    @pl.when(turn == pl.num_programs(0) - 1)
-    def _():
-        depth = keep_ref.shape[1]
-        for index in range(2 * keep_ref.shape[0]):
-            start = pl.multiple_of(place[index] * depth, depth)
-            values = total[pl.ds(start, depth), :].astype(bf16)
-            (send_ref if index % 2 else keep_ref)[index // 2] = values
-
-
-def back(lay, slot, place, own, got, small, out_grad, conv_sum, conv_in, low, gate_grad, normed, w):
-    chans = low.shape[1]
-    count = slot.shape[0]
-    total, depth = normed.shape
-    rows = total // count
+    part_ref[...] = part.astype(bf16)
+
+
+def back(lay, own, got, small, out_grad, conv_sum, conv_in, low, gate_grad, w):
+    total, chans = low.shape
+    depth = w.shape[0]
+    rows = 256
+    count = total // rows
     at = lambda i: count - 1 - i
-    row = lambda a: pl.BlockSpec((rows, a.shape[1]), lambda i, *_: (at(i), 0))
-    column = lambda a: pl.BlockSpec((a.shape[0], rows), lambda i, *_: (0, at(i)))
-    half = place.shape[0] // 2
-    outs = [shape((rows, depth), bf16)] * count + [
-        shape((half, depth // half // 2, chans), bf16),
-        shape((half, depth // half // 2, chans), bf16),
+    row = lambda a: pl.BlockSpec((rows, a.shape[1]), lambda i: (at(i), 0))
+    column = lambda a: pl.BlockSpec((a.shape[0], rows), lambda i: (0, at(i)))
+    outs = [
+        shape((total, depth), bf16),
+        shape((total, chans), bf16),
         shape((lay.maps, chans), f32),
         shape((8, chans), f32),
     ]
     return pl.pallas_call(
-        functools.partial(back_kernel, lay, count),
+        functools.partial(back_kernel, lay),
+        grid=(count,),
+        in_specs=[
+            column(own),
+            column(got),
+            full(small),
+            row(out_grad),
+            row(conv_sum),
+            row(conv_in),
+            row(low),
+            row(gate_grad),
+            full(w),
+        ],
+        out_specs=[row(outs[0]), row(outs[1]), full(outs[2]), full(outs[3])],
+        out_shape=outs,
+        scratch_shapes=[pltpu.VMEM((rows + 8, chans), f32)],
+        compiler_params=params(),
+        cost_estimate=cost(11),
+        name="back",
+    )(own, got, small, out_grad, conv_sum, conv_in, low, gate_grad, w)
+
+
+def weights_kernel(pairs, half, place, *refs):
+    lefts, rights = refs[:pairs], refs[pairs : 2 * pairs]
+    w, keep_ref, send_ref, gain_ref, total = refs[2 * pairs :]
+    chans = rights[0].shape[1]
+    depth = keep_ref.shape[2]
+    for i in range(pairs):
+        values = dot(lefts[i][...], rights[i][...], TN)
+        total[...] = values
+        if i == 0:
+            product = values * w[:, half * chans : (half + 1) * chans].astype(f32)
+            gain_ref[...] = dot(jnp.ones((8, chans), bf16), product.astype(bf16), NT)
+        for index in range(2 * keep_ref.shape[0]):
+            start = pl.multiple_of(place[index] * depth, depth)
+            piece = total[pl.ds(start, depth), :].astype(bf16)
+            (send_ref if index % 2 else keep_ref)[index // 2, i] = piece
+
+
+def weights(place, half, lefts, rights, w):
+    depth = w.shape[0]
+    chans = rights[0].shape[1]
+    size = place.shape[0]
+    piece = shape((size // 2, len(lefts), depth // size, chans), bf16)
+    outs = [piece, piece, shape((8, depth), f32)]
+    return pl.pallas_call(
+        functools.partial(weights_kernel, len(lefts), half),
         grid_spec=pltpu.PrefetchScalarGridSpec(
-            num_scalar_prefetch=2,
-            grid=(count,),
-            in_specs=[
-                column(own),
-                column(got),
-                full(small),
-                row(out_grad),
-                row(conv_sum),
-                row(conv_in),
-                row(low),
-                row(gate_grad),
-                row(normed),
-                full(w),
-            ],
+            num_scalar_prefetch=1,
+            grid=(1,),
+            in_specs=[full(a) for a in (*lefts, *rights, w)],
             out_specs=[full(a) for a in outs],
-            scratch_shapes=[pltpu.VMEM((rows + 8, chans), f32), pltpu.VMEM((depth, chans), f32)],
+            scratch_shapes=[pltpu.VMEM((depth, chans), f32)],
         ),
         out_shape=outs,
         compiler_params=params(),
-        cost_estimate=cost(11),
-        name="back",
-    )(slot, place, own, got, small, out_grad, conv_sum, conv_in, low, gate_grad, normed, w)
+        cost_estimate=cost(3 * len(lefts)),
+        name="weights",
+    )(place, *lefts, *rights, w)
+
+
+def last_kernel(tokens, grad, normed_grad, gain, out_ref):
+    values = tokens[...].astype(f32)
+    inverse = lax.rsqrt(jnp.mean(values * values, axis=-1, keepdims=True) + epsilon)
+    hat = values * inverse
+    scaled = normed_grad[...].astype(f32) * gain[...]
+    out_ref[...] = grad[...].astype(f32) + inverse * (
+        scaled - hat * jnp.mean(scaled * hat, axis=-1, keepdims=True)
+    )
+
+
+def last(tokens, grad, normed_grad, gain):
+    total, depth = tokens.shape
+    rows = min(128, total)
+    row = pl.BlockSpec((rows, depth), lambda i: (i, 0))
+    return pl.pallas_call(
+        last_kernel,
+        grid=(total // rows,),
+        in_specs=[row, row, row, full(gain)],
+        out_specs=row,
+        out_shape=shape((total, depth), f32),
+        compiler_params=params(),
+        cost_estimate=cost(2),
+        name="last",
+    )(tokens, grad, normed_grad, gain)
 
 
 def exchange(values, axis, size, bits):
     return lax.ppermute(values, axis, [(i, i ^ bits) for i in range(size)])
-
-
-def relay(values, axis, size, beside):
-    up, down = [values], [values]
-    beside = list(beside)
-    for hop in range(1, size):
-        pairs = range(hop - 1, size - 1)
-        up.append(lax.ppermute(up[-1], axis, [(i, i + 1) for i in pairs]))
-        down.append(lax.ppermute(down[-1], axis, [(size - 1 - i, size - 2 - i) for i in pairs]))
-        if hop <= len(beside):
-            up[-1], down[-1], beside[hop - 1] = lax.optimization_barrier(
-                (up[-1], down[-1], beside[hop - 1])
-            )
-    return up, down, beside
-
-
-def chain_terms(sent, axis, size, after):
-    up, down = sent[size - 1], sent[1]
-    for hop in range(1, size):
-        up = lax.ppermute(up, axis, [(i, i + 1) for i in range(hop)])
-        down = lax.ppermute(down, axis, [(size - 1 - i, size - 2 - i) for i in range(hop)])
-        if hop == size - 2:
-            up, down, after = lax.optimization_barrier((up, down, after))
-        if hop < size - 1:
-            up = up + sent[size - 1 - hop]
-            down = down + sent[hop + 1]
-    return [sent[0], up, down], after
 
 
 def even_pieces(values, axis, size):
@@ -610,13 +591,6 @@
 
 def chip_terms(summed, axis, size):
     return [summed[0]] + [exchange(summed[m], axis, size, 2 * m) for m in range(1, size // 2)]
-
-
-def chunk_terms(sent, axis, size):
-    return [sent[0]] + [
-        lax.ppermute(sent[s], axis, [(i, (i + s) % size) for i in range(size)])
-        for s in range(1, size)
-    ]
 
 
 def total(terms):
@@ -640,11 +614,7 @@
     fsdp, tp, tokens, lengths, norm_gain, in_weight, conv_weight, conv_bias, x_weight, dt_weight,
     dt_bias, a_log, d_skip, out_weight, cotangent,
 ):
-    tp_me = lax.axis_index("tp")
     fs_me = lax.axis_index("fsdp")
-    chunks = jnp.arange(tp)
-    order = ((tp_me - chunks) % tp).astype(jnp.int32)
-    slot = ((chunks - tp_me) % tp).astype(jnp.int32)
     place = (fs_me ^ jnp.arange(fsdp)).astype(jnp.int32)
     depth = tokens.shape[2]
     part = conv_weight.shape[1]
@@ -652,7 +622,12 @@
     lay = Rows(x_weight.shape[1], a_log.shape[0], conv_weight.shape[0])
     maps, width, taps, rank, first = lay.maps, lay.width, lay.taps, lay.rank, lay.first
 
+    whole = lax.all_gather(tokens[0], "tp", axis=0, tiled=True)
     even = even_pieces(in_weight.reshape(in_weight.shape[0], 2 * chans), "fsdp", fsdp)
+    even, x_weight = lax.optimization_barrier((even, x_weight))
+    w = jnp.stack(all_pieces(even, "fsdp", fsdp))[place].reshape(depth, 2 * chans)
+    pieces = all_pieces(even_pieces(out_weight, "fsdp", fsdp), "fsdp", fsdp)
+    out_w = jnp.stack(pieces)[place].transpose(1, 0, 2).reshape(chans, depth)
     packed = jnp.concatenate(
         [
             x_weight.T,
@@ -668,47 +643,55 @@
         0,
     )
     gathered = lax.all_gather(packed, "fsdp", axis=0)
-    up, down, (gathered, even) = relay(tokens[0], "tp", tp, (gathered, even))
-    pieces = all_pieces(even, "fsdp", fsdp)
-    token_shards = up + down[1:]
-    source = jnp.where(chunks <= tp_me, tp_me - chunks, chunks - tp_me + tp - 1).astype(jnp.int32)
     small = gathered[:, : lay.count].transpose(1, 0, 2).reshape(lay.count, chans)
     dt_rows = dt_weight.size // part
     dt_w = gathered[:, lay.count : lay.count + dt_rows].reshape(rank, chans)
     gain = gathered[:, lay.count + dt_rows :].reshape(1, depth).astype(f32)
-    out_w = lax.all_gather(out_weight, "fsdp", axis=1, tiled=True)
-
-    normed, w, conv_in, gate, conv_sum, low, map_part, map_send = front(
-        lay, source, place, token_shards, gain, small, pieces
-    )
+
+    whole, out_w = lax.optimization_barrier((whole, out_w))
+    normed, conv_in, gate, conv_sum, low, map_part, map_send = front(lay, whole, gain, small, w)
     map_send, held = lax.optimization_barrier((map_send, cotangent[0]))
     grad_whole = lax.all_gather(held, "tp", axis=0, tiled=True)
     own, got, _ = sum_all(map_part, map_send, "tp", tp, ())
-    mixed, before, step, h, *sent = forward(
-        lay, lengths, slot, own, got, low, gate, dt_w, small, out_w
-    )
-    sent, grad_whole = lax.optimization_barrier((sent, grad_whole))
-    block_terms = chunk_terms(sent, "tp", tp)
+    mixed, before, step, h, sent = forward(
+        lay, lengths, own, got, low, gate, dt_w, small, out_w
+    )
+    block_sum = lax.psum_scatter(sent, "tp", scatter_dimension=0, tiled=True)
 
     map_part, map_send, conv_grad, gate_grad, rate_grad, dt_w_grad, bias_grad = backward(
         lay, lengths, own, got, low, gate, before, step, grad_whole, h, dt_w, small, out_w
     )
-    map_part, map_send, block_terms = lax.optimization_barrier((map_part, map_send, block_terms))
-    own_grad, got_grad, held = sum_all(map_part, map_send, "tp", tp, gate_grad)
-    pair = [
-        dot(a, b, TN).reshape(fsdp, 1, -1, chans)
-        for a, b in ((normed, held), (grad_whole, mixed))
-    ]
-    gate_half, out_weight_grad = lax.psum_scatter(
-        jnp.concatenate(pair, 1).astype(bf16), "fsdp", scatter_dimension=0, tiled=False
-    )
-    block_out = (tokens.astype(f32) + total(block_terms)[None]).astype(bf16)
-    own_grad, got_grad, block_out = lax.optimization_barrier((own_grad, got_grad, block_out))
-    *sent_back, keep, send, x_w_grad, taps_grad = back(
-        lay, slot, place, own_grad, got_grad, small, conv_grad, conv_sum, conv_in, low,
-        gate_grad, normed, w,
-    )
-    conv_half = total(chip_terms(pair_sum(keep, send, "fsdp", fsdp), "fsdp", fsdp))
+    *out_one, _ = weights(place, 0, (grad_whole,), (mixed,), w)
+    own_grad, got_grad, (held, out_one) = sum_all(
+        map_part, map_send, "tp", tp, (gate_grad, out_one)
+    )
+    *gate_one, gain_two = weights(place, 1, (normed,), (held,), w)
+    block_out = (tokens.astype(f32) + block_sum[None].astype(f32)).astype(bf16)
+    out_pairs = pair_sum(*out_one, "fsdp", fsdp)
+    own_grad, got_grad, gate_one, out_pairs = lax.optimization_barrier(
+        (own_grad, got_grad, gate_one, out_pairs)
+    )
+    normed_part, input_grad, x_w_grad, taps_grad = back(
+        lay, own_grad, got_grad, small, conv_grad, conv_sum, conv_in, low, gate_grad, w
+    )
+    normed_grad = lax.psum_scatter(normed_part, "tp", scatter_dimension=0, tiled=True)
+    *one, gain_one = weights(place, 0, (normed,), (input_grad,), w)
+    out_terms = chip_terms(out_pairs, "fsdp", fsdp)
+    gate_terms = chip_terms(pair_sum(*gate_one, "fsdp", fsdp), "fsdp", fsdp)
+    x_w_grad, taps_grad, out_terms, gate_terms = lax.optimization_barrier(
+        (x_w_grad, taps_grad, out_terms, gate_terms)
+    )
+    conv_terms = chip_terms(pair_sum(*one, "fsdp", fsdp), "fsdp", fsdp)
+    out_weight_grad, gate_half, conv_half = (
+        total(terms)[0] for terms in (out_terms, gate_terms, conv_terms)
+    )
+    in_weight_grad = jnp.stack([conv_half, gate_half], 1)
+    out_weight_grad = out_weight_grad.T
+    gain_grad = gain_one[:1] + gain_two[:1]
+    bits = 1
+    while bits < tp:
+        gain_grad = gain_grad + exchange(gain_grad, "tp", tp, 2 * bits - 1)
+        bits *= 2
     rows = jnp.concatenate(
         [x_w_grad, rate_grad * LN2, taps_grad[: taps + 1], bias_grad[:2]], 0
     ).astype(bf16)
@@ -717,35 +700,19 @@
         [
             rows.reshape(top, fsdp, part).transpose(1, 0, 2),
             dt_w_grad.astype(bf16).reshape(fsdp, -1, part),
+            gain_grad.astype(bf16).reshape(fsdp, -1, part),
         ],
         1,
     )[place]
     pairs = pair_sum(packed[0::2], packed[1::2], "fsdp", fsdp)
     small_grad = total(chip_terms(pairs, "fsdp", fsdp))
-    chain, (small_grad, gate_half, out_weight_grad) = chain_terms(
-        sent_back, "tp", tp, (small_grad, gate_half, out_weight_grad)
-    )
-    normed_grad = total(chain)
-    in_weight_grad = jnp.stack([conv_half, gate_half.astype(f32)], 1)
-    out_weight_grad = out_weight_grad.astype(f32).T
-    gain_out = jnp.sum(in_weight_grad * in_weight.astype(f32), axis=(1, 2), keepdims=True)
-    gain_out = (gain_out[:, 0] / norm_gain.astype(f32)[:, None]).reshape(1, -1)
-    bits = 1
-    while bits < tp:
-        gain_out = gain_out + exchange(gain_out, "tp", tp, 2 * bits - 1)
-        bits *= 2
-
-    own_values = tokens.astype(f32)
-    own_inverse = lax.rsqrt(jnp.mean(own_values * own_values, axis=-1, keepdims=True) + epsilon)
-    own_hat = own_values * own_inverse
-    scaled = normed_grad[None] * gain[None]
-    input_grads = cotangent.astype(f32) + own_inverse * (
-        scaled - own_hat * jnp.mean(scaled * own_hat, axis=-1, keepdims=True)
-    )
+    gain_out = small_grad[top + dt_rows :].reshape(-1) / norm_gain.astype(f32)
+
+    input_grads = last(tokens[0], cotangent[0], normed_grad, gain)[None]
     return (
         block_out,
         input_grads,
-        gain_out.reshape(-1),
+        gain_out,
         in_weight_grad,
         small_grad[first : first + taps],
         small_grad[first + taps],

time: 283 us -> 252 us (0.89)
  waiting for transfers between devices: 67.6 us -> 46.4 us
  starting transfers between devices: 56.9 us -> 37.7 us
  local copies, waits for them, and re-layouts: 23.4 us -> 34.7 us
  Pallas kernels: 87.7 us -> 98.6 us
  other arithmetic: 16.9 us -> 9.55 us
  matrix products: 4.57 us -> 0 us
    ppermute x15 -> x0, starting transfers between devices: 36.8 us -> none  [the longest x3 13.4 us: chain_terms(): up = lax.ppermute(up, axis, [(i, i + 1) for i in range(hop)])]
    ppermute x15 -> x0, waiting for transfers between devices: 26.9 us -> none  [the longest x3 13.5 us: chain_terms(): up = lax.ppermute(up, axis, [(i, i + 1) for i in range(hop)])]
    ppermute x21 -> x36, starting transfers between devices: 20 us -> 37.4 us  [exchange(): return lax.ppermute(values, axis, [(i, i ^ bits) for i in range(size)])]
    pallas_call x3 -> x7, Pallas kernels: 48.3 us -> 59.2 us  [the longest x1 21.9 us: forward(): pl.pallas_call(functools.partial(forward_kernel, lay), grid_spec=pltpu.Pr...]
    unnamed x49 -> x46, local copies, waits for them, and re-layouts: 8.04 us -> 16 us
    add x5 -> x2, other arithmetic: 5.61 us -> 0.84 us  [the longest x1 0.84 us: shards(): gain_grad = gain_one[:1] + gain_two[:1]]
    dot_general x2 -> x0, matrix products: 4.57 us -> none  [dot(): return lax.dot_general(a, b, dims, preferred_element_type=f32)]
    all_gather x1, waiting for transfers between devices: 0.01 us -> 4.41 us  [shards(): whole = lax.all_gather(tokens[0], 'tp', axis=0, tiled=True)]
  transfers between devices with their start and end apart: 39 -> 40, of which waited for: 13 -> 15; matrix products, arithmetic and copies ran while one was open for 13% -> 17% of each run, Pallas kernels for 31% -> 35%
where the time goes in v5:
time: 252 us; the launch traced here: 251 us
  Pallas kernels  98.6 us (39%)
  waiting for transfers between devices  46.4 us (18%)
  starting transfers between devices  37.7 us (15%)
  local copies, waits for them, and re-layouts  34.7 us (14%)
  between operations  14.9 us (6%)
  other arithmetic  9.55 us (4%)
  blocking collectives  9.29 us (4%)
    pallas_call x1, Pallas kernels, backward(): pl.pallas_call(functools.partial(backward_kernel, lay), grid_spec=pltpu.P...  39.4 us
    ppermute x36, starting transfers between devices, exchange(): return lax.ppermute(values, axis, [(i, i ^ bits) for i in range(size)])  37.4 us
    ppermute x36, waiting for transfers between devices, exchange(): return lax.ppermute(values, axis, [(i, i ^ bits) for i in range(size)])  33.5 us
    pallas_call x1, Pallas kernels, forward(): pl.pallas_call(functools.partial(forward_kernel, lay), grid_spec=pltpu.Pr...  21.9 us
    pallas_call x3, Pallas kernels, weights(): pl.pallas_call(functools.partial(weights_kernel, len(lefts), half), grid_...  17 us
    unnamed x46, local copies, waits for them, and re-layouts  16 us
    pallas_call x1, Pallas kernels, back(): pl.pallas_call(functools.partial(back_kernel, lay), grid=(count,), in_spe...  9.93 us
    all_gather x1, blocking collectives, shards(): gathered = lax.all_gather(packed, 'fsdp', axis=0)  9.29 us
  transfers between devices with their start and end apart: 40, of which 15 were waited for; matrix products, arithmetic and copies ran while one was open for 17% of the time, Pallas kernels for 35%

profile of v5, /device:TPU:0, one launch (start us, length us, event | category | flops | bytes accessed | tf_op | source)
XLA Modules:
  0.0 251.1 jit_solution(17723340242083612084)
XLA Ops:
  7.2 3.0 %collective-permute-start.1 = (bf16[512,128]{1,0:T(8,128)(2,1)}, bf16[512,128]{1,0:T(8,128)(2,1)S(1)}, u32[]{:S(2)}, u32[]{:S(2)}) collective-permute-start(bf16[512,128]{1,0:T(8,128)(2,1)} %param.24), channel_id=1, source_target_pairs={{0,8},{4,12},{8,0},{12,4},{16,24},{20,28},{24,16},{28,20},{1,9},{5... | collective-permute-start | bytes 393224 | tf_op jit(solution)/shard_map/ppermute | solution.py:576
  10.2 1.5 collective-permute-start.5
  11.7 1.7 copy.149
  13.4 1.4 collective-permute-start.9
  14.8 1.5 collective-permute-start.8
  23.8 8.1 %collective-permute-done.3 = bf16[512,128]{1,0:T(8,128)(2,1)S(1)} collective-permute-done((bf16[512,128]{1,0:T(8,128)(2,1)}, bf16[512,128]{1,0:T(8,128)(2,1)S(1)}, u32[]{:S(2)}, u32[]{:S(2)}) %collective-permute-start.3) | collective-permute-done | bytes 131104 | tf_op jit(solution)/shard_map/ppermute | solution.py:576
  33.4 9.3 %all-gather.2 = bf16[8,194,64]{1,2,0:T(8,128)(2,1)S(1)} all-gather(bf16[1,194,64]{1,2,0:T(8,128)(2,1)S(1)} %bitcast.126), channel_id=3, replica_groups=mesh['fsdp'=8,'tp'=4] {'fsdp'}, dimensions={0}, use_global_device_ids=true | all-gather | bytes 223488 | tf_op jit(solution)/shard_map/all_gather | solution.py:645
  46.4 1.0 bitcast_dynamic-update-slice_fusion.7
  47.3 1.1 copy_bitcast_fusion.out_w
  48.5 1.0 bitcast_dynamic-update-slice_fusion.6
  49.4 1.0 bitcast_dynamic-update-slice_fusion.5
  50.4 1.0 bitcast_dynamic-update-slice_fusion.4
  51.4 1.0 bitcast_dynamic-update-slice_fusion.3
  52.4 1.0 bitcast_dynamic-update-slice_fusion.2
  53.4 1.0 bitcast_dynamic-update-slice_fusion.1
  55.3 2.0 gather_fusion.1
  57.3 4.4 %all-gather.8.cloned.1.call-done = bf16[1,1024,1024]{2,1,0:T(8,128)(2,1)} async-done(((bf16[1,256,1024]{2,1,0:T(8,128)(2,1)}), bf16[1,1024,1024]{2,1,0:T(8,128)(2,1)}) %all-gather.8.cloned.1.call-update) | async-done | bytes 2097168 | tf_op jit(solution)/shard_map/all_gather | solution.py:625
  61.8 7.9 %front.1 = (bf16[1024,1024]{1,0:T(8,128)(2,1)}, f32[1024,512]{1,0:T(8,128)}, f32[1024,512]{1,0:T(8,128)}, f32[1024,512]{1,0:T(8,128)}, bf16[1024,512]{1,0:T(8,12...) custom-call(bf16[1024,1024]{1,0:T(8,128)(2,1)} %bitcast.131, f32[1,1024]{1,0:T(1,128)} %reshape.126.gain, ...), custom_call_target="tpu_custom_call" | custom-call | flops 8999999488 | bytes 27000000 | tf_op jit(solution)/shard_map/front/pallas_call | solution.py:164
  69.8 6.9 %collective-permute-done.14 = bf16[96,1024]{1,0:T(8,128)(2,1)S(1)} collective-permute-done((bf16[96,1024]{1,0:T(8,128)(2,1)}, bf16[96,1024]{1,0:T(8,128)(2,1)S(1)}, u32[]{:S(2)}, u32[]{:S(2)}) %collective-permute-start.14) | collective-permute-done | bytes 196640 | tf_op jit(solution)/shard_map/ppermute | solution.py:576
  76.7 1.8 fusion.8
  78.5 1.4 collective-permute-start.15
  82.0 9.5 %collective-permute-done.15.got = bf16[96,1024]{1,0:T(8,128)(2,1)S(1)} collective-permute-done((bf16[96,1024]{1,0:T(8,128)(2,1)S(1)}, bf16[96,1024]{1,0:T(8,128)(2,1)S(1)}, u32[]{:S(2)}, u32[]{:S(2)}) %collective-permute-start.15) | collective-permute-done | bytes 196640 | tf_op jit(solution)/shard_map/ppermute | solution.py:576
  92.2 21.9 %forward.1 = (bf16[1024,512]{1,0:T(8,128)(2,1)}, f32[1024,512]{1,0:T(8,128)}, f32[1024,512]{1,0:T(8,128)}, bf16[16384,512]{1,0:T(8,128)(2,1)}, bf16[1024,1024]{1,0:T(8,128)(2,1)}) custom-call(s32[1]{0:T(128)S(6)} %copy.165.length, f32[96,1024]{1,0:T(8,128)} %get-tuple-element.196.own, bf16[96,1024]{1,0:T(8,128)(2,1)} %copy-done.9, ...), custom_call_target="tpu_custom_call" | custom-call | flops 24000000000 | bytes 72000000 | tf_op jit(solution)/shard_map/forward/pallas_call | solution.py:248
  114.3 8.4 %all-gather.6.cloned.1.call-done.grad.refs_0_ = bf16[1024,1024]{1,0:T(8,128)(2,1)} async-done(((bf16[256,1024]{1,0:T(8,128)(2,1)}), bf16[1024,1024]{1,0:T(8,128)(2,1)}) %all-gather.6.cloned.1.call-update) | async-done | bytes 2097168 | tf_op jit(solution)/shard_map/all_gather | solution.py:654
  122.7 39.4 %backward.1 = (f32[96,1024]{1,0:T(8,128)}, bf16[96,1024]{1,0:T(8,128)(2,1)}, f32[1024,512]{1,0:T(8,128)}, bf16[1024,512]{1,0:T(8,128)(2,1)}, f32[16,512]{1,0:T(8...) custom-call(s32[1]{0:T(128)S(6)} %copy.165.length, f32[96,1024]{1,0:T(8,128)} %get-tuple-element.196.own, ...), custom_call_target="tpu_custom_call" | custom-call | flops 40000000000 | bytes 120000000 | tf_op jit(solution)/shard_map/backward/pallas_call | solution.py:395
  162.1 2.3 collective-permute-start.16
  164.4 5.7 %weights.3 = (bf16[4,1,128,512]{3,2,1,0:T(8,128)(2,1)}, bf16[4,1,128,512]{3,2,1,0:T(8,128)(2,1)}, f32[8,1024]{1,0:T(8,128)}) custom-call(s32[8]{0:T(128)} %iota_xor_fusion.place, bf16[1024,1024]{1,0:T(8,128)(2,1)} %all-gather.6.cloned.1.call-done.grad.refs_0_, bf16[1024,512]{1,0:T(8,128)(2,1)} %get-tuple-element.91.refs_1_, bf16[1024,1024]{1,0:T(8,128)(2,1)} %bitcast.114), custom_call_target="tpu_custom_call" | custom-call | flops 3000000000 | bytes 9000000 | tf_op jit(solution)/shard_map/weights/pallas_call | solution.py:533
  171.4 2.5 %collective-permute-start.17 = (bf16[96,1024]{1,0:T(8,128)(2,1)S(1)}, bf16[96,1024]{1,0:T(8,128)(2,1)S(1)}, u32[]{:S(2)}, u32[]{:S(2)}) collective-permute-start(bf16[96,1024]{1,0:T(8,128)(2,1)S(1)} %get-tuple-element.193), channel_id=1, source_target_pairs={{0,3},{1,2},{2,1},{3,0},{4,7},{5,6},{6,5},{7,4},{8,11},{9,10},{10,... | collective-permute-start | bytes 589832 | tf_op jit(solution)/shard_map/ppermute | solution.py:576
  173.9 5.7 %weights.4 = (bf16[4,1,128,512]{3,2,1,0:T(8,128)(2,1)}, bf16[4,1,128,512]{3,2,1,0:T(8,128)(2,1)}, f32[8,1024]{1,0:T(8,128)}) custom-call(s32[8]{0:T(128)} %iota_xor_fusion.place, bf16[1024,1024]{1,0:T(8,128)(2,1)} %get-tuple-element.95.refs_0_, bf16[1024,512]{1,0:T(8,128)(2,1)} %get-tuple-element.96.refs_1_.gate_grad, bf16[1024,1024]{1,0:T(8,128)(2,1)} %bitcast.115), custom_call_target="tpu_custom_call" | custom-call | flops 3000000000 | bytes 9000000 | tf_op jit(solution)/shard_map/weights/pallas_call | solution.py:533
  181.3 9.9 %back.1 = (bf16[1024,1024]{1,0:T(8,128)(2,1)}, bf16[1024,512]{1,0:T(8,128)(2,1)}, f32[96,512]{1,0:T(8,128)}, f32[8,512]{1,0:T(8,128)}) custom-call(f32[96,1024]{1,0:T(8,128)} %get-tuple-element.101.own, bf16[96,1024]{1,0:T(8,128)(2,1)} %copy-done.10, bf16[128,512]{1,0:T(8,128)(2,1)} %copy.127.small, f32[1024,512]{1,0:T(8,128)} %get-tuple-element.103.out_grad, ...), custom_call_target="tpu_custom_call" | custom-call | flops 11000000512 | bytes 33000000 | tf_op jit(solution)/shard_map/back/pallas_call | solution.py:487
  191.3 5.7 %weights.5 = (bf16[4,1,128,512]{3,2,1,0:T(8,128)(2,1)}, bf16[4,1,128,512]{3,2,1,0:T(8,128)(2,1)}, f32[8,1024]{1,0:T(8,128)}) custom-call(s32[8]{0:T(128)} %iota_xor_fusion.place, bf16[1024,1024]{1,0:T(8,128)(2,1)} %get-tuple-element.95.refs_0_, bf16[1024,512]{1,0:T(8,128)(2,1)} %get-tuple-element.117.refs_1_, bf16[1024,1024]{1,0:T(8,128)(2,1)} %bitcast.117), custom_call_target="tpu_custom_call" | custom-call | flops 3000000000 | bytes 9000000 | tf_op jit(solution)/shard_map/weights/pallas_call | solution.py:533
  197.8 3.2 %collective-permute-start.26 = (f32[1,1024]{1,0:T(1,128)S(1)}, f32[1,1024]{1,0:T(1,128)S(1)}, u32[]{:S(2)}, u32[]{:S(2)}) collective-permute-start(f32[1,1024]{1,0:T(1,128)S(1)} %slice_add_fusion.1), channel_id=1, source_target_pairs={{0,1},{1,0},{2,3},{3,2},{4,5},{5,4},{6,7},{7,6},{8,9},{9,8},{10,11... | collective-permute-start | bytes 12296 | tf_op jit(solution)/shard_map/ppermute | solution.py:576
  202.9 3.4 %collective-permute-start.27 = (f32[1,1024]{1,0:T(1,128)S(1)}, f32[1,1024]{1,0:T(1,128)S(1)}, u32[]{:S(2)}, u32[]{:S(2)}) collective-permute-start(f32[1,1024]{1,0:T(1,128)S(1)} %add.89), channel_id=1, source_target_pairs={{0,3},{1,2},{2,1},{3,0},{4,7},{5,6},{6,5},{7,4},{8,11},{9,10},{10,... | collective-permute-start | bytes 12296 | tf_op jit(solution)/shard_map/ppermute | solution.py:576
  207.1 1.7 collective-permute-start.21
  209.3 1.3 collective-permute-start.19
  211.1 1.7 collective-permute-start.25
  214.2 1.1 collective-permute-start.23
  216.0 2.3 collective-permute-done.20
  218.7 1.4 collective-permute-start.35
  220.2 1.6 collective-permute-start.34
  223.8 1.0 add_bitcast_fusion
  225.2 2.3 collective-permute-done.35
  227.9 1.0 fusion.3
  229.0 1.2 copy.140
  231.1 1.2 collective-permute-start.29
  232.3 1.5 collective-permute-start.31
  234.6 2.0 fusion
  242.1 2.5 last.1
  (163 shorter events, 35.9 us)
Async XLA Ops:
  7.2 54.6 %all-gather.8.cloned.1.call-start = ((), (), s32[]{:S(2)}) async-start(), calls=%async_computation.5 | async-start | bytes 2621440 | tf_op jit(solution)/shard_map/all_gather | solution.py:625
  7.2 16.4 %collective-permute-start.1 = (bf16[512,128]{1,0:T(8,128)(2,1)}, bf16[512,128]{1,0:T(8,128)(2,1)S(1)}, u32[]{:S(2)}, u32[]{:S(2)}) collective-permute-start(bf16[512,128]{1,0:T(8,128)(2,1)} %param.24), channel_id=1, source_target_pairs={{0,8},{4,12},{8,0},{12,4},{16,24},{20,28},{24,16},{28,20},{1,9},{5... | collective-permute-start | bytes 393224 | tf_op jit(solution)/shard_map/ppermute | solution.py:576
  10.2 12.8 %collective-permute-start = (bf16[512,128]{1,0:T(8,128)(2,1)}, bf16[512,128]{1,0:T(8,128)(2,1)S(1)}, u32[]{:S(2)}, u32[]{:S(2)}) collective-permute-start(bf16[512,128]{1,0:T(8,128)(2,1)} %param.24), channel_id=1, source_target_pairs={{0,4},{4,0},{8,12},{12,8},{16,20},{20,16},{24,28},{28,24},{1,5},{5... | collective-permute-start | bytes 393224 | tf_op jit(solution)/shard_map/ppermute | solution.py:576
  10.2 13.6 %collective-permute-start.5 = (bf16[512,128]{1,0:T(8,128)(2,1)}, bf16[512,128]{1,0:T(8,128)(2,1)S(1)}, u32[]{:S(2)}, u32[]{:S(2)}) collective-permute-start(bf16[512,128]{1,0:T(8,128)(2,1)} %param.24), channel_id=1, source_target_pairs={{0,24},{4,28},{8,16},{12,20},{16,8},{20,12},{24,0},{28,4},{1,25},{... | collective-permute-start | bytes 393224 | tf_op jit(solution)/shard_map/ppermute | solution.py:576
  13.4 18.7 %collective-permute-start.9 = (bf16[128,1024]{1,0:T(8,128)(2,1)}, bf16[128,1024]{1,0:T(8,128)(2,1)}, u32[]{:S(2)}, u32[]{:S(2)}) collective-permute-start(bf16[128,1024]{1,0:T(8,128)(2,1)} %bitcast.65), channel_id=1, source_target_pairs={{0,24},{4,28},{8,16},{12,20},{16,8},{20,12},{24,0},{28,4},{1,25},{... | collective-permute-start | bytes 786440 | tf_op jit(solution)/shard_map/ppermute | solution.py:576
  14.8 17.7 %collective-permute-start.8 = (bf16[128,1024]{1,0:T(8,128)(2,1)}, bf16[128,1024]{1,0:T(8,128)(2,1)}, u32[]{:S(2)}, u32[]{:S(2)}) collective-permute-start(bf16[128,1024]{1,0:T(8,128)(2,1)} %bitcast.65), channel_id=1, source_target_pairs={{0,16},{4,20},{8,24},{12,28},{16,0},{20,4},{24,8},{28,12},{1,17},{... | collective-permute-start | bytes 786440 | tf_op jit(solution)/shard_map/ppermute | solution.py:576
  16.4 106.3 %all-gather.6.cloned.1.call-start = ((), (), s32[]{:S(2)}) async-start(), calls=%async_computation.3 | async-start | bytes 2621440 | tf_op jit(solution)/shard_map/all_gather | solution.py:654
  23.0 9.5 %collective-permute-start.7 = (bf16[128,1024]{1,0:T(8,128)(2,1)}, bf16[128,1024]{1,0:T(8,128)(2,1)}, u32[]{:S(2)}, u32[]{:S(2)}) collective-permute-start(bf16[128,1024]{1,0:T(8,128)(2,1)} %bitcast.65), channel_id=1, source_target_pairs={{0,8},{4,12},{8,0},{12,4},{16,24},{20,28},{24,16},{28,20},{1,9},{5... | collective-permute-start | bytes 786440 | tf_op jit(solution)/shard_map/ppermute | solution.py:576
  23.6 8.4 %collective-permute-start.3 = (bf16[512,128]{1,0:T(8,128)(2,1)}, bf16[512,128]{1,0:T(8,128)(2,1)S(1)}, u32[]{:S(2)}, u32[]{:S(2)}) collective-permute-start(bf16[512,128]{1,0:T(8,128)(2,1)} %param.24), channel_id=1, source_target_pairs={{0,16},{4,20},{8,24},{12,28},{16,0},{20,4},{24,8},{28,12},{1,17},{... | collective-permute-start | bytes 393224 | tf_op jit(solution)/shard_map/ppermute | solution.py:576
  23.8 21.1 %collective-permute-start.2 = (bf16[512,128]{1,0:T(8,128)(2,1)S(1)}, bf16[512,128]{1,0:T(8,128)(2,1)S(1)}, u32[]{:S(2)}, u32[]{:S(2)}) collective-permute-start(bf16[512,128]{1,0:T(8,128)(2,1)S(1)} %collective-permute-done.1), channel_id=1, source_target_pairs={{0,4},{4,0},{8,12},{12,8},{16,20},{20,16},{24,28},{28,24},{1,5},{5... | collective-permute-start | bytes 393224 | tf_op jit(solution)/shard_map/ppermute | solution.py:576
  32.0 13.6 %collective-permute-start.6 = (bf16[512,128]{1,0:T(8,128)(2,1)S(1)}, bf16[512,128]{1,0:T(8,128)(2,1)S(1)}, u32[]{:S(2)}, u32[]{:S(2)}) collective-permute-start(bf16[512,128]{1,0:T(8,128)(2,1)S(1)} %collective-permute-done.5), channel_id=1, source_target_pairs={{0,4},{4,0},{8,12},{12,8},{16,20},{20,16},{24,28},{28,24},{1,5},{5... | collective-permute-start | bytes 393224 | tf_op jit(solution)/shard_map/ppermute | solution.py:576
  32.1 13.2 %collective-permute-start.4 = (bf16[512,128]{1,0:T(8,128)(2,1)S(1)}, bf16[512,128]{1,0:T(8,128)(2,1)S(1)}, u32[]{:S(2)}, u32[]{:S(2)}) collective-permute-start(bf16[512,128]{1,0:T(8,128)(2,1)S(1)} %collective-permute-done.3), channel_id=1, source_target_pairs={{0,4},{4,0},{8,12},{12,8},{16,20},{20,16},{24,28},{28,24},{1,5},{5... | collective-permute-start | bytes 393224 | tf_op jit(solution)/shard_map/ppermute | solution.py:576
  44.4 4.1 %collective-permute-start.10 = (bf16[128,1024]{1,0:T(8,128)(2,1)}, bf16[128,1024]{1,0:T(8,128)(2,1)}, u32[]{:S(2)}, u32[]{:S(2)}) collective-permute-start(bf16[128,1024]{1,0:T(8,128)(2,1)} %bitcast.65), channel_id=1, source_target_pairs={{0,4},{4,0},{8,12},{12,8},{16,20},{20,16},{24,28},{28,24},{1,5},{5... | collective-permute-start | bytes 786440 | tf_op jit(solution)/shard_map/ppermute | solution.py:576
  44.7 5.7 %collective-permute-start.11 = (bf16[128,1024]{1,0:T(8,128)(2,1)}, bf16[128,1024]{1,0:T(8,128)(2,1)}, u32[]{:S(2)}, u32[]{:S(2)}) collective-permute-start(bf16[128,1024]{1,0:T(8,128)(2,1)} %collective-permute-done.7), channel_id=1, source_target_pairs={{0,4},{4,0},{8,12},{12,8},{16,20},{20,16},{24,28},{28,24},{1,5},{5... | collective-permute-start | bytes 786440 | tf_op jit(solution)/shard_map/ppermute | solution.py:576
  44.9 7.5 %collective-permute-start.12 = (bf16[128,1024]{1,0:T(8,128)(2,1)}, bf16[128,1024]{1,0:T(8,128)(2,1)}, u32[]{:S(2)}, u32[]{:S(2)}) collective-permute-start(bf16[128,1024]{1,0:T(8,128)(2,1)} %collective-permute-done.8), channel_id=1, source_target_pairs={{0,4},{4,0},{8,12},{12,8},{16,20},{20,16},{24,28},{28,24},{1,5},{5... | collective-permute-start | bytes 786440 | tf_op jit(solution)/shard_map/ppermute | solution.py:576
  45.3 9.0 %collective-permute-start.13 = (bf16[128,1024]{1,0:T(8,128)(2,1)}, bf16[128,1024]{1,0:T(8,128)(2,1)}, u32[]{:S(2)}, u32[]{:S(2)}) collective-permute-start(bf16[128,1024]{1,0:T(8,128)(2,1)} %collective-permute-done.9), channel_id=1, source_target_pairs={{0,4},{4,0},{8,12},{12,8},{16,20},{20,16},{24,28},{28,24},{1,5},{5... | collective-permute-start | bytes 786440 | tf_op jit(solution)/shard_map/ppermute | solution.py:576
  69.7 164.9 %reduce-scatter.3.cloned.1.call-start = ((), (), s32[]{:S(2)}) async-start(), calls=%async_computation.2 | async-start | bytes 2621440 | tf_op jit(solution)/shard_map/reduce_scatter | solution.py:659
  69.7 7.0 %collective-permute-start.14 = (bf16[96,1024]{1,0:T(8,128)(2,1)}, bf16[96,1024]{1,0:T(8,128)(2,1)S(1)}, u32[]{:S(2)}, u32[]{:S(2)}) collective-permute-start(bf16[96,1024]{1,0:T(8,128)(2,1)} %get-tuple-element.79), channel_id=1, source_target_pairs={{0,1},{1,0},{2,3},{3,2},{4,5},{5,4},{6,7},{7,6},{8,9},{9,8},{10,11... | collective-permute-start | bytes 589832 | tf_op jit(solution)/shard_map/ppermute | solution.py:576
  78.5 13.0 %collective-permute-start.15 = (bf16[96,1024]{1,0:T(8,128)(2,1)S(1)}, bf16[96,1024]{1,0:T(8,128)(2,1)S(1)}, u32[]{:S(2)}, u32[]{:S(2)}) collective-permute-start(bf16[96,1024]{1,0:T(8,128)(2,1)S(1)} %get-tuple-element.195), channel_id=1, source_target_pairs={{0,3},{1,2},{2,1},{3,0},{4,7},{5,6},{6,5},{7,4},{8,11},{9,10},{10,... | collective-permute-start | bytes 589832 | tf_op jit(solution)/shard_map/ppermute | solution.py:576
  114.1 128.0 %reduce-scatter.5.cloned.1.call-start = ((), (), s32[]{:S(2)}) async-start(), calls=%async_computation.4 | async-start | bytes 2621440 | tf_op jit(solution)/shard_map/reduce_scatter | solution.py:677
  162.1 8.4 %collective-permute-start.16 = (bf16[96,1024]{1,0:T(8,128)(2,1)}, bf16[96,1024]{1,0:T(8,128)(2,1)S(1)}, u32[]{:S(2)}, u32[]{:S(2)}) collective-permute-start(bf16[96,1024]{1,0:T(8,128)(2,1)} %get-tuple-element.89), channel_id=1, source_target_pairs={{0,1},{1,0},{2,3},{3,2},{4,5},{5,4},{6,7},{7,6},{8,9},{9,8},{10,11... | collective-permute-start | bytes 589832 | tf_op jit(solution)/shard_map/ppermute | solution.py:576
  170.6 9.0 %collective-permute-start.18 = (bf16[4,1,128,512]{3,2,1,0:T(8,128)(2,1)}, bf16[4,1,128,512]{3,2,1,0:T(8,128)(2,1)S(1)}, u32[]{:S(2)}, u32[]{:S(2)}) collective-permute-start(bf16[4,1,128,512]{3,2,1,0:T(8,128)(2,1)} %get-tuple-element.100), channel_id=1, source_target_pairs={{0,4},{4,0},{8,12},{12,8},{16,20},{20,16},{24,28},{28,24},{1,5},{5... | collective-permute-start | bytes 1572872 | tf_op jit(solution)/shard_map/ppermute | solution.py:576
  171.4 9.2 %collective-permute-start.17 = (bf16[96,1024]{1,0:T(8,128)(2,1)S(1)}, bf16[96,1024]{1,0:T(8,128)(2,1)S(1)}, u32[]{:S(2)}, u32[]{:S(2)}) collective-permute-start(bf16[96,1024]{1,0:T(8,128)(2,1)S(1)} %get-tuple-element.193), channel_id=1, source_target_pairs={{0,3},{1,2},{2,1},{3,0},{4,7},{5,6},{6,5},{7,4},{8,11},{9,10},{10,... | collective-permute-start | bytes 589832 | tf_op jit(solution)/shard_map/ppermute | solution.py:576
  191.2 9.8 %copy-start.7 = (f32[16,512]{1,0:T(8,128)S(1)}, f32[16,512]{1,0:T(8,128)}, u32[]{:S(2)}) copy-start(f32[16,512]{1,0:T(8,128)} %get-tuple-element.113) | copy-start | bytes 98308
  191.2 10.5 %copy-start.6 = (f32[64,512]{1,0:T(8,128)S(1)}, f32[64,512]{1,0:T(8,128)}, u32[]{:S(2)}) copy-start(f32[64,512]{1,0:T(8,128)} %get-tuple-element.116) | copy-start | bytes 393220
  196.9 14.0 %copy-start.1 = (bf16[4,1,128,512]{3,2,1,0:T(8,128)(2,1)S(1)}, bf16[4,1,128,512]{3,2,1,0:T(8,128)(2,1)}, u32[]{:S(2)}) copy-start(bf16[4,1,128,512]{3,2,1,0:T(8,128)(2,1)} %get-tuple-element.110) | copy-start | bytes 1572868
  197.8 5.2 %collective-permute-start.26 = (f32[1,1024]{1,0:T(1,128)S(1)}, f32[1,1024]{1,0:T(1,128)S(1)}, u32[]{:S(2)}, u32[]{:S(2)}) collective-permute-start(f32[1,1024]{1,0:T(1,128)S(1)} %slice_add_fusion.1), channel_id=1, source_target_pairs={{0,1},{1,0},{2,3},{3,2},{4,5},{5,4},{6,7},{7,6},{8,9},{9,8},{10,11... | collective-permute-start | bytes 12296 | tf_op jit(solution)/shard_map/ppermute | solution.py:576
  201.0 9.9 %collective-permute-start.22 = (bf16[4,1,128,512]{3,2,1,0:T(8,128)(2,1)}, bf16[4,1,128,512]{3,2,1,0:T(8,128)(2,1)S(1)}, u32[]{:S(2)}, u32[]{:S(2)}) collective-permute-start(bf16[4,1,128,512]{3,2,1,0:T(8,128)(2,1)} %get-tuple-element.111), channel_id=1, source_target_pairs={{0,4},{4,0},{8,12},{12,8},{16,20},{20,16},{24,28},{28,24},{1,5},{5... | collective-permute-start | bytes 1572872 | tf_op jit(solution)/shard_map/ppermute | solution.py:576
  202.0 11.4 %copy-start.2 = (bf16[4,1,128,512]{3,2,1,0:T(8,128)(2,1)S(1)}, bf16[4,1,128,512]{3,2,1,0:T(8,128)(2,1)}, u32[]{:S(2)}) copy-start(bf16[4,1,128,512]{3,2,1,0:T(8,128)(2,1)} %get-tuple-element.120) | copy-start | bytes 1572868
  202.3 10.5 %collective-permute-start.32 = (bf16[4,1,128,512]{3,2,1,0:T(8,128)(2,1)}, bf16[4,1,128,512]{3,2,1,0:T(8,128)(2,1)S(1)}, u32[]{:S(2)}, u32[]{:S(2)}) collective-permute-start(bf16[4,1,128,512]{3,2,1,0:T(8,128)(2,1)} %get-tuple-element.121), channel_id=1, source_target_pairs={{0,4},{4,0},{8,12},{12,8},{16,20},{20,16},{24,28},{28,24},{1,5},{5... | collective-permute-start | bytes 1572872 | tf_op jit(solution)/shard_map/ppermute | solution.py:576
  202.9 6.4 %collective-permute-start.27 = (f32[1,1024]{1,0:T(1,128)S(1)}, f32[1,1024]{1,0:T(1,128)S(1)}, u32[]{:S(2)}, u32[]{:S(2)}) collective-permute-start(f32[1,1024]{1,0:T(1,128)S(1)} %add.89), channel_id=1, source_target_pairs={{0,3},{1,2},{2,1},{3,0},{4,7},{5,6},{6,5},{7,4},{8,11},{9,10},{10,... | collective-permute-start | bytes 12296 | tf_op jit(solution)/shard_map/ppermute | solution.py:576
  207.1 7.1 %collective-permute-start.21 = (bf16[1,128,512]{2,1,0:T(8,128)(2,1)}, bf16[1,128,512]{2,1,0:T(8,128)(2,1)S(1)}, u32[]{:S(2)}, u32[]{:S(2)}) collective-permute-start(bf16[1,128,512]{2,1,0:T(8,128)(2,1)} %get-tuple-element.204), channel_id=1, source_target_pairs={{0,24},{4,28},{8,16},{12,20},{16,8},{20,12},{24,0},{28,4},{1,25},{... | collective-permute-start | bytes 393224 | tf_op jit(solution)/shard_map/ppermute | solution.py:576
  208.8 9.5 %collective-permute-start.20 = (bf16[1,128,512]{2,1,0:T(8,128)(2,1)}, bf16[1,128,512]{2,1,0:T(8,128)(2,1)S(1)}, u32[]{:S(2)}, u32[]{:S(2)}) collective-permute-start(bf16[1,128,512]{2,1,0:T(8,128)(2,1)} %get-tuple-element.205), channel_id=1, source_target_pairs={{0,16},{4,20},{8,24},{12,28},{16,0},{20,4},{24,8},{28,12},{1,17},{... | collective-permute-start | bytes 393224 | tf_op jit(solution)/shard_map/ppermute | solution.py:576
  209.3 9.4 %collective-permute-start.19 = (bf16[1,128,512]{2,1,0:T(8,128)(2,1)}, bf16[1,128,512]{2,1,0:T(8,128)(2,1)}, u32[]{:S(2)}, u32[]{:S(2)}) collective-permute-start(bf16[1,128,512]{2,1,0:T(8,128)(2,1)} %get-tuple-element.206), channel_id=1, source_target_pairs={{0,8},{4,12},{8,0},{12,4},{16,24},{20,28},{24,16},{28,20},{1,9},{5... | collective-permute-start | bytes 393224 | tf_op jit(solution)/shard_map/ppermute | solution.py:576
  211.0 11.3 %copy-start.5 = (f32[96,512]{1,0:T(8,128)S(1)}, f32[96,512]{1,0:T(8,128)}, u32[]{:S(2)}) copy-start(f32[96,512]{1,0:T(8,128)} %get-tuple-element.112) | copy-start | bytes 589828
  211.1 11.3 %copy-start.8 = (f32[8,512]{1,0:T(8,128)S(1)}, f32[8,512]{1,0:T(8,128)}, u32[]{:S(2)}) copy-start(f32[8,512]{1,0:T(8,128)} %get-tuple-element.114) | copy-start | bytes 49156
  211.1 9.1 %collective-permute-start.25 = (bf16[1,128,512]{2,1,0:T(8,128)(2,1)S(1)}, bf16[1,128,512]{2,1,0:T(8,128)(2,1)S(1)}, u32[]{:S(2)}, u32[]{:S(2)}) collective-permute-start(bf16[1,128,512]{2,1,0:T(8,128)(2,1)S(1)} %get-tuple-element.200), channel_id=1, source_target_pairs={{0,24},{4,28},{8,16},{12,20},{16,8},{20,12},{24,0},{28,4},{1,25},{... | collective-permute-start | bytes 393224 | tf_op jit(solution)/shard_map/ppermute | solution.py:576
  212.9 9.0 %collective-permute-start.24 = (bf16[1,128,512]{2,1,0:T(8,128)(2,1)S(1)}, bf16[1,128,512]{2,1,0:T(8,128)(2,1)S(1)}, u32[]{:S(2)}, u32[]{:S(2)}) collective-permute-start(bf16[1,128,512]{2,1,0:T(8,128)(2,1)S(1)} %get-tuple-element.201), channel_id=1, source_target_pairs={{0,16},{4,20},{8,24},{12,28},{16,0},{20,4},{24,8},{28,12},{1,17},{... | collective-permute-start | bytes 393224 | tf_op jit(solution)/shard_map/ppermute | solution.py:576
  214.2 8.1 %collective-permute-start.23 = (bf16[1,128,512]{2,1,0:T(8,128)(2,1)S(1)}, bf16[1,128,512]{2,1,0:T(8,128)(2,1)S(1)}, u32[]{:S(2)}, u32[]{:S(2)}) collective-permute-start(bf16[1,128,512]{2,1,0:T(8,128)(2,1)S(1)} %get-tuple-element.202), channel_id=1, source_target_pairs={{0,8},{4,12},{8,0},{12,4},{16,24},{20,28},{24,16},{28,20},{1,9},{5... | collective-permute-start | bytes 393224 | tf_op jit(solution)/shard_map/ppermute | solution.py:576
  218.3 6.9 %collective-permute-start.33 = (bf16[1,128,512]{2,1,0:T(8,128)(2,1)}, bf16[1,128,512]{2,1,0:T(8,128)(2,1)S(1)}, u32[]{:S(2)}, u32[]{:S(2)}) collective-permute-start(bf16[1,128,512]{2,1,0:T(8,128)(2,1)} %get-tuple-element.197), channel_id=1, source_target_pairs={{0,8},{4,12},{8,0},{12,4},{16,24},{20,28},{24,16},{28,20},{1,9},{5... | collective-permute-start | bytes 393224 | tf_op jit(solution)/shard_map/ppermute | solution.py:576
  218.7 8.7 %collective-permute-start.35 = (bf16[1,128,512]{2,1,0:T(8,128)(2,1)S(1)}, bf16[1,128,512]{2,1,0:T(8,128)(2,1)}, u32[]{:S(2)}, u32[]{:S(2)}) collective-permute-start(bf16[1,128,512]{2,1,0:T(8,128)(2,1)S(1)} %get-tuple-element.198), channel_id=1, source_target_pairs={{0,24},{4,28},{8,16},{12,20},{16,8},{20,12},{24,0},{28,4},{1,25},{... | collective-permute-start | bytes 393224 | tf_op jit(solution)/shard_map/ppermute | solution.py:576
  220.2 7.7 %collective-permute-start.34 = (bf16[1,128,512]{2,1,0:T(8,128)(2,1)S(1)}, bf16[1,128,512]{2,1,0:T(8,128)(2,1)}, u32[]{:S(2)}, u32[]{:S(2)}) collective-permute-start(bf16[1,128,512]{2,1,0:T(8,128)(2,1)S(1)} %get-tuple-element.199), channel_id=1, source_target_pairs={{0,16},{4,20},{8,24},{12,28},{16,0},{20,4},{24,8},{28,12},{1,17},{... | collective-permute-start | bytes 393224 | tf_op jit(solution)/shard_map/ppermute | solution.py:576
  223.7 7.3 %collective-permute-start.28 = (bf16[4,185,64]{1,2,0:T(8,128)(2,1)S(1)}, bf16[4,185,64]{1,2,0:T(8,128)(2,1)S(1)}, u32[]{:S(2)}, u32[]{:S(2)}) collective-permute-start(bf16[4,185,64]{1,2,0:T(8,128)(2,1)S(1)} %slice.117), channel_id=1, source_target_pairs={{0,4},{4,0},{8,12},{12,8},{16,20},{20,16},{24,28},{28,24},{1,5},{5... | collective-permute-start | bytes 284168 | tf_op jit(solution)/shard_map/ppermute | solution.py:576
  224.8 9.8 %copy-start = (bf16[1,256,1024]{2,1,0:T(8,128)(2,1)S(1)}, bf16[1,256,1024]{2,1,0:T(8,128)(2,1)}, u32[]{:S(2)}) copy-start(bf16[1,256,1024]{2,1,0:T(8,128)(2,1)} %param.13) | copy-start | bytes 1572868
  229.0 12.0 %copy-start.11 = (bf16[128]{0:T(256)(128)(2,1)S(1)}, bf16[128]{0:T(256)(128)(2,1)}, u32[]{:S(2)}) copy-start(bf16[128]{0:T(256)(128)(2,1)} %param.15) | copy-start | bytes 772
  231.1 5.6 %collective-permute-start.29 = (bf16[185,64]{0,1:T(8,128)(2,1)S(1)}, bf16[185,64]{0,1:T(8,128)(2,1)S(1)}, u32[]{:S(2)}, u32[]{:S(2)}) collective-permute-start(bf16[185,64]{0,1:T(8,128)(2,1)S(1)} %get-tuple-element.208), channel_id=1, source_target_pairs={{0,8},{4,12},{8,0},{12,4},{16,24},{20,28},{24,16},{28,20},{1,9},{5... | collective-permute-start | bytes 71048 | tf_op jit(solution)/shard_map/ppermute | solution.py:576
  232.3 4.8 %collective-permute-start.31 = (bf16[185,64]{0,1:T(8,128)(2,1)S(1)}, bf16[185,64]{0,1:T(8,128)(2,1)S(1)}, u32[]{:S(2)}, u32[]{:S(2)}) collective-permute-start(bf16[185,64]{0,1:T(8,128)(2,1)S(1)} %get-tuple-element.209), channel_id=1, source_target_pairs={{0,24},{4,28},{8,16},{12,20},{16,8},{20,12},{24,0},{28,4},{1,25},{... | collective-permute-start | bytes 71048 | tf_op jit(solution)/shard_map/ppermute | solution.py:576
  233.7 3.9 %collective-permute-start.30 = (bf16[185,64]{0,1:T(8,128)(2,1)S(1)}, bf16[185,64]{0,1:T(8,128)(2,1)S(1)}, u32[]{:S(2)}, u32[]{:S(2)}) collective-permute-start(bf16[185,64]{0,1:T(8,128)(2,1)S(1)} %get-tuple-element.210), channel_id=1, source_target_pairs={{0,16},{4,20},{8,24},{12,28},{16,0},{20,4},{24,8},{28,12},{1,17},{... | collective-permute-start | bytes 71048 | tf_op jit(solution)/shard_map/ppermute | solution.py:576
  (4 other events, 13.2 us)
Sparse Core Ops, SparseCore 0:
  16.5 45.1 all-gather.7
  69.8 52.8 all-gather.5
  125.0 43.2 reduce-scatter.2
  191.4 45.9 reduce-scatter.4

commit v6 on v5

--- a/solution.py
+++ b/solution.py
@@ -11,7 +11,7 @@
 f32 = jnp.float32
 LOG2E = 1.4426950408889634
 LN2 = 0.6931471805599453
-ROWS = 128
+ROWS = 256
 STEPS = 16
 LANES = 128
 SCALE = 1.0
@@ -85,6 +85,10 @@
 
 def lane_sums(values, width):
     rows = values.shape[0] // width
+    if rows > LANES:
+        step = LANES * width
+        parts = [values[i : i + step] for i in range(0, values.shape[0], step)]
+        return jnp.concatenate([lane_sums(part, width) for part in parts], 1)
     sums = dot(values, jnp.ones((LANES, rows), bf16))
     lane = iota((width, rows), 1)
     kept = [jnp.zeros((width, rows), f32)] * 4
@@ -281,7 +285,7 @@
 
 
 def backward_kernel(
-    lay, length, own, got, low, gate, before_ref, step_ref, grad, h_ref, last_ref, dt_w, small, out_w,
+    lay, length, own, got, low, gate, before_ref, step_ref, grad, h_ref, last_ref, dt_w, small, out_w_t,
     map_ref, send_ref, out_ref, gate_ref, rate_ref, dt_w_ref, bias_ref,
     carry, grads, terms, drive, scan_grad, lanes, cross_b, cross_c, step_rows, drive_rows, grad_rows,
 ):
@@ -300,7 +304,7 @@
     live = live_rows(length[0], (turns - 1 - turn) * rows, rows)
     rest = lay.rest(small)
     conv_out = low[...].astype(f32)
-    masked = dot(grad[...], out_w[...], NT) * live
+    masked = dot(grad[...], out_w_t[...]) * live
     gates = gate[...]
     sigma = jax.nn.sigmoid(gates)
     gate_ref[...] = (
@@ -376,7 +380,7 @@
     out_ref[...] = out_scan * rest[taps + 2 : taps + 3] + step_ref[...] * weighted
 
 
-def backward(lay, length, own, got, low, gate, before, step, grad, h, dt_w, small, out_w):
+def backward(lay, length, own, got, low, gate, before, step, grad, h, dt_w, small, out_w_t):
     total, chans = low.shape
     width = lay.width
     turns = total // ROWS
@@ -408,7 +412,7 @@
                 pl.BlockSpec((ROWS * width, chans), lambda i, *_: (at(i), 0)),
                 pl.BlockSpec((width, chans), lambda i, *_: (jnp.maximum(at(i) * ROWS - 1, 0), 0)),
             ]
-            + [full(a) for a in (dt_w, small, out_w)],
+            + [full(a) for a in (dt_w, small, out_w_t)],
             out_specs=[column(lay.maps), column(lay.maps), row(chans), row(chans)]
             + [full(a) for a in outs[4:]],
             scratch_shapes=[
@@ -429,7 +433,7 @@
         compiler_params=params(),
         cost_estimate=cost(40),
         name="backward",
-    )(length, own, got, low, gate, before, step, grad, h, h, dt_w, small, out_w)
+    )(length, own, got, low, gate, before, step, grad, h, h, dt_w, small, out_w_t)
 
 
 def back_kernel(
@@ -627,7 +631,9 @@
     even, x_weight = lax.optimization_barrier((even, x_weight))
     w = jnp.stack(all_pieces(even, "fsdp", fsdp))[place].reshape(depth, 2 * chans)
     pieces = all_pieces(even_pieces(out_weight, "fsdp", fsdp), "fsdp", fsdp)
-    out_w = jnp.stack(pieces)[place].transpose(1, 0, 2).reshape(chans, depth)
+    ordered = jnp.stack(pieces)[place]
+    out_w = ordered.transpose(1, 0, 2).reshape(chans, depth)
+    out_w_t = ordered.transpose(0, 2, 1).reshape(depth, chans)
     packed = jnp.concatenate(
         [
             x_weight.T,
@@ -648,25 +654,23 @@
     dt_w = gathered[:, lay.count : lay.count + dt_rows].reshape(rank, chans)
     gain = gathered[:, lay.count + dt_rows :].reshape(1, depth).astype(f32)
 
-    whole, out_w = lax.optimization_barrier((whole, out_w))
+    whole, out_w, out_w_t = lax.optimization_barrier((whole, out_w, out_w_t))
     normed, conv_in, gate, conv_sum, low, map_part, map_send = front(lay, whole, gain, small, w)
-    map_send, held = lax.optimization_barrier((map_send, cotangent[0]))
+    own, got, held = sum_all(map_part, map_send, "tp", tp, cotangent[0])
     grad_whole = lax.all_gather(held, "tp", axis=0, tiled=True)
-    own, got, _ = sum_all(map_part, map_send, "tp", tp, ())
     mixed, before, step, h, sent = forward(
         lay, lengths, own, got, low, gate, dt_w, small, out_w
     )
     block_sum = lax.psum_scatter(sent, "tp", scatter_dimension=0, tiled=True)
 
     map_part, map_send, conv_grad, gate_grad, rate_grad, dt_w_grad, bias_grad = backward(
-        lay, lengths, own, got, low, gate, before, step, grad_whole, h, dt_w, small, out_w
+        lay, lengths, own, got, low, gate, before, step, grad_whole, h, dt_w, small, out_w_t
     )
     *out_one, _ = weights(place, 0, (grad_whole,), (mixed,), w)
     own_grad, got_grad, (held, out_one) = sum_all(
         map_part, map_send, "tp", tp, (gate_grad, out_one)
     )
     *gate_one, gain_two = weights(place, 1, (normed,), (held,), w)
-    block_out = (tokens.astype(f32) + block_sum[None].astype(f32)).astype(bf16)
     out_pairs = pair_sum(*out_one, "fsdp", fsdp)
     own_grad, got_grad, gate_one, out_pairs = lax.optimization_barrier(
         (own_grad, got_grad, gate_one, out_pairs)
@@ -682,11 +686,6 @@
         (x_w_grad, taps_grad, out_terms, gate_terms)
     )
     conv_terms = chip_terms(pair_sum(*one, "fsdp", fsdp), "fsdp", fsdp)
-    out_weight_grad, gate_half, conv_half = (
-        total(terms)[0] for terms in (out_terms, gate_terms, conv_terms)
-    )
-    in_weight_grad = jnp.stack([conv_half, gate_half], 1)
-    out_weight_grad = out_weight_grad.T
     gain_grad = gain_one[:1] + gain_two[:1]
     bits = 1
     while bits < tp:
@@ -705,7 +704,14 @@
         1,
     )[place]
     pairs = pair_sum(packed[0::2], packed[1::2], "fsdp", fsdp)
-    small_grad = total(chip_terms(pairs, "fsdp", fsdp))
+    small_terms = chip_terms(pairs, "fsdp", fsdp)
+    out_terms, gate_terms, conv_terms, small_terms, block_sum = lax.optimization_barrier(
+        (out_terms, gate_terms, conv_terms, small_terms, block_sum)
+    )
+    small_grad = total(small_terms)
+    out_weight_grad = total(out_terms)[0].T
+    in_weight_grad = jnp.stack([total(conv_terms)[0], total(gate_terms)[0]], 1)
+    block_out = (tokens.astype(f32) + block_sum[None].astype(f32)).astype(bf16)
     gain_out = small_grad[top + dt_rows :].reshape(-1) / norm_gain.astype(f32)
 
     input_grads = last(tokens[0], cotangent[0], normed_grad, gain)[None]

time: 252 us -> 249 us (0.988)
  waiting for transfers between devices: 46.4 us -> 53.7 us
  Pallas kernels: 98.6 us -> 92.8 us
  other arithmetic: 9.55 us -> 6.55 us
    all_gather x1, waiting for transfers between devices: 8.35 us -> 16.4 us  [shards(): grad_whole = lax.all_gather(held, 'tp', axis=0, tiled=True)]
    pallas_call x1, Pallas kernels: 39.4 us -> 36.1 us  [backward(): pl.pallas_call(functools.partial(backward_kernel, lay), grid_spec=pltpu.P...]
    pallas_call x1, Pallas kernels: 21.9 us -> 19.3 us  [forward(): pl.pallas_call(functools.partial(forward_kernel, lay), grid_spec=pltpu.Pr...]
    unnamed x46 -> x48, local copies, waits for them, and re-layouts: 16 us -> 16 us
  transfers between devices with their start and end apart: 40 -> 40, of which waited for: 15 -> 15; matrix products, arithmetic and copies ran while one was open for 17% -> 17% of each run, Pallas kernels for 35% -> 33%
where the time goes in v6:
time: 249 us; the launch traced here: 248 us
  Pallas kernels  92.8 us (37%)
  waiting for transfers between devices  53.7 us (22%)
  local copies, waits for them, and re-layouts  36 us (14%)
  starting transfers between devices  35.2 us (14%)
  between operations  14.9 us (6%)
  blocking collectives  9.29 us (4%)
  other arithmetic  6.55 us (3%)
    pallas_call x1, Pallas kernels, backward(): pl.pallas_call(functools.partial(backward_kernel, lay), grid_spec=pltpu.P...  36.1 us
    ppermute x36, starting transfers between devices, exchange(): return lax.ppermute(values, axis, [(i, i ^ bits) for i in range(size)])  34.9 us
    ppermute x36, waiting for transfers between devices, exchange(): return lax.ppermute(values, axis, [(i, i ^ bits) for i in range(size)])  34.1 us
    pallas_call x1, Pallas kernels, forward(): pl.pallas_call(functools.partial(forward_kernel, lay), grid_spec=pltpu.Pr...  19.3 us
    pallas_call x3, Pallas kernels, weights(): pl.pallas_call(functools.partial(weights_kernel, len(lefts), half), grid_...  17 us
    all_gather x1, waiting for transfers between devices, shards(): grad_whole = lax.all_gather(held, 'tp', axis=0, tiled=True)  16.4 us
    unnamed x48, local copies, waits for them, and re-layouts  16 us
    pallas_call x1, Pallas kernels, back(): pl.pallas_call(functools.partial(back_kernel, lay), grid=(count,), in_spe...  9.93 us
  transfers between devices with their start and end apart: 40, of which 15 were waited for; matrix products, arithmetic and copies ran while one was open for 17% of the time, Pallas kernels for 33%

profile of v6, /device:TPU:0, one launch (start us, length us, event | category | flops | bytes accessed | tf_op | source)
XLA Modules:
  0.0 248.4 jit_solution(7904732515312637717)
XLA Ops:
  7.2 3.0 %collective-permute-start.1 = (bf16[512,128]{1,0:T(8,128)(2,1)}, bf16[512,128]{1,0:T(8,128)(2,1)S(1)}, u32[]{:S(2)}, u32[]{:S(2)}) collective-permute-start(bf16[512,128]{1,0:T(8,128)(2,1)} %param.24), channel_id=1, source_target_pairs={{0,8},{4,12},{8,0},{12,4},{16,24},{20,28},{24,16},{28,20},{1,9},{5... | collective-permute-start | bytes 393224 | tf_op jit(solution)/shard_map/ppermute | solution.py:580
  10.2 1.5 collective-permute-start.5
  11.7 1.7 copy.154
  13.4 1.4 collective-permute-start.9
  14.8 1.5 collective-permute-start.8
  23.8 8.1 %collective-permute-done.3 = bf16[512,128]{1,0:T(8,128)(2,1)S(1)} collective-permute-done((bf16[512,128]{1,0:T(8,128)(2,1)}, bf16[512,128]{1,0:T(8,128)(2,1)S(1)}, u32[]{:S(2)}, u32[]{:S(2)}) %collective-permute-start.3) | collective-permute-done | bytes 131104 | tf_op jit(solution)/shard_map/ppermute | solution.py:580
  33.4 9.3 %all-gather.2 = bf16[8,194,64]{1,2,0:T(8,128)(2,1)S(1)} all-gather(bf16[1,194,64]{1,2,0:T(8,128)(2,1)S(1)} %bitcast.124), channel_id=3, replica_groups=mesh['fsdp'=8,'tp'=4] {'fsdp'}, dimensions={0}, use_global_device_ids=true | all-gather | bytes 223488 | tf_op jit(solution)/shard_map/all_gather | solution.py:651
  46.4 1.3 copy.122
  47.7 1.0 bitcast_dynamic-update-slice_fusion.7
  48.6 1.1 copy_bitcast_fusion.out_w
  49.8 1.0 bitcast_dynamic-update-slice_fusion.6
  50.7 1.0 bitcast_dynamic-update-slice_fusion.5
  51.7 1.0 bitcast_dynamic-update-slice_fusion.4
  52.7 1.0 bitcast_dynamic-update-slice_fusion.3
  53.7 1.0 bitcast_dynamic-update-slice_fusion.2
  54.6 1.0 bitcast_dynamic-update-slice_fusion.1
  55.6 1.0 bitcast_dynamic-update-slice_fusion
  56.6 2.0 gather_fusion.1
  58.6 3.1 %all-gather.8.cloned.1.call-done = bf16[1,1024,1024]{2,1,0:T(8,128)(2,1)} async-done(((bf16[1,256,1024]{2,1,0:T(8,128)(2,1)}), bf16[1,1024,1024]{2,1,0:T(8,128)(2,1)}) %all-gather.8.cloned.1.call-update) | async-done | bytes 2097168 | tf_op jit(solution)/shard_map/all_gather | solution.py:629
  61.8 7.9 %front.1 = (bf16[1024,1024]{1,0:T(8,128)(2,1)}, f32[1024,512]{1,0:T(8,128)}, f32[1024,512]{1,0:T(8,128)}, f32[1024,512]{1,0:T(8,128)}, bf16[1024,512]{1,0:T(8,12...) custom-call(bf16[1024,1024]{1,0:T(8,128)(2,1)} %bitcast.129, f32[1,1024]{1,0:T(1,128)} %reshape.114.gain, ...), custom_call_target="tpu_custom_call" | custom-call | flops 8999999488 | bytes 27000000 | tf_op jit(solution)/shard_map/front/pallas_call | solution.py:168
  69.7 6.9 %collective-permute-done.14 = bf16[96,1024]{1,0:T(8,128)(2,1)S(1)} collective-permute-done((bf16[96,1024]{1,0:T(8,128)(2,1)}, bf16[96,1024]{1,0:T(8,128)(2,1)S(1)}, u32[]{:S(2)}, u32[]{:S(2)}) %collective-permute-start.14) | collective-permute-done | bytes 196640 | tf_op jit(solution)/shard_map/ppermute | solution.py:580
  76.7 1.8 fusion.3
  78.5 1.4 collective-permute-start.15
  82.0 4.2 %collective-permute-done.15.got = bf16[96,1024]{1,0:T(8,128)(2,1)S(1)} collective-permute-done((bf16[96,1024]{1,0:T(8,128)(2,1)S(1)}, bf16[96,1024]{1,0:T(8,128)(2,1)S(1)}, u32[]{:S(2)}, u32[]{:S(2)}) %collective-permute-start.15) | collective-permute-done | bytes 196640 | tf_op jit(solution)/shard_map/ppermute | solution.py:580
  86.9 19.3 %forward.1 = (bf16[1024,512]{1,0:T(8,128)(2,1)}, f32[1024,512]{1,0:T(8,128)}, f32[1024,512]{1,0:T(8,128)}, bf16[16384,512]{1,0:T(8,128)(2,1)}, bf16[1024,1024]{1,0:T(8,128)(2,1)}) custom-call(s32[1]{0:T(128)S(6)} %copy.170.length, f32[96,1024]{1,0:T(8,128)} %get-tuple-element.232.own, bf16[96,1024]{1,0:T(8,128)(2,1)} %copy-done.10, ...), custom_call_target="tpu_custom_call" | custom-call | flops 24000000000 | bytes 72000000 | tf_op jit(solution)/shard_map/forward/pallas_call | solution.py:252
  106.4 16.4 %all-gather.6.cloned.1.call-done.grad.refs_0_ = bf16[1024,1024]{1,0:T(8,128)(2,1)} async-done(((bf16[256,1024]{1,0:T(8,128)(2,1)}), bf16[1024,1024]{1,0:T(8,128)(2,1)}) %all-gather.6.cloned.1.call-update) | async-done | bytes 2097168 | tf_op jit(solution)/shard_map/all_gather | solution.py:660
  122.8 36.1 %backward.1 = (f32[96,1024]{1,0:T(8,128)}, bf16[96,1024]{1,0:T(8,128)(2,1)}, f32[1024,512]{1,0:T(8,128)}, bf16[1024,512]{1,0:T(8,128)(2,1)}, f32[16,512]{1,0:T(8...) custom-call(s32[1]{0:T(128)S(6)} %copy.170.length, f32[96,1024]{1,0:T(8,128)} %get-tuple-element.232.own, ...), custom_call_target="tpu_custom_call" | custom-call | flops 40000000000 | bytes 120000000 | tf_op jit(solution)/shard_map/backward/pallas_call | solution.py:399
  159.0 5.7 %weights.3 = (bf16[4,1,128,512]{3,2,1,0:T(8,128)(2,1)}, bf16[4,1,128,512]{3,2,1,0:T(8,128)(2,1)}, f32[8,1024]{1,0:T(8,128)}) custom-call(s32[8]{0:T(128)} %iota_xor_fusion.place, bf16[1024,1024]{1,0:T(8,128)(2,1)} %all-gather.6.cloned.1.call-done.grad.refs_0_, bf16[1024,512]{1,0:T(8,128)(2,1)} %get-tuple-element.109.refs_1_, bf16[1024,1024]{1,0:T(8,128)(2,1)} %bitcast.111), custom_call_target="tpu_custom_call" | custom-call | flops 3000000000 | bytes 9000000 | tf_op jit(solution)/shard_map/weights/pallas_call | solution.py:537
  164.7 4.6 %collective-permute-done.16 = bf16[96,1024]{1,0:T(8,128)(2,1)S(1)} collective-permute-done((bf16[96,1024]{1,0:T(8,128)(2,1)}, bf16[96,1024]{1,0:T(8,128)(2,1)S(1)}, u32[]{:S(2)}, u32[]{:S(2)}) %collective-permute-start.16) | collective-permute-done | bytes 196640 | tf_op jit(solution)/shard_map/ppermute | solution.py:580
  170.1 3.1 %collective-permute-start.17 = (bf16[96,1024]{1,0:T(8,128)(2,1)S(1)}, bf16[96,1024]{1,0:T(8,128)(2,1)S(1)}, u32[]{:S(2)}, u32[]{:S(2)}) collective-permute-start(bf16[96,1024]{1,0:T(8,128)(2,1)S(1)} %get-tuple-element.229), channel_id=1, source_target_pairs={{0,3},{1,2},{2,1},{3,0},{4,7},{5,6},{6,5},{7,4},{8,11},{9,10},{10,... | collective-permute-start | bytes 589832 | tf_op jit(solution)/shard_map/ppermute | solution.py:580
  173.2 5.7 %weights.4 = (bf16[4,1,128,512]{3,2,1,0:T(8,128)(2,1)}, bf16[4,1,128,512]{3,2,1,0:T(8,128)(2,1)}, f32[8,1024]{1,0:T(8,128)}) custom-call(s32[8]{0:T(128)} %iota_xor_fusion.place, bf16[1024,1024]{1,0:T(8,128)(2,1)} %get-tuple-element.113.refs_0_, bf16[1024,512]{1,0:T(8,128)(2,1)} %get-tuple-element.114.refs_1_.gate_grad, bf16[1024,1024]{1,0:T(8,128)(2,1)} %bitcast.112), custom_call_target="tpu_custom_call" | custom-call | flops 3000000000 | bytes 9000000 | tf_op jit(solution)/shard_map/weights/pallas_call | solution.py:537
  180.0 9.9 %back.1 = (bf16[1024,1024]{1,0:T(8,128)(2,1)}, bf16[1024,512]{1,0:T(8,128)(2,1)}, f32[96,512]{1,0:T(8,128)}, f32[8,512]{1,0:T(8,128)}) custom-call(f32[96,1024]{1,0:T(8,128)} %get-tuple-element.119.own, bf16[96,1024]{1,0:T(8,128)(2,1)} %copy-done.11, bf16[128,512]{1,0:T(8,128)(2,1)} %copy.132.small, f32[1024,512]{1,0:T(8,128)} %get-tuple-element.121.out_grad, ...), custom_call_target="tpu_custom_call" | custom-call | flops 11000000512 | bytes 33000000 | tf_op jit(solution)/shard_map/back/pallas_call | solution.py:491
  190.0 5.7 %weights.5 = (bf16[4,1,128,512]{3,2,1,0:T(8,128)(2,1)}, bf16[4,1,128,512]{3,2,1,0:T(8,128)(2,1)}, f32[8,1024]{1,0:T(8,128)}) custom-call(s32[8]{0:T(128)} %iota_xor_fusion.place, bf16[1024,1024]{1,0:T(8,128)(2,1)} %get-tuple-element.113.refs_0_, bf16[1024,512]{1,0:T(8,128)(2,1)} %get-tuple-element.137.refs_1_, bf16[1024,1024]{1,0:T(8,128)(2,1)} %bitcast.114), custom_call_target="tpu_custom_call" | custom-call | flops 3000000000 | bytes 9000000 | tf_op jit(solution)/shard_map/weights/pallas_call | solution.py:537
  197.0 4.0 %collective-permute-start.30 = (f32[1,1024]{1,0:T(1,128)S(1)}, f32[1,1024]{1,0:T(1,128)S(1)}, u32[]{:S(2)}, u32[]{:S(2)}) collective-permute-start(f32[1,1024]{1,0:T(1,128)S(1)} %slice_add_fusion.1), channel_id=1, source_target_pairs={{0,1},{1,0},{2,3},{3,2},{4,5},{5,4},{6,7},{7,6},{8,9},{9,8},{10,11... | collective-permute-start | bytes 12296 | tf_op jit(solution)/shard_map/ppermute | solution.py:580
  201.7 2.4 collective-permute-start.21
  205.2 2.1 collective-permute-start.31
  208.2 2.6 %collective-permute-done.31 = f32[1,1024]{1,0:T(1,128)S(1)} collective-permute-done((f32[1,1024]{1,0:T(1,128)S(1)}, f32[1,1024]{1,0:T(1,128)S(1)}, u32[]{:S(2)}, u32[]{:S(2)}) %collective-permute-start.31) | collective-permute-done | bytes 4128 | tf_op jit(solution)/shard_map/ppermute | solution.py:580
  210.8 2.4 collective-permute-start.25
  216.1 1.8 collective-permute-done.25
  217.9 1.1 collective-permute-done.24
  220.4 1.5 collective-permute-start.29
  222.8 1.2 collective-permute-start.27
  224.0 1.5 collective-permute-start.35
  226.4 1.3 collective-permute-done.29
  228.5 2.0 collective-permute-done.28
  235.3 1.2 copy.145
  238.4 1.0 fusion
  239.4 2.5 last.1
  (165 shorter events, 34.6 us)
Async XLA Ops:
  7.2 54.6 %all-gather.8.cloned.1.call-start = ((), (), s32[]{:S(2)}) async-start(), calls=%async_computation.5 | async-start | bytes 2621440 | tf_op jit(solution)/shard_map/all_gather | solution.py:629
  7.2 16.4 %collective-permute-start.1 = (bf16[512,128]{1,0:T(8,128)(2,1)}, bf16[512,128]{1,0:T(8,128)(2,1)S(1)}, u32[]{:S(2)}, u32[]{:S(2)}) collective-permute-start(bf16[512,128]{1,0:T(8,128)(2,1)} %param.24), channel_id=1, source_target_pairs={{0,8},{4,12},{8,0},{12,4},{16,24},{20,28},{24,16},{28,20},{1,9},{5... | collective-permute-start | bytes 393224 | tf_op jit(solution)/shard_map/ppermute | solution.py:580
  10.2 12.8 %collective-permute-start = (bf16[512,128]{1,0:T(8,128)(2,1)}, bf16[512,128]{1,0:T(8,128)(2,1)S(1)}, u32[]{:S(2)}, u32[]{:S(2)}) collective-permute-start(bf16[512,128]{1,0:T(8,128)(2,1)} %param.24), channel_id=1, source_target_pairs={{0,4},{4,0},{8,12},{12,8},{16,20},{20,16},{24,28},{28,24},{1,5},{5... | collective-permute-start | bytes 393224 | tf_op jit(solution)/shard_map/ppermute | solution.py:580
  10.2 13.6 %collective-permute-start.5 = (bf16[512,128]{1,0:T(8,128)(2,1)}, bf16[512,128]{1,0:T(8,128)(2,1)S(1)}, u32[]{:S(2)}, u32[]{:S(2)}) collective-permute-start(bf16[512,128]{1,0:T(8,128)(2,1)} %param.24), channel_id=1, source_target_pairs={{0,24},{4,28},{8,16},{12,20},{16,8},{20,12},{24,0},{28,4},{1,25},{... | collective-permute-start | bytes 393224 | tf_op jit(solution)/shard_map/ppermute | solution.py:580
  13.4 18.7 %collective-permute-start.9 = (bf16[128,1024]{1,0:T(8,128)(2,1)}, bf16[128,1024]{1,0:T(8,128)(2,1)}, u32[]{:S(2)}, u32[]{:S(2)}) collective-permute-start(bf16[128,1024]{1,0:T(8,128)(2,1)} %bitcast.65), channel_id=1, source_target_pairs={{0,24},{4,28},{8,16},{12,20},{16,8},{20,12},{24,0},{28,4},{1,25},{... | collective-permute-start | bytes 786440 | tf_op jit(solution)/shard_map/ppermute | solution.py:580
  14.8 17.7 %collective-permute-start.8 = (bf16[128,1024]{1,0:T(8,128)(2,1)}, bf16[128,1024]{1,0:T(8,128)(2,1)}, u32[]{:S(2)}, u32[]{:S(2)}) collective-permute-start(bf16[128,1024]{1,0:T(8,128)(2,1)} %bitcast.65), channel_id=1, source_target_pairs={{0,16},{4,20},{8,24},{12,28},{16,0},{20,4},{24,8},{28,12},{1,17},{... | collective-permute-start | bytes 786440 | tf_op jit(solution)/shard_map/ppermute | solution.py:580
  16.4 106.4 %all-gather.6.cloned.1.call-start = ((), (), s32[]{:S(2)}) async-start(), calls=%async_computation.2 | async-start | bytes 2621440 | tf_op jit(solution)/shard_map/all_gather | solution.py:660
  23.0 9.5 %collective-permute-start.7 = (bf16[128,1024]{1,0:T(8,128)(2,1)}, bf16[128,1024]{1,0:T(8,128)(2,1)}, u32[]{:S(2)}, u32[]{:S(2)}) collective-permute-start(bf16[128,1024]{1,0:T(8,128)(2,1)} %bitcast.65), channel_id=1, source_target_pairs={{0,8},{4,12},{8,0},{12,4},{16,24},{20,28},{24,16},{28,20},{1,9},{5... | collective-permute-start | bytes 786440 | tf_op jit(solution)/shard_map/ppermute | solution.py:580
  23.6 8.4 %collective-permute-start.3 = (bf16[512,128]{1,0:T(8,128)(2,1)}, bf16[512,128]{1,0:T(8,128)(2,1)S(1)}, u32[]{:S(2)}, u32[]{:S(2)}) collective-permute-start(bf16[512,128]{1,0:T(8,128)(2,1)} %param.24), channel_id=1, source_target_pairs={{0,16},{4,20},{8,24},{12,28},{16,0},{20,4},{24,8},{28,12},{1,17},{... | collective-permute-start | bytes 393224 | tf_op jit(solution)/shard_map/ppermute | solution.py:580
  23.8 21.1 %collective-permute-start.2 = (bf16[512,128]{1,0:T(8,128)(2,1)S(1)}, bf16[512,128]{1,0:T(8,128)(2,1)S(1)}, u32[]{:S(2)}, u32[]{:S(2)}) collective-permute-start(bf16[512,128]{1,0:T(8,128)(2,1)S(1)} %collective-permute-done.1), channel_id=1, source_target_pairs={{0,4},{4,0},{8,12},{12,8},{16,20},{20,16},{24,28},{28,24},{1,5},{5... | collective-permute-start | bytes 393224 | tf_op jit(solution)/shard_map/ppermute | solution.py:580
  32.0 13.6 %collective-permute-start.6 = (bf16[512,128]{1,0:T(8,128)(2,1)S(1)}, bf16[512,128]{1,0:T(8,128)(2,1)S(1)}, u32[]{:S(2)}, u32[]{:S(2)}) collective-permute-start(bf16[512,128]{1,0:T(8,128)(2,1)S(1)} %collective-permute-done.5), channel_id=1, source_target_pairs={{0,4},{4,0},{8,12},{12,8},{16,20},{20,16},{24,28},{28,24},{1,5},{5... | collective-permute-start | bytes 393224 | tf_op jit(solution)/shard_map/ppermute | solution.py:580
  32.1 13.2 %collective-permute-start.4 = (bf16[512,128]{1,0:T(8,128)(2,1)S(1)}, bf16[512,128]{1,0:T(8,128)(2,1)S(1)}, u32[]{:S(2)}, u32[]{:S(2)}) collective-permute-start(bf16[512,128]{1,0:T(8,128)(2,1)S(1)} %collective-permute-done.3), channel_id=1, source_target_pairs={{0,4},{4,0},{8,12},{12,8},{16,20},{20,16},{24,28},{28,24},{1,5},{5... | collective-permute-start | bytes 393224 | tf_op jit(solution)/shard_map/ppermute | solution.py:580
  44.4 5.4 %collective-permute-start.10 = (bf16[128,1024]{1,0:T(8,128)(2,1)}, bf16[128,1024]{1,0:T(8,128)(2,1)}, u32[]{:S(2)}, u32[]{:S(2)}) collective-permute-start(bf16[128,1024]{1,0:T(8,128)(2,1)} %bitcast.65), channel_id=1, source_target_pairs={{0,4},{4,0},{8,12},{12,8},{16,20},{20,16},{24,28},{28,24},{1,5},{5... | collective-permute-start | bytes 786440 | tf_op jit(solution)/shard_map/ppermute | solution.py:580
  44.7 7.0 %collective-permute-start.11 = (bf16[128,1024]{1,0:T(8,128)(2,1)}, bf16[128,1024]{1,0:T(8,128)(2,1)}, u32[]{:S(2)}, u32[]{:S(2)}) collective-permute-start(bf16[128,1024]{1,0:T(8,128)(2,1)} %collective-permute-done.7), channel_id=1, source_target_pairs={{0,4},{4,0},{8,12},{12,8},{16,20},{20,16},{24,28},{28,24},{1,5},{5... | collective-permute-start | bytes 786440 | tf_op jit(solution)/shard_map/ppermute | solution.py:580
  44.9 8.8 %collective-permute-start.12 = (bf16[128,1024]{1,0:T(8,128)(2,1)}, bf16[128,1024]{1,0:T(8,128)(2,1)}, u32[]{:S(2)}, u32[]{:S(2)}) collective-permute-start(bf16[128,1024]{1,0:T(8,128)(2,1)} %collective-permute-done.8), channel_id=1, source_target_pairs={{0,4},{4,0},{8,12},{12,8},{16,20},{20,16},{24,28},{28,24},{1,5},{5... | collective-permute-start | bytes 786440 | tf_op jit(solution)/shard_map/ppermute | solution.py:580
  45.3 10.3 %collective-permute-start.13 = (bf16[128,1024]{1,0:T(8,128)(2,1)}, bf16[128,1024]{1,0:T(8,128)(2,1)}, u32[]{:S(2)}, u32[]{:S(2)}) collective-permute-start(bf16[128,1024]{1,0:T(8,128)(2,1)} %collective-permute-done.9), channel_id=1, source_target_pairs={{0,4},{4,0},{8,12},{12,8},{16,20},{20,16},{24,28},{28,24},{1,5},{5... | collective-permute-start | bytes 786440 | tf_op jit(solution)/shard_map/ppermute | solution.py:580
  69.6 6.9 %collective-permute-start.14 = (bf16[96,1024]{1,0:T(8,128)(2,1)}, bf16[96,1024]{1,0:T(8,128)(2,1)S(1)}, u32[]{:S(2)}, u32[]{:S(2)}) collective-permute-start(bf16[96,1024]{1,0:T(8,128)(2,1)} %get-tuple-element.96), channel_id=1, source_target_pairs={{0,1},{1,0},{2,3},{3,2},{4,5},{5,4},{6,7},{7,6},{8,9},{9,8},{10,11... | collective-permute-start | bytes 589832 | tf_op jit(solution)/shard_map/ppermute | solution.py:580
  76.6 151.9 %reduce-scatter.3.cloned.1.call-start = ((), (), s32[]{:S(2)}) async-start(), calls=%async_computation.3 | async-start | bytes 2621440 | tf_op jit(solution)/shard_map/reduce_scatter | solution.py:664
  78.5 7.7 %collective-permute-start.15 = (bf16[96,1024]{1,0:T(8,128)(2,1)S(1)}, bf16[96,1024]{1,0:T(8,128)(2,1)S(1)}, u32[]{:S(2)}, u32[]{:S(2)}) collective-permute-start(bf16[96,1024]{1,0:T(8,128)(2,1)S(1)} %get-tuple-element.231), channel_id=1, source_target_pairs={{0,3},{1,2},{2,1},{3,0},{4,7},{5,6},{6,5},{7,4},{8,11},{9,10},{10,... | collective-permute-start | bytes 589832 | tf_op jit(solution)/shard_map/ppermute | solution.py:580
  106.2 133.2 %reduce-scatter.5.cloned.1.call-start = ((), (), s32[]{:S(2)}) async-start(), calls=%async_computation.4 | async-start | bytes 2621440 | tf_op jit(solution)/shard_map/reduce_scatter | solution.py:681
  158.9 10.4 %collective-permute-start.16 = (bf16[96,1024]{1,0:T(8,128)(2,1)}, bf16[96,1024]{1,0:T(8,128)(2,1)S(1)}, u32[]{:S(2)}, u32[]{:S(2)}) collective-permute-start(bf16[96,1024]{1,0:T(8,128)(2,1)} %get-tuple-element.107), channel_id=1, source_target_pairs={{0,1},{1,0},{2,3},{3,2},{4,5},{5,4},{6,7},{7,6},{8,9},{9,8},{10,11... | collective-permute-start | bytes 589832 | tf_op jit(solution)/shard_map/ppermute | solution.py:580
  159.0 10.3 %copy-start.5 = (f32[96,1024]{1,0:T(8,128)S(1)}, f32[96,1024]{1,0:T(8,128)}, u32[]{:S(2)}) copy-start(f32[96,1024]{1,0:T(8,128)} %get-tuple-element.106) | copy-start | bytes 1179652
  169.3 9.5 %collective-permute-start.18 = (bf16[4,1,128,512]{3,2,1,0:T(8,128)(2,1)}, bf16[4,1,128,512]{3,2,1,0:T(8,128)(2,1)S(1)}, u32[]{:S(2)}, u32[]{:S(2)}) collective-permute-start(bf16[4,1,128,512]{3,2,1,0:T(8,128)(2,1)} %get-tuple-element.118), channel_id=1, source_target_pairs={{0,4},{4,0},{8,12},{12,8},{16,20},{20,16},{24,28},{28,24},{1,5},{5... | collective-permute-start | bytes 1572872 | tf_op jit(solution)/shard_map/ppermute | solution.py:580
  170.1 9.2 %collective-permute-start.17 = (bf16[96,1024]{1,0:T(8,128)(2,1)S(1)}, bf16[96,1024]{1,0:T(8,128)(2,1)S(1)}, u32[]{:S(2)}, u32[]{:S(2)}) collective-permute-start(bf16[96,1024]{1,0:T(8,128)(2,1)S(1)} %get-tuple-element.229), channel_id=1, source_target_pairs={{0,3},{1,2},{2,1},{3,0},{4,7},{5,6},{6,5},{7,4},{8,11},{9,10},{10,... | collective-permute-start | bytes 589832 | tf_op jit(solution)/shard_map/ppermute | solution.py:580
  173.2 5.7 %copy-start.4 = (bf16[4,1,128,512]{3,2,1,0:T(8,128)(2,1)S(1)}, bf16[4,1,128,512]{3,2,1,0:T(8,128)(2,1)}, u32[]{:S(2)}) copy-start(bf16[4,1,128,512]{3,2,1,0:T(8,128)(2,1)} %get-tuple-element.117) | copy-start | bytes 1572868
  190.0 15.2 %collective-permute-start.22 = (bf16[4,1,128,512]{3,2,1,0:T(8,128)(2,1)}, bf16[4,1,128,512]{3,2,1,0:T(8,128)(2,1)S(1)}, u32[]{:S(2)}, u32[]{:S(2)}) collective-permute-start(bf16[4,1,128,512]{3,2,1,0:T(8,128)(2,1)} %get-tuple-element.128), channel_id=1, source_target_pairs={{0,4},{4,0},{8,12},{12,8},{16,20},{20,16},{24,28},{28,24},{1,5},{5... | collective-permute-start | bytes 1572872 | tf_op jit(solution)/shard_map/ppermute | solution.py:580
  190.0 17.3 %copy-start.3 = (bf16[4,1,128,512]{3,2,1,0:T(8,128)(2,1)S(1)}, bf16[4,1,128,512]{3,2,1,0:T(8,128)(2,1)}, u32[]{:S(2)}) copy-start(bf16[4,1,128,512]{3,2,1,0:T(8,128)(2,1)} %get-tuple-element.127) | copy-start | bytes 1572868
  195.7 18.6 %copy-start.8 = (f32[16,512]{1,0:T(8,128)S(1)}, f32[16,512]{1,0:T(8,128)}, u32[]{:S(2)}) copy-start(f32[16,512]{1,0:T(8,128)} %get-tuple-element.141) | copy-start | bytes 98308
  195.7 19.3 %copy-start.7 = (f32[64,512]{1,0:T(8,128)S(1)}, f32[64,512]{1,0:T(8,128)}, u32[]{:S(2)}) copy-start(f32[64,512]{1,0:T(8,128)} %get-tuple-element.144) | copy-start | bytes 393220
  195.7 18.0 %collective-permute-start.26 = (bf16[4,1,128,512]{3,2,1,0:T(8,128)(2,1)}, bf16[4,1,128,512]{3,2,1,0:T(8,128)(2,1)S(1)}, u32[]{:S(2)}, u32[]{:S(2)}) collective-permute-start(bf16[4,1,128,512]{3,2,1,0:T(8,128)(2,1)} %get-tuple-element.139), channel_id=1, source_target_pairs={{0,4},{4,0},{8,12},{12,8},{16,20},{20,16},{24,28},{28,24},{1,5},{5... | collective-permute-start | bytes 1572872 | tf_op jit(solution)/shard_map/ppermute | solution.py:580
  197.0 7.7 %collective-permute-start.30 = (f32[1,1024]{1,0:T(1,128)S(1)}, f32[1,1024]{1,0:T(1,128)S(1)}, u32[]{:S(2)}, u32[]{:S(2)}) collective-permute-start(f32[1,1024]{1,0:T(1,128)S(1)} %slice_add_fusion.1), channel_id=1, source_target_pairs={{0,1},{1,0},{2,3},{3,2},{4,5},{5,4},{6,7},{7,6},{8,9},{9,8},{10,11... | collective-permute-start | bytes 12296 | tf_op jit(solution)/shard_map/ppermute | solution.py:580
  201.7 14.2 %copy-start.2 = (bf16[4,1,128,512]{3,2,1,0:T(8,128)(2,1)S(1)}, bf16[4,1,128,512]{3,2,1,0:T(8,128)(2,1)}, u32[]{:S(2)}) copy-start(bf16[4,1,128,512]{3,2,1,0:T(8,128)(2,1)} %get-tuple-element.138) | copy-start | bytes 1572868
  201.7 11.5 %collective-permute-start.21 = (bf16[1,128,512]{2,1,0:T(8,128)(2,1)S(1)}, bf16[1,128,512]{2,1,0:T(8,128)(2,1)S(1)}, u32[]{:S(2)}, u32[]{:S(2)}) collective-permute-start(bf16[1,128,512]{2,1,0:T(8,128)(2,1)S(1)} %get-tuple-element.241), channel_id=1, source_target_pairs={{0,24},{4,28},{8,16},{12,20},{16,8},{20,12},{24,0},{28,4},{1,25},{... | collective-permute-start | bytes 393224 | tf_op jit(solution)/shard_map/ppermute | solution.py:580
  204.0 12.0 %collective-permute-start.20 = (bf16[1,128,512]{2,1,0:T(8,128)(2,1)}, bf16[1,128,512]{2,1,0:T(8,128)(2,1)S(1)}, u32[]{:S(2)}, u32[]{:S(2)}) collective-permute-start(bf16[1,128,512]{2,1,0:T(8,128)(2,1)} %get-tuple-element.242), channel_id=1, source_target_pairs={{0,16},{4,20},{8,24},{12,28},{16,0},{20,4},{24,8},{28,12},{1,17},{... | collective-permute-start | bytes 393224 | tf_op jit(solution)/shard_map/ppermute | solution.py:580
  204.6 11.4 %collective-permute-start.19 = (bf16[1,128,512]{2,1,0:T(8,128)(2,1)S(1)}, bf16[1,128,512]{2,1,0:T(8,128)(2,1)S(1)}, u32[]{:S(2)}, u32[]{:S(2)}) collective-permute-start(bf16[1,128,512]{2,1,0:T(8,128)(2,1)S(1)} %get-tuple-element.243), channel_id=1, source_target_pairs={{0,8},{4,12},{8,0},{12,4},{16,24},{20,28},{24,16},{28,20},{1,9},{5... | collective-permute-start | bytes 393224 | tf_op jit(solution)/shard_map/ppermute | solution.py:580
  205.2 5.6 %collective-permute-start.31 = (f32[1,1024]{1,0:T(1,128)S(1)}, f32[1,1024]{1,0:T(1,128)S(1)}, u32[]{:S(2)}, u32[]{:S(2)}) collective-permute-start(f32[1,1024]{1,0:T(1,128)S(1)} %add.89), channel_id=1, source_target_pairs={{0,3},{1,2},{2,1},{3,0},{4,7},{5,6},{6,5},{7,4},{8,11},{9,10},{10,... | collective-permute-start | bytes 12296 | tf_op jit(solution)/shard_map/ppermute | solution.py:580
  207.4 11.5 %copy-start.9 = (f32[8,512]{1,0:T(8,128)S(1)}, f32[8,512]{1,0:T(8,128)}, u32[]{:S(2)}) copy-start(f32[8,512]{1,0:T(8,128)} %get-tuple-element.142) | copy-start | bytes 49156
  207.4 11.5 %copy-start.6 = (f32[96,512]{1,0:T(8,128)S(1)}, f32[96,512]{1,0:T(8,128)}, u32[]{:S(2)}) copy-start(f32[96,512]{1,0:T(8,128)} %get-tuple-element.140) | copy-start | bytes 589828
  210.8 7.1 %collective-permute-start.25 = (bf16[1,128,512]{2,1,0:T(8,128)(2,1)}, bf16[1,128,512]{2,1,0:T(8,128)(2,1)S(1)}, u32[]{:S(2)}, u32[]{:S(2)}) collective-permute-start(bf16[1,128,512]{2,1,0:T(8,128)(2,1)} %get-tuple-element.237), channel_id=1, source_target_pairs={{0,24},{4,28},{8,16},{12,20},{16,8},{20,12},{24,0},{28,4},{1,25},{... | collective-permute-start | bytes 393224 | tf_op jit(solution)/shard_map/ppermute | solution.py:580
  213.1 5.8 %collective-permute-start.24 = (bf16[1,128,512]{2,1,0:T(8,128)(2,1)}, bf16[1,128,512]{2,1,0:T(8,128)(2,1)S(1)}, u32[]{:S(2)}, u32[]{:S(2)}) collective-permute-start(bf16[1,128,512]{2,1,0:T(8,128)(2,1)} %get-tuple-element.238), channel_id=1, source_target_pairs={{0,16},{4,20},{8,24},{12,28},{16,0},{20,4},{24,8},{28,12},{1,17},{... | collective-permute-start | bytes 393224 | tf_op jit(solution)/shard_map/ppermute | solution.py:580
  213.8 5.2 %collective-permute-start.23 = (bf16[1,128,512]{2,1,0:T(8,128)(2,1)}, bf16[1,128,512]{2,1,0:T(8,128)(2,1)S(1)}, u32[]{:S(2)}, u32[]{:S(2)}) collective-permute-start(bf16[1,128,512]{2,1,0:T(8,128)(2,1)} %get-tuple-element.239), channel_id=1, source_target_pairs={{0,8},{4,12},{8,0},{12,4},{16,24},{20,28},{24,16},{28,20},{1,9},{5... | collective-permute-start | bytes 393224 | tf_op jit(solution)/shard_map/ppermute | solution.py:580
  220.3 3.7 %collective-permute-start.32 = (bf16[4,185,64]{1,2,0:T(8,128)(2,1)S(1)}, bf16[4,185,64]{1,2,0:T(8,128)(2,1)S(1)}, u32[]{:S(2)}, u32[]{:S(2)}) collective-permute-start(bf16[4,185,64]{1,2,0:T(8,128)(2,1)S(1)} %slice.121), channel_id=1, source_target_pairs={{0,4},{4,0},{8,12},{12,8},{16,20},{20,16},{24,28},{28,24},{1,5},{5... | collective-permute-start | bytes 284168 | tf_op jit(solution)/shard_map/ppermute | solution.py:580
  220.4 7.3 %collective-permute-start.29 = (bf16[1,128,512]{2,1,0:T(8,128)(2,1)S(1)}, bf16[1,128,512]{2,1,0:T(8,128)(2,1)S(1)}, u32[]{:S(2)}, u32[]{:S(2)}) collective-permute-start(bf16[1,128,512]{2,1,0:T(8,128)(2,1)S(1)} %get-tuple-element.233), channel_id=1, source_target_pairs={{0,24},{4,28},{8,16},{12,20},{16,8},{20,12},{24,0},{28,4},{1,25},{... | collective-permute-start | bytes 393224 | tf_op jit(solution)/shard_map/ppermute | solution.py:580
  221.9 8.6 %collective-permute-start.28 = (bf16[1,128,512]{2,1,0:T(8,128)(2,1)S(1)}, bf16[1,128,512]{2,1,0:T(8,128)(2,1)S(1)}, u32[]{:S(2)}, u32[]{:S(2)}) collective-permute-start(bf16[1,128,512]{2,1,0:T(8,128)(2,1)S(1)} %get-tuple-element.234), channel_id=1, source_target_pairs={{0,16},{4,20},{8,24},{12,28},{16,0},{20,4},{24,8},{28,12},{1,17},{... | collective-permute-start | bytes 393224 | tf_op jit(solution)/shard_map/ppermute | solution.py:580
  222.8 7.7 %collective-permute-start.27 = (bf16[1,128,512]{2,1,0:T(8,128)(2,1)S(1)}, bf16[1,128,512]{2,1,0:T(8,128)(2,1)S(1)}, u32[]{:S(2)}, u32[]{:S(2)}) collective-permute-start(bf16[1,128,512]{2,1,0:T(8,128)(2,1)S(1)} %get-tuple-element.235), channel_id=1, source_target_pairs={{0,8},{4,12},{8,0},{12,4},{16,24},{20,28},{24,16},{28,20},{1,9},{5... | collective-permute-start | bytes 393224 | tf_op jit(solution)/shard_map/ppermute | solution.py:580
  224.0 7.1 %collective-permute-start.35 = (bf16[185,64]{0,1:T(8,128)(2,1)S(1)}, bf16[185,64]{0,1:T(8,128)(2,1)S(1)}, u32[]{:S(2)}, u32[]{:S(2)}) collective-permute-start(bf16[185,64]{0,1:T(8,128)(2,1)S(1)} %get-tuple-element.245), channel_id=1, source_target_pairs={{0,24},{4,28},{8,16},{12,20},{16,8},{20,12},{24,0},{28,4},{1,25},{... | collective-permute-start | bytes 71048 | tf_op jit(solution)/shard_map/ppermute | solution.py:580
  225.5 6.0 %collective-permute-start.34 = (bf16[185,64]{0,1:T(8,128)(2,1)S(1)}, bf16[185,64]{0,1:T(8,128)(2,1)S(1)}, u32[]{:S(2)}, u32[]{:S(2)}) collective-permute-start(bf16[185,64]{0,1:T(8,128)(2,1)S(1)} %get-tuple-element.246), channel_id=1, source_target_pairs={{0,16},{4,20},{8,24},{12,28},{16,0},{20,4},{24,8},{28,12},{1,17},{... | collective-permute-start | bytes 71048 | tf_op jit(solution)/shard_map/ppermute | solution.py:580
  227.7 3.9 %collective-permute-start.33 = (bf16[185,64]{0,1:T(8,128)(2,1)S(1)}, bf16[185,64]{0,1:T(8,128)(2,1)S(1)}, u32[]{:S(2)}, u32[]{:S(2)}) collective-permute-start(bf16[185,64]{0,1:T(8,128)(2,1)S(1)} %get-tuple-element.247), channel_id=1, source_target_pairs={{0,8},{4,12},{8,0},{12,4},{16,24},{20,28},{24,16},{28,20},{1,9},{5... | collective-permute-start | bytes 71048 | tf_op jit(solution)/shard_map/ppermute | solution.py:580
  (5 other events, 12.6 us)
Sparse Core Ops, SparseCore 0:
  16.5 45.1 all-gather.7
  76.7 45.9 all-gather.5
  125.1 47.5 reduce-scatter.2
  190.1 46.1 reduce-scatter.4

commit v7 on v6

--- a/solution.py
+++ b/solution.py
@@ -124,19 +124,34 @@
         return ref[self.first :, :].astype(f32)
 
 
-def front_kernel(
-    lay, tokens, gain, small, w,
-    normed_ref, input_ref, gate_ref, sum_ref, low_ref, map_ref, send_ref, halo,
-):
-    rows = tokens.shape[0]
+def front_kernel(lay, shards, pieces, order, place, tokens, gain, small, *refs):
+    shard_refs = refs[:shards]
+    piece_refs = refs[shards : shards + pieces]
+    (
+        normed_ref, w, input_ref, gate_ref, sum_ref, low_ref, map_ref, send_ref, halo, values,
+    ) = refs[shards + pieces :]
+    rows = normed_ref.shape[0]
+    cut = tokens.shape[0]
     chans = small.shape[1]
     taps = lay.taps
-
-    @pl.when(pl.program_id(0) == 0)
+    turn = pl.program_id(0)
+
+    @pl.when(turn == 0)
     def _():
+        for index in range(pieces):
+            depth = piece_refs[index].shape[0]
+            start = pl.multiple_of(place[index] * depth, depth)
+            w[pl.ds(start, depth), :] = piece_refs[index][...]
         halo[:8] = jnp.zeros_like(halo[:8])
 
-    values = tokens[...].astype(f32)
+    for index in range(shards):
+
+        @pl.when(order[turn] == index)
+        def _(index=index):
+            values[cut:] = shard_refs[index][...].astype(f32)
+
+    values[:cut] = tokens[...].astype(f32)
+    values = values[...]
     inverse = lax.rsqrt(jnp.mean(values * values, axis=-1, keepdims=True) + epsilon)
     normed = (values * inverse * gain[...]).astype(bf16)
     normed_ref[...] = normed
@@ -159,19 +174,31 @@
     send_ref[...] = mapped.astype(bf16)
 
 
-def front(lay, tokens, gain, small, w):
-    total, depth = tokens.shape
-    rows = 256
+def front(lay, order, place, tokens, shards, gain, small, pieces):
+    count = len(shards)
+    cut = tokens.shape[0] // count
+    rows = cut + shards[0].shape[0]
+    depth = tokens.shape[1]
+    total = count * rows
     chans = small.shape[1]
-    row = lambda w: pl.BlockSpec((rows, w), lambda i: (i, 0))
-    column = lambda w: pl.BlockSpec((w, rows), lambda i: (0, i))
+    both = pieces[0].shape[1]
+    row = lambda w: pl.BlockSpec((rows, w), lambda i, *_: (i, 0))
+    column = lambda w: pl.BlockSpec((w, rows), lambda i, *_: (0, i))
     return pl.pallas_call(
-        functools.partial(front_kernel, lay),
-        grid=(total // rows,),
-        in_specs=[row(depth)] + [full(a) for a in (gain, small, w)],
-        out_specs=[row(depth)] + [row(chans)] * 4 + [column(lay.maps)] * 2,
+        functools.partial(front_kernel, lay, count, len(pieces)),
+        grid_spec=pltpu.PrefetchScalarGridSpec(
+            num_scalar_prefetch=2,
+            grid=(count,),
+            in_specs=[pl.BlockSpec((cut, depth), lambda i, *_: (i, 0))]
+            + [full(a) for a in (gain, small, *shards, *pieces)],
+            out_specs=[row(depth), pl.BlockSpec((depth, both), lambda i, *_: (0, 0))]
+            + [row(chans)] * 4
+            + [column(lay.maps)] * 2,
+            scratch_shapes=[pltpu.VMEM((rows + 8, chans), f32), pltpu.VMEM((rows, depth), f32)],
+        ),
         out_shape=[
             shape((total, depth), bf16),
+            shape((depth, both), bf16),
             shape((total, chans), f32),
             shape((total, chans), f32),
             shape((total, chans), f32),
@@ -179,11 +206,10 @@
             shape((lay.maps, total), f32),
             shape((lay.maps, total), bf16),
         ],
-        scratch_shapes=[pltpu.VMEM((rows + 8, chans), f32)],
         compiler_params=params(),
         cost_estimate=cost(9),
         name="front",
-    )(tokens, gain, small, w)
+    )(order, place, tokens, gain, small, *shards, *pieces)
 
 
 def forward_kernel(
@@ -626,10 +652,22 @@
     lay = Rows(x_weight.shape[1], a_log.shape[0], conv_weight.shape[0])
     maps, width, taps, rank, first = lay.maps, lay.width, lay.taps, lay.rank, lay.first
 
-    whole = lax.all_gather(tokens[0], "tp", axis=0, tiled=True)
+    cut = tokens.shape[1] * 3 // 4
+    whole = lax.all_gather(tokens[0, :cut], "tp", axis=0, tiled=True)
+    order = ((lax.axis_index("tp") - jnp.arange(tp)) % tp).astype(jnp.int32)
+    direct = [tokens[0, cut:]] + [
+        lax.ppermute(tokens[0, cut:], "tp", [(i, (i + k) % tp) for i in range(tp)])
+        for k in range(1, tp)
+    ]
     even = even_pieces(in_weight.reshape(in_weight.shape[0], 2 * chans), "fsdp", fsdp)
-    even, x_weight = lax.optimization_barrier((even, x_weight))
-    w = jnp.stack(all_pieces(even, "fsdp", fsdp))[place].reshape(depth, 2 * chans)
+    even, direct, x_weight, a_log, conv_weight, conv_bias, dt_bias, d_skip, dt_weight, gain_part = (
+        lax.optimization_barrier(
+            (
+                even, direct, x_weight, a_log, conv_weight, conv_bias, dt_bias, d_skip, dt_weight,
+                norm_gain,
+            )
+        )
+    )
     pieces = all_pieces(even_pieces(out_weight, "fsdp", fsdp), "fsdp", fsdp)
     ordered = jnp.stack(pieces)[place]
     out_w = ordered.transpose(1, 0, 2).reshape(chans, depth)
@@ -644,19 +682,24 @@
             d_skip[None],
             jnp.zeros((lay.count - first - taps - 3, part), bf16),
             dt_weight.reshape(-1, part),
-            norm_gain.reshape(-1, part),
+            gain_part.reshape(-1, part),
         ],
         0,
     )
     gathered = lax.all_gather(packed, "fsdp", axis=0)
+    w_pieces = all_pieces(even, "fsdp", fsdp)
+    gathered, w_pieces = lax.optimization_barrier((gathered, w_pieces))
     small = gathered[:, : lay.count].transpose(1, 0, 2).reshape(lay.count, chans)
     dt_rows = dt_weight.size // part
     dt_w = gathered[:, lay.count : lay.count + dt_rows].reshape(rank, chans)
     gain = gathered[:, lay.count + dt_rows :].reshape(1, depth).astype(f32)
 
-    whole, out_w, out_w_t = lax.optimization_barrier((whole, out_w, out_w_t))
-    normed, conv_in, gate, conv_sum, low, map_part, map_send = front(lay, whole, gain, small, w)
-    own, got, held = sum_all(map_part, map_send, "tp", tp, cotangent[0])
+    normed, w, conv_in, gate, conv_sum, low, map_part, map_send = front(
+        lay, order, place, whole, direct, gain, small, w_pieces
+    )
+    own, got, (held, out_w, out_w_t) = sum_all(
+        map_part, map_send, "tp", tp, (cotangent[0], out_w, out_w_t)
+    )
     grad_whole = lax.all_gather(held, "tp", axis=0, tiled=True)
     mixed, before, step, h, sent = forward(
         lay, lengths, own, got, low, gate, dt_w, small, out_w

time: 249 us -> 247 us (level)
  local copies, waits for them, and re-layouts: 36 us -> 23.1 us
  starting transfers between devices: 35.2 us -> 44.3 us
    unnamed x48 -> x72, local copies, waits for them, and re-layouts: 16 us -> 6.85 us
    ppermute x0 -> x3, starting transfers between devices: none -> 6.11 us  [shards(): lax.ppermute(tokens[0, cut:], 'tp', [(i, (i + k) % tp) for i in range(tp)])]
    all_gather x1, waiting for transfers between devices: 3.13 us -> 0.01 us  [shards(): whole = lax.all_gather(tokens[0, :cut], 'tp', axis=0, tiled=True)]
    ppermute x36, starting transfers between devices: 34.9 us -> 37.8 us  [exchange(): return lax.ppermute(values, axis, [(i, i ^ bits) for i in range(size)])]
  transfers between devices with their start and end apart: 40 -> 43, of which waited for: 15 -> 15; matrix products, arithmetic and copies ran while one was open for 17% -> 11% of each run, Pallas kernels for 33% -> 34%
where the time goes in v7:
time: 247 us
  Pallas kernels  94.1 us (38%)
  waiting for transfers between devices  54.6 us (22%)
  starting transfers between devices  44.3 us (18%)
  local copies, waits for them, and re-layouts  23.1 us (9%)
  between operations  15.1 us (6%)
  blocking collectives  9.32 us (4%)
  other arithmetic  6.06 us (2%)
    ppermute x36, starting transfers between devices, exchange(): return lax.ppermute(values, axis, [(i, i ^ bits) for i in range(size)])  37.8 us
    pallas_call x1, Pallas kernels, backward(): pl.pallas_call(functools.partial(backward_kernel, lay), grid_spec=pltpu.P...  36.2 us
    ppermute x36, waiting for transfers between devices, exchange(): return lax.ppermute(values, axis, [(i, i ^ bits) for i in range(size)])  35 us
    pallas_call x1, Pallas kernels, forward(): pl.pallas_call(functools.partial(forward_kernel, lay), grid_spec=pltpu.Pr...  19.4 us
    all_gather x1, waiting for transfers between devices, shards(): grad_whole = lax.all_gather(held, 'tp', axis=0, tiled=True)  17.2 us
    pallas_call x3, Pallas kernels, weights(): pl.pallas_call(functools.partial(weights_kernel, len(lefts), half), grid_...  17.1 us
    pallas_call x1, Pallas kernels, back(): pl.pallas_call(functools.partial(back_kernel, lay), grid=(count,), in_spe...  9.91 us
    all_gather x1, blocking collectives, shards(): gathered = lax.all_gather(packed, 'fsdp', axis=0)  9.32 us
  transfers between devices with their start and end apart: 43, of which 15 were waited for; matrix products, arithmetic and copies ran while one was open for 11% of the time, Pallas kernels for 34%

profile of v7, /device:TPU:0, one launch (start us, length us, event | category | flops | bytes accessed | tf_op | source)
XLA Modules:
  0.0 246.5 jit_solution(15331342432297963080)
XLA Ops:
  7.3 0.9 slice_bitcast_fusion.12.refs_0_
  8.3 5.1 %collective-permute-start.5 = (bf16[64,1024]{1,0:T(8,128)(2,1)S(1)}, bf16[64,1024]{1,0:T(8,128)(2,1)S(1)}, u32[]{:S(2)}, u32[]{:S(2)}) collective-permute-start(bf16[64,1024]{1,0:T(8,128)(2,1)S(1)} %slice_bitcast_fusion.12.refs_0_), channel_id=1, source_target_pairs={{0,3},{1,0},{2,1},{3,2},{4,7},{5,4},{6,5},{7,6},{8,11},{9,8},{10,9... | collective-permute-start | bytes 393224 | tf_op jit(solution)/shard_map/ppermute | solution.py:659
  13.4 1.0 collective-permute-start.3
  14.4 1.5 collective-permute-start.12
  15.9 1.8 slice.110
  18.2 0.9 bitcast_dynamic-update-slice_fusion.7
  19.7 1.0 copy.153
  20.7 1.6 collective-permute-start.16
  22.3 2.3 collective-permute-done.4.refs_2_
  24.6 2.4 collective-permute-start.2
  28.1 1.6 collective-permute-start.14
  29.7 11.9 %collective-permute-done.14 = bf16[512,128]{1,0:T(8,128)(2,1)S(1)} collective-permute-done((bf16[512,128]{1,0:T(8,128)(2,1)S(1)}, bf16[512,128]{1,0:T(8,128)(2,1)S(1)}, u32[]{:S(2)}, u32[]{:S(2)}) %collective-permute-start.14) | collective-permute-done | bytes 131104 | tf_op jit(solution)/shard_map/ppermute | solution.py:606
  45.3 1.3 copy.132
  46.8 9.3 %all-gather.2 = bf16[8,194,64]{1,2,0:T(8,128)(2,1)S(1)} all-gather(bf16[1,194,64]{1,2,0:T(8,128)(2,1)S(1)} %bitcast.109), channel_id=3, replica_groups=mesh['fsdp'=8,'tp'=4] {'fsdp'}, dimensions={0}, use_global_device_ids=true | all-gather | bytes 223488 | tf_op jit(solution)/shard_map/all_gather | solution.py:689
  57.9 9.1 %front.1 = (bf16[1024,1024]{1,0:T(8,128)(2,1)}, bf16[1024,1024]{1,0:T(8,128)(2,1)}, f32[1024,512]{1,0:T(8,128)}, f32[1024,512]{1,0:T(8,128)}, f32[1024,512]{1,0:...) custom-call(s32[4]{0:T(128)} %and_select_fusion.order, s32[8]{0:T(128)} %iota_xor_fusion.place, ...), custom_call_target="tpu_custom_call" | custom-call | flops 8999999488 | bytes 27000000 | tf_op jit(solution)/shard_map/front/pallas_call | solution.py:187
  67.0 2.5 %collective-permute-start.10 = (bf16[96,1024]{1,0:T(8,128)(2,1)}, bf16[96,1024]{1,0:T(8,128)(2,1)S(1)}, u32[]{:S(2)}, u32[]{:S(2)}) collective-permute-start(bf16[96,1024]{1,0:T(8,128)(2,1)} %get-tuple-element.135), channel_id=1, source_target_pairs={{0,1},{1,0},{2,3},{3,2},{4,5},{5,4},{6,7},{7,6},{8,9},{9,8},{10,11... | collective-permute-start | bytes 589832 | tf_op jit(solution)/shard_map/ppermute | solution.py:606
  69.6 1.2 copy_bitcast_fusion.out_w
  70.7 4.5 %collective-permute-done.10 = bf16[96,1024]{1,0:T(8,128)(2,1)S(1)} collective-permute-done((bf16[96,1024]{1,0:T(8,128)(2,1)}, bf16[96,1024]{1,0:T(8,128)(2,1)S(1)}, u32[]{:S(2)}, u32[]{:S(2)}) %collective-permute-start.10) | collective-permute-done | bytes 196640 | tf_op jit(solution)/shard_map/ppermute | solution.py:606
  76.1 2.1 collective-permute-start.18
  79.8 4.8 %collective-permute-done.18.got = bf16[96,1024]{1,0:T(8,128)(2,1)S(1)} collective-permute-done((bf16[96,1024]{1,0:T(8,128)(2,1)S(1)}, bf16[96,1024]{1,0:T(8,128)(2,1)S(1)}, u32[]{:S(2)}, u32[]{:S(2)}) %collective-permute-start.18) | collective-permute-done | bytes 196640 | tf_op jit(solution)/shard_map/ppermute | solution.py:606
  85.3 19.4 %forward.1 = (bf16[1024,512]{1,0:T(8,128)(2,1)}, f32[1024,512]{1,0:T(8,128)}, f32[1024,512]{1,0:T(8,128)}, bf16[16384,512]{1,0:T(8,128)(2,1)}, bf16[1024,1024]{1,0:T(8,128)(2,1)}) custom-call(s32[1]{0:T(128)S(6)} %copy.162.length, f32[96,1024]{1,0:T(8,128)} %get-tuple-element.272.own, bf16[96,1024]{1,0:T(8,128)(2,1)} %copy-done.24, ...), custom_call_target="tpu_custom_call" | custom-call | flops 24000000000 | bytes 72000000 | tf_op jit(solution)/shard_map/forward/pallas_call | solution.py:278
  104.9 17.2 %all-gather.6.cloned.1.call-done.grad.refs_0_ = bf16[1024,1024]{1,0:T(8,128)(2,1)} async-done(((bf16[256,1024]{1,0:T(8,128)(2,1)}), bf16[1024,1024]{1,0:T(8,128)(2,1)}) %all-gather.6.cloned.1.call-update) | async-done | bytes 2097168 | tf_op jit(solution)/shard_map/all_gather | solution.py:703
  122.1 36.2 %backward.1 = (f32[96,1024]{1,0:T(8,128)}, bf16[96,1024]{1,0:T(8,128)(2,1)}, f32[1024,512]{1,0:T(8,128)}, bf16[1024,512]{1,0:T(8,128)(2,1)}, f32[16,512]{1,0:T(8...) custom-call(s32[1]{0:T(128)S(6)} %copy.162.length, f32[96,1024]{1,0:T(8,128)} %get-tuple-element.272.own, ...), custom_call_target="tpu_custom_call" | custom-call | flops 40000000000 | bytes 120000000 | tf_op jit(solution)/shard_map/backward/pallas_call | solution.py:425
  158.4 5.7 %weights.3 = (bf16[4,1,128,512]{3,2,1,0:T(8,128)(2,1)}, bf16[4,1,128,512]{3,2,1,0:T(8,128)(2,1)}, f32[8,1024]{1,0:T(8,128)}) custom-call(s32[8]{0:T(128)} %iota_xor_fusion.place, bf16[1024,1024]{1,0:T(8,128)(2,1)} %all-gather.6.cloned.1.call-done.grad.refs_0_, bf16[1024,512]{1,0:T(8,128)(2,1)} %get-tuple-element.148.refs_1_, ...), custom_call_target="tpu_custom_call" | custom-call | flops 3000000000 | bytes 9000000 | tf_op jit(solution)/shard_map/weights/pallas_call | solution.py:563
  164.1 3.8 %collective-permute-done.19 = bf16[96,1024]{1,0:T(8,128)(2,1)S(1)} collective-permute-done((bf16[96,1024]{1,0:T(8,128)(2,1)}, bf16[96,1024]{1,0:T(8,128)(2,1)S(1)}, u32[]{:S(2)}, u32[]{:S(2)}) %collective-permute-start.19) | collective-permute-done | bytes 196640 | tf_op jit(solution)/shard_map/ppermute | solution.py:606
  167.9 0.8 fusion.3
  168.8 2.7 %collective-permute-start.20 = (bf16[96,1024]{1,0:T(8,128)(2,1)S(1)}, bf16[96,1024]{1,0:T(8,128)(2,1)S(1)}, u32[]{:S(2)}, u32[]{:S(2)}) collective-permute-start(bf16[96,1024]{1,0:T(8,128)(2,1)S(1)} %get-tuple-element.269), channel_id=1, source_target_pairs={{0,3},{1,2},{2,1},{3,0},{4,7},{5,6},{6,5},{7,4},{8,11},{9,10},{10,... | collective-permute-start | bytes 589832 | tf_op jit(solution)/shard_map/ppermute | solution.py:606
  171.5 5.7 %weights.4 = (bf16[4,1,128,512]{3,2,1,0:T(8,128)(2,1)}, bf16[4,1,128,512]{3,2,1,0:T(8,128)(2,1)}, f32[8,1024]{1,0:T(8,128)}) custom-call(s32[8]{0:T(128)} %iota_xor_fusion.place, bf16[1024,1024]{1,0:T(8,128)(2,1)} %get-tuple-element.153.refs_0_, bf16[1024,512]{1,0:T(8,128)(2,1)} %get-tuple-element.154.refs_1_.gate_grad, ...), custom_call_target="tpu_custom_call" | custom-call | flops 3000000000 | bytes 9000000 | tf_op jit(solution)/shard_map/weights/pallas_call | solution.py:563
  178.6 9.9 %back.1 = (bf16[1024,1024]{1,0:T(8,128)(2,1)}, bf16[1024,512]{1,0:T(8,128)(2,1)}, f32[96,512]{1,0:T(8,128)}, f32[8,512]{1,0:T(8,128)}) custom-call(f32[96,1024]{1,0:T(8,128)} %get-tuple-element.159.own, bf16[96,1024]{1,0:T(8,128)(2,1)} %copy-done.25, bf16[128,512]{1,0:T(8,128)(2,1)} %copy.130.small, f32[1024,512]{1,0:T(8,128)} %get-tuple-element.161.out_grad, ...), custom_call_target="tpu_custom_call" | custom-call | flops 11000000512 | bytes 33000000 | tf_op jit(solution)/shard_map/back/pallas_call | solution.py:517
  188.6 5.7 %weights.5 = (bf16[4,1,128,512]{3,2,1,0:T(8,128)(2,1)}, bf16[4,1,128,512]{3,2,1,0:T(8,128)(2,1)}, f32[8,1024]{1,0:T(8,128)}) custom-call(s32[8]{0:T(128)} %iota_xor_fusion.place, bf16[1024,1024]{1,0:T(8,128)(2,1)} %get-tuple-element.153.refs_0_, bf16[1024,512]{1,0:T(8,128)(2,1)} %get-tuple-element.177.refs_1_, bf16[1024,1024]{1,0:T(8,128)(2,1)} %get-tuple-element.149.refs_2_.w), custom_call_target="tpu_custom_call" | custom-call | flops 3000000000 | bytes 9000000 | tf_op jit(solution)/shard_map/weights/pallas_call | solution.py:563
  195.6 3.5 %collective-permute-start.33 = (f32[1,1024]{1,0:T(1,128)S(1)}, f32[1,1024]{1,0:T(1,128)S(1)}, u32[]{:S(2)}, u32[]{:S(2)}) collective-permute-start(f32[1,1024]{1,0:T(1,128)S(1)} %slice_add_fusion.1), channel_id=1, source_target_pairs={{0,1},{1,0},{2,3},{3,2},{4,5},{5,4},{6,7},{7,6},{8,9},{9,8},{10,11... | collective-permute-start | bytes 12296 | tf_op jit(solution)/shard_map/ppermute | solution.py:606
  199.8 2.4 collective-permute-start.24
  203.3 2.7 %collective-permute-start.34 = (f32[1,1024]{1,0:T(1,128)S(1)}, f32[1,1024]{1,0:T(1,128)S(1)}, u32[]{:S(2)}, u32[]{:S(2)}) collective-permute-start(f32[1,1024]{1,0:T(1,128)S(1)} %add.95), channel_id=1, source_target_pairs={{0,3},{1,2},{2,1},{3,0},{4,7},{5,6},{6,5},{7,4},{8,11},{9,10},{10,... | collective-permute-start | bytes 12296 | tf_op jit(solution)/shard_map/ppermute | solution.py:606
  206.9 2.0 collective-permute-done.34
  208.9 2.4 collective-permute-start.28
  214.2 1.9 collective-permute-done.28
  216.0 1.1 collective-permute-done.27
  218.5 1.5 collective-permute-start.32
  220.0 0.9 collective-permute-start.31
  220.9 1.2 collective-permute-start.30
  222.1 1.5 collective-permute-start.38
  223.6 0.9 collective-permute-start.37
  224.5 1.4 collective-permute-done.32
  226.6 2.0 collective-permute-done.31
  232.4 0.8 copy.148
  233.4 1.2 copy.145
  236.5 1.0 fusion
  237.5 2.5 %last.1 = f32[256,1024]{1,0:T(8,128)} custom-call(bf16[256,1024]{1,0:T(8,128)(2,1)} %bitcast.94, bf16[256,1024]{1,0:T(8,128)(2,1)} %bitcast.101, bf16[256,1024]{1,0:T(8,128)(2,1)} %reduce-scatter.5.cloned.1.call-done.normed_grad, f32[1,1024]{1,0:T(1,128)} %reshape.110.gain), custom_call_target="tpu_custom_call" | custom-call | flops 2000000000 | bytes 6000000 | tf_op jit(solution)/shard_map/last/pallas_call | solution.py:593
  (199 shorter events, 27.0 us)
Async XLA Ops:
  7.2 35.7 %copy-start.20 = (bf16[64]{0:T(256)(128)(2,1)S(1)}, bf16[64]{0:T(256)(128)(2,1)}, u32[]{:S(2)}) copy-start(bf16[64]{0:T(256)(128)(2,1)} %param.23) | copy-start | bytes 388
  7.2 35.6 %copy-start.19 = (bf16[64]{0:T(256)(128)(2,1)S(1)}, bf16[64]{0:T(256)(128)(2,1)}, u32[]{:S(2)}) copy-start(bf16[64]{0:T(256)(128)(2,1)} %param.21) | copy-start | bytes 388
  7.2 35.8 %copy-start.14 = (bf16[8,512]{1,0:T(8,128)(2,1)S(1)}, bf16[8,512]{1,0:T(8,128)(2,1)}, u32[]{:S(2)}) copy-start(bf16[8,512]{1,0:T(8,128)(2,1)} %param.20) | copy-start | bytes 24580
  7.2 35.4 %copy-start.18 = (bf16[64]{0:T(256)(128)(2,1)S(1)}, bf16[64]{0:T(256)(128)(2,1)}, u32[]{:S(2)}) copy-start(bf16[64]{0:T(256)(128)(2,1)} %param.18) | copy-start | bytes 388
  7.3 50.7 %all-gather.8.cloned.1.call-start = ((), (), s32[]{:S(2)}) async-start(), calls=%async_computation.5 | async-start | bytes 1966080 | tf_op jit(solution)/shard_map/all_gather | solution.py:656
  8.3 37.0 %copy-start.11 = (bf16[64,1024]{1,0:T(8,128)(2,1)}, bf16[64,1024]{1,0:T(8,128)(2,1)S(1)}, u32[]{:S(2)}) copy-start(bf16[64,1024]{1,0:T(8,128)(2,1)S(1)} %slice_bitcast_fusion.12.refs_0_) | copy-start | bytes 393220
  8.3 12.4 %collective-permute-start.5 = (bf16[64,1024]{1,0:T(8,128)(2,1)S(1)}, bf16[64,1024]{1,0:T(8,128)(2,1)S(1)}, u32[]{:S(2)}, u32[]{:S(2)}) collective-permute-start(bf16[64,1024]{1,0:T(8,128)(2,1)S(1)} %slice_bitcast_fusion.12.refs_0_), channel_id=1, source_target_pairs={{0,3},{1,0},{2,1},{3,2},{4,7},{5,4},{6,5},{7,6},{8,11},{9,8},{10,9... | collective-permute-start | bytes 393224 | tf_op jit(solution)/shard_map/ppermute | solution.py:659
  13.4 11.2 %collective-permute-start.4 = (bf16[64,1024]{1,0:T(8,128)(2,1)S(1)}, bf16[64,1024]{1,0:T(8,128)(2,1)S(1)}, u32[]{:S(2)}, u32[]{:S(2)}) collective-permute-start(bf16[64,1024]{1,0:T(8,128)(2,1)S(1)} %slice_bitcast_fusion.12.refs_0_), channel_id=1, source_target_pairs={{0,2},{1,3},{2,0},{3,1},{4,6},{5,7},{6,4},{7,5},{8,10},{9,11},{10,... | collective-permute-start | bytes 393224 | tf_op jit(solution)/shard_map/ppermute | solution.py:659
  13.4 13.7 %collective-permute-start.3 = (bf16[64,1024]{1,0:T(8,128)(2,1)S(1)}, bf16[64,1024]{1,0:T(8,128)(2,1)S(1)}, u32[]{:S(2)}, u32[]{:S(2)}) collective-permute-start(bf16[64,1024]{1,0:T(8,128)(2,1)S(1)} %slice_bitcast_fusion.12.refs_0_), channel_id=1, source_target_pairs={{0,1},{1,2},{2,3},{3,0},{4,5},{5,6},{6,7},{7,4},{8,9},{9,10},{10,1... | collective-permute-start | bytes 393224 | tf_op jit(solution)/shard_map/ppermute | solution.py:659
  14.4 13.7 %collective-permute-start.12 = (bf16[512,128]{1,0:T(8,128)(2,1)}, bf16[512,128]{1,0:T(8,128)(2,1)S(1)}, u32[]{:S(2)}, u32[]{:S(2)}) collective-permute-start(bf16[512,128]{1,0:T(8,128)(2,1)} %param.24), channel_id=1, source_target_pairs={{0,8},{4,12},{8,0},{12,4},{16,24},{20,28},{24,16},{28,20},{1,9},{5... | collective-permute-start | bytes 393224 | tf_op jit(solution)/shard_map/ppermute | solution.py:606
  15.9 11.7 %collective-permute-start.11 = (bf16[512,128]{1,0:T(8,128)(2,1)}, bf16[512,128]{1,0:T(8,128)(2,1)S(1)}, u32[]{:S(2)}, u32[]{:S(2)}) collective-permute-start(bf16[512,128]{1,0:T(8,128)(2,1)} %param.24), channel_id=1, source_target_pairs={{0,4},{4,0},{8,12},{12,8},{16,20},{20,16},{24,28},{28,24},{1,5},{5... | collective-permute-start | bytes 393224 | tf_op jit(solution)/shard_map/ppermute | solution.py:606
  17.7 104.4 %all-gather.6.cloned.1.call-start = ((), (), s32[]{:S(2)}) async-start(), calls=%async_computation.2 | async-start | bytes 2621440 | tf_op jit(solution)/shard_map/all_gather | solution.py:703
  20.7 9.0 %collective-permute-start.16 = (bf16[512,128]{1,0:T(8,128)(2,1)S(1)}, bf16[512,128]{1,0:T(8,128)(2,1)S(1)}, u32[]{:S(2)}, u32[]{:S(2)}) collective-permute-start(bf16[512,128]{1,0:T(8,128)(2,1)S(1)} %copy-done.10), channel_id=1, source_target_pairs={{0,24},{4,28},{8,16},{12,20},{16,8},{20,12},{24,0},{28,4},{1,25},{... | collective-permute-start | bytes 393224 | tf_op jit(solution)/shard_map/ppermute | solution.py:606
  24.6 17.2 %collective-permute-start.2 = (bf16[128,1024]{1,0:T(8,128)(2,1)S(1)}, bf16[128,1024]{1,0:T(8,128)(2,1)S(1)}, u32[]{:S(2)}, u32[]{:S(2)}) collective-permute-start(bf16[128,1024]{1,0:T(8,128)(2,1)S(1)} %bitcast.104), channel_id=1, source_target_pairs={{0,24},{4,28},{8,16},{12,20},{16,8},{20,12},{24,0},{28,4},{1,25},{... | collective-permute-start | bytes 786440 | tf_op jit(solution)/shard_map/ppermute | solution.py:606
  27.0 15.2 %collective-permute-start.1 = (bf16[128,1024]{1,0:T(8,128)(2,1)S(1)}, bf16[128,1024]{1,0:T(8,128)(2,1)S(1)}, u32[]{:S(2)}, u32[]{:S(2)}) collective-permute-start(bf16[128,1024]{1,0:T(8,128)(2,1)S(1)} %bitcast.105), channel_id=1, source_target_pairs={{0,16},{4,20},{8,24},{12,28},{16,0},{20,4},{24,8},{28,12},{1,17},{... | collective-permute-start | bytes 786440 | tf_op jit(solution)/shard_map/ppermute | solution.py:606
  27.5 14.7 %collective-permute-start = (bf16[128,1024]{1,0:T(8,128)(2,1)S(1)}, bf16[128,1024]{1,0:T(8,128)(2,1)S(1)}, u32[]{:S(2)}, u32[]{:S(2)}) collective-permute-start(bf16[128,1024]{1,0:T(8,128)(2,1)S(1)} %bitcast.106), channel_id=1, source_target_pairs={{0,8},{4,12},{8,0},{12,4},{16,24},{20,28},{24,16},{28,20},{1,9},{5... | collective-permute-start | bytes 786440 | tf_op jit(solution)/shard_map/ppermute | solution.py:606
  28.1 13.5 %collective-permute-start.14 = (bf16[512,128]{1,0:T(8,128)(2,1)S(1)}, bf16[512,128]{1,0:T(8,128)(2,1)S(1)}, u32[]{:S(2)}, u32[]{:S(2)}) collective-permute-start(bf16[512,128]{1,0:T(8,128)(2,1)S(1)} %copy-done.10), channel_id=1, source_target_pairs={{0,16},{4,20},{8,24},{12,28},{16,0},{20,4},{24,8},{28,12},{1,17},{... | collective-permute-start | bytes 393224 | tf_op jit(solution)/shard_map/ppermute | solution.py:606
  29.7 14.1 %collective-permute-start.13 = (bf16[512,128]{1,0:T(8,128)(2,1)S(1)}, bf16[512,128]{1,0:T(8,128)(2,1)S(1)}, u32[]{:S(2)}, u32[]{:S(2)}) collective-permute-start(bf16[512,128]{1,0:T(8,128)(2,1)S(1)} %collective-permute-done.12), channel_id=1, source_target_pairs={{0,4},{4,0},{8,12},{12,8},{16,20},{20,16},{24,28},{28,24},{1,5},{5... | collective-permute-start | bytes 393224 | tf_op jit(solution)/shard_map/ppermute | solution.py:606
  41.6 2.8 %collective-permute-start.17 = (bf16[512,128]{1,0:T(8,128)(2,1)S(1)}, bf16[512,128]{1,0:T(8,128)(2,1)S(1)}, u32[]{:S(2)}, u32[]{:S(2)}) collective-permute-start(bf16[512,128]{1,0:T(8,128)(2,1)S(1)} %collective-permute-done.16), channel_id=1, source_target_pairs={{0,4},{4,0},{8,12},{12,8},{16,20},{20,16},{24,28},{28,24},{1,5},{5... | collective-permute-start | bytes 393224 | tf_op jit(solution)/shard_map/ppermute | solution.py:606
  41.8 2.2 collective-permute-start.15
  43.2 12.9 %collective-permute-start.6 = (bf16[128,1024]{1,0:T(8,128)(2,1)S(1)}, bf16[128,1024]{1,0:T(8,128)(2,1)}, u32[]{:S(2)}, u32[]{:S(2)}) collective-permute-start(bf16[128,1024]{1,0:T(8,128)(2,1)S(1)} %bitcast.107), channel_id=1, source_target_pairs={{0,4},{4,0},{8,12},{12,8},{16,20},{20,16},{24,28},{28,24},{1,5},{5... | collective-permute-start | bytes 786440 | tf_op jit(solution)/shard_map/ppermute | solution.py:606
  43.4 12.7 %collective-permute-start.7 = (bf16[128,1024]{1,0:T(8,128)(2,1)S(1)}, bf16[128,1024]{1,0:T(8,128)(2,1)}, u32[]{:S(2)}, u32[]{:S(2)}) collective-permute-start(bf16[128,1024]{1,0:T(8,128)(2,1)S(1)} %collective-permute-done.refs_6_), channel_id=1, source_target_pairs={{0,4},{4,0},{8,12},{12,8},{16,20},{20,16},{24,28},{28,24},{1,5},{5... | collective-permute-start | bytes 786440 | tf_op jit(solution)/shard_map/ppermute | solution.py:606
  43.8 12.3 %collective-permute-start.8 = (bf16[128,1024]{1,0:T(8,128)(2,1)S(1)}, bf16[128,1024]{1,0:T(8,128)(2,1)}, u32[]{:S(2)}, u32[]{:S(2)}) collective-permute-start(bf16[128,1024]{1,0:T(8,128)(2,1)S(1)} %collective-permute-done.1.refs_8_), channel_id=1, source_target_pairs={{0,4},{4,0},{8,12},{12,8},{16,20},{20,16},{24,28},{28,24},{1,5},{5... | collective-permute-start | bytes 786440 | tf_op jit(solution)/shard_map/ppermute | solution.py:606
  44.0 12.2 %collective-permute-start.9 = (bf16[128,1024]{1,0:T(8,128)(2,1)S(1)}, bf16[128,1024]{1,0:T(8,128)(2,1)}, u32[]{:S(2)}, u32[]{:S(2)}) collective-permute-start(bf16[128,1024]{1,0:T(8,128)(2,1)S(1)} %collective-permute-done.2.refs_10_), channel_id=1, source_target_pairs={{0,4},{4,0},{8,12},{12,8},{16,20},{20,16},{24,28},{28,24},{1,5},{5... | collective-permute-start | bytes 786440 | tf_op jit(solution)/shard_map/ppermute | solution.py:606
  67.0 8.2 %collective-permute-start.10 = (bf16[96,1024]{1,0:T(8,128)(2,1)}, bf16[96,1024]{1,0:T(8,128)(2,1)S(1)}, u32[]{:S(2)}, u32[]{:S(2)}) collective-permute-start(bf16[96,1024]{1,0:T(8,128)(2,1)} %get-tuple-element.135), channel_id=1, source_target_pairs={{0,1},{1,0},{2,3},{3,2},{4,5},{5,4},{6,7},{7,6},{8,9},{9,8},{10,11... | collective-permute-start | bytes 589832 | tf_op jit(solution)/shard_map/ppermute | solution.py:606
  75.2 151.4 %reduce-scatter.3.cloned.1.call-start = ((), (), s32[]{:S(2)}) async-start(), calls=%async_computation.3 | async-start | bytes 2621440 | tf_op jit(solution)/shard_map/reduce_scatter | solution.py:707
  76.1 8.5 %collective-permute-start.18 = (bf16[96,1024]{1,0:T(8,128)(2,1)S(1)}, bf16[96,1024]{1,0:T(8,128)(2,1)S(1)}, u32[]{:S(2)}, u32[]{:S(2)}) collective-permute-start(bf16[96,1024]{1,0:T(8,128)(2,1)S(1)} %get-tuple-element.271), channel_id=1, source_target_pairs={{0,3},{1,2},{2,1},{3,0},{4,7},{5,6},{6,5},{7,4},{8,11},{9,10},{10,... | collective-permute-start | bytes 589832 | tf_op jit(solution)/shard_map/ppermute | solution.py:606
  104.7 132.8 %reduce-scatter.5.cloned.1.call-start = ((), (), s32[]{:S(2)}) async-start(), calls=%async_computation.4 | async-start | bytes 2621440 | tf_op jit(solution)/shard_map/reduce_scatter | solution.py:724
  158.3 9.6 %collective-permute-start.19 = (bf16[96,1024]{1,0:T(8,128)(2,1)}, bf16[96,1024]{1,0:T(8,128)(2,1)S(1)}, u32[]{:S(2)}, u32[]{:S(2)}) collective-permute-start(bf16[96,1024]{1,0:T(8,128)(2,1)} %get-tuple-element.146), channel_id=1, source_target_pairs={{0,1},{1,0},{2,3},{3,2},{4,5},{5,4},{6,7},{7,6},{8,9},{9,8},{10,11... | collective-permute-start | bytes 589832 | tf_op jit(solution)/shard_map/ppermute | solution.py:606
  167.9 9.3 %collective-permute-start.21 = (bf16[4,1,128,512]{3,2,1,0:T(8,128)(2,1)}, bf16[4,1,128,512]{3,2,1,0:T(8,128)(2,1)S(1)}, u32[]{:S(2)}, u32[]{:S(2)}) collective-permute-start(bf16[4,1,128,512]{3,2,1,0:T(8,128)(2,1)} %get-tuple-element.158), channel_id=1, source_target_pairs={{0,4},{4,0},{8,12},{12,8},{16,20},{20,16},{24,28},{28,24},{1,5},{5... | collective-permute-start | bytes 1572872 | tf_op jit(solution)/shard_map/ppermute | solution.py:606
  168.8 9.2 %collective-permute-start.20 = (bf16[96,1024]{1,0:T(8,128)(2,1)S(1)}, bf16[96,1024]{1,0:T(8,128)(2,1)S(1)}, u32[]{:S(2)}, u32[]{:S(2)}) collective-permute-start(bf16[96,1024]{1,0:T(8,128)(2,1)S(1)} %get-tuple-element.269), channel_id=1, source_target_pairs={{0,3},{1,2},{2,1},{3,0},{4,7},{5,6},{6,5},{7,4},{8,11},{9,10},{10,... | collective-permute-start | bytes 589832 | tf_op jit(solution)/shard_map/ppermute | solution.py:606
  188.5 14.7 %collective-permute-start.25 = (bf16[4,1,128,512]{3,2,1,0:T(8,128)(2,1)}, bf16[4,1,128,512]{3,2,1,0:T(8,128)(2,1)S(1)}, u32[]{:S(2)}, u32[]{:S(2)}) collective-permute-start(bf16[4,1,128,512]{3,2,1,0:T(8,128)(2,1)} %get-tuple-element.168), channel_id=1, source_target_pairs={{0,4},{4,0},{8,12},{12,8},{16,20},{20,16},{24,28},{28,24},{1,5},{5... | collective-permute-start | bytes 1572872 | tf_op jit(solution)/shard_map/ppermute | solution.py:606
  194.3 17.5 %collective-permute-start.29 = (bf16[4,1,128,512]{3,2,1,0:T(8,128)(2,1)}, bf16[4,1,128,512]{3,2,1,0:T(8,128)(2,1)S(1)}, u32[]{:S(2)}, u32[]{:S(2)}) collective-permute-start(bf16[4,1,128,512]{3,2,1,0:T(8,128)(2,1)} %get-tuple-element.179), channel_id=1, source_target_pairs={{0,4},{4,0},{8,12},{12,8},{16,20},{20,16},{24,28},{28,24},{1,5},{5... | collective-permute-start | bytes 1572872 | tf_op jit(solution)/shard_map/ppermute | solution.py:606
  195.6 7.1 %collective-permute-start.33 = (f32[1,1024]{1,0:T(1,128)S(1)}, f32[1,1024]{1,0:T(1,128)S(1)}, u32[]{:S(2)}, u32[]{:S(2)}) collective-permute-start(f32[1,1024]{1,0:T(1,128)S(1)} %slice_add_fusion.1), channel_id=1, source_target_pairs={{0,1},{1,0},{2,3},{3,2},{4,5},{5,4},{6,7},{7,6},{8,9},{9,8},{10,11... | collective-permute-start | bytes 12296 | tf_op jit(solution)/shard_map/ppermute | solution.py:606
  199.8 11.5 %collective-permute-start.24 = (bf16[1,128,512]{2,1,0:T(8,128)(2,1)S(1)}, bf16[1,128,512]{2,1,0:T(8,128)(2,1)S(1)}, u32[]{:S(2)}, u32[]{:S(2)}) collective-permute-start(bf16[1,128,512]{2,1,0:T(8,128)(2,1)S(1)} %get-tuple-element.281), channel_id=1, source_target_pairs={{0,24},{4,28},{8,16},{12,20},{16,8},{20,12},{24,0},{28,4},{1,25},{... | collective-permute-start | bytes 393224 | tf_op jit(solution)/shard_map/ppermute | solution.py:606
  202.1 12.0 %collective-permute-start.23 = (bf16[1,128,512]{2,1,0:T(8,128)(2,1)}, bf16[1,128,512]{2,1,0:T(8,128)(2,1)S(1)}, u32[]{:S(2)}, u32[]{:S(2)}) collective-permute-start(bf16[1,128,512]{2,1,0:T(8,128)(2,1)} %get-tuple-element.282), channel_id=1, source_target_pairs={{0,16},{4,20},{8,24},{12,28},{16,0},{20,4},{24,8},{28,12},{1,17},{... | collective-permute-start | bytes 393224 | tf_op jit(solution)/shard_map/ppermute | solution.py:606
  202.7 11.5 %collective-permute-start.22 = (bf16[1,128,512]{2,1,0:T(8,128)(2,1)S(1)}, bf16[1,128,512]{2,1,0:T(8,128)(2,1)S(1)}, u32[]{:S(2)}, u32[]{:S(2)}) collective-permute-start(bf16[1,128,512]{2,1,0:T(8,128)(2,1)S(1)} %get-tuple-element.283), channel_id=1, source_target_pairs={{0,8},{4,12},{8,0},{12,4},{16,24},{20,28},{24,16},{28,20},{1,9},{5... | collective-permute-start | bytes 393224 | tf_op jit(solution)/shard_map/ppermute | solution.py:606
  203.3 5.6 %collective-permute-start.34 = (f32[1,1024]{1,0:T(1,128)S(1)}, f32[1,1024]{1,0:T(1,128)S(1)}, u32[]{:S(2)}, u32[]{:S(2)}) collective-permute-start(f32[1,1024]{1,0:T(1,128)S(1)} %add.95), channel_id=1, source_target_pairs={{0,3},{1,2},{2,1},{3,0},{4,7},{5,6},{6,5},{7,4},{8,11},{9,10},{10,... | collective-permute-start | bytes 12296 | tf_op jit(solution)/shard_map/ppermute | solution.py:606
  208.9 7.1 %collective-permute-start.28 = (bf16[1,128,512]{2,1,0:T(8,128)(2,1)}, bf16[1,128,512]{2,1,0:T(8,128)(2,1)S(1)}, u32[]{:S(2)}, u32[]{:S(2)}) collective-permute-start(bf16[1,128,512]{2,1,0:T(8,128)(2,1)} %get-tuple-element.277), channel_id=1, source_target_pairs={{0,24},{4,28},{8,16},{12,20},{16,8},{20,12},{24,0},{28,4},{1,25},{... | collective-permute-start | bytes 393224 | tf_op jit(solution)/shard_map/ppermute | solution.py:606
  211.3 5.8 %collective-permute-start.27 = (bf16[1,128,512]{2,1,0:T(8,128)(2,1)}, bf16[1,128,512]{2,1,0:T(8,128)(2,1)S(1)}, u32[]{:S(2)}, u32[]{:S(2)}) collective-permute-start(bf16[1,128,512]{2,1,0:T(8,128)(2,1)} %get-tuple-element.278), channel_id=1, source_target_pairs={{0,16},{4,20},{8,24},{12,28},{16,0},{20,4},{24,8},{28,12},{1,17},{... | collective-permute-start | bytes 393224 | tf_op jit(solution)/shard_map/ppermute | solution.py:606
  211.8 5.3 %collective-permute-start.26 = (bf16[1,128,512]{2,1,0:T(8,128)(2,1)}, bf16[1,128,512]{2,1,0:T(8,128)(2,1)S(1)}, u32[]{:S(2)}, u32[]{:S(2)}) collective-permute-start(bf16[1,128,512]{2,1,0:T(8,128)(2,1)} %get-tuple-element.279), channel_id=1, source_target_pairs={{0,8},{4,12},{8,0},{12,4},{16,24},{20,28},{24,16},{28,20},{1,9},{5... | collective-permute-start | bytes 393224 | tf_op jit(solution)/shard_map/ppermute | solution.py:606
  218.4 3.7 %collective-permute-start.35 = (bf16[4,185,64]{1,2,0:T(8,128)(2,1)S(1)}, bf16[4,185,64]{1,2,0:T(8,128)(2,1)S(1)}, u32[]{:S(2)}, u32[]{:S(2)}) collective-permute-start(bf16[4,185,64]{1,2,0:T(8,128)(2,1)S(1)} %slice.132), channel_id=1, source_target_pairs={{0,4},{4,0},{8,12},{12,8},{16,20},{20,16},{24,28},{28,24},{1,5},{5... | collective-permute-start | bytes 284168 | tf_op jit(solution)/shard_map/ppermute | solution.py:606
  218.5 7.3 %collective-permute-start.32 = (bf16[1,128,512]{2,1,0:T(8,128)(2,1)S(1)}, bf16[1,128,512]{2,1,0:T(8,128)(2,1)S(1)}, u32[]{:S(2)}, u32[]{:S(2)}) collective-permute-start(bf16[1,128,512]{2,1,0:T(8,128)(2,1)S(1)} %get-tuple-element.273), channel_id=1, source_target_pairs={{0,24},{4,28},{8,16},{12,20},{16,8},{20,12},{24,0},{28,4},{1,25},{... | collective-permute-start | bytes 393224 | tf_op jit(solution)/shard_map/ppermute | solution.py:606
  220.0 8.6 %collective-permute-start.31 = (bf16[1,128,512]{2,1,0:T(8,128)(2,1)S(1)}, bf16[1,128,512]{2,1,0:T(8,128)(2,1)S(1)}, u32[]{:S(2)}, u32[]{:S(2)}) collective-permute-start(bf16[1,128,512]{2,1,0:T(8,128)(2,1)S(1)} %get-tuple-element.274), channel_id=1, source_target_pairs={{0,16},{4,20},{8,24},{12,28},{16,0},{20,4},{24,8},{28,12},{1,17},{... | collective-permute-start | bytes 393224 | tf_op jit(solution)/shard_map/ppermute | solution.py:606
  220.9 7.7 %collective-permute-start.30 = (bf16[1,128,512]{2,1,0:T(8,128)(2,1)S(1)}, bf16[1,128,512]{2,1,0:T(8,128)(2,1)S(1)}, u32[]{:S(2)}, u32[]{:S(2)}) collective-permute-start(bf16[1,128,512]{2,1,0:T(8,128)(2,1)S(1)} %get-tuple-element.275), channel_id=1, source_target_pairs={{0,8},{4,12},{8,0},{12,4},{16,24},{20,28},{24,16},{28,20},{1,9},{5... | collective-permute-start | bytes 393224 | tf_op jit(solution)/shard_map/ppermute | solution.py:606
  222.1 7.1 %collective-permute-start.38 = (bf16[185,64]{0,1:T(8,128)(2,1)S(1)}, bf16[185,64]{0,1:T(8,128)(2,1)S(1)}, u32[]{:S(2)}, u32[]{:S(2)}) collective-permute-start(bf16[185,64]{0,1:T(8,128)(2,1)S(1)} %get-tuple-element.285), channel_id=1, source_target_pairs={{0,24},{4,28},{8,16},{12,20},{16,8},{20,12},{24,0},{28,4},{1,25},{... | collective-permute-start | bytes 71048 | tf_op jit(solution)/shard_map/ppermute | solution.py:606
  223.6 6.0 %collective-permute-start.37 = (bf16[185,64]{0,1:T(8,128)(2,1)S(1)}, bf16[185,64]{0,1:T(8,128)(2,1)S(1)}, u32[]{:S(2)}, u32[]{:S(2)}) collective-permute-start(bf16[185,64]{0,1:T(8,128)(2,1)S(1)} %get-tuple-element.286), channel_id=1, source_target_pairs={{0,16},{4,20},{8,24},{12,28},{16,0},{20,4},{24,8},{28,12},{1,17},{... | collective-permute-start | bytes 71048 | tf_op jit(solution)/shard_map/ppermute | solution.py:606
  225.8 3.9 %collective-permute-start.36 = (bf16[185,64]{0,1:T(8,128)(2,1)S(1)}, bf16[185,64]{0,1:T(8,128)(2,1)S(1)}, u32[]{:S(2)}, u32[]{:S(2)}) collective-permute-start(bf16[185,64]{0,1:T(8,128)(2,1)S(1)} %get-tuple-element.287), channel_id=1, source_target_pairs={{0,8},{4,12},{8,0},{12,4},{16,24},{20,28},{24,16},{28,20},{1,9},{5... | collective-permute-start | bytes 71048 | tf_op jit(solution)/shard_map/ppermute | solution.py:606
  (25 other events, 328.0 us)
Sparse Core Ops, SparseCore 0:
  17.8 36.7 all-gather.7
  75.4 46.6 all-gather.5
  124.4 45.5 reduce-scatter.2
  188.7 45.4 reduce-scatter.4

commit v8 on v7

--- a/solution.py
+++ b/solution.py
@@ -660,11 +660,11 @@
         for k in range(1, tp)
     ]
     even = even_pieces(in_weight.reshape(in_weight.shape[0], 2 * chans), "fsdp", fsdp)
-    even, direct, x_weight, a_log, conv_weight, conv_bias, dt_bias, d_skip, dt_weight, gain_part = (
+    even, direct, x_weight, a_log, conv_weight, conv_bias, dt_bias, d_skip, dt_weight, gain_part, out_weight = (
         lax.optimization_barrier(
             (
                 even, direct, x_weight, a_log, conv_weight, conv_bias, dt_bias, d_skip, dt_weight,
-                norm_gain,
+                norm_gain, out_weight,
             )
         )
     )

time: 247 us -> 245 us (level)
  starting transfers between devices: 44.3 us -> 41.5 us
    ppermute x36, waiting for transfers between devices: 35 us -> 30.7 us  [exchange(): return lax.ppermute(values, axis, [(i, i ^ bits) for i in range(size)])]
    ppermute x3, waiting for transfers between devices: 2.3 us -> 5.22 us  [shards(): lax.ppermute(tokens[0, cut:], 'tp', [(i, (i + k) % tp) for i in range(tp)])]
    ppermute x36, starting transfers between devices: 37.8 us -> 35 us  [exchange(): return lax.ppermute(values, axis, [(i, i ^ bits) for i in range(size)])]
    unnamed x72 -> x74, local copies, waits for them, and re-layouts: 6.85 us -> 8.26 us
  transfers between devices with their start and end apart: 43 -> 43, of which waited for: 15 -> 18; matrix products, arithmetic and copies ran while one was open for 11% -> 11% of each run, Pallas kernels for 34% -> 34%
where the time goes in v8:
time: 245 us; the launch traced here: 244 us
  Pallas kernels  94.1 us (38%)
  waiting for transfers between devices  54.6 us (22%)
  starting transfers between devices  41.5 us (17%)
  local copies, waits for them, and re-layouts  24.4 us (10%)
  between operations  15.1 us (6%)
  blocking collectives  8.59 us (4%)
  other arithmetic  6.07 us (2%)
    pallas_call x1, Pallas kernels, backward(): pl.pallas_call(functools.partial(backward_kernel, lay), grid_spec=pltpu.P...  36.2 us
    ppermute x36, starting transfers between devices, exchange(): return lax.ppermute(values, axis, [(i, i ^ bits) for i in range(size)])  35 us
    ppermute x36, waiting for transfers between devices, exchange(): return lax.ppermute(values, axis, [(i, i ^ bits) for i in range(size)])  30.7 us
    pallas_call x1, Pallas kernels, forward(): pl.pallas_call(functools.partial(forward_kernel, lay), grid_spec=pltpu.Pr...  19.4 us
    pallas_call x3, Pallas kernels, weights(): pl.pallas_call(functools.partial(weights_kernel, len(lefts), half), grid_...  17 us
    all_gather x1, waiting for transfers between devices, shards(): grad_whole = lax.all_gather(held, 'tp', axis=0, tiled=True)  16.5 us
    pallas_call x1, Pallas kernels, back(): pl.pallas_call(functools.partial(back_kernel, lay), grid=(count,), in_spe...  9.92 us
    pallas_call x1, Pallas kernels, front(): pl.pallas_call(functools.partial(front_kernel, lay, count, len(pieces)),...  9.08 us
  transfers between devices with their start and end apart: 43, of which 18 were waited for; matrix products, arithmetic and copies ran while one was open for 11% of the time, Pallas kernels for 34%

profile of v8, /device:TPU:0, one launch (start us, length us, event | category | flops | bytes accessed | tf_op | source)
XLA Modules:
  0.0 244.3 jit_solution(7390578402174063443)
XLA Ops:
  7.3 0.9 slice_bitcast_fusion.12.refs_0_
  8.3 5.1 %collective-permute-start.5 = (bf16[64,1024]{1,0:T(8,128)(2,1)S(1)}, bf16[64,1024]{1,0:T(8,128)(2,1)S(1)}, u32[]{:S(2)}, u32[]{:S(2)}) collective-permute-start(bf16[64,1024]{1,0:T(8,128)(2,1)S(1)} %slice_bitcast_fusion.12.refs_0_), channel_id=1, source_target_pairs={{0,3},{1,0},{2,1},{3,2},{4,7},{5,4},{6,5},{7,6},{8,11},{9,8},{10,9... | collective-permute-start | bytes 393224 | tf_op jit(solution)/shard_map/ppermute | solution.py:659
  13.4 1.0 copy.153
  14.4 2.5 %collective-permute-start.2 = (bf16[128,1024]{1,0:T(8,128)(2,1)S(1)}, bf16[128,1024]{1,0:T(8,128)(2,1)S(1)}, u32[]{:S(2)}, u32[]{:S(2)}) collective-permute-start(bf16[128,1024]{1,0:T(8,128)(2,1)S(1)} %bitcast.104), channel_id=1, source_target_pairs={{0,24},{4,28},{8,16},{12,20},{16,8},{20,12},{24,0},{28,4},{1,25},{... | collective-permute-start | bytes 786440 | tf_op jit(solution)/shard_map/ppermute | solution.py:606
  17.9 1.8 slice.110
  20.3 1.1 collective-permute-start.3
  21.9 5.2 %collective-permute-done.3.refs_1_ = bf16[64,1024]{1,0:T(8,128)(2,1)S(1)} collective-permute-done((bf16[64,1024]{1,0:T(8,128)(2,1)S(1)}, bf16[64,1024]{1,0:T(8,128)(2,1)S(1)}, u32[]{:S(2)}, u32[]{:S(2)}) %collective-permute-start.3) | collective-permute-done | bytes 131104 | tf_op jit(solution)/shard_map/ppermute | solution.py:659
  27.1 1.6 collective-permute-done.1.refs_8_
  28.9 1.5 collective-permute-start.16
  30.5 1.2 collective-permute-start.12
  31.7 0.9 bitcast_dynamic-update-slice_fusion.7
  34.4 8.6 %all-gather.2 = bf16[8,194,64]{1,2,0:T(8,128)(2,1)S(1)} all-gather(bf16[1,194,64]{1,2,0:T(8,128)(2,1)S(1)} %bitcast.109), channel_id=3, replica_groups=mesh['fsdp'=8,'tp'=4] {'fsdp'}, dimensions={0}, use_global_device_ids=true | all-gather | bytes 223488 | tf_op jit(solution)/shard_map/all_gather | solution.py:689
  43.6 1.5 collective-permute-start.14
  45.1 4.4 %collective-permute-done.14 = bf16[512,128]{1,0:T(8,128)(2,1)S(1)} collective-permute-done((bf16[512,128]{1,0:T(8,128)(2,1)S(1)}, bf16[512,128]{1,0:T(8,128)(2,1)S(1)}, u32[]{:S(2)}, u32[]{:S(2)}) %collective-permute-start.14) | collective-permute-done | bytes 131104 | tf_op jit(solution)/shard_map/ppermute | solution.py:606
  54.2 1.3 copy.132
  55.5 2.1 all-gather.8.cloned.1.call-done
  57.5 9.1 %front.1 = (bf16[1024,1024]{1,0:T(8,128)(2,1)}, bf16[1024,1024]{1,0:T(8,128)(2,1)}, f32[1024,512]{1,0:T(8,128)}, f32[1024,512]{1,0:T(8,128)}, f32[1024,512]{1,0:...) custom-call(s32[4]{0:T(128)} %and_select_fusion.order, s32[8]{0:T(128)} %iota_xor_fusion.place, ...), custom_call_target="tpu_custom_call" | custom-call | flops 8999999488 | bytes 27000000 | tf_op jit(solution)/shard_map/front/pallas_call | solution.py:187
  67.2 1.1 copy_bitcast_fusion.out_w
  68.3 5.1 %collective-permute-done.10 = bf16[96,1024]{1,0:T(8,128)(2,1)S(1)} collective-permute-done((bf16[96,1024]{1,0:T(8,128)(2,1)}, bf16[96,1024]{1,0:T(8,128)(2,1)S(1)}, u32[]{:S(2)}, u32[]{:S(2)}) %collective-permute-start.10) | collective-permute-done | bytes 196640 | tf_op jit(solution)/shard_map/ppermute | solution.py:606
  74.3 1.3 collective-permute-start.18
  77.2 4.6 %collective-permute-done.18.got = bf16[96,1024]{1,0:T(8,128)(2,1)S(1)} collective-permute-done((bf16[96,1024]{1,0:T(8,128)(2,1)S(1)}, bf16[96,1024]{1,0:T(8,128)(2,1)S(1)}, u32[]{:S(2)}, u32[]{:S(2)}) %collective-permute-start.18) | collective-permute-done | bytes 196640 | tf_op jit(solution)/shard_map/ppermute | solution.py:606
  82.5 19.4 %forward.1 = (bf16[1024,512]{1,0:T(8,128)(2,1)}, f32[1024,512]{1,0:T(8,128)}, f32[1024,512]{1,0:T(8,128)}, bf16[16384,512]{1,0:T(8,128)(2,1)}, bf16[1024,1024]{1,0:T(8,128)(2,1)}) custom-call(s32[1]{0:T(128)S(6)} %copy.162.length, f32[96,1024]{1,0:T(8,128)} %get-tuple-element.274.own, bf16[96,1024]{1,0:T(8,128)(2,1)} %copy-done.25, ...), custom_call_target="tpu_custom_call" | custom-call | flops 24000000000 | bytes 72000000 | tf_op jit(solution)/shard_map/forward/pallas_call | solution.py:278
  102.2 16.5 %all-gather.6.cloned.1.call-done.grad.refs_0_ = bf16[1024,1024]{1,0:T(8,128)(2,1)} async-done(((bf16[256,1024]{1,0:T(8,128)(2,1)}), bf16[1024,1024]{1,0:T(8,128)(2,1)}) %all-gather.6.cloned.1.call-update) | async-done | bytes 2097168 | tf_op jit(solution)/shard_map/all_gather | solution.py:703
  118.7 36.2 %backward.1 = (f32[96,1024]{1,0:T(8,128)}, bf16[96,1024]{1,0:T(8,128)(2,1)}, f32[1024,512]{1,0:T(8,128)}, bf16[1024,512]{1,0:T(8,128)(2,1)}, f32[16,512]{1,0:T(8...) custom-call(s32[1]{0:T(128)S(6)} %copy.162.length, f32[96,1024]{1,0:T(8,128)} %get-tuple-element.274.own, ...), custom_call_target="tpu_custom_call" | custom-call | flops 40000000000 | bytes 120000000 | tf_op jit(solution)/shard_map/backward/pallas_call | solution.py:425
  155.0 5.7 %weights.3 = (bf16[4,1,128,512]{3,2,1,0:T(8,128)(2,1)}, bf16[4,1,128,512]{3,2,1,0:T(8,128)(2,1)}, f32[8,1024]{1,0:T(8,128)}) custom-call(s32[8]{0:T(128)} %iota_xor_fusion.place, bf16[1024,1024]{1,0:T(8,128)(2,1)} %all-gather.6.cloned.1.call-done.grad.refs_0_, bf16[1024,512]{1,0:T(8,128)(2,1)} %get-tuple-element.150.refs_1_, ...), custom_call_target="tpu_custom_call" | custom-call | flops 3000000000 | bytes 9000000 | tf_op jit(solution)/shard_map/weights/pallas_call | solution.py:563
  160.7 4.8 %collective-permute-done.19 = bf16[96,1024]{1,0:T(8,128)(2,1)S(1)} collective-permute-done((bf16[96,1024]{1,0:T(8,128)(2,1)}, bf16[96,1024]{1,0:T(8,128)(2,1)S(1)}, u32[]{:S(2)}, u32[]{:S(2)}) %collective-permute-start.19) | collective-permute-done | bytes 196640 | tf_op jit(solution)/shard_map/ppermute | solution.py:606
  166.3 2.8 %collective-permute-start.20 = (bf16[96,1024]{1,0:T(8,128)(2,1)S(1)}, bf16[96,1024]{1,0:T(8,128)(2,1)S(1)}, u32[]{:S(2)}, u32[]{:S(2)}) collective-permute-start(bf16[96,1024]{1,0:T(8,128)(2,1)S(1)} %get-tuple-element.271), channel_id=1, source_target_pairs={{0,3},{1,2},{2,1},{3,0},{4,7},{5,6},{6,5},{7,4},{8,11},{9,10},{10,... | collective-permute-start | bytes 589832 | tf_op jit(solution)/shard_map/ppermute | solution.py:606
  169.1 5.7 %weights.4 = (bf16[4,1,128,512]{3,2,1,0:T(8,128)(2,1)}, bf16[4,1,128,512]{3,2,1,0:T(8,128)(2,1)}, f32[8,1024]{1,0:T(8,128)}) custom-call(s32[8]{0:T(128)} %iota_xor_fusion.place, bf16[1024,1024]{1,0:T(8,128)(2,1)} %get-tuple-element.155.refs_0_, bf16[1024,512]{1,0:T(8,128)(2,1)} %get-tuple-element.156.refs_1_.gate_grad, ...), custom_call_target="tpu_custom_call" | custom-call | flops 3000000000 | bytes 9000000 | tf_op jit(solution)/shard_map/weights/pallas_call | solution.py:563
  176.2 9.9 %back.1 = (bf16[1024,1024]{1,0:T(8,128)(2,1)}, bf16[1024,512]{1,0:T(8,128)(2,1)}, f32[96,512]{1,0:T(8,128)}, f32[8,512]{1,0:T(8,128)}) custom-call(f32[96,1024]{1,0:T(8,128)} %get-tuple-element.161.own, bf16[96,1024]{1,0:T(8,128)(2,1)} %copy-done.26, bf16[128,512]{1,0:T(8,128)(2,1)} %copy.130.small, f32[1024,512]{1,0:T(8,128)} %get-tuple-element.163.out_grad, ...), custom_call_target="tpu_custom_call" | custom-call | flops 11000000512 | bytes 33000000 | tf_op jit(solution)/shard_map/back/pallas_call | solution.py:517
  186.3 5.7 %weights.5 = (bf16[4,1,128,512]{3,2,1,0:T(8,128)(2,1)}, bf16[4,1,128,512]{3,2,1,0:T(8,128)(2,1)}, f32[8,1024]{1,0:T(8,128)}) custom-call(s32[8]{0:T(128)} %iota_xor_fusion.place, bf16[1024,1024]{1,0:T(8,128)(2,1)} %get-tuple-element.155.refs_0_, bf16[1024,512]{1,0:T(8,128)(2,1)} %get-tuple-element.179.refs_1_, bf16[1024,1024]{1,0:T(8,128)(2,1)} %get-tuple-element.151.refs_2_.w), custom_call_target="tpu_custom_call" | custom-call | flops 3000000000 | bytes 9000000 | tf_op jit(solution)/shard_map/weights/pallas_call | solution.py:563
  193.2 3.8 %collective-permute-start.33 = (f32[1,1024]{1,0:T(1,128)S(1)}, f32[1,1024]{1,0:T(1,128)S(1)}, u32[]{:S(2)}, u32[]{:S(2)}) collective-permute-start(f32[1,1024]{1,0:T(1,128)S(1)} %slice_add_fusion.1), channel_id=1, source_target_pairs={{0,1},{1,0},{2,3},{3,2},{4,5},{5,4},{6,7},{7,6},{8,9},{9,8},{10,11... | collective-permute-start | bytes 12296 | tf_op jit(solution)/shard_map/ppermute | solution.py:606
  197.7 2.4 collective-permute-start.24
  201.2 2.6 %collective-permute-start.34 = (f32[1,1024]{1,0:T(1,128)S(1)}, f32[1,1024]{1,0:T(1,128)S(1)}, u32[]{:S(2)}, u32[]{:S(2)}) collective-permute-start(f32[1,1024]{1,0:T(1,128)S(1)} %add.95), channel_id=1, source_target_pairs={{0,3},{1,2},{2,1},{3,0},{4,7},{5,6},{6,5},{7,4},{8,11},{9,10},{10,... | collective-permute-start | bytes 12296 | tf_op jit(solution)/shard_map/ppermute | solution.py:606
  204.6 2.1 collective-permute-done.34
  206.7 2.4 collective-permute-start.28
  212.0 1.9 collective-permute-done.28
  213.9 1.0 collective-permute-done.27
  216.4 1.5 collective-permute-start.32
  217.8 1.0 collective-permute-start.31
  218.8 1.1 collective-permute-start.30
  220.0 1.5 collective-permute-start.38
  221.4 1.0 collective-permute-start.37
  222.4 1.3 collective-permute-done.32
  223.7 0.9 collective-permute-start.36
  224.6 1.9 collective-permute-done.31
  231.3 1.2 copy.145
  234.3 1.0 fusion
  235.3 2.5 %last.1 = f32[256,1024]{1,0:T(8,128)} custom-call(bf16[256,1024]{1,0:T(8,128)(2,1)} %bitcast.94, bf16[256,1024]{1,0:T(8,128)(2,1)} %bitcast.101, bf16[256,1024]{1,0:T(8,128)(2,1)} %reduce-scatter.5.cloned.1.call-done.normed_grad, f32[1,1024]{1,0:T(1,128)} %reshape.110.gain), custom_call_target="tpu_custom_call" | custom-call | flops 2000000000 | bytes 6000000 | tf_op jit(solution)/shard_map/last/pallas_call | solution.py:593
  (201 shorter events, 29.9 us)
Async XLA Ops:
  7.2 36.4 %copy-start.10 = (bf16[512,128]{1,0:T(8,128)(2,1)S(1)}, bf16[512,128]{1,0:T(8,128)(2,1)}, u32[]{:S(2)}) copy-start(bf16[512,128]{1,0:T(8,128)(2,1)} %param.24) | copy-start | bytes 393220
  7.2 27.0 %copy-start.13 = (bf16[64,96]{1,0:T(8,128)(2,1)S(1)}, bf16[64,96]{1,0:T(8,128)(2,1)}, u32[]{:S(2)}) copy-start(bf16[64,96]{1,0:T(8,128)(2,1)} %param.19) | copy-start | bytes 36868
  7.3 50.3 %all-gather.8.cloned.1.call-start = ((), (), s32[]{:S(2)}) async-start(), calls=%async_computation.5 | async-start | bytes 1966080 | tf_op jit(solution)/shard_map/all_gather | solution.py:656
  8.3 44.3 %copy-start.11 = (bf16[64,1024]{1,0:T(8,128)(2,1)}, bf16[64,1024]{1,0:T(8,128)(2,1)S(1)}, u32[]{:S(2)}) copy-start(bf16[64,1024]{1,0:T(8,128)(2,1)S(1)} %slice_bitcast_fusion.12.refs_0_) | copy-start | bytes 393220
  8.3 12.0 %collective-permute-start.5 = (bf16[64,1024]{1,0:T(8,128)(2,1)S(1)}, bf16[64,1024]{1,0:T(8,128)(2,1)S(1)}, u32[]{:S(2)}, u32[]{:S(2)}) collective-permute-start(bf16[64,1024]{1,0:T(8,128)(2,1)S(1)} %slice_bitcast_fusion.12.refs_0_), channel_id=1, source_target_pairs={{0,3},{1,0},{2,1},{3,2},{4,7},{5,4},{6,5},{7,6},{8,11},{9,8},{10,9... | collective-permute-start | bytes 393224 | tf_op jit(solution)/shard_map/ppermute | solution.py:659
  13.4 8.5 %collective-permute-start.4 = (bf16[64,1024]{1,0:T(8,128)(2,1)S(1)}, bf16[64,1024]{1,0:T(8,128)(2,1)S(1)}, u32[]{:S(2)}, u32[]{:S(2)}) collective-permute-start(bf16[64,1024]{1,0:T(8,128)(2,1)S(1)} %slice_bitcast_fusion.12.refs_0_), channel_id=1, source_target_pairs={{0,2},{1,3},{2,0},{3,1},{4,6},{5,7},{6,4},{7,5},{8,10},{9,11},{10,... | collective-permute-start | bytes 393224 | tf_op jit(solution)/shard_map/ppermute | solution.py:659
  14.4 38.9 %copy-start.7 = (bf16[16,8,2,512]{3,1,2,0:T(8,128)(2,1)}, bf16[16,8,2,512]{3,1,2,0:T(8,128)(2,1)S(1)}, u32[]{:S(2)}) copy-start(bf16[16,8,2,512]{3,1,2,0:T(8,128)(2,1)S(1)} %copy.153) | copy-start | bytes 786436
  14.4 12.8 %collective-permute-start.2 = (bf16[128,1024]{1,0:T(8,128)(2,1)S(1)}, bf16[128,1024]{1,0:T(8,128)(2,1)S(1)}, u32[]{:S(2)}, u32[]{:S(2)}) collective-permute-start(bf16[128,1024]{1,0:T(8,128)(2,1)S(1)} %bitcast.104), channel_id=1, source_target_pairs={{0,24},{4,28},{8,16},{12,20},{16,8},{20,12},{24,0},{28,4},{1,25},{... | collective-permute-start | bytes 786440 | tf_op jit(solution)/shard_map/ppermute | solution.py:606
  16.9 11.8 %collective-permute-start.1 = (bf16[128,1024]{1,0:T(8,128)(2,1)S(1)}, bf16[128,1024]{1,0:T(8,128)(2,1)S(1)}, u32[]{:S(2)}, u32[]{:S(2)}) collective-permute-start(bf16[128,1024]{1,0:T(8,128)(2,1)S(1)} %bitcast.105), channel_id=1, source_target_pairs={{0,16},{4,20},{8,24},{12,28},{16,0},{20,4},{24,8},{28,12},{1,17},{... | collective-permute-start | bytes 786440 | tf_op jit(solution)/shard_map/ppermute | solution.py:606
  17.4 11.5 %collective-permute-start = (bf16[128,1024]{1,0:T(8,128)(2,1)S(1)}, bf16[128,1024]{1,0:T(8,128)(2,1)}, u32[]{:S(2)}, u32[]{:S(2)}) collective-permute-start(bf16[128,1024]{1,0:T(8,128)(2,1)S(1)} %bitcast.106), channel_id=1, source_target_pairs={{0,8},{4,12},{8,0},{12,4},{16,24},{20,28},{24,16},{28,20},{1,9},{5... | collective-permute-start | bytes 786440 | tf_op jit(solution)/shard_map/ppermute | solution.py:606
  19.7 99.0 %all-gather.6.cloned.1.call-start = ((), (), s32[]{:S(2)}) async-start(), calls=%async_computation.2 | async-start | bytes 2621440 | tf_op jit(solution)/shard_map/all_gather | solution.py:703
  20.3 6.8 %collective-permute-start.3 = (bf16[64,1024]{1,0:T(8,128)(2,1)S(1)}, bf16[64,1024]{1,0:T(8,128)(2,1)S(1)}, u32[]{:S(2)}, u32[]{:S(2)}) collective-permute-start(bf16[64,1024]{1,0:T(8,128)(2,1)S(1)} %slice_bitcast_fusion.12.refs_0_), channel_id=1, source_target_pairs={{0,1},{1,2},{2,3},{3,0},{4,5},{5,6},{6,7},{7,4},{8,9},{9,10},{10,1... | collective-permute-start | bytes 393224 | tf_op jit(solution)/shard_map/ppermute | solution.py:659
  21.9 27.6 %copy-start.28 = (bf16[64,1024]{1,0:T(8,128)(2,1)}, bf16[64,1024]{1,0:T(8,128)(2,1)S(1)}, u32[]{:S(2)}) copy-start(bf16[64,1024]{1,0:T(8,128)(2,1)S(1)} %collective-permute-done.4.refs_2_) | copy-start | bytes 393220
  28.9 14.1 %collective-permute-start.16 = (bf16[512,128]{1,0:T(8,128)(2,1)}, bf16[512,128]{1,0:T(8,128)(2,1)S(1)}, u32[]{:S(2)}, u32[]{:S(2)}) collective-permute-start(bf16[512,128]{1,0:T(8,128)(2,1)} %param.24), channel_id=1, source_target_pairs={{0,24},{4,28},{8,16},{12,20},{16,8},{20,12},{24,0},{28,4},{1,25},{... | collective-permute-start | bytes 393224 | tf_op jit(solution)/shard_map/ppermute | solution.py:606
  30.5 13.1 %collective-permute-start.12 = (bf16[512,128]{1,0:T(8,128)(2,1)}, bf16[512,128]{1,0:T(8,128)(2,1)S(1)}, u32[]{:S(2)}, u32[]{:S(2)}) collective-permute-start(bf16[512,128]{1,0:T(8,128)(2,1)} %param.24), channel_id=1, source_target_pairs={{0,8},{4,12},{8,0},{12,4},{16,24},{20,28},{24,16},{28,20},{1,9},{5... | collective-permute-start | bytes 393224 | tf_op jit(solution)/shard_map/ppermute | solution.py:606
  31.7 11.7 %collective-permute-start.11 = (bf16[512,128]{1,0:T(8,128)(2,1)}, bf16[512,128]{1,0:T(8,128)(2,1)S(1)}, u32[]{:S(2)}, u32[]{:S(2)}) collective-permute-start(bf16[512,128]{1,0:T(8,128)(2,1)} %param.24), channel_id=1, source_target_pairs={{0,4},{4,0},{8,12},{12,8},{16,20},{20,16},{24,28},{28,24},{1,5},{5... | collective-permute-start | bytes 393224 | tf_op jit(solution)/shard_map/ppermute | solution.py:606
  33.7 15.8 %collective-permute-start.6 = (bf16[128,1024]{1,0:T(8,128)(2,1)S(1)}, bf16[128,1024]{1,0:T(8,128)(2,1)}, u32[]{:S(2)}, u32[]{:S(2)}) collective-permute-start(bf16[128,1024]{1,0:T(8,128)(2,1)S(1)} %bitcast.107), channel_id=1, source_target_pairs={{0,4},{4,0},{8,12},{12,8},{16,20},{20,16},{24,28},{28,24},{1,5},{5... | collective-permute-start | bytes 786440 | tf_op jit(solution)/shard_map/ppermute | solution.py:606
  34.2 15.8 %collective-permute-start.7 = (bf16[128,1024]{1,0:T(8,128)(2,1)}, bf16[128,1024]{1,0:T(8,128)(2,1)}, u32[]{:S(2)}, u32[]{:S(2)}) collective-permute-start(bf16[128,1024]{1,0:T(8,128)(2,1)} %collective-permute-done.refs_6_), channel_id=1, source_target_pairs={{0,4},{4,0},{8,12},{12,8},{16,20},{20,16},{24,28},{28,24},{1,5},{5... | collective-permute-start | bytes 786440 | tf_op jit(solution)/shard_map/ppermute | solution.py:606
  43.0 7.1 %collective-permute-start.8 = (bf16[128,1024]{1,0:T(8,128)(2,1)S(1)}, bf16[128,1024]{1,0:T(8,128)(2,1)S(1)}, u32[]{:S(2)}, u32[]{:S(2)}) collective-permute-start(bf16[128,1024]{1,0:T(8,128)(2,1)S(1)} %collective-permute-done.1.refs_8_), channel_id=1, source_target_pairs={{0,4},{4,0},{8,12},{12,8},{16,20},{20,16},{24,28},{28,24},{1,5},{5... | collective-permute-start | bytes 786440 | tf_op jit(solution)/shard_map/ppermute | solution.py:606
  43.4 6.6 %collective-permute-start.9 = (bf16[128,1024]{1,0:T(8,128)(2,1)S(1)}, bf16[128,1024]{1,0:T(8,128)(2,1)S(1)}, u32[]{:S(2)}, u32[]{:S(2)}) collective-permute-start(bf16[128,1024]{1,0:T(8,128)(2,1)S(1)} %collective-permute-done.2.refs_10_), channel_id=1, source_target_pairs={{0,4},{4,0},{8,12},{12,8},{16,20},{20,16},{24,28},{28,24},{1,5},{5... | collective-permute-start | bytes 786440 | tf_op jit(solution)/shard_map/ppermute | solution.py:606
  43.6 5.9 %collective-permute-start.14 = (bf16[512,128]{1,0:T(8,128)(2,1)S(1)}, bf16[512,128]{1,0:T(8,128)(2,1)S(1)}, u32[]{:S(2)}, u32[]{:S(2)}) collective-permute-start(bf16[512,128]{1,0:T(8,128)(2,1)S(1)} %copy-done.10), channel_id=1, source_target_pairs={{0,16},{4,20},{8,24},{12,28},{16,0},{20,4},{24,8},{28,12},{1,17},{... | collective-permute-start | bytes 393224 | tf_op jit(solution)/shard_map/ppermute | solution.py:606
  49.5 3.8 %collective-permute-start.13 = (bf16[512,128]{1,0:T(8,128)(2,1)S(1)}, bf16[512,128]{1,0:T(8,128)(2,1)S(1)}, u32[]{:S(2)}, u32[]{:S(2)}) collective-permute-start(bf16[512,128]{1,0:T(8,128)(2,1)S(1)} %collective-permute-done.12), channel_id=1, source_target_pairs={{0,4},{4,0},{8,12},{12,8},{16,20},{20,16},{24,28},{28,24},{1,5},{5... | collective-permute-start | bytes 393224 | tf_op jit(solution)/shard_map/ppermute | solution.py:606
  49.5 3.9 %collective-permute-start.17 = (bf16[512,128]{1,0:T(8,128)(2,1)S(1)}, bf16[512,128]{1,0:T(8,128)(2,1)S(1)}, u32[]{:S(2)}, u32[]{:S(2)}) collective-permute-start(bf16[512,128]{1,0:T(8,128)(2,1)S(1)} %collective-permute-done.16), channel_id=1, source_target_pairs={{0,4},{4,0},{8,12},{12,8},{16,20},{20,16},{24,28},{28,24},{1,5},{5... | collective-permute-start | bytes 393224 | tf_op jit(solution)/shard_map/ppermute | solution.py:606
  50.0 3.3 %collective-permute-start.15 = (bf16[512,128]{1,0:T(8,128)(2,1)S(1)}, bf16[512,128]{1,0:T(8,128)(2,1)S(1)}, u32[]{:S(2)}, u32[]{:S(2)}) collective-permute-start(bf16[512,128]{1,0:T(8,128)(2,1)S(1)} %collective-permute-done.14), channel_id=1, source_target_pairs={{0,4},{4,0},{8,12},{12,8},{16,20},{20,16},{24,28},{28,24},{1,5},{5... | collective-permute-start | bytes 393224 | tf_op jit(solution)/shard_map/ppermute | solution.py:606
  66.6 6.8 %collective-permute-start.10 = (bf16[96,1024]{1,0:T(8,128)(2,1)}, bf16[96,1024]{1,0:T(8,128)(2,1)S(1)}, u32[]{:S(2)}, u32[]{:S(2)}) collective-permute-start(bf16[96,1024]{1,0:T(8,128)(2,1)} %get-tuple-element.136), channel_id=1, source_target_pairs={{0,1},{1,0},{2,3},{3,2},{4,5},{5,4},{6,7},{7,6},{8,9},{9,8},{10,11... | collective-permute-start | bytes 589832 | tf_op jit(solution)/shard_map/ppermute | solution.py:606
  73.5 151.1 %reduce-scatter.3.cloned.1.call-start = ((), (), s32[]{:S(2)}) async-start(), calls=%async_computation.3 | async-start | bytes 2621440 | tf_op jit(solution)/shard_map/reduce_scatter | solution.py:707
  74.3 7.5 %collective-permute-start.18 = (bf16[96,1024]{1,0:T(8,128)(2,1)S(1)}, bf16[96,1024]{1,0:T(8,128)(2,1)S(1)}, u32[]{:S(2)}, u32[]{:S(2)}) collective-permute-start(bf16[96,1024]{1,0:T(8,128)(2,1)S(1)} %get-tuple-element.273), channel_id=1, source_target_pairs={{0,3},{1,2},{2,1},{3,0},{4,7},{5,6},{6,5},{7,4},{8,11},{9,10},{10,... | collective-permute-start | bytes 589832 | tf_op jit(solution)/shard_map/ppermute | solution.py:606
  101.9 133.4 %reduce-scatter.5.cloned.1.call-start = ((), (), s32[]{:S(2)}) async-start(), calls=%async_computation.4 | async-start | bytes 2621440 | tf_op jit(solution)/shard_map/reduce_scatter | solution.py:724
  154.9 10.6 %collective-permute-start.19 = (bf16[96,1024]{1,0:T(8,128)(2,1)}, bf16[96,1024]{1,0:T(8,128)(2,1)S(1)}, u32[]{:S(2)}, u32[]{:S(2)}) collective-permute-start(bf16[96,1024]{1,0:T(8,128)(2,1)} %get-tuple-element.148), channel_id=1, source_target_pairs={{0,1},{1,0},{2,3},{3,2},{4,5},{5,4},{6,7},{7,6},{8,9},{9,8},{10,11... | collective-permute-start | bytes 589832 | tf_op jit(solution)/shard_map/ppermute | solution.py:606
  165.5 9.3 %collective-permute-start.21 = (bf16[4,1,128,512]{3,2,1,0:T(8,128)(2,1)}, bf16[4,1,128,512]{3,2,1,0:T(8,128)(2,1)S(1)}, u32[]{:S(2)}, u32[]{:S(2)}) collective-permute-start(bf16[4,1,128,512]{3,2,1,0:T(8,128)(2,1)} %get-tuple-element.160), channel_id=1, source_target_pairs={{0,4},{4,0},{8,12},{12,8},{16,20},{20,16},{24,28},{28,24},{1,5},{5... | collective-permute-start | bytes 1572872 | tf_op jit(solution)/shard_map/ppermute | solution.py:606
  166.3 9.2 %collective-permute-start.20 = (bf16[96,1024]{1,0:T(8,128)(2,1)S(1)}, bf16[96,1024]{1,0:T(8,128)(2,1)S(1)}, u32[]{:S(2)}, u32[]{:S(2)}) collective-permute-start(bf16[96,1024]{1,0:T(8,128)(2,1)S(1)} %get-tuple-element.271), channel_id=1, source_target_pairs={{0,3},{1,2},{2,1},{3,0},{4,7},{5,6},{6,5},{7,4},{8,11},{9,10},{10,... | collective-permute-start | bytes 589832 | tf_op jit(solution)/shard_map/ppermute | solution.py:606
  186.2 15.0 %collective-permute-start.25 = (bf16[4,1,128,512]{3,2,1,0:T(8,128)(2,1)}, bf16[4,1,128,512]{3,2,1,0:T(8,128)(2,1)S(1)}, u32[]{:S(2)}, u32[]{:S(2)}) collective-permute-start(bf16[4,1,128,512]{3,2,1,0:T(8,128)(2,1)} %get-tuple-element.170), channel_id=1, source_target_pairs={{0,4},{4,0},{8,12},{12,8},{16,20},{20,16},{24,28},{28,24},{1,5},{5... | collective-permute-start | bytes 1572872 | tf_op jit(solution)/shard_map/ppermute | solution.py:606
  191.9 17.8 %collective-permute-start.29 = (bf16[4,1,128,512]{3,2,1,0:T(8,128)(2,1)}, bf16[4,1,128,512]{3,2,1,0:T(8,128)(2,1)S(1)}, u32[]{:S(2)}, u32[]{:S(2)}) collective-permute-start(bf16[4,1,128,512]{3,2,1,0:T(8,128)(2,1)} %get-tuple-element.181), channel_id=1, source_target_pairs={{0,4},{4,0},{8,12},{12,8},{16,20},{20,16},{24,28},{28,24},{1,5},{5... | collective-permute-start | bytes 1572872 | tf_op jit(solution)/shard_map/ppermute | solution.py:606
  193.2 7.4 %collective-permute-start.33 = (f32[1,1024]{1,0:T(1,128)S(1)}, f32[1,1024]{1,0:T(1,128)S(1)}, u32[]{:S(2)}, u32[]{:S(2)}) collective-permute-start(f32[1,1024]{1,0:T(1,128)S(1)} %slice_add_fusion.1), channel_id=1, source_target_pairs={{0,1},{1,0},{2,3},{3,2},{4,5},{5,4},{6,7},{7,6},{8,9},{9,8},{10,11... | collective-permute-start | bytes 12296 | tf_op jit(solution)/shard_map/ppermute | solution.py:606
  197.7 11.4 %collective-permute-start.24 = (bf16[1,128,512]{2,1,0:T(8,128)(2,1)S(1)}, bf16[1,128,512]{2,1,0:T(8,128)(2,1)S(1)}, u32[]{:S(2)}, u32[]{:S(2)}) collective-permute-start(bf16[1,128,512]{2,1,0:T(8,128)(2,1)S(1)} %get-tuple-element.283), channel_id=1, source_target_pairs={{0,24},{4,28},{8,16},{12,20},{16,8},{20,12},{24,0},{28,4},{1,25},{... | collective-permute-start | bytes 393224 | tf_op jit(solution)/shard_map/ppermute | solution.py:606
  200.0 12.0 %collective-permute-start.23 = (bf16[1,128,512]{2,1,0:T(8,128)(2,1)}, bf16[1,128,512]{2,1,0:T(8,128)(2,1)S(1)}, u32[]{:S(2)}, u32[]{:S(2)}) collective-permute-start(bf16[1,128,512]{2,1,0:T(8,128)(2,1)} %get-tuple-element.284), channel_id=1, source_target_pairs={{0,16},{4,20},{8,24},{12,28},{16,0},{20,4},{24,8},{28,12},{1,17},{... | collective-permute-start | bytes 393224 | tf_op jit(solution)/shard_map/ppermute | solution.py:606
  200.6 11.4 %collective-permute-start.22 = (bf16[1,128,512]{2,1,0:T(8,128)(2,1)S(1)}, bf16[1,128,512]{2,1,0:T(8,128)(2,1)S(1)}, u32[]{:S(2)}, u32[]{:S(2)}) collective-permute-start(bf16[1,128,512]{2,1,0:T(8,128)(2,1)S(1)} %get-tuple-element.285), channel_id=1, source_target_pairs={{0,8},{4,12},{8,0},{12,4},{16,24},{20,28},{24,16},{28,20},{1,9},{5... | collective-permute-start | bytes 393224 | tf_op jit(solution)/shard_map/ppermute | solution.py:606
  201.2 5.6 %collective-permute-start.34 = (f32[1,1024]{1,0:T(1,128)S(1)}, f32[1,1024]{1,0:T(1,128)S(1)}, u32[]{:S(2)}, u32[]{:S(2)}) collective-permute-start(f32[1,1024]{1,0:T(1,128)S(1)} %add.95), channel_id=1, source_target_pairs={{0,3},{1,2},{2,1},{3,0},{4,7},{5,6},{6,5},{7,4},{8,11},{9,10},{10,... | collective-permute-start | bytes 12296 | tf_op jit(solution)/shard_map/ppermute | solution.py:606
  206.7 7.1 %collective-permute-start.28 = (bf16[1,128,512]{2,1,0:T(8,128)(2,1)}, bf16[1,128,512]{2,1,0:T(8,128)(2,1)S(1)}, u32[]{:S(2)}, u32[]{:S(2)}) collective-permute-start(bf16[1,128,512]{2,1,0:T(8,128)(2,1)} %get-tuple-element.279), channel_id=1, source_target_pairs={{0,24},{4,28},{8,16},{12,20},{16,8},{20,12},{24,0},{28,4},{1,25},{... | collective-permute-start | bytes 393224 | tf_op jit(solution)/shard_map/ppermute | solution.py:606
  209.1 5.8 %collective-permute-start.27 = (bf16[1,128,512]{2,1,0:T(8,128)(2,1)}, bf16[1,128,512]{2,1,0:T(8,128)(2,1)S(1)}, u32[]{:S(2)}, u32[]{:S(2)}) collective-permute-start(bf16[1,128,512]{2,1,0:T(8,128)(2,1)} %get-tuple-element.280), channel_id=1, source_target_pairs={{0,16},{4,20},{8,24},{12,28},{16,0},{20,4},{24,8},{28,12},{1,17},{... | collective-permute-start | bytes 393224 | tf_op jit(solution)/shard_map/ppermute | solution.py:606
  209.7 5.2 %collective-permute-start.26 = (bf16[1,128,512]{2,1,0:T(8,128)(2,1)}, bf16[1,128,512]{2,1,0:T(8,128)(2,1)S(1)}, u32[]{:S(2)}, u32[]{:S(2)}) collective-permute-start(bf16[1,128,512]{2,1,0:T(8,128)(2,1)} %get-tuple-element.281), channel_id=1, source_target_pairs={{0,8},{4,12},{8,0},{12,4},{16,24},{20,28},{24,16},{28,20},{1,9},{5... | collective-permute-start | bytes 393224 | tf_op jit(solution)/shard_map/ppermute | solution.py:606
  216.2 3.7 %collective-permute-start.35 = (bf16[4,185,64]{1,2,0:T(8,128)(2,1)S(1)}, bf16[4,185,64]{1,2,0:T(8,128)(2,1)S(1)}, u32[]{:S(2)}, u32[]{:S(2)}) collective-permute-start(bf16[4,185,64]{1,2,0:T(8,128)(2,1)S(1)} %slice.132), channel_id=1, source_target_pairs={{0,4},{4,0},{8,12},{12,8},{16,20},{20,16},{24,28},{28,24},{1,5},{5... | collective-permute-start | bytes 284168 | tf_op jit(solution)/shard_map/ppermute | solution.py:606
  216.4 7.3 %collective-permute-start.32 = (bf16[1,128,512]{2,1,0:T(8,128)(2,1)S(1)}, bf16[1,128,512]{2,1,0:T(8,128)(2,1)S(1)}, u32[]{:S(2)}, u32[]{:S(2)}) collective-permute-start(bf16[1,128,512]{2,1,0:T(8,128)(2,1)S(1)} %get-tuple-element.275), channel_id=1, source_target_pairs={{0,24},{4,28},{8,16},{12,20},{16,8},{20,12},{24,0},{28,4},{1,25},{... | collective-permute-start | bytes 393224 | tf_op jit(solution)/shard_map/ppermute | solution.py:606
  217.8 8.6 %collective-permute-start.31 = (bf16[1,128,512]{2,1,0:T(8,128)(2,1)S(1)}, bf16[1,128,512]{2,1,0:T(8,128)(2,1)S(1)}, u32[]{:S(2)}, u32[]{:S(2)}) collective-permute-start(bf16[1,128,512]{2,1,0:T(8,128)(2,1)S(1)} %get-tuple-element.276), channel_id=1, source_target_pairs={{0,16},{4,20},{8,24},{12,28},{16,0},{20,4},{24,8},{28,12},{1,17},{... | collective-permute-start | bytes 393224 | tf_op jit(solution)/shard_map/ppermute | solution.py:606
  218.8 7.7 %collective-permute-start.30 = (bf16[1,128,512]{2,1,0:T(8,128)(2,1)S(1)}, bf16[1,128,512]{2,1,0:T(8,128)(2,1)S(1)}, u32[]{:S(2)}, u32[]{:S(2)}) collective-permute-start(bf16[1,128,512]{2,1,0:T(8,128)(2,1)S(1)} %get-tuple-element.277), channel_id=1, source_target_pairs={{0,8},{4,12},{8,0},{12,4},{16,24},{20,28},{24,16},{28,20},{1,9},{5... | collective-permute-start | bytes 393224 | tf_op jit(solution)/shard_map/ppermute | solution.py:606
  220.0 7.0 %collective-permute-start.38 = (bf16[185,64]{0,1:T(8,128)(2,1)S(1)}, bf16[185,64]{0,1:T(8,128)(2,1)S(1)}, u32[]{:S(2)}, u32[]{:S(2)}) collective-permute-start(bf16[185,64]{0,1:T(8,128)(2,1)S(1)} %get-tuple-element.287), channel_id=1, source_target_pairs={{0,24},{4,28},{8,16},{12,20},{16,8},{20,12},{24,0},{28,4},{1,25},{... | collective-permute-start | bytes 71048 | tf_op jit(solution)/shard_map/ppermute | solution.py:606
  221.4 6.0 %collective-permute-start.37 = (bf16[185,64]{0,1:T(8,128)(2,1)S(1)}, bf16[185,64]{0,1:T(8,128)(2,1)S(1)}, u32[]{:S(2)}, u32[]{:S(2)}) collective-permute-start(bf16[185,64]{0,1:T(8,128)(2,1)S(1)} %get-tuple-element.288), channel_id=1, source_target_pairs={{0,16},{4,20},{8,24},{12,28},{16,0},{20,4},{24,8},{28,12},{1,17},{... | collective-permute-start | bytes 71048 | tf_op jit(solution)/shard_map/ppermute | solution.py:606
  223.7 3.9 %collective-permute-start.36 = (bf16[185,64]{0,1:T(8,128)(2,1)S(1)}, bf16[185,64]{0,1:T(8,128)(2,1)S(1)}, u32[]{:S(2)}, u32[]{:S(2)}) collective-permute-start(bf16[185,64]{0,1:T(8,128)(2,1)S(1)} %get-tuple-element.289), channel_id=1, source_target_pairs={{0,8},{4,12},{8,0},{12,4},{16,24},{20,28},{24,16},{28,20},{1,9},{5... | collective-permute-start | bytes 71048 | tf_op jit(solution)/shard_map/ppermute | solution.py:606
  (26 other events, 385.0 us)
Sparse Core Ops, SparseCore 0:
  19.8 37.6 all-gather.7
  73.6 45.0 all-gather.5
  121.0 47.7 reduce-scatter.2
  186.3 46.3 reduce-scatter.4
